TPU v7x, 32 devices: a whole 2x2x4 slice. The times are simulated.
32 devices in a mesh: section: 2 (over x), dp: 4 (over z), tensor: 4 (over y, core).
Axes of the slice: x: 2, y: 2, z: 4, core: 2. Of those that a mesh axis runs over, the one named last changes fastest.
Arguments:
- section_input: bfloat16 [2, 4, 736, 1152], P(None, 'dp', 'tensor'), may hold values from -6 to 6
- final_cotangent: bfloat16 [2, 4, 736, 1152], P(None, 'dp', 'tensor'), may hold values from -6 to 6
- lengths: int32 [2, 4], P(None, 'dp'), may hold values from 368 to 736, as said below
- qkv_weight: bfloat16 [2, 3, 1152, 1152], P('section', None, 'dp', 'tensor'), may hold values from -0.1875 to 0.1875
- out_weight: bfloat16 [2, 1152, 1152], P('section', 'tensor', 'dp'), may hold values from -2.5 to 2.5
- up_weight: bfloat16 [2, 1152, 4304], P('section', 'dp', 'tensor'), may hold values from -0.1875 to 0.1875
- down_weight: bfloat16 [2, 4304, 1152], P('section', 'tensor', 'dp'), may hold values from -0.09375 to 0.09375
- norm_gains: float32 [2, 2, 1152], P('section', None, ('dp', 'tensor')), may hold values from 0.1 to 1.9
- biases: float32 [2, 6, 1152], P('section', None, ('dp', 'tensor')), may hold values from -3 to 3
- up_bias: float32 [2, 4304], P('section', 'tensor'), may hold values from -3 to 3
Outputs:
- section_output: bfloat16 [2, 2, 4, 736, 1152], P('section', None, 'dp', 'tensor')
- input_grad: bfloat16 [2, 2, 4, 736, 1152], P('section', None, 'dp', 'tensor')
- qkv_grad: float32 [2, 3, 1152, 1152], P('section', None, 'dp', 'tensor')
- out_grad: float32 [2, 1152, 1152], P('section', 'tensor', 'dp')
- up_grad: float32 [2, 1152, 4304], P('section', 'dp', 'tensor')
- down_grad: float32 [2, 4304, 1152], P('section', 'tensor', 'dp')
- gains_grad: float32 [2, 2, 1152], P('section', None, ('dp', 'tensor'))
- biases_grad: float32 [2, 6, 1152], P('section', None, ('dp', 'tensor'))
- up_bias_grad: float32 [2, 4304], P('section', 'tensor')
Inputs may be any that keep to these rules, and one draw needn't show every extreme that they name: `lengths`: in every micro-batch at least one image has all 736 token slots valid; every image has 368 valid slots or more.
All inputs are finite; a program needn't handle non-finite values.
Results may differ from a plain program's by a relative error of at most 0.018.
Values may be sent and summed in bfloat16 or wider, within the bound.
A program may use at most 192 MiB of HBM per device.

v0:
```python
import math

import jax
import jax.numpy as jnp
from jax import lax
from jax.sharding import PartitionSpec as P

HEAD = 72


norm_eps = 1e-06
masked_score = -1000000000.0


def shifted(x, axis, by):
    length = lax.axis_size(axis)
    pairs = [(i, i + by) for i in range(length) if 0 <= i + by < length]
    return lax.ppermute(x, axis, pairs)


def layer_norm(rows, gain_vec, shift_vec):
    centred = rows - jnp.mean(rows, axis=-1, keepdims=True)
    spread = jnp.mean(centred * centred, axis=-1, keepdims=True)
    return centred * lax.rsqrt(spread + norm_eps) * gain_vec + shift_vec


def gelu_tanh(value):
    return jax.nn.gelu(value, approximate=True)


def rows_gather(pieces):
    return lax.all_gather(pieces, "tensor", axis=1, tiled=True)


def grads_gather(pieces):
    return lax.all_gather(pieces, "tensor", axis=1, tiled=True)


def grads_reduce(partial_value):
    return lax.psum_scatter(
        partial_value.astype(jnp.bfloat16), "tensor", scatter_dimension=1, tiled=True
    ).astype(jnp.float32)


def gather_weights(qkv_part, out_part, up_part, down_part):
    return (
        lax.all_gather(qkv_part, "dp", axis=1, tiled=True),
        lax.all_gather(out_part, "dp", axis=1, tiled=True),
        lax.all_gather(up_part, "dp", axis=0, tiled=True),
        lax.all_gather(down_part, "dp", axis=1, tiled=True),
    )


def gather_again(qkv_part, out_part, up_part, down_part):
    return (
        lax.all_gather(qkv_part, "dp", axis=1, tiled=True),
        lax.all_gather(out_part, "dp", axis=1, tiled=True),
        lax.all_gather(up_part, "dp", axis=0, tiled=True),
        lax.all_gather(down_part, "dp", axis=1, tiled=True),
    )


def head_scores(queries, keys_all, length):
    seq_len = queries.shape[0]
    split = (seq_len, queries.shape[1] // HEAD, HEAD)
    scores = jnp.einsum(
        "qhe,khe->hqk",
        queries.reshape(split),
        keys_all.reshape(split),
        preferred_element_type=jnp.float32,
    ) / math.sqrt(HEAD)
    valid = jnp.arange(seq_len, dtype=jnp.int32)[None, None, :] < length
    return (jnp.where(valid, scores, masked_score), split)


def attend_forward(pieces):
    queries, keys_all, values, length = pieces
    scores, split = head_scores(queries, keys_all, length)
    top_score = jnp.max(scores, axis=-1, keepdims=True)
    exp_scores = jnp.exp(scores - top_score)
    total = jnp.sum(exp_scores, axis=-1, keepdims=True)
    probs = (exp_scores / total).astype(jnp.bfloat16)
    mixed = jnp.einsum(
        "hqk,khe->qhe", probs, values.reshape(split), preferred_element_type=jnp.float32
    )
    log_total = (top_score + jnp.log(total))[..., 0]
    return (mixed.reshape(queries.shape).astype(jnp.bfloat16), log_total)


def attend_backward(pieces):
    queries, keys_all, values, log_total, grad_mixed, length = pieces
    scores, split = head_scores(queries, keys_all, length)
    probs = jnp.exp(scores - log_total[..., None])
    probs_low = probs.astype(jnp.bfloat16)
    grad_split = grad_mixed.reshape(split)
    grad_values = jnp.einsum(
        "hqk,qhe->khe", probs_low, grad_split, preferred_element_type=jnp.float32
    )
    grad_probs = jnp.einsum(
        "qhe,khe->hqk", grad_split, values.reshape(split), preferred_element_type=jnp.float32
    )
    inner = jnp.sum(grad_probs * probs, axis=-1, keepdims=True)
    grad_scores = (probs * (grad_probs - inner)).astype(jnp.bfloat16)
    grad_queries = jnp.einsum(
        "hqk,khe->qhe", grad_scores, keys_all.reshape(split), preferred_element_type=jnp.float32
    ) / math.sqrt(HEAD)
    grad_keys = jnp.einsum(
        "hqk,qhe->khe", grad_scores, queries.reshape(split), preferred_element_type=jnp.float32
    ) / math.sqrt(HEAD)
    flat = queries.shape
    return (
        grad_queries.reshape(flat).astype(jnp.bfloat16),
        grad_keys.reshape(flat).astype(jnp.bfloat16),
        grad_values.reshape(flat).astype(jnp.bfloat16),
    )


def layer_forward(inputs_low, lengths_here, weights, vectors):
    qkv_full, out_part, up_part, down_part = weights
    gains, shifts, up_bias_here, bias_query, bias_value = vectors
    inputs = inputs_low.astype(jnp.float32)
    normed = layer_norm(inputs, gains[0], shifts[0]).astype(jnp.bfloat16)
    normed_full = rows_gather(normed)
    projected = jnp.einsum(
        "nsd,cde->cnse", normed_full, qkv_full, preferred_element_type=jnp.float32
    )
    queries = (projected[0] + bias_query).astype(jnp.bfloat16)
    keys_all = projected[1].astype(jnp.bfloat16)
    values = (projected[2] + bias_value).astype(jnp.bfloat16)
    mixed, log_total = lax.map(attend_forward, (queries, keys_all, values, lengths_here))
    partial_value = jnp.einsum("nsh,hd->nsd", mixed, out_part, preferred_element_type=jnp.float32)
    branch = lax.psum_scatter(
        partial_value.astype(jnp.bfloat16), "tensor", scatter_dimension=1, tiled=True
    ).astype(jnp.float32)
    hidden = inputs + branch + shifts[3]
    normed_two = layer_norm(hidden, gains[1], shifts[4]).astype(jnp.bfloat16)
    second_full = rows_gather(normed_two)
    upper = (
        jnp.einsum("nsd,df->nsf", second_full, up_part, preferred_element_type=jnp.float32)
        + up_bias_here
    )
    active = gelu_tanh(upper).astype(jnp.bfloat16)
    down_terms = jnp.einsum("nsf,fd->nsd", active, down_part, preferred_element_type=jnp.float32)
    outputs = (
        hidden
        + lax.psum_scatter(
            down_terms.astype(jnp.bfloat16), "tensor", scatter_dimension=1, tiled=True
        ).astype(jnp.float32)
        + shifts[5]
    ).astype(jnp.bfloat16)
    kept = (
        inputs_low,
        normed_full,
        queries,
        keys_all,
        values,
        log_total,
        mixed,
        hidden,
        second_full,
        upper,
        active,
    )
    return (outputs, kept)


def layer_backward(grad_low, kept, lengths_here, weights, vectors):
    qkv_full, out_part, up_part, down_part = weights
    gains, shifts, up_bias_here, bias_query, bias_value = vectors
    (
        inputs_low,
        normed_full,
        queries,
        keys_all,
        values,
        log_total,
        mixed,
        hidden,
        second_full,
        upper,
        active,
    ) = kept
    grad_rows = grad_low.astype(jnp.float32)
    grad_full = grads_gather(grad_low)
    grad_down_bias = jnp.sum(grad_rows, axis=(0, 1))
    grad_down = jnp.einsum("nsf,nsd->fd", active, grad_full, preferred_element_type=jnp.float32)
    grad_active = jnp.einsum(
        "nsd,fd->nsf", grad_full, down_part, preferred_element_type=jnp.float32
    )
    gelu_back = jax.vjp(gelu_tanh, upper)[1]
    grad_upper = gelu_back(grad_active)[0].astype(jnp.bfloat16)
    grad_up_bias = jnp.sum(grad_upper.astype(jnp.float32), axis=(0, 1))
    grad_up = jnp.einsum("nsd,nsf->df", second_full, grad_upper, preferred_element_type=jnp.float32)
    grad_normed_two = grads_reduce(
        jnp.einsum("nsf,df->nsd", grad_upper, up_part, preferred_element_type=jnp.float32)
    )
    norm_back_two = jax.vjp(layer_norm, hidden, gains[1], shifts[4])[1]
    grad_hidden_norm, grad_gain_two, grad_shift_two = norm_back_two(grad_normed_two)
    grad_hidden = grad_rows + grad_hidden_norm
    grad_branch = grad_hidden.astype(jnp.bfloat16)
    grad_out_bias = jnp.sum(grad_branch.astype(jnp.float32), axis=(0, 1))
    branch_full = grads_gather(grad_branch)
    grad_outw = jnp.einsum("nsh,nsd->hd", mixed, branch_full, preferred_element_type=jnp.float32)
    grad_mixed = jnp.einsum(
        "nsd,hd->nsh", branch_full, out_part, preferred_element_type=jnp.float32
    ).astype(jnp.bfloat16)
    grad_queries, grad_keys, grad_values = lax.map(
        attend_backward, (queries, keys_all, values, log_total, grad_mixed, lengths_here)
    )
    grad_bias_query = jnp.sum(grad_queries.astype(jnp.float32), axis=(0, 1))
    grad_bias_value = jnp.sum(grad_values.astype(jnp.float32), axis=(0, 1))
    stacked = jnp.stack([grad_queries, grad_keys, grad_values])
    grad_qkv = jnp.einsum("nsd,cnse->cde", normed_full, stacked, preferred_element_type=jnp.float32)
    grad_normed = grads_reduce(
        jnp.einsum("cnse,cde->nsd", stacked, qkv_full, preferred_element_type=jnp.float32)
    )
    norm_back_one = jax.vjp(layer_norm, inputs_low.astype(jnp.float32), gains[0], shifts[0])[1]
    grad_input_norm, grad_gain_one, grad_shift_one = norm_back_one(grad_normed)
    grad_inputs = (grad_hidden + grad_input_norm).astype(jnp.bfloat16)
    matrices = (grad_qkv, grad_outw, grad_up, grad_down)
    gain_terms = jnp.stack([grad_gain_one, grad_gain_two])
    shift_terms = (
        grad_shift_one,
        grad_bias_query,
        grad_bias_value,
        grad_out_bias,
        grad_shift_two,
        grad_down_bias,
    )
    return (grad_inputs, (matrices, gain_terms, shift_terms, grad_up_bias))


def shards(
    section_input,
    final_cotangent,
    lengths,
    qkv_weight,
    out_weight,
    up_weight,
    down_weight,
    norm_gains,
    biases,
    up_bias,
):
    section_id = lax.axis_index("section")
    sections = lax.axis_size("section")
    micro_count = section_input.shape[0]
    ticks = micro_count + sections - 1
    weights = gather_weights(qkv_weight[0], out_weight[0], up_weight[0], down_weight[0])
    gains, shifts = (
        lax.all_gather(norm_gains[0], ("dp", "tensor"), axis=1, tiled=True),
        lax.all_gather(biases[0], ("dp", "tensor"), axis=1, tiled=True),
    )
    head_width = qkv_weight.shape[3]
    head_start = lax.axis_index("tensor") * head_width
    bias_query = lax.dynamic_slice_in_dim(shifts[1], head_start, head_width, 0)
    bias_value = lax.dynamic_slice_in_dim(shifts[2], head_start, head_width, 0)
    vectors = (gains, shifts, up_bias[0], bias_query, bias_value)
    zero_rows = jnp.zeros(section_input.shape[1:], jnp.bfloat16)
    received = zero_rows
    outputs_all = []
    kept_all = []
    for tick in range(ticks):
        source = section_input[tick] if tick < micro_count else zero_rows
        layer_in = jnp.where(section_id == 0, source, received)
        micro = jnp.clip(tick - section_id, 0, micro_count - 1)
        lengths_here = lax.dynamic_index_in_dim(lengths, micro, 0, keepdims=False)
        produced, kept = layer_forward(layer_in, lengths_here, weights, vectors)
        outputs_all.append(produced)
        kept_all.append(kept)
        if tick + 1 < ticks:
            received = shifted(produced, "section", 1)
    section_output = lax.dynamic_slice_in_dim(jnp.stack(outputs_all), section_id, micro_count, 0)
    kept_stack = jax.tree.map(lambda *items: jnp.stack(items), *kept_all)
    back_weights = gather_again(qkv_weight[0], out_weight[0], up_weight[0], down_weight[0])
    received_grad = zero_rows
    grads_total = None
    input_grads = []
    lag = sections - 1 - section_id
    for back_tick in range(ticks):
        micro_raw = back_tick - lag
        micro = jnp.clip(micro_raw, 0, micro_count - 1)
        slot = jnp.clip(micro_raw + section_id, 0, ticks - 1)
        kept = jax.tree.map(
            lambda stacked: lax.dynamic_index_in_dim(stacked, slot, 0, keepdims=False), kept_stack
        )
        source = final_cotangent[back_tick] if back_tick < micro_count else zero_rows
        incoming = jnp.where(section_id == sections - 1, source, received_grad)
        live = (micro_raw >= 0) & (micro_raw < micro_count)
        incoming = jnp.where(live, incoming, zero_rows)
        lengths_here = lax.dynamic_index_in_dim(lengths, micro, 0, keepdims=False)
        grad_rows, grads_now = layer_backward(incoming, kept, lengths_here, back_weights, vectors)
        grads_total = (
            grads_now if grads_total is None else jax.tree.map(jnp.add, grads_total, grads_now)
        )
        input_grads.append(grad_rows)
        if back_tick + 1 < ticks:
            received_grad = shifted(grad_rows, "section", -1)
    input_grad = lax.dynamic_slice_in_dim(jnp.stack(input_grads), lag, micro_count, 0)
    matrices, gain_terms, shift_terms, up_bias_term = grads_total
    width = shifts.shape[1]
    zero_width = jnp.zeros((width,), jnp.float32)
    query_full = lax.dynamic_update_slice_in_dim(zero_width, shift_terms[1], head_start, 0)
    value_full = lax.dynamic_update_slice_in_dim(zero_width, shift_terms[2], head_start, 0)
    shift_full = jnp.stack(
        [shift_terms[0], query_full, value_full, shift_terms[3], shift_terms[4], shift_terms[5]]
    )
    qkv_sum, out_sum, up_sum, down_sum = (
        lax.psum_scatter(
            matrices[0].astype(jnp.bfloat16), "dp", scatter_dimension=1, tiled=True
        ).astype(jnp.float32),
        lax.psum_scatter(
            matrices[1].astype(jnp.bfloat16), "dp", scatter_dimension=1, tiled=True
        ).astype(jnp.float32),
        lax.psum_scatter(
            matrices[2].astype(jnp.bfloat16), "dp", scatter_dimension=0, tiled=True
        ).astype(jnp.float32),
        lax.psum_scatter(
            matrices[3].astype(jnp.bfloat16), "dp", scatter_dimension=1, tiled=True
        ).astype(jnp.float32),
    )
    gains_sum, shifts_sum = (
        lax.psum_scatter(gain_terms, ("dp", "tensor"), scatter_dimension=1, tiled=True),
        lax.psum_scatter(shift_full, ("dp", "tensor"), scatter_dimension=1, tiled=True),
    )
    up_bias_sum = lax.psum(up_bias_term, "dp")
    return (
        section_output[None],
        input_grad[None],
        qkv_sum[None],
        out_sum[None],
        up_sum[None],
        down_sum[None],
        gains_sum[None],
        shifts_sum[None],
        up_bias_sum[None],
    )


def solution(mesh):
    in_specs = (
        P(None, "dp", "tensor", None),
        P(None, "dp", "tensor", None),
        P(None, "dp"),
        P("section", None, "dp", "tensor"),
        P("section", "tensor", "dp"),
        P("section", "dp", "tensor"),
        P("section", "tensor", "dp"),
        P("section", None, ("dp", "tensor")),
        P("section", None, ("dp", "tensor")),
        P("section", "tensor"),
    )
    out_specs = (
        P("section", None, "dp", "tensor", None),
        P("section", None, "dp", "tensor", None),
        P("section", None, "dp", "tensor"),
        P("section", "tensor", "dp"),
        P("section", "dp", "tensor"),
        P("section", "tensor", "dp"),
        P("section", None, ("dp", "tensor")),
        P("section", None, ("dp", "tensor")),
        P("section", "tensor"),
    )
    return jax.shard_map(shards, mesh=mesh, in_specs=in_specs, out_specs=out_specs, check_vma=False)
```

profile of v0, /device:TPU:0, one launch (start us, length us, event | category | flops | bytes accessed | tf_op | source)
XLA Modules:
  0.0 1310.9 jit_solution(832372325527382517)
XLA Ops:
  11.4 27.2 %all-gather = f32[1,2,1152]{1,0,2:T(1,128)S(1)} all-gather(f32[1,2,72]{1,0,2:T(1,128)S(1)} %copy.70), channel_id=2, replica_groups=mesh['section'=2,'dp'=4,'tensor'=4] {'dp','tensor'}, dimensions={2}, use_global_device_ids=true | all-gather | bytes 9792 | tf_op jit(solution)/shard_map/all_gather | solution.py:251
  38.6 22.9 %all-gather.1 = f32[1,6,1152]{1,0,2:T(1,128)S(1)} all-gather(f32[1,6,72]{1,0,2:T(1,128)S(1)} %copy.71), channel_id=3, replica_groups=mesh['section'=2,'dp'=4,'tensor'=4] {'dp','tensor'}, dimensions={2}, use_global_device_ids=true | all-gather | bytes 29376 | tf_op jit(solution)/shard_map/all_gather | solution.py:252
  62.0 18.9 %slice_reduce_fusion.2 = (f32[1152]{0:T(1024)S(1)}, f32[1152]{0:T(1024)S(1)}) fusion(f32[1,2,1152]{1,0,2:T(1,128)S(1)} %all-gather), kind=kLoop, calls=%fused_computation.424 | loop fusion | bytes 18432 | tf_op jit(solution)/shard_map/slice | solution.py:136
  80.9 22.3 %fusion.357 = (f32[1,1,1152]{1,0,2:T(1,128)S(1)}, f32[1,1,1152]{1,0,2:T(1,128)S(1)}, f32[1152]{0:T(1024)S(1)}, f32[1152]{0:T(1024)S(1)}, f32[1152]{0:T(1024)S(1)}, /*index=5*/f32[1152]{0:T(1024)S(1)}) fusion(f32[1,6,1152]{1,0,2:T(1,128)S(1)} %all-gather.1), kind=kLoop, calls=%fused_computation.585 | loop fusion | bytes 55296 | tf_op jit(solution)/shard_map/slice | solution.py:257
  106.5 33.2 %all-gather.3 = bf16[1,288,1152]{1,0,2:T(2,128)(2,1)S(1)} all-gather(bf16[1,288,288]{1,0,2:T(2,128)(2,1)S(1)} %copy.75), channel_id=5, replica_groups=mesh['section'=2,'dp'=4,'tensor'=4] {'dp'}, dimensions={2}, use_global_device_ids=true | all-gather | bytes 829440 | tf_op jit(solution)/shard_map/all_gather | solution.py:48
  166.7 26.4 %reduce-scatter.67.cloned.1.call-done = bf16[1,184,1152]{2,1,0:T(8,128)(2,1)} async-done(((bf16[1,736,1152]{2,1,0:T(8,128)(2,1)}), bf16[1,184,1152]{2,1,0:T(8,128)(2,1)}) %reduce-scatter.67.cloned.1.call-update) | async-done | bytes 423952
  199.5 50.5 %all-gather.47.cloned.1.call-done = bf16[1,1152,1076]{2,1,0:T(8,128)(2,1)} async-done(((bf16[1,288,1076]{2,1,0:T(8,128)(2,1)}), bf16[1,1152,1076]{2,1,0:T(8,128)(2,1)}) %all-gather.47.cloned.1.call-update) | async-done | bytes 2479120 | tf_op jit(solution)/shard_map/all_gather | solution.py:49
  249.9 21.1 %all-gather.25.cloned.1.call-done = bf16[1,736,1152]{2,1,0:T(8,128)(2,1)} async-done(((bf16[1,184,1152]{2,1,0:T(8,128)(2,1)}), bf16[1,736,1152]{2,1,0:T(8,128)(2,1)}) %all-gather.25.cloned.1.call-update) | async-done | bytes 1695760 | tf_op jit(solution)/shard_map/all_gather | solution.py:32
  277.4 50.4 %all-gather.49.cloned.1.call-done = bf16[1,1076,1152]{1,2,0:T(8,128)(2,1)} async-done(((bf16[1,1076,288]{1,2,0:T(8,128)(2,1)}), bf16[1,1076,1152]{1,2,0:T(8,128)(2,1)}) %all-gather.49.cloned.1.call-update) | async-done | bytes 2479120 | tf_op jit(solution)/shard_map/all_gather | solution.py:50
  335.0 27.6 %reduce-scatter.69.cloned.1.call-done = bf16[1,184,1152]{2,1,0:T(8,128)(2,1)} async-done(((bf16[1,736,1152]{2,1,0:T(8,128)(2,1)}), bf16[1,184,1152]{2,1,0:T(8,128)(2,1)}) %reduce-scatter.69.cloned.1.call-update) | async-done | bytes 423952
  379.5 20.6 %all-gather.27.cloned.1.call-done = bf16[1,736,1152]{2,1,0:T(8,128)(2,1)} async-done(((bf16[1,184,1152]{2,1,0:T(8,128)(2,1)}), bf16[1,736,1152]{2,1,0:T(8,128)(2,1)}) %all-gather.27.cloned.1.call-update) | async-done | bytes 1695760 | tf_op jit(solution)/shard_map/all_gather | solution.py:32
  414.2 28.9 %reduce-scatter.71.cloned.1.call-done = bf16[1,184,1152]{2,1,0:T(8,128)(2,1)} async-done(((bf16[1,736,1152]{2,1,0:T(8,128)(2,1)}), bf16[1,184,1152]{2,1,0:T(8,128)(2,1)}) %reduce-scatter.71.cloned.1.call-update) | async-done | bytes 423952
  448.7 20.2 %all-gather.29.cloned.1.call-done = bf16[1,736,1152]{2,1,0:T(8,128)(2,1)} async-done(((bf16[1,184,1152]{2,1,0:T(8,128)(2,1)}), bf16[1,736,1152]{2,1,0:T(8,128)(2,1)}) %all-gather.29.cloned.1.call-update) | async-done | bytes 1695760 | tf_op jit(solution)/shard_map/all_gather | solution.py:32
  480.0 28.8 %reduce-scatter.73.cloned.1.call-done = bf16[1,184,1152]{2,1,0:T(8,128)(2,1)} async-done(((bf16[1,736,1152]{2,1,0:T(8,128)(2,1)}), bf16[1,184,1152]{2,1,0:T(8,128)(2,1)}) %reduce-scatter.73.cloned.1.call-update) | async-done | bytes 423952
  524.9 20.3 %all-gather.31.cloned.1.call-done = bf16[1,736,1152]{2,1,0:T(8,128)(2,1)} async-done(((bf16[1,184,1152]{2,1,0:T(8,128)(2,1)}), bf16[1,736,1152]{2,1,0:T(8,128)(2,1)}) %all-gather.31.cloned.1.call-update) | async-done | bytes 1695760 | tf_op jit(solution)/shard_map/all_gather | solution.py:32
  560.6 28.9 %reduce-scatter.75.cloned.1.call-done = bf16[1,184,1152]{2,1,0:T(8,128)(2,1)} async-done(((bf16[1,736,1152]{2,1,0:T(8,128)(2,1)}), bf16[1,184,1152]{2,1,0:T(8,128)(2,1)}) %reduce-scatter.75.cloned.1.call-update) | async-done | bytes 423952
  596.8 18.7 %all-gather.33.cloned.1.call-done = bf16[1,736,1152]{2,1,0:T(8,128)(2,1)} async-done(((bf16[1,184,1152]{2,1,0:T(8,128)(2,1)}), bf16[1,736,1152]{2,1,0:T(8,128)(2,1)}) %all-gather.33.cloned.1.call-update) | async-done | bytes 1695760 | tf_op jit(solution)/shard_map/all_gather | solution.py:32
  653.2 26.5 %reduce-scatter.79.cloned.1.call-done = bf16[1,184,1152]{2,1,0:T(8,128)(2,1)} async-done(((bf16[1,736,1152]{2,1,0:T(8,128)(2,1)}), bf16[1,184,1152]{2,1,0:T(8,128)(2,1)}) %reduce-scatter.79.cloned.1.call-update) | async-done | bytes 423952
  731.1 26.3 %reduce-scatter.81.cloned.1.call-done = bf16[1,184,1152]{2,1,0:T(8,128)(2,1)} async-done(((bf16[1,736,1152]{2,1,0:T(8,128)(2,1)}), bf16[1,184,1152]{2,1,0:T(8,128)(2,1)}) %reduce-scatter.81.cloned.1.call-update) | async-done | bytes 423952
  765.7 12.1 collective-permute-done.2
  780.9 19.1 %all-gather.37.cloned.1.call-done = bf16[1,736,1152]{2,1,0:T(8,128)(2,1)} async-done(((bf16[1,184,1152]{2,1,0:T(8,128)(2,1)}), bf16[1,736,1152]{2,1,0:T(8,128)(2,1)}) %all-gather.37.cloned.1.call-update) | async-done | bytes 1695760 | tf_op jit(solution)/shard_map/all_gather | solution.py:36
  813.5 28.8 %reduce-scatter.83.cloned.1.call-done = bf16[1,184,1152]{2,1,0:T(8,128)(2,1)} async-done(((bf16[1,736,1152]{2,1,0:T(8,128)(2,1)}), bf16[1,184,1152]{2,1,0:T(8,128)(2,1)}) %reduce-scatter.83.cloned.1.call-update) | async-done | bytes 423952
  855.3 13.6 %all-gather.39.cloned.1.call-done = bf16[1,736,1152]{2,1,0:T(8,128)(2,1)} async-done(((bf16[1,184,1152]{2,1,0:T(8,128)(2,1)}), bf16[1,736,1152]{2,1,0:T(8,128)(2,1)}) %all-gather.39.cloned.1.call-update) | async-done | bytes 1695760 | tf_op jit(solution)/shard_map/all_gather | solution.py:36
  891.3 28.6 %reduce-scatter.85.cloned.1.call-done = bf16[1,184,1152]{2,1,0:T(8,128)(2,1)} async-done(((bf16[1,736,1152]{2,1,0:T(8,128)(2,1)}), bf16[1,184,1152]{2,1,0:T(8,128)(2,1)}) %reduce-scatter.85.cloned.1.call-update) | async-done | bytes 423952
  928.2 12.1 collective-permute-done.3
  941.9 19.5 %all-gather.41.cloned.1.call-done = bf16[1,736,1152]{2,1,0:T(8,128)(2,1)} async-done(((bf16[1,184,1152]{2,1,0:T(8,128)(2,1)}), bf16[1,736,1152]{2,1,0:T(8,128)(2,1)}) %all-gather.41.cloned.1.call-update) | async-done | bytes 1695760 | tf_op jit(solution)/shard_map/all_gather | solution.py:36
  974.9 28.9 %reduce-scatter.87.cloned.1.call-done = bf16[1,184,1152]{2,1,0:T(8,128)(2,1)} async-done(((bf16[1,736,1152]{2,1,0:T(8,128)(2,1)}), bf16[1,184,1152]{2,1,0:T(8,128)(2,1)}) %reduce-scatter.87.cloned.1.call-update) | async-done | bytes 423952
  1113.1 12.6 psum.7
  1146.2 24.8 %reduce-scatter.61.cloned.1.call-done = bf16[1076,288]{0,1:T(8,128)(2,1)} async-done(((bf16[1076,1152]{0,1:T(8,128)(2,1)}), bf16[1076,288]{0,1:T(8,128)(2,1)}) %reduce-scatter.61.cloned.1.call-update) | async-done | bytes 619792 | tf_op jit(solution)/shard_map/reduce_scatter | solution.py:318
  1173.8 23.8 %reduce-scatter.65.cloned.1.call-done = bf16[288,288]{1,0:T(8,128)(2,1)} async-done(((bf16[1152,288]{1,0:T(8,128)(2,1)}), bf16[288,288]{1,0:T(8,128)(2,1)}) %reduce-scatter.65.cloned.1.call-update) | async-done | bytes 165904
  1199.5 28.3 %reduce-scatter.89.cloned.1.call-done = bf16[1,184,1152]{2,1,0:T(8,128)(2,1)} async-done(((bf16[1,736,1152]{2,1,0:T(8,128)(2,1)}), bf16[1,184,1152]{2,1,0:T(8,128)(2,1)}) %reduce-scatter.89.cloned.1.call-update) | async-done | bytes 423952
  1231.1 62.4 %all-reduce.14 = (f32[2,1152]{1,0:T(2,128)S(1)}, f32[6,1152]{1,0:T(8,128)S(1)}) all-reduce(f32[2,1152]{1,0:T(2,128)S(1)} %fusion.319, f32[6,1152]{1,0:T(8,128)S(1)} %stack.226), channel_id=25, replica_groups=mesh['section'=2,'dp'=4,'tensor'=4] {'dp','tensor'}, use_global_device_ids=true, to_apply=%region_67.68.clone | all-reduce | flops 9216 | bytes 73728
  (592 shorter events, 459.1 us)
Async XLA Ops:
  7.2 138.1 %all-gather.45.cloned.1.call-start = ((), (), s32[]{:S(2)}) async-start(), calls=%async_computation.29 | async-start | bytes 4423680 | tf_op jit(solution)/shard_map/all_gather | solution.py:47
  9.8 141.6 %all-gather.23.cloned.1.call-start = ((), (), s32[]{:S(2)}) async-start(), calls=%async_computation.16 | async-start | bytes 2119680 | tf_op jit(solution)/shard_map/all_gather | solution.py:32
  104.2 89.0 %reduce-scatter.67.cloned.1.call-start = ((), (), s32[]{:S(2)}) async-start(), calls=%async_computation.35 | async-start | bytes 2119680
  166.1 83.8 %all-gather.47.cloned.1.call-start = ((), (), s32[]{:S(2)}) async-start(), calls=%async_computation.30 | async-start | bytes 3317760 | tf_op jit(solution)/shard_map/all_gather | solution.py:49
  166.7 104.3 %all-gather.25.cloned.1.call-start = ((), (), s32[]{:S(2)}) async-start(), calls=%async_computation.17 | async-start | bytes 2119680 | tf_op jit(solution)/shard_map/all_gather | solution.py:32
  198.6 129.2 %all-gather.49.cloned.1.call-start = ((), (), s32[]{:S(2)}) async-start(), calls=%async_computation.31 | async-start | bytes 3317760 | tf_op jit(solution)/shard_map/all_gather | solution.py:50
  199.2 163.4 %reduce-scatter.69.cloned.1.call-start = ((), (), s32[]{:S(2)}) async-start(), calls=%async_computation.36 | async-start | bytes 2119680
  334.9 65.2 %all-gather.27.cloned.1.call-start = ((), (), s32[]{:S(2)}) async-start(), calls=%async_computation.18 | async-start | bytes 2119680 | tf_op jit(solution)/shard_map/all_gather | solution.py:32
  378.6 64.4 %reduce-scatter.71.cloned.1.call-start = ((), (), s32[]{:S(2)}) async-start(), calls=%async_computation.37 | async-start | bytes 2119680
  414.1 54.8 %all-gather.29.cloned.1.call-start = ((), (), s32[]{:S(2)}) async-start(), calls=%async_computation.19 | async-start | bytes 2119680 | tf_op jit(solution)/shard_map/all_gather | solution.py:32
  448.4 60.4 %reduce-scatter.73.cloned.1.call-start = ((), (), s32[]{:S(2)}) async-start(), calls=%async_computation.38 | async-start | bytes 2119680
  479.9 65.3 %all-gather.31.cloned.1.call-start = ((), (), s32[]{:S(2)}) async-start(), calls=%async_computation.20 | async-start | bytes 2119680 | tf_op jit(solution)/shard_map/all_gather | solution.py:32
  523.7 65.8 %reduce-scatter.75.cloned.1.call-start = ((), (), s32[]{:S(2)}) async-start(), calls=%async_computation.39 | async-start | bytes 2119680
  560.6 54.9 %all-gather.33.cloned.1.call-start = ((), (), s32[]{:S(2)}) async-start(), calls=%async_computation.21 | async-start | bytes 2119680 | tf_op jit(solution)/shard_map/all_gather | solution.py:32
  595.0 42.2 %all-gather.51.cloned.1.call-start = ((), (), s32[]{:S(2)}) async-start(), calls=%async_computation.32 | async-start | bytes 2119680 | tf_op jit(solution)/shard_map/all_gather | solution.py:36
  596.6 83.1 %reduce-scatter.79.cloned.1.call-start = ((), (), s32[]{:S(2)}) async-start(), calls=%async_computation.41 | async-start | bytes 2119680
  650.8 55.4 %all-gather.35.cloned.1.call-start = ((), (), s32[]{:S(2)}) async-start(), calls=%async_computation.22 | async-start | bytes 2119680 | tf_op jit(solution)/shard_map/all_gather | solution.py:36
  685.7 71.7 %reduce-scatter.81.cloned.1.call-start = ((), (), s32[]{:S(2)}) async-start(), calls=%async_computation.42 | async-start | bytes 2119680
  728.6 71.4 %all-gather.37.cloned.1.call-start = ((), (), s32[]{:S(2)}) async-start(), calls=%async_computation.23 | async-start | bytes 2119680 | tf_op jit(solution)/shard_map/all_gather | solution.py:36
  780.4 62.0 %reduce-scatter.83.cloned.1.call-start = ((), (), s32[]{:S(2)}) async-start(), calls=%async_computation.43 | async-start | bytes 2119680
  813.4 55.5 %all-gather.39.cloned.1.call-start = ((), (), s32[]{:S(2)}) async-start(), calls=%async_computation.24 | async-start | bytes 2119680 | tf_op jit(solution)/shard_map/all_gather | solution.py:36
  848.4 71.5 %reduce-scatter.85.cloned.1.call-start = ((), (), s32[]{:S(2)}) async-start(), calls=%async_computation.44 | async-start | bytes 2119680
  891.0 70.4 %all-gather.41.cloned.1.call-start = ((), (), s32[]{:S(2)}) async-start(), calls=%async_computation.25 | async-start | bytes 2119680 | tf_op jit(solution)/shard_map/all_gather | solution.py:36
  926.9 13.4 %collective-permute-start.3 = (bf16[1,184,1152]{2,1,0:T(8,128)(2,1)}, bf16[1,184,1152]{2,1,0:T(8,128)(2,1)S(1)}, u32[]{:S(2)}, u32[]{:S(2)}) collective-permute-start(bf16[1,184,1152]{2,1,0:T(8,128)(2,1)} %add_convert_fusion.13), channel_id=1, source_target_pairs={{16,0},{17,1},{18,2},{19,3},{20,4},{21,5},{22,6},{23,7},{24,8},{25... | collective-permute-start | bytes 1271816 | tf_op jit(solution)/shard_map/ppermute | solution.py:18
  941.8 62.0 %reduce-scatter.87.cloned.1.call-start = ((), (), s32[]{:S(2)}) async-start(), calls=%async_computation.45 | async-start | bytes 2119680
  974.9 81.7 %all-gather.43.cloned.1.call-start = ((), (), s32[]{:S(2)}) async-start(), calls=%async_computation.26 | async-start | bytes 2119680 | tf_op jit(solution)/shard_map/all_gather | solution.py:36
  1009.7 89.6 %reduce-scatter.77.cloned.1.call-start = ((), (), s32[]{:S(2)}) async-start(), calls=%async_computation.40 | async-start | bytes 2119680
  1017.5 126.3 %reduce-scatter.59.cloned.1.call-start = ((), (), s32[]{:S(2)}) async-start(), calls=%async_computation.27 | async-start | bytes 3317760 | tf_op jit(solution)/shard_map/reduce_scatter | solution.py:315
  1029.5 141.4 %reduce-scatter.61.cloned.1.call-start = ((), (), s32[]{:S(2)}) async-start(), calls=%async_computation.28 | async-start | bytes 3317760 | tf_op jit(solution)/shard_map/reduce_scatter | solution.py:318
  1045.9 151.7 %reduce-scatter.65.cloned.1.call-start = ((), (), s32[]{:S(2)}) async-start(), calls=%async_computation.34 | async-start | bytes 1105920
  1078.3 149.5 %reduce-scatter.89.cloned.1.call-start = ((), (), s32[]{:S(2)}) async-start(), calls=%async_computation.46 | async-start | bytes 2119680
  1093.5 205.2 %reduce-scatter.63.cloned.1.call-start = ((), (), s32[]{:S(2)}) async-start(), calls=%async_computation.33 | async-start | bytes 2580480
  (146 other events, 4227.1 us)
Sparse Core Ops, SparseCore 0:
  10.1 75.2 all-gather.44
  104.3 17.9 all-gather.22
  166.2 26.8 reduce-scatter.66
  194.6 55.2 all-gather.46
  251.9 19.0 all-gather.24
  272.5 55.2 all-gather.48
  335.1 27.4 reduce-scatter.68
  378.7 21.3 all-gather.26
  414.2 28.7 reduce-scatter.70
  448.5 20.2 all-gather.28
  480.0 28.7 reduce-scatter.72
  523.8 21.3 all-gather.30
  560.7 28.7 reduce-scatter.74
  595.1 20.3 all-gather.32
  616.9 20.3 all-gather.50
  650.9 28.7 reduce-scatter.78
  685.9 20.3 all-gather.34
  728.7 28.7 reduce-scatter.80
  780.5 19.4 all-gather.36
  813.5 28.7 reduce-scatter.82
  848.5 20.3 all-gather.38
  891.1 28.7 reduce-scatter.84
  941.9 19.4 all-gather.40
  975.0 28.7 reduce-scatter.86
  1009.8 20.3 all-gather.42
  1032.6 28.7 reduce-scatter.76
  1063.5 52.7 reduce-scatter.58
  1118.6 52.3 reduce-scatter.60
  1173.3 24.2 reduce-scatter.64
  1200.0 27.7 reduce-scatter.88
  1230.2 43.5 reduce-scatter.62
where the time goes:
time: 1320 us; the launch traced here: 1310 us
  waiting for transfers between devices  672 us (51%)
  matrix products  220 us (17%)
  blocking collectives  158 us (12%)
  other arithmetic  122 us (9%)
  local copies, waits for them, and re-layouts  106 us (8%)
  between operations  17.3 us (1%)
  starting transfers between devices  14.2 us (1%)
    unnamed x45, waiting for transfers between devices  333 us
    all_gather x6, waiting for transfers between devices, rows_gather(): return lax.all_gather(pieces, 'tensor', axis=1, tiled=True)  101 us
    all_gather x6, waiting for transfers between devices, grads_gather(): return lax.all_gather(pieces, 'tensor', axis=1, tiled=True)  70.2 us
    unnamed x1, blocking collectives  62.4 us
    all_gather x1, waiting for transfers between devices, gather_weights(): lax.all_gather(up_part, 'dp', axis=0, tiled=True)  50.5 us
    all_gather x1, waiting for transfers between devices, gather_weights(): lax.all_gather(down_part, 'dp', axis=1, tiled=True)  50.4 us
    unnamed x299, local copies, waits for them, and re-layouts  43.5 us
    ppermute x4, waiting for transfers between devices, shifted(): return lax.ppermute(x, axis, pairs)  41.9 us
  transfers between devices with their start and end apart: 35, of which 29 were waited for; matrix products, arithmetic and copies ran while one was open for 18% of the time, Pallas kernels for 0%

commit v1 on v0

v1 whole, which is shorter than its diff:
```python
import math

import jax
import jax.numpy as jnp
from jax import lax
from jax.experimental import pallas as pl
from jax.experimental.pallas import tpu as pltpu
from jax.sharding import PartitionSpec as P

HEAD = 72
LANES = 128
norm_eps = 1e-06
masked_score = -1000000000.0
score_scale = 1.0 / math.sqrt(HEAD)
SWAP = [(0, 1), (1, 0)]
GELU_A = math.sqrt(2.0 / math.pi)
GELU_B = 0.044715
EVERY = ("section", "dp", "tensor")


def round_up(value, step):
    return -(-value // step) * step


def dot(left, right, left_dim, right_dim):
    return lax.dot_general(
        left, right, (((left_dim,), (right_dim,)), ((), ())), preferred_element_type=jnp.float32
    )


def low(value):
    return value.astype(jnp.bfloat16)


def layer_norm(rows, gain_vec, shift_vec):
    centred = rows - jnp.mean(rows, axis=-1, keepdims=True)
    spread = jnp.mean(centred * centred, axis=-1, keepdims=True)
    return centred * lax.rsqrt(spread + norm_eps) * gain_vec + shift_vec


def norm_back(rows, gain_vec, grads):
    centred = rows - jnp.mean(rows, axis=-1, keepdims=True)
    spread = jnp.mean(centred * centred, axis=-1, keepdims=True)
    inverse = lax.rsqrt(spread + norm_eps)
    xhat = centred * inverse
    e = grads * gain_vec
    back = inverse * (
        e
        - jnp.mean(e, axis=-1, keepdims=True)
        - xhat * jnp.mean(e * xhat, axis=-1, keepdims=True)
    )
    return back, grads * xhat


def gelu_tanh(value):
    return jax.nn.gelu(value, approximate=True)


def pad_heads(flat, heads):
    split = flat.reshape(flat.shape[:-1] + (heads, HEAD))
    padded = jnp.pad(split, [(0, 0)] * (split.ndim - 1) + [(0, LANES - HEAD)])
    return padded.reshape(flat.shape[:-1] + (heads * LANES,))


def drop_heads(padded):
    heads = padded.shape[-1] // LANES
    split = padded.reshape(padded.shape[:-1] + (heads, LANES))[..., :HEAD]
    return split.reshape(padded.shape[:-1] + (heads * HEAD,))


MESH = pl.DeviceIdType.MESH
VMEM_BYTES = 64_000_000
LOG2E = 1.0 / math.log(2.0)
TILE = 256


class Slab:
    def __init__(self, half_rows):
        self.half_rows = half_rows
        section = lax.axis_index("section")
        tensor = lax.axis_index("tensor")
        core = lax.rem(tensor, 2)
        self.mine = self.around(section, tensor, core)
        self.theirs = self.around(section, tensor + 1 - 2 * core, 1 - core)
        self.mate = self.theirs[0]

    @staticmethod
    def around(section, tensor, core):
        over = lax.rem(tensor + 2, 4)
        turn = 1 - 2 * section
        first = (section + (1 - core) * turn, tensor + core * (over - tensor))
        second = (section + core * turn, tensor + (1 - core) * (over - tensor))
        return [(section, tensor), first, second, (1 - section, over)]

    def rows(self, ref, at):
        start = pl.multiple_of((2 * at[1] + at[0]) * self.half_rows, self.half_rows)
        return ref.at[pl.ds(start, self.half_rows)]

    def greet(self):
        barrier = pltpu.get_barrier_semaphore()
        for peer in (self.mine[1], self.mine[2], self.mate):
            pl.semaphore_signal(barrier, inc=1, device_id=named(peer), device_id_type=MESH)
        pl.semaphore_wait(barrier, 3)


def named(at):
    return {"section": at[0], "tensor": at[1]}


class Moves:
    def __init__(self, slab, send_sems, recv_sems):
        self.slab, self.send_sems, self.recv_sems = slab, send_sems, recv_sems
        self.sent = []

    def copy(self, src, dst, role, peer):
        return pltpu.make_async_remote_copy(
            src_ref=src,
            dst_ref=dst,
            send_sem=self.send_sems.at[role],
            recv_sem=self.recv_sems.at[role],
            device_id=named(peer),
            device_id_type=MESH,
        )

    def send(self, src, dst, role, peer):
        copy = self.copy(src, dst, role, peer)
        copy.start()
        self.sent.append(copy)

    def arrived(self, dst, role):
        self.copy(dst, dst, role, self.slab.mate).wait_recv()

    def drain(self):
        for copy in self.sent:
            copy.wait_send()


class Gather(Moves):
    def __init__(self, slab, whole, send_sems, recv_sems):
        super().__init__(slab, send_sems, recv_sems)
        self.whole = whole

    def pass_on(self, at, role, peer):
        part = self.slab.rows(self.whole, at)
        self.send(part, part, role, peer)

    def arrive(self, at, role):
        self.arrived(self.slab.rows(self.whole, at), role)

    def start(self):
        mine = self.slab.mine
        self.pass_on(mine[0], 0, mine[1])
        self.pass_on(mine[0], 1, mine[2])
        self.pass_on(mine[0], 3, self.slab.mate)

    def forward(self):
        mine, mate = self.slab.mine, self.slab.mate
        self.arrive(mine[1], 0)
        self.pass_on(mine[1], 2, mine[2])
        self.pass_on(mine[1], 4, mate)

    def to_mate(self):
        mine, mate = self.slab.mine, self.slab.mate
        self.arrive(mine[2], 1)
        self.pass_on(mine[2], 5, mate)
        self.arrive(mine[3], 2)
        self.pass_on(mine[3], 6, mate)

    def finish(self):
        for k in range(4):
            self.arrive(self.slab.theirs[k], 3 + k)
        self.drain()


class Scatter(Moves):
    def __init__(self, slab, terms, from_mate, outgoing, from_second, from_first, send_sems, recv_sems):
        super().__init__(slab, send_sems, recv_sems)
        self.terms, self.from_mate, self.outgoing = terms, from_mate, outgoing
        self.from_second, self.from_first = from_second, from_first

    def start(self):
        for k in (3, 2, 1, 0):
            part = self.slab.rows(self.terms, self.slab.theirs[k])
            self.send(part, self.from_mate.at[k], k, self.slab.mate)

    def chip_sum(self, k, rows):
        part = self.slab.rows(self.terms, self.slab.mine[k])
        return part[rows].astype(jnp.float32) + self.from_mate[k, rows].astype(jnp.float32)

    def blocks(self):
        return [pl.ds(start, 32) for start in range(0, self.slab.half_rows, 32)]

    def second_hop(self):
        second = self.slab.mine[2]
        for k, slot in ((3, 1), (2, 0)):
            self.arrived(self.from_mate.at[k], k)
            for rows in self.blocks():
                self.outgoing[slot, rows] = low(self.chip_sum(k, rows))
            self.send(self.outgoing.at[slot], self.from_second.at[slot], 4 + slot, second)

    def first_hop(self):
        self.arrived(self.from_mate.at[1], 1)
        self.arrived(self.from_second.at[1], 5)
        for rows in self.blocks():
            term = self.from_second[1, rows].astype(jnp.float32)
            self.outgoing[2, rows] = low(self.chip_sum(1, rows) + term)
        self.send(self.outgoing.at[2], self.from_first, 6, self.slab.mine[1])

    def finish(self):
        self.arrived(self.from_mate.at[0], 0)
        self.arrived(self.from_second.at[0], 4)
        self.arrived(self.from_first, 6)
        self.drain()

    def total(self, rows):
        other = self.from_second[0, rows].astype(jnp.float32)
        last = self.from_first[rows].astype(jnp.float32)
        return self.chip_sum(0, rows) + other + last


def scatter_scratch(micro, seq, half_rows, width):
    return [
        pltpu.VMEM((micro, seq, width), jnp.bfloat16),
        pltpu.VMEM((micro, 4, half_rows, width), jnp.bfloat16),
        pltpu.VMEM((micro, 3, half_rows, width), jnp.bfloat16),
        pltpu.VMEM((micro, 2, half_rows, width), jnp.bfloat16),
        pltpu.VMEM((micro, half_rows, width), jnp.bfloat16),
        pltpu.SemaphoreType.DMA((micro, 7)),
        pltpu.SemaphoreType.DMA((micro, 7)),
    ]


def gather_scratch(micro, seq, width):
    return [
        pltpu.VMEM((micro, seq, width), jnp.bfloat16),
        pltpu.SemaphoreType.DMA((micro, 7)),
        pltpu.SemaphoreType.DMA((micro, 7)),
    ]


def make_scatters(slab, refs, micro):
    terms, from_mate, outgoing, from_second, from_first, send_sems, recv_sems = refs
    return [
        Scatter(
            slab,
            terms.at[m],
            from_mate.at[m],
            outgoing.at[m],
            from_second.at[m],
            from_first.at[m],
            send_sems.at[m],
            recv_sems.at[m],
        )
        for m in range(micro)
    ]


def make_gathers(slab, refs, micro):
    whole, send_sems, recv_sems = refs
    return [
        Gather(slab, whole.at[m], send_sems.at[m], recv_sems.at[m]) for m in range(micro)
    ]


def step_rows(i, size):
    return pl.ds(pl.multiple_of(i * size, size), size)


def repeat(count, body):
    def one(i, carry):
        body(i)
        return carry

    lax.fori_loop(0, count, one, 0)


def widen(packed, wide):
    heads = packed.shape[1] // HEAD

    def block(i):
        rows = step_rows(i, 128)
        for h in range(heads):
            piece = packed[rows, h * HEAD : (h + 1) * HEAD]
            blank = jnp.zeros((128, LANES - HEAD), jnp.bfloat16)
            wide[rows, h * LANES : (h + 1) * LANES] = jnp.concatenate([piece, blank], axis=1)

    repeat(packed.shape[0] // 128, block)


def attn_forward_kernel(
    rows_ref, vec, bias, mask, packed_hbm, hidden_ref, lse_ref, normed_hbm, qkv_hbm, mixed_hbm, *rest
):
    micro, half_rows, width = rows_ref.shape
    gathered, gather_refs = rest[0], rest[0:3]
    scatter_refs = rest[3:10]
    terms = rest[3]
    packed, wide, qkv, mixed, load_sem, keep_sems = rest[10:]
    seq = qkv.shape[1]
    pair = mixed.shape[2]
    heads = pair // LANES
    load = pltpu.make_async_copy(packed_hbm, packed, load_sem)
    load.start()
    slab = Slab(half_rows)
    gathers = make_gathers(slab, gather_refs, micro)
    scatters = make_scatters(slab, scatter_refs, micro)
    slab.greet()
    for m in range(micro):
        own = slab.rows(gathered.at[m], slab.mine[0])
        for start in range(0, half_rows, 32):
            block = rows_ref[m, pl.ds(start, 32)].astype(jnp.float32)
            own[pl.ds(start, 32)] = low(layer_norm(block, vec[0:1], vec[2:3]))
        gathers[m].start()
    load.wait()
    widen(packed, wide)
    keeps = []

    def keep(src, dst, i):
        copy = pltpu.make_async_copy(src, dst, keep_sems.at[i])
        copy.start()
        keeps.append(copy)

    def project(m):
        def block(i):
            rows = step_rows(i, TILE)
            out = dot(gathered[m, rows], wide[:, : 3 * pair], 1, 0)
            qkv[m, rows] = low(out + bias[...])

        repeat(seq // TILE, block)

    def attend(m, h):
        def block(i):
            rows = step_rows(i, LANES)
            q = qkv[m, rows, h * LANES : (h + 1) * LANES]
            k = qkv[m, :, pair + h * LANES : pair + (h + 1) * LANES]
            v = qkv[m, :, 2 * pair + h * LANES : 2 * pair + (h + 1) * LANES]
            scores = dot(q, k, 1, 1) * (score_scale * LOG2E) + mask[m : m + 1]
            top = jnp.max(scores, axis=-1, keepdims=True)
            exp_scores = jnp.exp2(scores - top)
            total = jnp.sum(exp_scores, axis=-1, keepdims=True)
            probs = low(exp_scores * (1.0 / total))
            mixed[m, rows, h * LANES : (h + 1) * LANES] = low(dot(probs, v, 1, 0))
            lse = jnp.broadcast_to(top + jnp.log(total) * LOG2E, (LANES, LANES)).T
            lse_ref[m, h : h + 1, rows] = lse[0:1]

        repeat(seq // LANES, block)

    def output(m):
        def block(i):
            rows = step_rows(i, TILE)
            terms[m, rows] = low(dot(mixed[m, rows], wide[:, 3 * pair :], 1, 1))

        repeat(seq // TILE, block)

    def close(m):
        scatters[m].finish()
        for rows in scatters[m].blocks():
            start = rows_ref[m, rows].astype(jnp.float32)
            hidden_ref[m, rows] = start + scatters[m].total(rows) + vec[5:6]

    gathers[0].forward()
    gathers[0].to_mate()
    gathers[1].forward()
    gathers[0].finish()
    keep(gathered.at[0], normed_hbm.at[0], 0)
    project(0)
    gathers[1].to_mate()
    attend(0, 0)
    gathers[1].finish()
    keep(gathered.at[1], normed_hbm.at[1], 1)
    for h in range(1, heads):
        attend(0, h)
    output(0)
    scatters[0].start()
    keep(qkv.at[0], qkv_hbm.at[0], 2)
    keep(mixed.at[0], mixed_hbm.at[0], 3)
    project(1)
    scatters[0].second_hop()
    for h in range(heads):
        attend(1, h)
        if h == 0:
            scatters[0].first_hop()
    output(1)
    scatters[1].start()
    keep(qkv.at[1], qkv_hbm.at[1], 4)
    keep(mixed.at[1], mixed_hbm.at[1], 5)
    close(0)
    scatters[1].second_hop()
    scatters[1].first_hop()
    close(1)
    for copy in keeps:
        copy.wait()


def ffn_forward_kernel(
    hidden_ref, vec, up_bias, packed_hbm, out_ref, second_hbm, upper_hbm, *rest
):
    micro, half_rows, width = hidden_ref.shape
    gathered, gather_refs = rest[0], rest[0:3]
    scatter_refs = rest[3:10]
    terms = rest[3]
    packed, upper, load_sem, keep_sems = rest[10:]
    seq, ff = upper.shape[1:]
    load = pltpu.make_async_copy(packed_hbm, packed, load_sem)
    load.start()
    slab = Slab(half_rows)
    gathers = make_gathers(slab, gather_refs, micro)
    scatters = make_scatters(slab, scatter_refs, micro)
    slab.greet()
    for m in range(micro):
        own = slab.rows(gathered.at[m], slab.mine[0])
        for start in range(0, half_rows, 32):
            block = hidden_ref[m, pl.ds(start, 32)]
            own[pl.ds(start, 32)] = low(layer_norm(block, vec[1:2], vec[6:7]))
        gathers[m].start()
    load.wait()
    keeps = []

    def keep(src, dst, i):
        copy = pltpu.make_async_copy(src, dst, keep_sems.at[i])
        copy.start()
        keeps.append(copy)

    def compute(m, i):
        rows = step_rows(i, TILE)
        value = dot(gathered[m, rows], packed[:, :ff], 1, 0) + up_bias[...]
        upper[m, rows] = value
        active = low(gelu_tanh(value))
        terms[m, rows] = low(dot(active, packed[:, ff:], 1, 1))

    def close(m):
        scatters[m].finish()
        for rows in scatters[m].blocks():
            out_ref[m, rows] = low(hidden_ref[m, rows] + scatters[m].total(rows) + vec[7:8])

    count = seq // TILE
    gathers[0].forward()
    gathers[0].to_mate()
    gathers[1].forward()
    gathers[0].finish()
    keep(gathered.at[0], second_hbm.at[0], 0)
    repeat(count, lambda i: compute(0, i))
    scatters[0].start()
    keep(upper.at[0], upper_hbm.at[0], 1)
    gathers[1].to_mate()
    gathers[1].finish()
    keep(gathered.at[1], second_hbm.at[1], 2)
    scatters[0].second_hop()
    repeat(count, lambda i: compute(1, i))
    scatters[1].start()
    keep(upper.at[1], upper_hbm.at[1], 3)
    scatters[0].first_hop()
    scatters[1].second_hop()
    close(0)
    scatters[1].first_hop()
    close(1)
    for copy in keeps:
        copy.wait()


def ffn_backward_kernel(
    grad_ref, hidden_ref, vec, second_hbm, upper_hbm, packed_hbm,
    out_ref, grads_ref, small_ref, up_bias_ref, *rest
):
    micro, half_rows, width = hidden_ref.shape
    gathered, gather_refs = rest[0], rest[0:3]
    scatter_refs = rest[3:10]
    terms = rest[3]
    packed, second, upper, grad_upper, active, sums, load_sems = rest[10:]
    seq, ff = upper.shape[1:]
    loads = [pltpu.make_async_copy(packed_hbm, packed, load_sems.at[0])]
    for m in range(micro):
        loads.append(pltpu.make_async_copy(upper_hbm.at[m], upper.at[m], load_sems.at[1 + 2 * m]))
        loads.append(pltpu.make_async_copy(second_hbm.at[m], second.at[m], load_sems.at[2 + 2 * m]))
    for load in loads:
        load.start()
    slab = Slab(half_rows)
    gathers = make_gathers(slab, gather_refs, micro)
    scatters = make_scatters(slab, scatter_refs, micro)
    slab.greet()
    for m in range(micro):
        own = slab.rows(gathered.at[m], slab.mine[0])
        for start in range(0, half_rows, 32):
            own[pl.ds(start, 32)] = grad_ref[m, pl.ds(start, 32)]
        gathers[m].start()
    small_ref[...] = jnp.zeros_like(small_ref)
    up_bias_ref[...] = jnp.zeros_like(up_bias_ref)
    for load in loads:
        load.wait()

    def compute(m, i):
        rows = step_rows(i, TILE)
        value = upper[m, rows]
        square = value * value
        bent = jnp.tanh(GELU_A * value * (1.0 + GELU_B * square))
        half = 0.5 * (1.0 + bent)
        active[m, rows] = low(value * half)
        slope = half + (0.5 * GELU_A) * value * (1.0 - bent * bent) * (1.0 + 3.0 * GELU_B * square)
        grad_active = dot(gathered[m, rows], packed[:, ff:], 1, 0)
        grad = low(grad_active * slope)
        grad_upper[m, rows] = grad
        up_bias_ref[0:1] += jnp.sum(grad.astype(jnp.float32), axis=0, keepdims=True)
        terms[m, rows] = low(dot(grad, packed[:, :ff], 1, 1))

    def weight_grads(m):
        def block(i):
            cols = step_rows(i, LANES)
            up = dot(second[m, :, cols], grad_upper[m], 0, 0)
            down = dot(gathered[m, :, cols], active[m], 0, 0)
            if m == 0:
                sums[cols, :ff] = up
                sums[cols, ff:] = down
            else:
                grads_ref[cols, :ff] = low(sums[cols, :ff] + up)
                grads_ref[cols, ff:] = low(sums[cols, ff:] + down)

        repeat(width // LANES, block)

    def close(m):
        scatters[m].finish()
        for rows in scatters[m].blocks():
            grad_normed = scatters[m].total(rows)
            back, gain_terms = norm_back(hidden_ref[m, rows], vec[1:2], grad_normed)
            grad_rows = grad_ref[m, rows].astype(jnp.float32)
            grad_hidden = grad_rows + back
            out_ref[m, rows] = grad_hidden
            branch = low(grad_hidden).astype(jnp.float32)
            for j, item in enumerate((gain_terms, grad_normed, grad_rows, branch)):
                small_ref[j : j + 1] += jnp.sum(item, axis=0, keepdims=True)

    count = seq // TILE
    gathers[0].forward()
    gathers[0].to_mate()
    gathers[1].forward()
    gathers[0].finish()
    repeat(count, lambda i: compute(0, i))
    scatters[0].start()
    gathers[1].to_mate()
    gathers[1].finish()
    scatters[0].second_hop()
    repeat(count, lambda i: compute(1, i))
    scatters[1].start()
    scatters[0].first_hop()
    weight_grads(0)
    scatters[1].second_hop()
    close(0)
    scatters[1].first_hop()
    weight_grads(1)
    close(1)


def attn_backward_kernel(
    grad_ref, rows_ref, vec, lse, mask, normed_hbm, qkv_hbm, mixed_hbm, packed_hbm,
    out_ref, grads_ref, small_ref, bias_ref, *rest
):
    micro, half_rows, width = grad_ref.shape
    gathered, gather_refs = rest[0], rest[0:3]
    scatter_refs = rest[3:10]
    terms = rest[3]
    packed, wide, normed, qkv, mixed, grad_mixed, grad_qkv, turned, sums, load_sems = rest[10:]
    seq, pair = mixed.shape[1:]
    heads = pair // LANES
    loads = [pltpu.make_async_copy(packed_hbm, packed, load_sems.at[0])]
    for m in range(micro):
        loads.append(pltpu.make_async_copy(qkv_hbm.at[m], qkv.at[m], load_sems.at[1 + 3 * m]))
        loads.append(pltpu.make_async_copy(mixed_hbm.at[m], mixed.at[m], load_sems.at[2 + 3 * m]))
        loads.append(pltpu.make_async_copy(normed_hbm.at[m], normed.at[m], load_sems.at[3 + 3 * m]))
    for load in loads:
        load.start()
    slab = Slab(half_rows)
    gathers = make_gathers(slab, gather_refs, micro)
    scatters = make_scatters(slab, scatter_refs, micro)
    slab.greet()
    for m in range(micro):
        own = slab.rows(gathered.at[m], slab.mine[0])
        for start in range(0, half_rows, 32):
            own[pl.ds(start, 32)] = low(grad_ref[m, pl.ds(start, 32)])
        gathers[m].start()
    small_ref[...] = jnp.zeros_like(small_ref)
    bias_ref[...] = jnp.zeros_like(bias_ref)
    for load in loads:
        load.wait()
    widen(packed, wide)

    def head(h, part=0):
        return slice(part * pair + h * LANES, part * pair + (h + 1) * LANES)

    for m in range(micro):
        for h in range(heads):
            turned[m, h] = low(qkv[m, :, head(h, 1)].astype(jnp.float32).T)

    def mix_grads(m):
        def block(i):
            rows = step_rows(i, TILE)
            grad_mixed[m, rows] = low(dot(gathered[m, rows], wide[:, 3 * pair :], 1, 0))

        repeat(seq // TILE, block)

    def attend(m, h):
        keys, values = qkv[m, :, head(h, 1)], qkv[m, :, head(h, 2)]
        shut = mask[m]

        def block(i, carry):
            grad_keys, grad_values = carry
            rows = step_rows(i, LANES)
            queries = qkv[m, rows, head(h)]
            grads = grad_mixed[m, rows, head(h)]
            scores = dot(keys, queries, 1, 1) * (score_scale * LOG2E) + shut
            probs = jnp.exp2(scores - lse[m, h : h + 1, rows])
            grad_probs = dot(values, grads, 1, 1)
            inner = jnp.sum(grad_probs * probs, axis=0, keepdims=True)
            grad_scores = low(probs * (grad_probs - inner))
            turn = dot(turned[m, h], grad_scores, 1, 0).T
            grad_qkv[m, rows, head(h)] = low(turn * score_scale)
            grad_values = grad_values + dot(low(probs), grads, 1, 0)
            grad_keys = grad_keys + dot(grad_scores, queries, 1, 0)
            return grad_keys, grad_values

        zero = jnp.zeros((seq, LANES), jnp.float32)
        grad_keys, grad_values = lax.fori_loop(0, seq // LANES, block, (zero, zero))
        grad_qkv[m, :, head(h, 1)] = low(grad_keys * score_scale)
        grad_qkv[m, :, head(h, 2)] = low(grad_values)

    def back_project(m):
        def block(i):
            rows = step_rows(i, TILE)
            grads = grad_qkv[m, rows]
            terms[m, rows] = low(dot(grads, wide[:, : 3 * pair], 1, 1))
            for j, part in enumerate((0, 2)):
                piece = grads[:, part * pair : (part + 1) * pair].astype(jnp.float32)
                bias_ref[j : j + 1] += jnp.sum(piece, axis=0, keepdims=True)

        repeat(seq // TILE, block)

    def weight_grads(m):
        def block(i):
            cols = step_rows(i, LANES)
            first = dot(normed[m, :, cols], grad_qkv[m], 0, 0)
            last = dot(gathered[m, :, cols], mixed[m], 0, 0)
            if m == 0:
                sums[cols, : 3 * pair] = first
                sums[cols, 3 * pair :] = last
            else:
                total = low(
                    jnp.concatenate(
                        [sums[cols, : 3 * pair] + first, sums[cols, 3 * pair :] + last], axis=1
                    )
                )
                pieces = [
                    total[:, h * LANES : h * LANES + HEAD] for h in range(4 * heads)
                ]
                grads_ref[cols] = jnp.concatenate(pieces, axis=1)

        repeat(width // LANES, block)

    def close(m):
        scatters[m].finish()
        for rows in scatters[m].blocks():
            grad_normed = scatters[m].total(rows)
            back, gain_terms = norm_back(
                rows_ref[m, rows].astype(jnp.float32), vec[0:1], grad_normed
            )
            out_ref[m, rows] = low(grad_ref[m, rows] + back)
            for j, item in enumerate((gain_terms, grad_normed)):
                small_ref[j : j + 1] += jnp.sum(item, axis=0, keepdims=True)

    gathers[0].forward()
    gathers[0].to_mate()
    gathers[1].forward()
    gathers[0].finish()
    mix_grads(0)
    attend(0, 0)
    gathers[1].to_mate()
    for h in range(1, heads):
        attend(0, h)
    gathers[1].finish()
    back_project(0)
    scatters[0].start()
    mix_grads(1)
    attend(1, 0)
    scatters[0].second_hop()
    for h in range(1, heads):
        attend(1, h)
        if h == 1:
            scatters[0].first_hop()
    back_project(1)
    scatters[1].start()
    weight_grads(0)
    scatters[1].second_hop()
    close(0)
    scatters[1].first_hop()
    weight_grads(1)
    close(1)


def any_spec():
    return pl.BlockSpec(memory_space=pl.ANY)


def vmem_spec():
    return pl.BlockSpec(memory_space=pltpu.VMEM)


def shape_of(shape, dtype):
    return jax.ShapeDtypeStruct(shape, dtype)


def params(collective):
    return pltpu.CompilerParams(
        collective_id=collective, has_side_effects=True, vmem_limit_bytes=VMEM_BYTES
    )


def attn_forward(rows_low, vec, bias_qv, packed, mask):
    micro, half_rows, width = rows_low.shape
    seq = mask.shape[1]
    pair = bias_qv.shape[1]
    heads = pair // LANES
    bias = jnp.concatenate([bias_qv[0], jnp.zeros((pair,), jnp.float32), bias_qv[1]])[None]
    low_type, high_type = jnp.bfloat16, jnp.float32
    hidden, lse, normed, qkv, mixed = pl.pallas_call(
        attn_forward_kernel,
        out_shape=[
            shape_of((micro, half_rows, width), high_type),
            shape_of((micro, heads, seq), high_type),
            shape_of((micro, seq, width), low_type),
            shape_of((micro, seq, 3 * pair), low_type),
            shape_of((micro, seq, pair), low_type),
        ],
        in_specs=[vmem_spec()] * 4 + [any_spec()],
        out_specs=[vmem_spec()] * 2 + [any_spec()] * 3,
        scratch_shapes=gather_scratch(micro, seq, width)
        + scatter_scratch(micro, seq, half_rows, width)
        + [
            pltpu.VMEM(packed.shape, low_type),
            pltpu.VMEM((width, 4 * pair), low_type),
            pltpu.VMEM((micro, seq, 3 * pair), low_type),
            pltpu.VMEM((micro, seq, pair), low_type),
            pltpu.SemaphoreType.DMA,
            pltpu.SemaphoreType.DMA((6,)),
        ],
        compiler_params=params(0),
        name="attn_forward",
    )(rows_low, vec, bias, mask, packed)
    return hidden, (normed, qkv, lse, mixed)


def ffn_forward(hidden, vec, up_bias, packed, seq):
    micro, half_rows, width = hidden.shape
    ff = up_bias.shape[0]
    low_type, high_type = jnp.bfloat16, jnp.float32
    out, second, upper = pl.pallas_call(
        ffn_forward_kernel,
        out_shape=[
            shape_of((micro, half_rows, width), low_type),
            shape_of((micro, seq, width), low_type),
            shape_of((micro, seq, ff), high_type),
        ],
        in_specs=[vmem_spec()] * 3 + [any_spec()],
        out_specs=[vmem_spec()] + [any_spec()] * 2,
        scratch_shapes=gather_scratch(micro, seq, width)
        + scatter_scratch(micro, seq, half_rows, width)
        + [
            pltpu.VMEM(packed.shape, low_type),
            pltpu.VMEM((micro, seq, ff), high_type),
            pltpu.SemaphoreType.DMA,
            pltpu.SemaphoreType.DMA((4,)),
        ],
        compiler_params=params(1),
        name="ffn_forward",
    )(hidden, vec, up_bias[None], packed)
    return out, (second, upper)


def ffn_backward(grad_low, hidden, kept, vec, packed):
    second, upper = kept
    micro, half_rows, width = hidden.shape
    seq, ff = upper.shape[1:]
    low_type, high_type = jnp.bfloat16, jnp.float32
    grad_hidden, grads, small, up_bias = pl.pallas_call(
        ffn_backward_kernel,
        out_shape=[
            shape_of((micro, half_rows, width), high_type),
            shape_of((width, 2 * ff), low_type),
            shape_of((8, width), high_type),
            shape_of((8, ff), high_type),
        ],
        in_specs=[vmem_spec()] * 3 + [any_spec()] * 3,
        out_specs=[vmem_spec()] * 4,
        scratch_shapes=gather_scratch(micro, seq, width)
        + scatter_scratch(micro, seq, half_rows, width)
        + [
            pltpu.VMEM(packed.shape, low_type),
            pltpu.VMEM((micro, seq, width), low_type),
            pltpu.VMEM((micro, seq, ff), high_type),
            pltpu.VMEM((micro, seq, ff), low_type),
            pltpu.VMEM((micro, seq, ff), low_type),
            pltpu.VMEM((width, 2 * ff), high_type),
            pltpu.SemaphoreType.DMA((1 + 2 * micro,)),
        ],
        compiler_params=params(2),
        name="ffn_backward",
    )(grad_low, hidden, vec, second, upper, packed)
    return grad_hidden, grads, small, up_bias[0]


def attn_backward(grad_hidden, rows_low, kept, vec, packed, mask):
    normed, qkv, lse, mixed = kept
    micro, half_rows, width = grad_hidden.shape
    seq, pair = mixed.shape[1:]
    heads = pair // LANES
    low_type, high_type = jnp.bfloat16, jnp.float32
    out, grads, small, bias = pl.pallas_call(
        attn_backward_kernel,
        out_shape=[
            shape_of((micro, half_rows, width), low_type),
            shape_of(packed.shape, low_type),
            shape_of((8, width), high_type),
            shape_of((8, pair), high_type),
        ],
        in_specs=[vmem_spec()] * 5 + [any_spec()] * 4,
        out_specs=[vmem_spec()] * 4,
        scratch_shapes=gather_scratch(micro, seq, width)
        + scatter_scratch(micro, seq, half_rows, width)
        + [
            pltpu.VMEM(packed.shape, low_type),
            pltpu.VMEM((width, 4 * pair), low_type),
            pltpu.VMEM((micro, seq, width), low_type),
            pltpu.VMEM((micro, seq, 3 * pair), low_type),
            pltpu.VMEM((micro, seq, pair), low_type),
            pltpu.VMEM((micro, seq, pair), low_type),
            pltpu.VMEM((micro, seq, 3 * pair), low_type),
            pltpu.VMEM((micro, heads, LANES, seq), low_type),
            pltpu.VMEM((width, 4 * pair), high_type),
            pltpu.SemaphoreType.DMA((1 + 3 * micro,)),
        ],
        compiler_params=params(3),
        name="attn_backward",
    )(grad_hidden, rows_low, vec, lse, mask, normed, qkv, mixed, packed)
    return out, grads, small, bias[:2]


def shards(
    section_input,
    final_cotangent,
    lengths,
    qkv_weight,
    out_weight,
    up_weight,
    down_weight,
    norm_gains,
    biases,
    up_bias,
):
    here = lax.axis_index("section")
    tensor = lax.axis_index("tensor")
    sections = lax.axis_size("section")
    micro, _, own_rows, width = section_input.shape
    head_cols = qkv_weight.shape[3]
    pair_cols = head_cols // sections
    heads = pair_cols // HEAD
    ff_cols = up_weight.shape[2]
    half_ff = ff_cols // sections
    ff_wide = round_up(half_ff, LANES)
    half_rows = round_up(-(-own_rows // sections), 32)
    full_rows = half_rows * sections
    seq = full_rows * lax.axis_size("tensor")

    def pick(two, index):
        return lax.dynamic_index_in_dim(two, index, 0, keepdims=False)

    def by_layer(mine, other):
        return [jnp.where(here == 0, mine, other), jnp.where(here == 0, other, mine)]

    def swap(value):
        return lax.ppermute(value, "section", SWAP)

    part_rows = qkv_weight.shape[2]
    heads_first = jnp.concatenate([jnp.moveaxis(qkv_weight[0], 1, 0), out_weight[0].T[:, None]], 1)
    halves = heads_first.reshape(part_rows, 4, sections, pair_cols)
    attn_parts = jnp.moveaxis(halves, 2, 0).reshape(sections, part_rows, 4 * pair_cols)
    ff_parts = jnp.stack([up_weight[0], down_weight[0].T], 1)
    ff_parts = ff_parts.reshape(part_rows, 2, sections, half_ff)
    ff_parts = jnp.pad(ff_parts, [(0, 0)] * 3 + [(0, ff_wide - half_ff)])
    ff_parts = jnp.moveaxis(ff_parts, 2, 0).reshape(sections, part_rows, 2 * ff_wide)
    attn_layers = by_layer(pick(attn_parts, here), swap(pick(attn_parts, 1 - here)))
    ff_layers = by_layer(pick(ff_parts, here), swap(pick(ff_parts, 1 - here)))
    attn_packed, ff_packed = [], []
    for layer in range(2):
        attn_packed.append(lax.all_gather(attn_layers[layer], "dp", axis=0, tiled=True))
        ff_packed.append(lax.all_gather(ff_layers[layer], "dp", axis=0, tiled=True))

    small = jnp.concatenate([norm_gains[0], biases[0]], 0)
    vectors = lax.all_gather(small, EVERY, axis=0, tiled=False)
    vectors = vectors.reshape((sections, -1) + small.shape)
    vectors = jnp.moveaxis(vectors, 1, 2).reshape(sections, small.shape[0], width)
    up_biases = lax.all_gather(up_bias[0], "section", axis=0, tiled=False)
    up_biases = lax.dynamic_slice_in_dim(up_biases, here * half_ff, half_ff, 1)
    up_biases = jnp.pad(up_biases, [(0, 0), (0, ff_wide - half_ff)])
    head_start = tensor * head_cols + here * pair_cols
    bias_qv = lax.dynamic_slice_in_dim(vectors[:, 3:5], head_start, pair_cols, 2)
    bias_qv = pad_heads(bias_qv, heads)

    place = jnp.arange(seq, dtype=jnp.int32)
    within = place % full_rows
    token = (place // full_rows) * own_rows + within
    live = (within < own_rows)[None] & (token[None] < lengths)
    mask = jnp.where(live, 0.0, masked_score).astype(jnp.float32)
    mask_columns = jnp.broadcast_to(mask[:, :, None], (micro, seq, LANES))

    def my_rows(value):
        padded = jnp.pad(value[:, 0], [(0, 0), (0, full_rows - own_rows), (0, 0)])
        return lax.dynamic_slice_in_dim(padded, here * half_rows, half_rows, 1)

    def whole_rows(first, second):
        mine, other = jnp.where(here == 0, first, second), jnp.where(here == 0, second, first)
        got = swap(other)
        low_half, high_half = by_layer(mine, got)
        return jnp.concatenate([low_half, high_half], 1)[:, None, :own_rows]

    rows = my_rows(section_input)
    inputs, hiddens, attn_kept, ff_kept, outputs = [], [], [], [], []
    for layer in range(2):
        inputs.append(rows)
        hidden, kept = attn_forward(
            rows, vectors[layer], bias_qv[layer], attn_packed[layer], mask
        )
        hiddens.append(hidden)
        attn_kept.append(kept)
        rows, kept = ffn_forward(
            hidden, vectors[layer], up_biases[layer], ff_packed[layer], seq
        )
        ff_kept.append(kept)
        outputs.append(rows)
    section_output = whole_rows(outputs[0], outputs[1])

    grads = my_rows(final_cotangent)
    zero_row = jnp.zeros((width,), jnp.float32)
    attn_sums, ff_sums, small_sums, up_sums, input_grads = {}, {}, {}, {}, {}
    for layer in (1, 0):
        grad_hidden, ff_grad, small_two, up_sums[layer] = ffn_backward(
            grads, hiddens[layer], ff_kept[layer], vectors[layer], ff_packed[layer]
        )
        ff_sums[layer] = lax.psum_scatter(ff_grad, "dp", scatter_dimension=0, tiled=True)
        grads, attn_grad, small_one, bias_grad = attn_backward(
            grad_hidden,
            inputs[layer],
            attn_kept[layer],
            vectors[layer],
            attn_packed[layer],
            mask_columns,
        )
        attn_sums[layer] = lax.psum_scatter(attn_grad, "dp", scatter_dimension=0, tiled=True)
        input_grads[layer] = grads
        bias_grad = drop_heads(bias_grad)
        bias_rows = [
            lax.dynamic_update_slice_in_dim(zero_row, bias_grad[i], head_start, 0) for i in (0, 1)
        ]
        small_sums[layer] = jnp.stack(
            [
                small_one[0],
                small_two[0],
                small_one[1],
                bias_rows[0],
                bias_rows[1],
                small_two[3],
                small_two[1],
                small_two[2],
            ]
        )
    input_grad = whole_rows(input_grads[0], input_grads[1])

    def own_layer(sums):
        mine, other = by_layer(sums[0], sums[1])
        return jnp.stack(by_layer(mine, swap(other)), 1)

    attn_total = own_layer(attn_sums).astype(jnp.float32)
    attn_total = attn_total.reshape(part_rows, sections, 4, pair_cols)
    attn_total = jnp.moveaxis(attn_total, 2, 0).reshape(4, part_rows, head_cols)
    ff_total = own_layer(ff_sums).astype(jnp.float32)
    ff_total = ff_total.reshape(part_rows, sections, 2, ff_wide)[..., :half_ff]
    ff_total = jnp.moveaxis(ff_total, 2, 0).reshape(2, part_rows, ff_cols)

    small_all = jnp.stack([small_sums[0], small_sums[1]])
    small_all = small_all.reshape(small_all.shape[:2] + (-1, small.shape[1]))
    small_all = jnp.moveaxis(small_all, 2, 1).reshape((-1,) + small.shape)
    small_mine = lax.psum_scatter(small_all, EVERY, scatter_dimension=0, tiled=True)
    up_all = lax.psum(jnp.stack([up_sums[0], up_sums[1]])[:, :half_ff], "dp")
    up_mine, up_other = by_layer(up_all[0], up_all[1])
    up_total = jnp.stack(by_layer(up_mine, swap(up_other))).reshape(1, ff_cols)
    gains = norm_gains.shape[1]
    return (
        section_output[None],
        input_grad[None],
        attn_total[None, :3],
        attn_total[3].T[None],
        ff_total[0][None],
        ff_total[1].T[None],
        small_mine[:, :gains],
        small_mine[:, gains:],
        up_total,
    )


def solution(mesh):
    in_specs = (
        P(None, "dp", "tensor", None),
        P(None, "dp", "tensor", None),
        P(None, "dp"),
        P("section", None, "dp", "tensor"),
        P("section", "tensor", "dp"),
        P("section", "dp", "tensor"),
        P("section", "tensor", "dp"),
        P("section", None, ("dp", "tensor")),
        P("section", None, ("dp", "tensor")),
        P("section", "tensor"),
    )
    out_specs = (
        P("section", None, "dp", "tensor", None),
        P("section", None, "dp", "tensor", None),
        P("section", None, "dp", "tensor"),
        P("section", "tensor", "dp"),
        P("section", "dp", "tensor"),
        P("section", "tensor", "dp"),
        P("section", None, ("dp", "tensor")),
        P("section", None, ("dp", "tensor")),
        P("section", "tensor"),
    )
    return jax.shard_map(shards, mesh=mesh, in_specs=in_specs, out_specs=out_specs, check_vma=False)
```

time: 1320 us -> 865 us (0.66)
  Pallas kernels: 0 us -> 399 us
  waiting for transfers between devices: 672 us -> 326 us
  matrix products: 220 us -> 0 us
  other arithmetic: 122 us -> 14.5 us
  blocking collectives: 158 us -> 56.8 us
  local copies, waits for them, and re-layouts: 106 us -> 35.8 us
    pallas_call x0 -> x8, Pallas kernels: none -> 399 us  [the longest x2 116 us: attn_backward(): pl.pallas_call(attn_backward_kernel, out_shape=[shape_of((micro, half_row...]
    all_gather x15 -> x4, waiting for transfers between devices: 272 us -> 0.06 us  [the longest x2 0.04 us: shards(): ff_packed.append(lax.all_gather(ff_layers[layer], 'dp', axis=0, tiled=True))]
    unnamed x45 -> x10, waiting for transfers between devices: 333 us -> 108 us
    dot_general x57 -> x0, matrix products: 220 us -> none  [the longest x3 25.1 us: layer_backward(): jnp.einsum('nsd,fd->nsf', grad_full, down_part, preferred_element_type=jn...]
    reduce_scatter x2 -> x4, waiting for transfers between devices: 24.8 us -> 184 us  [the longest x2 115 us: shards(): lax.psum_scatter(ff_grad, 'dp', scatter_dimension=0, tiled=True)]
    unnamed x1 -> x0, blocking collectives: 62.4 us -> none
    reduce_sum x33 -> x0, other arithmetic: 46.9 us -> none  [the longest x6 12.1 us: layer_norm(): return centred * lax.rsqrt(spread + norm_eps) * gain_vec + shift_vec]
    unnamed x299 -> x42, local copies, waits for them, and re-layouts: 43.5 us -> 4.36 us
  transfers between devices with their start and end apart: 35 -> 16, of which waited for: 29 -> 8; matrix products, arithmetic and copies ran while one was open for 18% -> 3% of each run, Pallas kernels for 0% -> 17%
where the time goes in v1:
time: 865 us; the launch traced here: 859 us
  Pallas kernels  399 us (46%)
  waiting for transfers between devices  326 us (38%)
  blocking collectives  56.8 us (7%)
  local copies, waits for them, and re-layouts  35.8 us (4%)
  between operations  14.9 us (2%)
  other arithmetic  14.5 us (2%)
  starting transfers between devices  11.6 us (1%)
    pallas_call x2, Pallas kernels, attn_backward(): pl.pallas_call(attn_backward_kernel, out_shape=[shape_of((micro, half_row...  116 us
    reduce_scatter x2, waiting for transfers between devices, shards(): lax.psum_scatter(ff_grad, 'dp', scatter_dimension=0, tiled=True)  115 us
    unnamed x10, waiting for transfers between devices  108 us
    pallas_call x2, Pallas kernels, attn_forward(): pl.pallas_call(attn_forward_kernel, out_shape=[shape_of((micro, half_rows...  106 us
    pallas_call x2, Pallas kernels, ffn_backward(): pl.pallas_call(ffn_backward_kernel, out_shape=[shape_of((micro, half_rows...  92.7 us
    pallas_call x2, Pallas kernels, ffn_forward(): pl.pallas_call(ffn_forward_kernel, out_shape=[shape_of((micro, half_rows,...  85.4 us
    reduce_scatter x2, waiting for transfers between devices, shards(): lax.psum_scatter(attn_grad, 'dp', scatter_dimension=0, tiled=True)  68.1 us
    all_gather x1, blocking collectives, shards(): vectors = lax.all_gather(small, EVERY, axis=0, tiled=False)  43.7 us
  transfers between devices with their start and end apart: 16, of which 8 were waited for; matrix products, arithmetic and copies ran while one was open for 3% of the time, Pallas kernels for 17%

profile of v1, /device:TPU:0, one launch (start us, length us, event | category | flops | bytes accessed | tf_op | source)
XLA Modules:
  0.0 858.6 jit_solution(11173330977215140703)
XLA Ops:
  7.2 1.4 copy.48
  10.9 3.0 collective-permute-start
  15.6 7.1 collective-permute-done
  23.7 1.6 fusion.3
  25.3 1.5 copy.52
  27.9 1.8 collective-permute-start.1
  29.7 15.9 %collective-permute-done.1 = bf16[288,1280]{1,0:T(8,128)(2,1)S(1)} collective-permute-done((bf16[288,1280]{1,0:T(8,128)(2,1)S(1)}, bf16[288,1280]{1,0:T(8,128)(2,1)S(1)}, u32[]{:S(2)}, u32[]{:S(2)}) %collective-permute-start.1) | collective-permute-done | bytes 737312 | tf_op jit(solution)/shard_map/ppermute | solution.py:875
  48.3 43.7 %all-gather = f32[256,72]{1,0:T(8,128)S(1)} all-gather(f32[8,72]{1,0:T(8,128)S(1)} %pad_maximum_fusion.7), channel_id=2, replica_groups=mesh['section'=2,'dp'=4,'tensor'=4] {'section','dp','tensor'}, dimensions={0}, use_global_device_ids=true | all-gather | bytes 76032 | tf_op jit(solution)/shard_map/all_gather | solution.py:893
  93.6 4.4 all-gather.1
  102.3 52.5 %attn_forward.2 = (f32[2,96,1152]{2,1,0:T(8,128)}, f32[2,2,768]{2,1,0:T(2,128)}, bf16[2,768,1152]{2,1,0:T(8,128)(2,1)}, bf16[2,768,768]{2,1,0:T(8,128)(2,1)}, bf16[2,768,256]{2,1,0:T(8,128)(2,1)}) custom-call(bf16[2,96,1152]{2,1,0:T(8,128)(2,1)} %pad_dynamic-slice_fusion.1.rows_ref, f32[8,1152]{1,0:T(8,128)} %squeeze.76.vec, ...), custom_call_target="tpu_custom_call" | custom-call | tf_op jit(solution)/shard_map/attn_forward/pallas_call | solution.py:720
  154.8 42.8 %ffn_forward.2 = (bf16[2,96,1152]{2,1,0:T(8,128)(2,1)}, bf16[2,768,1152]{2,1,0:T(8,128)(2,1)}, f32[2,768,640]{2,1,0:T(8,128)}) custom-call(f32[2,96,1152]{2,1,0:T(8,128)} %get-tuple-element.41.hidden_ref, f32[8,1152]{1,0:T(8,128)} %squeeze.76.vec, f32[1,640]{1,0:T(1,128)} %get-tuple-element.131.up_bias, ...), custom_call_target="tpu_custom_call" | custom-call | tf_op jit(solution)/shard_map/ffn_forward/pallas_call | solution.py:751
  197.7 53.0 %attn_forward.3 = (f32[2,96,1152]{2,1,0:T(8,128)}, f32[2,2,768]{2,1,0:T(2,128)}, bf16[2,768,1152]{2,1,0:T(8,128)(2,1)}, bf16[2,768,768]{2,1,0:T(8,128)(2,1)}, bf16[2,768,256]{2,1,0:T(8,128)(2,1)}) custom-call(bf16[2,96,1152]{2,1,0:T(8,128)(2,1)} %get-tuple-element.42.rows_ref, f32[8,1152]{1,0:T(8,128)} %squeeze.86.vec, f32[1,768]{1,0:T(1,128)} %broadcast_in_dim.38.bias, ...), custom_call_target="tpu_custom_call" | custom-call | tf_op jit(solution)/shard_map/attn_forward/pallas_call | solution.py:720
  250.7 42.6 %ffn_forward.3 = (bf16[2,96,1152]{2,1,0:T(8,128)(2,1)}, bf16[2,768,1152]{2,1,0:T(8,128)(2,1)}, f32[2,768,640]{2,1,0:T(8,128)}) custom-call(f32[2,96,1152]{2,1,0:T(8,128)} %get-tuple-element.43.hidden_ref, f32[8,1152]{1,0:T(8,128)} %squeeze.86.vec, f32[1,640]{1,0:T(1,128)} %get-tuple-element.130.up_bias, ...), custom_call_target="tpu_custom_call" | custom-call | tf_op jit(solution)/shard_map/ffn_forward/pallas_call | solution.py:751
  293.3 46.3 %ffn_backward.2 = (f32[2,96,1152]{2,1,0:T(8,128)}, bf16[1152,1280]{1,0:T(8,128)(2,1)}, f32[8,1152]{1,0:T(8,128)}, f32[8,640]{1,0:T(8,128)}) custom-call(bf16[2,96,1152]{2,1,0:T(8,128)(2,1)} %pad_dynamic-slice_fusion.grad_ref, f32[2,96,1152]{2,1,0:T(8,128)} %get-tuple-element.43.hidden_ref, f32[8,1152]{1,0:T(8,128)} %squeeze.86.vec, ...), custom_call_target="tpu_custom_call" | custom-call | tf_op jit(solution)/shard_map/ffn_backward/pallas_call | solution.py:779
  340.8 57.8 %attn_backward.2 = (bf16[2,96,1152]{2,1,0:T(8,128)(2,1)}, bf16[1152,576]{1,0:T(8,128)(2,1)}, f32[8,1152]{1,0:T(8,128)}, f32[8,256]{1,0:T(8,128)}) custom-call(f32[2,96,1152]{2,1,0:T(8,128)} %get-tuple-element.47.grad_ref, bf16[2,96,1152]{2,1,0:T(8,128)(2,1)} %get-tuple-element.42.rows_ref, f32[8,1152]{1,0:T(8,128)} %squeeze.86.vec, ...), custom_call_target="tpu_custom_call" | custom-call | tf_op jit(solution)/shard_map/attn_backward/pallas_call | solution.py:812
  398.6 46.4 %ffn_backward.3 = (f32[2,96,1152]{2,1,0:T(8,128)}, bf16[1152,1280]{1,0:T(8,128)(2,1)}, f32[8,1152]{1,0:T(8,128)}, f32[8,640]{1,0:T(8,128)}) custom-call(bf16[2,96,1152]{2,1,0:T(8,128)(2,1)} %get-tuple-element.52.grad_ref, f32[2,96,1152]{2,1,0:T(8,128)} %get-tuple-element.41.hidden_ref, f32[8,1152]{1,0:T(8,128)} %squeeze.76.vec, ...), custom_call_target="tpu_custom_call" | custom-call | tf_op jit(solution)/shard_map/ffn_backward/pallas_call | solution.py:779
  446.6 57.8 %attn_backward.3 = (bf16[2,96,1152]{2,1,0:T(8,128)(2,1)}, bf16[1152,576]{1,0:T(8,128)(2,1)}, f32[8,1152]{1,0:T(8,128)}, f32[8,256]{1,0:T(8,128)}) custom-call(f32[2,96,1152]{2,1,0:T(8,128)} %get-tuple-element.55.grad_ref, bf16[2,96,1152]{2,1,0:T(8,128)(2,1)} %pad_dynamic-slice_fusion.1.rows_ref, f32[8,1152]{1,0:T(8,128)} %squeeze.76.vec, ...), custom_call_target="tpu_custom_call" | custom-call | tf_op jit(solution)/shard_map/attn_backward/pallas_call | solution.py:812
  513.9 8.8 %psum.7 = f32[2,538]{1,0:T(2,128)S(1)} all-reduce(f32[2,538]{1,0:T(2,128)S(1)} %pad_maximum_fusion.5), channel_id=1, replica_groups=mesh['section'=2,'dp'=4,'tensor'=4] {'dp'}, use_global_device_ids=true, to_apply=%region_5.6 | all-reduce | flops 1076 | bytes 8608 | tf_op jit(solution)/shard_map/psum | solution.py:987
  522.7 1.4 collective-permute-start.6
  527.8 104.1 %all-reduce.8.cloned.1.call-done = f32[32,8,72]{2,1,0:T(8,128)} async-done(((f32[32,8,72]{2,1,0:T(8,128)}), f32[32,8,72]{2,1,0:T(8,128)}) %all-reduce.8.cloned.1.call-update) | async-done | bytes 73744
  634.0 33.1 %reduce-scatter.5.cloned.1.call-done = bf16[288,576]{1,0:T(8,128)(2,1)} async-done(((bf16[1152,576]{1,0:T(8,128)(2,1)}), bf16[288,576]{1,0:T(8,128)(2,1)}) %reduce-scatter.5.cloned.1.call-update) | async-done | bytes 331792 | tf_op jit(solution)/shard_map/reduce_scatter | solution.py:952
  667.1 35.0 %reduce-scatter.7.cloned.1.call-done = bf16[288,576]{1,0:T(8,128)(2,1)} async-done(((bf16[1152,576]{1,0:T(8,128)(2,1)}), bf16[288,576]{1,0:T(8,128)(2,1)}) %reduce-scatter.7.cloned.1.call-update) | async-done | bytes 331792 | tf_op jit(solution)/shard_map/reduce_scatter | solution.py:952
  703.2 1.5 collective-permute-start.4
  704.7 55.9 %reduce-scatter.9.cloned.1.call-done = bf16[288,1280]{1,0:T(8,128)(2,1)} async-done(((bf16[1152,1280]{1,0:T(8,128)(2,1)}), bf16[288,1280]{1,0:T(8,128)(2,1)}) %reduce-scatter.9.cloned.1.call-update) | async-done | bytes 737296 | tf_op jit(solution)/shard_map/reduce_scatter | solution.py:943
  760.6 59.5 %reduce-scatter.11.cloned.1.call-done = bf16[288,1280]{1,0:T(8,128)(2,1)} async-done(((bf16[1152,1280]{1,0:T(8,128)(2,1)}), bf16[288,1280]{1,0:T(8,128)(2,1)}) %reduce-scatter.11.cloned.1.call-update) | async-done | bytes 737296 | tf_op jit(solution)/shard_map/reduce_scatter | solution.py:943
  820.1 2.1 broadcast_select_fusion.2
  822.1 1.5 collective-permute-start.5
  827.3 1.6 copy.61
  828.9 11.4 %collective-permute-done.5 = bf16[288,1280]{1,0:T(8,128)(2,1)} collective-permute-done((bf16[288,1280]{1,0:T(8,128)(2,1)}, bf16[288,1280]{1,0:T(8,128)(2,1)}, u32[]{:S(2)}, u32[]{:S(2)}) %collective-permute-start.5) | collective-permute-done | bytes 737312 | tf_op jit(solution)/shard_map/ppermute | solution.py:875
  843.1 2.3 fusion.22
  846.6 2.0 squeeze.91
  849.7 2.0 slice.173
  (162 shorter events, 42.3 us)
Async XLA Ops:
  7.2 95.1 %all-gather.7.cloned.1.call-start = ((), (), s32[]{:S(2)}) async-start(), calls=%async_computation.4 | async-start | bytes 1843200 | tf_op jit(solution)/shard_map/all_gather | solution.py:889
  9.9 4.3 copy-start.10
  10.0 4.9 copy-start.11
  10.9 11.8 %collective-permute-start = (bf16[288,576]{1,0:T(8,128)(2,1)}, bf16[288,576]{1,0:T(8,128)(2,1)S(1)}, u32[]{:S(2)}, u32[]{:S(2)}) collective-permute-start(bf16[288,576]{1,0:T(8,128)(2,1)} %bitcast.16), channel_id=1, source_target_pairs={{0,16},{16,0},{1,17},{17,1},{2,18},{18,2},{3,19},{19,3},{4,20},{20... | collective-permute-start | bytes 995336 | tf_op jit(solution)/shard_map/ppermute | solution.py:875
  23.7 131.1 %all-gather.9.cloned.1.call-start = ((), (), s32[]{:S(2)}) async-start(), calls=%async_computation.5 | async-start | bytes 3686400 | tf_op jit(solution)/shard_map/all_gather | solution.py:890
  27.9 20.4 %copy-start.15 = (f32[1,6,72]{2,0,1:T(1,128)S(1)}, f32[1,6,72]{2,0,1:T(1,128)}, u32[]{:S(2)}) copy-start(f32[1,6,72]{2,0,1:T(1,128)} %param.18) | copy-start | bytes 5188
  27.9 20.4 %copy-start.16 = (f32[1,2,72]{2,1,0:T(2,128)S(1)}, f32[1,2,72]{2,1,0:T(2,128)}, u32[]{:S(2)}) copy-start(f32[1,2,72]{2,1,0:T(2,128)} %param.17) | copy-start | bytes 1732
  27.9 17.7 %collective-permute-start.1 = (bf16[288,1280]{1,0:T(8,128)(2,1)S(1)}, bf16[288,1280]{1,0:T(8,128)(2,1)S(1)}, u32[]{:S(2)}, u32[]{:S(2)}) collective-permute-start(bf16[288,1280]{1,0:T(8,128)(2,1)S(1)} %dynamic-slice_bitcast_fusion), channel_id=1, source_target_pairs={{0,16},{16,0},{1,17},{17,1},{2,18},{18,2},{3,19},{19,3},{4,20},{20... | collective-permute-start | bytes 2211848 | tf_op jit(solution)/shard_map/ppermute | solution.py:875
  46.8 46.8 %copy-start.14 = (f32[1,1076]{1,0:T(1,128)S(1)}, f32[1,1076]{1,0:T(1,128)}, u32[]{:S(2)}) copy-start(f32[1,1076]{1,0:T(1,128)} %param.19) | copy-start | bytes 12916
  46.8 53.1 %copy-start.17 = (s32[2,1]{0,1:T(1,128)S(1)}, s32[2,1]{0,1:T(1,128)}, u32[]{:S(2)}) copy-start(s32[2,1]{0,1:T(1,128)} %param.12) | copy-start | bytes 28
  46.8 53.8 %copy-start.8 = (bf16[2,1,184,1152]{3,2,1,0:T(8,128)(2,1)S(1)}, bf16[2,1,184,1152]{3,2,1,0:T(8,128)(2,1)}, u32[]{:S(2)}) copy-start(bf16[2,1,184,1152]{3,2,1,0:T(8,128)(2,1)} %param.10) | copy-start | bytes 2543620
  46.9 150.8 %all-gather.11.cloned.1.call-start = ((), (), s32[]{:S(2)}) async-start(), calls=%async_computation.6 | async-start | bytes 1843200 | tf_op jit(solution)/shard_map/all_gather | solution.py:889
  47.6 53.8 %copy-start.9 = (bf16[2,1,184,1152]{3,2,1,0:T(8,128)(2,1)S(1)}, bf16[2,1,184,1152]{3,2,1,0:T(8,128)(2,1)}, u32[]{:S(2)}) copy-start(bf16[2,1,184,1152]{3,2,1,0:T(8,128)(2,1)} %param.11) | copy-start | bytes 2543620
  47.6 203.1 %all-gather.13.cloned.1.call-start = ((), (), s32[]{:S(2)}) async-start(), calls=%async_computation.7 | async-start | bytes 3686400 | tf_op jit(solution)/shard_map/all_gather | solution.py:890
  48.2 583.7 %all-reduce.8.cloned.1.call-start = ((), (), s32[]{:S(2)}) async-start(), calls=%async_computation.12 | async-start | bytes 262144
  293.3 46.3 %copy-start.12 = (f32[2,768]{1,0:T(2,128)S(1)}, f32[2,768]{1,0:T(2,128)}, u32[]{:S(2)}) copy-start(f32[2,768]{1,0:T(2,128)} %and_select_fusion.mask) | copy-start | bytes 18436
  398.5 48.0 %copy-start.13 = (f32[8,1152]{1,0:T(8,128)S(1)}, f32[8,1152]{1,0:T(8,128)}, u32[]{:S(2)}) copy-start(f32[8,1152]{1,0:T(8,128)} %get-tuple-element.69) | copy-start | bytes 110596
  509.6 157.4 %reduce-scatter.5.cloned.1.call-start = ((), (), s32[]{:S(2)}) async-start(), calls=%async_computation.8 | async-start | bytes 1843200 | tf_op jit(solution)/shard_map/reduce_scatter | solution.py:952
  510.2 191.9 %reduce-scatter.7.cloned.1.call-start = ((), (), s32[]{:S(2)}) async-start(), calls=%async_computation.9 | async-start | bytes 1843200 | tf_op jit(solution)/shard_map/reduce_scatter | solution.py:952
  511.0 249.6 %reduce-scatter.9.cloned.1.call-start = ((), (), s32[]{:S(2)}) async-start(), calls=%async_computation.10 | async-start | bytes 3686400 | tf_op jit(solution)/shard_map/reduce_scatter | solution.py:943
  511.7 12.4 %copy-start.1 = (bf16[2,96,1152]{2,1,0:T(8,128)(2,1)S(1)}, bf16[2,96,1152]{2,1,0:T(8,128)(2,1)}, u32[]{:S(2)}) copy-start(bf16[2,96,1152]{2,1,0:T(8,128)(2,1)} %get-tuple-element.52.grad_ref) | copy-start | bytes 1327108
  511.7 12.4 %copy-start.5 = (bf16[2,96,1152]{2,1,0:T(8,128)(2,1)S(1)}, bf16[2,96,1152]{2,1,0:T(8,128)(2,1)}, u32[]{:S(2)}) copy-start(bf16[2,96,1152]{2,1,0:T(8,128)(2,1)} %get-tuple-element.60) | copy-start | bytes 1327108
  511.7 308.3 %reduce-scatter.11.cloned.1.call-start = ((), (), s32[]{:S(2)}) async-start(), calls=%async_computation.11 | async-start | bytes 3686400 | tf_op jit(solution)/shard_map/reduce_scatter | solution.py:943
  511.8 13.2 %copy-start = (bf16[2,96,1152]{2,1,0:T(8,128)(2,1)S(1)}, bf16[2,96,1152]{2,1,0:T(8,128)(2,1)}, u32[]{:S(2)}) copy-start(bf16[2,96,1152]{2,1,0:T(8,128)(2,1)} %get-tuple-element.42.rows_ref) | copy-start | bytes 1327108
  511.8 13.2 %copy-start.4 = (bf16[2,96,1152]{2,1,0:T(8,128)(2,1)S(1)}, bf16[2,96,1152]{2,1,0:T(8,128)(2,1)}, u32[]{:S(2)}) copy-start(bf16[2,96,1152]{2,1,0:T(8,128)(2,1)} %get-tuple-element.44) | copy-start | bytes 1327108
  522.7 4.3 collective-permute-start.6
  524.2 109.6 %collective-permute-start.3 = (bf16[2,96,1152]{2,1,0:T(8,128)(2,1)S(1)}, bf16[2,96,1152]{2,1,0:T(8,128)(2,1)S(1)}, u32[]{:S(2)}, u32[]{:S(2)}) collective-permute-start(bf16[2,96,1152]{2,1,0:T(8,128)(2,1)S(1)} %broadcast_select_fusion.6), channel_id=1, source_target_pairs={{0,16},{16,0},{1,17},{17,1},{2,18},{18,2},{3,19},{19,3},{4,20},{20... | collective-permute-start | bytes 1327112 | tf_op jit(solution)/shard_map/ppermute | solution.py:875
  525.8 108.1 %collective-permute-start.2 = (bf16[2,96,1152]{2,1,0:T(8,128)(2,1)}, bf16[2,96,1152]{2,1,0:T(8,128)(2,1)S(1)}, u32[]{:S(2)}, u32[]{:S(2)}) collective-permute-start(bf16[2,96,1152]{2,1,0:T(8,128)(2,1)} %broadcast_select_fusion.10), channel_id=1, source_target_pairs={{0,16},{16,0},{1,17},{17,1},{2,18},{18,2},{3,19},{19,3},{4,20},{20... | collective-permute-start | bytes 1327112 | tf_op jit(solution)/shard_map/ppermute | solution.py:875
  703.2 122.4 %collective-permute-start.4 = (bf16[288,576]{1,0:T(8,128)(2,1)S(1)}, bf16[288,576]{1,0:T(8,128)(2,1)S(1)}, u32[]{:S(2)}, u32[]{:S(2)}) collective-permute-start(bf16[288,576]{1,0:T(8,128)(2,1)S(1)} %broadcast_select_fusion.14), channel_id=1, source_target_pairs={{0,16},{16,0},{1,17},{17,1},{2,18},{18,2},{3,19},{19,3},{4,20},{20... | collective-permute-start | bytes 995336 | tf_op jit(solution)/shard_map/ppermute | solution.py:875
  822.1 18.1 %collective-permute-start.5 = (bf16[288,1280]{1,0:T(8,128)(2,1)}, bf16[288,1280]{1,0:T(8,128)(2,1)}, u32[]{:S(2)}, u32[]{:S(2)}) collective-permute-start(bf16[288,1280]{1,0:T(8,128)(2,1)} %broadcast_select_fusion.2), channel_id=1, source_target_pairs={{0,16},{16,0},{1,17},{17,1},{2,18},{18,2},{3,19},{19,3},{4,20},{20... | collective-permute-start | bytes 2211848 | tf_op jit(solution)/shard_map/ppermute | solution.py:875
  827.3 13.0 %copy-start.2 = (bf16[288,1280]{1,0:T(8,128)(2,1)S(1)}, bf16[288,1280]{1,0:T(8,128)(2,1)}, u32[]{:S(2)}) copy-start(bf16[288,1280]{1,0:T(8,128)(2,1)} %reduce-scatter.9.cloned.1.call-done) | copy-start | bytes 2211844
  827.3 13.0 %copy-start.3 = (bf16[288,1280]{1,0:T(8,128)(2,1)S(1)}, bf16[288,1280]{1,0:T(8,128)(2,1)}, u32[]{:S(2)}) copy-start(bf16[288,1280]{1,0:T(8,128)(2,1)} %reduce-scatter.11.cloned.1.call-done) | copy-start | bytes 2211844
  (2 other events, 3.9 us)
Sparse Core Ops, SparseCore 0:
  23.8 37.0 all-gather.6
  63.1 59.0 all-gather.8
  124.3 34.2 all-gather.10
  160.6 59.1 all-gather.12
  509.8 122.1 all-reduce.7
  634.1 32.9 reduce-scatter.4
  669.4 32.6 reduce-scatter.6
  704.4 56.1 reduce-scatter.8
  762.9 57.1 reduce-scatter.10

commit v2 on v1

v2 whole, which is shorter than its diff:
```python
import functools
import math

import jax
import jax.numpy as jnp
from jax import lax
from jax.experimental import pallas as pl
from jax.experimental.pallas import tpu as pltpu
from jax.sharding import PartitionSpec as P


HEAD = 72
LANES = 128
norm_eps = 1e-06
masked_score = -1000000000.0
score_scale = 1.0 / math.sqrt(HEAD)
GELU_A = math.sqrt(2.0 / math.pi)
GELU_B = 0.044715


def round_up(value, step):
    return -(-value // step) * step


def dot(left, right, left_dim, right_dim):
    return lax.dot_general(
        left, right, (((left_dim,), (right_dim,)), ((), ())), preferred_element_type=jnp.float32
    )


def low(value):
    return value.astype(jnp.bfloat16)


def layer_norm(rows, gain_vec, shift_vec):
    centred = rows - jnp.mean(rows, axis=-1, keepdims=True)
    spread = jnp.mean(centred * centred, axis=-1, keepdims=True)
    return centred * lax.rsqrt(spread + norm_eps) * gain_vec + shift_vec


def norm_back(rows, gain_vec, grads):
    centred = rows - jnp.mean(rows, axis=-1, keepdims=True)
    spread = jnp.mean(centred * centred, axis=-1, keepdims=True)
    inverse = lax.rsqrt(spread + norm_eps)
    xhat = centred * inverse
    e = grads * gain_vec
    back = inverse * (
        e
        - jnp.mean(e, axis=-1, keepdims=True)
        - xhat * jnp.mean(e * xhat, axis=-1, keepdims=True)
    )
    return back, grads * xhat


def gelu_tanh(value):
    return jax.nn.gelu(value, approximate=True)


MESH = pl.DeviceIdType.MESH
VMEM_BYTES = 64_000_000
COST = pl.CostEstimate(flops=20_000_000_000, transcendentals=0, bytes_accessed=100_000_000)
LOG2E = 1.0 / math.log(2.0)
TILE = 256


class Slab:
    def __init__(self, half_rows):
        self.half_rows = half_rows
        section = lax.axis_index("section")
        tensor = lax.axis_index("tensor")
        core = lax.rem(tensor, 2)
        self.core = core
        self.mine = self.around(section, tensor, core)
        self.theirs = self.around(section, tensor + 1 - 2 * core, 1 - core)
        self.mate = self.theirs[0]
        over = lax.rem(tensor + 2, 4)
        self.near, self.far = tensor, over
        self.mate_near, self.mate_far = self.mate[1], lax.rem(self.mate[1] + 2, 4)
        self.grid = self.places(section, self.near, self.far)
        self.mate_grid = self.places(section, self.mate_near, self.mate_far)
        self.across_y = self.grid[2]
        self.first, self.second = self.mine[1], self.mine[2]

    @staticmethod
    def places(section, near, far):
        flip = 1 - section
        return [(section, near), (flip, near), (section, far), (flip, far)]

    @staticmethod
    def around(section, tensor, core):
        over = lax.rem(tensor + 2, 4)
        turn = 1 - 2 * section
        first = (section + (1 - core) * turn, tensor + core * (over - tensor))
        second = (section + core * turn, tensor + (1 - core) * (over - tensor))
        return [(section, tensor), first, second, (1 - section, over)]

    def rows(self, ref, at):
        start = pl.multiple_of((2 * at[1] + at[0]) * self.half_rows, self.half_rows)
        return ref.at[pl.ds(start, self.half_rows)]

    def tile(self, tensor):
        size = 2 * self.half_rows
        return pl.ds(pl.multiple_of(tensor * size, size), size)

    def chip_tiles(self, far):
        return (self.mate_far, self.far) if far else (self.mate_near, self.near)

    def greet(self):
        barrier = pltpu.get_barrier_semaphore()
        for peer in (self.first, self.second, self.mate):
            pl.semaphore_signal(barrier, inc=1, device_id=named(peer), device_id_type=MESH)
        pl.semaphore_wait(barrier, 3)


def named(at):
    return {"section": at[0], "tensor": at[1]}


class Moves:
    def __init__(self, slab, send_sems, recv_sems):
        self.slab, self.send_sems, self.recv_sems = slab, send_sems, recv_sems
        self.sent = []

    def copy(self, src, dst, role, peer):
        return pltpu.make_async_remote_copy(
            src_ref=src,
            dst_ref=dst,
            send_sem=self.send_sems.at[role],
            recv_sem=self.recv_sems.at[role],
            device_id=named(peer),
            device_id_type=MESH,
        )

    def send(self, src, dst, role, peer):
        copy = self.copy(src, dst, role, peer)
        copy.start()
        self.sent.append(copy)

    def arrived(self, dst, role):
        self.copy(dst, dst, role, self.slab.mate).wait_recv()

    def drain(self):
        for copy in self.sent:
            copy.wait_send()


class Gather(Moves):
    def __init__(self, slab, whole, send_sems, recv_sems):
        super().__init__(slab, send_sems, recv_sems)
        self.whole = whole

    def pass_on(self, at, role, peer):
        part = self.slab.rows(self.whole, at)
        self.send(part, part, role, peer)

    def arrive(self, at, role):
        self.arrived(self.slab.rows(self.whole, at), role)

    def start(self):
        mine = self.slab.mine
        self.pass_on(mine[0], 0, mine[1])
        self.pass_on(mine[0], 3, self.slab.mate)

    def second(self):
        self.sent.pop(0).wait_send()
        self.pass_on(self.slab.mine[0], 1, self.slab.mine[2])

    def forward(self):
        mine, mate = self.slab.mine, self.slab.mate
        self.arrive(mine[1], 0)
        self.pass_on(mine[1], 2, mine[2])
        self.pass_on(mine[1], 4, mate)

    def to_mate(self):
        mine, mate = self.slab.mine, self.slab.mate
        self.arrive(mine[2], 1)
        self.pass_on(mine[2], 5, mate)
        self.arrive(mine[3], 2)
        self.pass_on(mine[3], 6, mate)

    def finish(self):
        for k in range(4):
            self.arrive(self.slab.theirs[k], 3 + k)
        self.drain()


class TileGather:
    def __init__(self, whole, send_sems, recv_sems):
        self.whole, self.send_sems, self.recv_sems = whole, send_sems, recv_sems
        self.tensor = lax.axis_index("tensor")
        self.over = lax.rem(self.tensor + 2, 4)
        self.mate = self.tensor + 1 - 2 * lax.rem(self.tensor, 2)
        self.micro, rows = whole.shape[0], whole.shape[1] // 4
        self.tile_rows = rows
        self.sent = []

    def tile(self, m, index):
        start = pl.multiple_of(index * self.tile_rows, self.tile_rows)
        return self.whole.at[m, pl.ds(start, self.tile_rows)]

    def copy(self, m, index, role, peer):
        part = self.tile(m, index)
        return remote(
            part, part, self.send_sems.at[m, role], self.recv_sems.at[m, role], {"tensor": peer}
        )

    def send(self, m, index, role, peer):
        copy = self.copy(m, index, role, peer)
        copy.start()
        self.sent.append(copy)

    def start(self):
        for m in range(self.micro):
            self.send(m, self.tensor, 0, self.over)
            self.send(m, self.tensor, 1, self.mate)

    def pass_on(self):
        for m in range(self.micro):
            self.copy(m, self.over, 0, self.over).wait_recv()
            self.send(m, self.over, 2, self.mate)

    def finish(self):
        for m in range(self.micro):
            self.copy(m, self.mate, 1, self.mate).wait_recv()
            self.copy(m, lax.rem(self.mate + 2, 4), 2, self.mate).wait_recv()

    def drain(self):
        for copy in self.sent:
            copy.wait_send()


class Scatter(Moves):
    def __init__(self, slab, terms, from_mate, outgoing, arrivals, send_sems, recv_sems):
        super().__init__(slab, send_sems, recv_sems)
        self.terms, self.from_mate, self.outgoing = terms, from_mate, outgoing
        self.relay, self.from_second, self.from_first = (arrivals.at[k] for k in range(3))

    def to_mate(self, at, role):
        self.send(self.slab.rows(self.terms, at), self.from_mate.at[role], role, self.slab.mate)

    def mate_far(self):
        self.to_mate(self.slab.mate_grid[3], 3)
        self.to_mate(self.slab.mate_grid[2], 1 + self.slab.core)

    def mate_near(self):
        self.to_mate(self.slab.mate_grid[1], 2 - self.slab.core)
        self.to_mate(self.slab.mate_grid[0], 0)

    def chip_sum(self, k, rows):
        part = self.slab.rows(self.terms, self.slab.mine[k])
        return part[rows].astype(jnp.float32) + self.from_mate[k, rows].astype(jnp.float32)

    def blocks(self):
        return [pl.ds(start, 32) for start in range(0, self.slab.half_rows, 32)]

    def hop(self, k, slot, dst, role, peer, ride=None):
        self.arrived(self.from_mate.at[k], k)
        if ride is not None:
            self.arrived(ride, 4)
        for rows in self.blocks():
            value = self.chip_sum(k, rows)
            if ride is not None:
                value = value + ride[rows].astype(jnp.float32)
            self.outgoing[slot, rows] = low(value)
        self.send(self.outgoing.at[slot], dst, role, peer)

    def far_hop(self):
        self.hop(3, 0, self.relay, 4, self.slab.second)

    def second_hop(self):
        self.hop(2, 1, self.from_second, 5, self.slab.second)

    def first_hop(self):
        self.hop(1, 2, self.from_first, 6, self.slab.first, self.relay)

    def finish(self):
        self.arrived(self.from_mate.at[0], 0)
        self.arrived(self.from_second, 5)
        self.arrived(self.from_first, 6)
        self.drain()

    def total(self, rows):
        other = self.from_second[rows].astype(jnp.float32) + self.from_first[rows].astype(
            jnp.float32
        )
        return self.chip_sum(0, rows) + other


def scatter_scratch(micro, seq, half_rows, width):
    return [
        pltpu.VMEM((micro, seq, width), jnp.bfloat16),
        pltpu.VMEM((micro, 4, half_rows, width), jnp.bfloat16),
        pltpu.VMEM((micro, 3, half_rows, width), jnp.bfloat16),
        pltpu.VMEM((micro, 3, half_rows, width), jnp.bfloat16),
        pltpu.SemaphoreType.DMA((micro, 7)),
        pltpu.SemaphoreType.DMA((micro, 7)),
    ]


def gather_scratch(micro, seq, width):
    return [
        pltpu.VMEM((micro, seq, width), jnp.bfloat16),
        pltpu.SemaphoreType.DMA((micro, 7)),
        pltpu.SemaphoreType.DMA((micro, 7)),
    ]


def make_scatters(slab, refs, micro):
    terms, from_mate, outgoing, arrivals, send_sems, recv_sems = refs
    return [
        Scatter(
            slab,
            terms.at[m],
            from_mate.at[m],
            outgoing.at[m],
            arrivals.at[m],
            send_sems.at[m],
            recv_sems.at[m],
        )
        for m in range(micro)
    ]


def make_gathers(slab, refs, micro):
    whole, send_sems, recv_sems = refs
    return [
        Gather(slab, whole.at[m], send_sems.at[m], recv_sems.at[m]) for m in range(micro)
    ]


def step_rows(i, size):
    return pl.ds(pl.multiple_of(i * size, size), size)


def repeat(count, body):
    def one(i, carry):
        body(i)
        return carry

    lax.fori_loop(0, count, one, 0)


def shut_keys(length, own_rows, full_rows, shape, dimension):
    place = lax.broadcasted_iota(jnp.int32, shape, dimension)
    step = jnp.zeros(shape, jnp.int32)
    for t in range(1, 4):
        step += (place >= t * full_rows).astype(jnp.int32)
    live = (place - step * full_rows < own_rows) & (
        place - step * (full_rows - own_rows) < length
    )
    return jnp.where(live, 0.0, masked_score)


def chip_rows(slab, far, compute):
    first, last = slab.chip_tiles(far)
    repeat(2, lambda i: compute(slab.tile(first + i * (last - first))))


def open_gathers(gathers, fill):
    fill(0)
    gathers[0].start()
    fill(1)
    gathers[0].second()
    gathers[1].start()
    gathers[0].forward()
    gathers[1].second()


def widen(packed, wide):
    heads = packed.shape[1] // HEAD

    def block(i):
        rows = step_rows(i, 128)
        for h in range(heads):
            piece = packed[rows, h * HEAD : (h + 1) * HEAD]
            blank = jnp.zeros((128, LANES - HEAD), jnp.bfloat16)
            wide[rows, h * LANES : (h + 1) * LANES] = jnp.concatenate([piece, blank], axis=1)

    repeat(packed.shape[0] // 128, block)


def split_tail(packed, tails, up_cols):
    start = packed.shape[1] - LANES

    def block(i):
        rows = step_rows(i, 128)
        for j in range(2):
            piece = packed[rows, start + j * up_cols : start + (j + 1) * up_cols]
            blank = jnp.zeros((128, LANES - up_cols), jnp.bfloat16)
            tails[rows, j * LANES : (j + 1) * LANES] = jnp.concatenate([piece, blank], axis=1)

    repeat(packed.shape[0] // 128, block)


def up_dot(rows, packed, tails):
    main = (packed.shape[1] - LANES) // 2
    first = dot(rows, packed[:, :main], 1, 0)
    return jnp.concatenate([first, dot(rows, tails[:, :LANES], 1, 0)], axis=1)


def up_back(grads, packed, tails):
    main = (packed.shape[1] - LANES) // 2
    return dot(grads[:, :main], packed[:, :main], 1, 1) + dot(
        grads[:, main:], tails[:, :LANES], 1, 1
    )


def down_dot(active, packed, tails):
    main = (packed.shape[1] - LANES) // 2
    return dot(active[:, :main], packed[:, main : 2 * main], 1, 1) + dot(
        active[:, main:], tails[:, LANES:], 1, 1
    )


def down_back(rows, packed, tails):
    main = (packed.shape[1] - LANES) // 2
    first = dot(rows, packed[:, main : 2 * main], 1, 0)
    return jnp.concatenate([first, dot(rows, tails[:, LANES:], 1, 0)], axis=1)


def attn_forward_kernel(
    ready, at, layer, own_rows, rows_ref, vectors, bias_ref, lengths, packed_hbm, given_hbm, grads_ref,
    hidden_ref, lse_ref, normed_hbm, qkv_hbm, mixed_hbm, *rest
):
    micro, half_rows, width = rows_ref.shape
    gathered, gather_refs = rest[0], rest[0:3]
    scatter_refs = rest[3:9]
    terms = rest[3]
    packed, wide, qkv, mixed, load_sem, keep_sems, given_sems, all_grads, tile_send, tile_recv = rest[9:]
    vec, bias = vectors.at[layer], bias_ref[layer]
    seq = qkv.shape[1]
    pair = mixed.shape[2]
    heads = pair // LANES
    load = pltpu.make_async_copy(
        packed_hbm.at[:, at : at + packed.shape[1]], packed, load_sem
    )
    load.start()
    slab = Slab(half_rows)
    gathers = make_gathers(slab, gather_refs, micro)
    scatters = make_scatters(slab, scatter_refs, micro)
    given = [
        pltpu.make_async_copy(given_hbm.at[m], gathered.at[m], given_sems.at[m])
        for m in range(micro if ready else 0)
    ]
    for copy in given:
        copy.start()
    slab.greet()
    if ready:
        tiles = TileGather(all_grads, tile_send, tile_recv)
        for m in range(micro):
            own = tiles.tile(m, tiles.tensor)
            count = grads_ref.shape[1]
            own[:count] = grads_ref[m]
            own[count:] = jnp.zeros((tiles.tile_rows - count, width), jnp.bfloat16)
        tiles.start()

    def fill(m):
        own = slab.rows(gathered.at[m], slab.mine[0])
        for start in range(0, half_rows, 32):
            block = rows_ref[m, pl.ds(start, 32)].astype(jnp.float32)
            own[pl.ds(start, 32)] = low(layer_norm(block, vec[0:1], vec[2:3]))

    if not ready:
        open_gathers(gathers, fill)
    load.wait()
    widen(packed, wide)
    keeps = []

    def keep(src, dst, i):
        copy = pltpu.make_async_copy(src, dst, keep_sems.at[i])
        copy.start()
        keeps.append(copy)

    def project(m):
        def block(i):
            rows = step_rows(i, TILE)
            out = dot(gathered[m, rows], wide[:, : 3 * pair], 1, 0)
            qkv[m, rows] = low(out + bias)

        repeat(seq // TILE, block)

    def attend(m, rows):
        shut = shut_keys(lengths[m], own_rows, 2 * half_rows, (1, seq), 1)
        for h in range(heads):
            cols = slice(h * LANES, (h + 1) * LANES)
            q = qkv[m, rows, cols]
            k = qkv[m, :, pair + h * LANES : pair + (h + 1) * LANES]
            v = qkv[m, :, 2 * pair + h * LANES : 2 * pair + (h + 1) * LANES]
            scores = dot(q, k, 1, 1) * (score_scale * LOG2E) + shut
            top = jnp.max(scores, axis=-1, keepdims=True)
            exp_scores = jnp.exp2(scores - top)
            total = jnp.sum(exp_scores, axis=-1, keepdims=True)
            probs = low(exp_scores * (1.0 / total))
            mixed[m, rows, cols] = low(dot(probs, v, 1, 0))
            lse_ref[m, h, rows] = jnp.broadcast_to(
                top + jnp.log(total) * LOG2E, (2 * half_rows, LANES)
            )
        terms[m, rows] = low(dot(mixed[m, rows], wide[:, 3 * pair :], 1, 1))

    def close(m):
        scatters[m].finish()
        for rows in scatters[m].blocks():
            start = rows_ref[m, rows].astype(jnp.float32)
            hidden_ref[m, rows] = start + scatters[m].total(rows) + vec[5:6]

    def gathered_rows(m):
        if ready:
            given[m].wait()
            return
        gathers[m].to_mate()
        gathers[m].finish()
        keep(gathered.at[m], normed_hbm.at[m], m)

    gathered_rows(0)
    project(0)
    if not ready:
        gathers[1].forward()
    chip_rows(slab, True, lambda rows: attend(0, rows))
    scatters[0].mate_far()
    gathered_rows(1)
    scatters[0].far_hop()
    chip_rows(slab, False, lambda rows: attend(0, rows))
    scatters[0].mate_near()
    keep(qkv.at[0], qkv_hbm.at[0], 2)
    keep(mixed.at[0], mixed_hbm.at[0], 3)
    project(1)
    scatters[0].second_hop()
    scatters[0].first_hop()
    if ready:
        tiles.pass_on()
    chip_rows(slab, True, lambda rows: attend(1, rows))
    scatters[1].mate_far()
    close(0)
    scatters[1].far_hop()
    if ready:
        tiles.finish()
        for m in range(micro):
            keep(all_grads.at[m], normed_hbm.at[m], m)
    chip_rows(slab, False, lambda rows: attend(1, rows))
    scatters[1].mate_near()
    keep(qkv.at[1], qkv_hbm.at[1], 4)
    keep(mixed.at[1], mixed_hbm.at[1], 5)
    scatters[1].second_hop()
    scatters[1].first_hop()
    close(1)
    if ready:
        tiles.drain()
    for copy in keeps:
        copy.wait()


def ffn_forward_kernel(
    half_ff, at, layer, hidden_ref, vectors, up_biases, packed_hbm, out_ref, second_hbm, upper_hbm, *rest
):
    micro, half_rows, _ = hidden_ref.shape
    gathered, gather_refs = rest[0], rest[0:3]
    scatter_refs = rest[3:9]
    terms = rest[3]
    packed, tails, upper, load_sem, keep_sems = rest[9:]
    vec, up_bias = vectors.at[layer], up_biases.at[layer]
    _, ff = upper.shape[1:]
    load = pltpu.make_async_copy(
        packed_hbm.at[:, at : at + packed.shape[1]], packed, load_sem
    )
    load.start()
    slab = Slab(half_rows)
    gathers = make_gathers(slab, gather_refs, micro)
    scatters = make_scatters(slab, scatter_refs, micro)
    slab.greet()

    def fill(m):
        own = slab.rows(gathered.at[m], slab.mine[0])
        for start in range(0, half_rows, 32):
            block = hidden_ref[m, pl.ds(start, 32)]
            own[pl.ds(start, 32)] = low(layer_norm(block, vec[1:2], vec[6:7]))

    open_gathers(gathers, fill)
    load.wait()
    split_tail(packed, tails, half_ff - ff + LANES)
    keeps = []

    def keep(src, dst, i):
        copy = pltpu.make_async_copy(src, dst, keep_sems.at[i])
        copy.start()
        keeps.append(copy)

    def compute(m, rows):
        value = up_dot(gathered[m, rows], packed, tails) + up_bias[...]
        upper[m, rows] = value
        active = low(gelu_tanh(value))
        terms[m, rows] = low(down_dot(active, packed, tails))

    def close(m):
        scatters[m].finish()
        for rows in scatters[m].blocks():
            out_ref[m, rows] = low(hidden_ref[m, rows] + scatters[m].total(rows) + vec[7:8])

    gathers[0].to_mate()
    gathers[0].finish()
    keep(gathered.at[0], second_hbm.at[0], 0)
    chip_rows(slab, True, lambda rows: compute(0, rows))
    scatters[0].mate_far()
    gathers[1].forward()
    scatters[0].far_hop()
    chip_rows(slab, False, lambda rows: compute(0, rows))
    scatters[0].mate_near()
    keep(upper.at[0], upper_hbm.at[0], 1)
    gathers[1].to_mate()
    scatters[0].second_hop()
    gathers[1].finish()
    keep(gathered.at[1], second_hbm.at[1], 2)
    chip_rows(slab, True, lambda rows: compute(1, rows))
    scatters[1].mate_far()
    scatters[0].first_hop()
    scatters[1].far_hop()
    chip_rows(slab, False, lambda rows: compute(1, rows))
    scatters[1].mate_near()
    keep(upper.at[1], upper_hbm.at[1], 3)
    scatters[1].second_hop()
    close(0)
    scatters[1].first_hop()
    close(1)
    for copy in keeps:
        copy.wait()


def ffn_backward_kernel(
    half_ff, at, layer, grad_ref, hidden_ref, vectors, second_hbm, upper_hbm, packed_hbm,
    out_ref, grads_ref, small_ref, up_bias_ref, *rest
):
    micro, half_rows, width = hidden_ref.shape
    gathered, gather_refs = rest[0], rest[0:3]
    scatter_refs = rest[3:9]
    terms = rest[3]
    packed, tails, second, upper, grad_upper, active, load_sems = rest[9:]
    vec = vectors.at[layer]
    seq, ff = upper.shape[1:]
    main = ff - LANES
    extra = half_ff - main
    load_packed = pltpu.make_async_copy(
        packed_hbm.at[:, at : at + packed.shape[1]], packed, load_sems.at[0]
    )
    load_packed.start()
    load_upper, load_second = [], []
    for m in range(micro):
        load_upper.append(
            pltpu.make_async_copy(upper_hbm.at[m], upper.at[m], load_sems.at[1 + m])
        )
        load_upper[m].start()
    for m in range(micro):
        load_second.append(
            pltpu.make_async_copy(second_hbm.at[m], second.at[m], load_sems.at[1 + micro + m])
        )
        load_second[m].start()
    slab = Slab(half_rows)
    gathers = make_gathers(slab, gather_refs, micro)
    scatters = make_scatters(slab, scatter_refs, micro)
    slab.greet()

    def fill(m):
        own = slab.rows(gathered.at[m], slab.mine[0])
        for start in range(0, half_rows, 32):
            own[pl.ds(start, 32)] = grad_ref[m, pl.ds(start, 32)]

    open_gathers(gathers, fill)
    small_ref[...] = jnp.zeros_like(small_ref)
    up_bias_ref[...] = jnp.zeros_like(up_bias_ref)
    load_packed.wait()
    split_tail(packed, tails, extra)

    def compute(m, rows):
        value = upper[m, rows]
        square = value * value
        bent = jnp.tanh(GELU_A * value * (1.0 + GELU_B * square))
        half = 0.5 * (1.0 + bent)
        active[m, rows] = low(value * half)
        slope = half + (0.5 * GELU_A) * value * (1.0 - bent * bent) * (1.0 + 3.0 * GELU_B * square)
        grad_active = down_back(gathered[m, rows], packed, tails)
        grad = low(grad_active * slope)
        grad_upper[m, rows] = grad
        up_bias_ref[0:1] += jnp.sum(grad.astype(jnp.float32), axis=0, keepdims=True)
        terms[m, rows] = low(up_back(grad, packed, tails))

    def stacked(ref, cols=slice(None)):
        return ref[:, :, cols].reshape(micro * seq, -1)

    def weight_grads(first, last):
        def block(i):
            cols = step_rows(i, LANES)
            up = dot(stacked(second, cols), stacked(grad_upper), 0, 0)
            down = dot(stacked(gathered, cols), stacked(active), 0, 0)
            grads_ref[cols, :main] = low(up[:, :main])
            grads_ref[cols, main : 2 * main] = low(down[:, :main])
            blank = jnp.zeros((LANES, LANES - 2 * extra), jnp.float32)
            rest_cols = [up[:, main : main + extra], down[:, main : main + extra], blank]
            grads_ref[cols, 2 * main :] = low(jnp.concatenate(rest_cols, axis=1))

        repeat(last - first, lambda i: block(first + i))

    def close(m):
        scatters[m].finish()
        for rows in scatters[m].blocks():
            grad_normed = scatters[m].total(rows)
            back, gain_terms = norm_back(hidden_ref[m, rows], vec[1:2], grad_normed)
            grad_rows = grad_ref[m, rows].astype(jnp.float32)
            grad_hidden = grad_rows + back
            out_ref[m, rows] = grad_hidden
            branch = low(grad_hidden).astype(jnp.float32)
            for j, item in enumerate((gain_terms, grad_normed, grad_rows, branch)):
                small_ref[j : j + 1] += jnp.sum(item, axis=0, keepdims=True)

    gathers[0].to_mate()
    gathers[0].finish()
    load_upper[0].wait()
    chip_rows(slab, True, lambda rows: compute(0, rows))
    scatters[0].mate_far()
    gathers[1].forward()
    scatters[0].far_hop()
    chip_rows(slab, False, lambda rows: compute(0, rows))
    scatters[0].mate_near()
    gathers[1].to_mate()
    scatters[0].second_hop()
    gathers[1].finish()
    load_upper[1].wait()
    chip_rows(slab, True, lambda rows: compute(1, rows))
    scatters[1].mate_far()
    scatters[0].first_hop()
    scatters[1].far_hop()
    chip_rows(slab, False, lambda rows: compute(1, rows))
    scatters[1].mate_near()
    scatters[1].second_hop()
    for load in load_second:
        load.wait()
    blocks = width // LANES
    weight_grads(0, blocks // 3)
    scatters[1].first_hop()
    close(0)
    weight_grads(blocks // 3, blocks)
    close(1)


def ffn_turn_kernel(
    half_ff, at, layer, hidden_ref, grad_ref, vectors, up_biases, given_hbm, packed_hbm,
    out_ref, grad_out_ref, grads_ref, small_ref, up_bias_ref, *rest
):
    micro, half_rows, width = hidden_ref.shape
    gathered, gather_refs = rest[0], rest[0:3]
    terms, back_terms = rest[3], rest[9]
    packed, tails, given, grad_upper, active, load_sem, given_sems = rest[15:]
    vec, up_bias = vectors.at[layer], up_biases.at[layer]
    seq, ff = active.shape[1:]
    main = ff - LANES
    extra = half_ff - main
    load = pltpu.make_async_copy(
        packed_hbm.at[:, at : at + packed.shape[1]], packed, load_sem
    )
    load.start()
    loads = [
        pltpu.make_async_copy(given_hbm.at[m], given.at[m], given_sems.at[m]) for m in range(micro)
    ]
    for copy in loads:
        copy.start()
    slab = Slab(half_rows)
    gathers = make_gathers(slab, gather_refs, micro)
    scatters = make_scatters(slab, rest[3:9], micro)
    backs = make_scatters(slab, rest[9:15], micro)
    slab.greet()

    def fill(m):
        own = slab.rows(gathered.at[m], slab.mine[0])
        for start in range(0, half_rows, 32):
            block = hidden_ref[m, pl.ds(start, 32)]
            own[pl.ds(start, 32)] = low(layer_norm(block, vec[1:2], vec[6:7]))

    open_gathers(gathers, fill)
    small_ref[...] = jnp.zeros_like(small_ref)
    up_bias_ref[...] = jnp.zeros_like(up_bias_ref)
    load.wait()
    split_tail(packed, tails, extra)

    def compute(m, rows):
        value = up_dot(gathered[m, rows], packed, tails) + up_bias[...]
        square = value * value
        bent = jnp.tanh(GELU_A * value * (1.0 + GELU_B * square))
        half = 0.5 * (1.0 + bent)
        shown = low(value * half)
        active[m, rows] = shown
        slope = half + (0.5 * GELU_A) * value * (1.0 - bent * bent) * (1.0 + 3.0 * GELU_B * square)
        grad = low(down_back(given[m, rows], packed, tails) * slope)
        grad_upper[m, rows] = grad
        up_bias_ref[0:1] += jnp.sum(grad.astype(jnp.float32), axis=0, keepdims=True)
        back_terms[m, rows] = low(up_back(grad, packed, tails))
        terms[m, rows] = low(down_dot(shown, packed, tails))

    def stacked(ref, cols=slice(None)):
        return ref[:, :, cols].reshape(micro * seq, -1)

    def weight_grads(first, last):
        def block(i):
            cols = step_rows(i, LANES)
            up = dot(stacked(gathered, cols), stacked(grad_upper), 0, 0)
            down = dot(stacked(given, cols), stacked(active), 0, 0)
            grads_ref[cols, :main] = low(up[:, :main])
            grads_ref[cols, main : 2 * main] = low(down[:, :main])
            blank = jnp.zeros((LANES, LANES - 2 * extra), jnp.float32)
            rest_cols = [up[:, main : main + extra], down[:, main : main + extra], blank]
            grads_ref[cols, 2 * main :] = low(jnp.concatenate(rest_cols, axis=1))

        repeat(last - first, lambda i: block(first + i))

    def close_back(m):
        backs[m].finish()
        for rows in backs[m].blocks():
            grad_normed = backs[m].total(rows)
            back, gain_terms = norm_back(hidden_ref[m, rows], vec[1:2], grad_normed)
            grad_rows = grad_ref[m, rows].astype(jnp.float32)
            grad_hidden = grad_rows + back
            grad_out_ref[m, rows] = grad_hidden
            branch = low(grad_hidden).astype(jnp.float32)
            for j, item in enumerate((gain_terms, grad_normed, grad_rows, branch)):
                small_ref[j : j + 1] += jnp.sum(item, axis=0, keepdims=True)

    def close(m):
        scatters[m].finish()
        for rows in scatters[m].blocks():
            out_ref[m, rows] = low(hidden_ref[m, rows] + scatters[m].total(rows) + vec[7:8])

    gathers[0].to_mate()
    gathers[0].finish()
    loads[0].wait()
    chip_rows(slab, True, lambda rows: compute(0, rows))
    backs[0].mate_far()
    scatters[0].mate_far()
    gathers[1].forward()
    backs[0].far_hop()
    chip_rows(slab, False, lambda rows: compute(0, rows))
    backs[0].mate_near()
    scatters[0].mate_near()
    gathers[1].to_mate()
    backs[0].second_hop()
    gathers[1].finish()
    loads[1].wait()
    chip_rows(slab, True, lambda rows: compute(1, rows))
    backs[1].mate_far()
    scatters[1].mate_far()
    backs[0].first_hop()
    backs[1].far_hop()
    chip_rows(slab, False, lambda rows: compute(1, rows))
    backs[1].mate_near()
    scatters[1].mate_near()
    backs[1].second_hop()
    for scatter in scatters:
        scatter.far_hop()
        scatter.second_hop()
    blocks = width // LANES
    weight_grads(0, blocks // 3)
    backs[1].first_hop()
    for scatter in scatters:
        scatter.first_hop()
    close_back(0)
    weight_grads(blocks // 3, blocks)
    close_back(1)
    for m in range(micro):
        close(m)


def attn_backward_kernel(
    at, layer, own_rows, grad_ref, rows_ref, vectors, lse, lengths, normed_hbm, qkv_hbm, mixed_hbm, packed_hbm,
    out_ref, grads_ref, small_ref, bias_ref, *rest
):
    micro, half_rows, width = grad_ref.shape
    gathered, gather_refs = rest[0], rest[0:3]
    scatter_refs = rest[3:9]
    terms = rest[3]
    packed, wide, normed, qkv, mixed, grad_mixed, grad_qkv, turned, shut = rest[9:18]
    low_probs, grad_scores, load_sems = rest[18:]
    vec = vectors.at[layer]
    seq, pair = mixed.shape[1:]
    heads = pair // LANES
    load_packed = pltpu.make_async_copy(
        packed_hbm.at[:, at : at + packed.shape[1]], packed, load_sems.at[0]
    )
    load_packed.start()
    load_qkv, load_rest = [], []
    for m in range(micro):
        load_qkv.append(pltpu.make_async_copy(qkv_hbm.at[m], qkv.at[m], load_sems.at[1 + 3 * m]))
        load_qkv[m].start()
    for m in range(micro):
        for k, (src, dst) in enumerate(((mixed_hbm, mixed), (normed_hbm, normed))):
            load = pltpu.make_async_copy(src.at[m], dst.at[m], load_sems.at[2 + k + 3 * m])
            load.start()
            load_rest.append(load)
    slab = Slab(half_rows)
    gathers = make_gathers(slab, gather_refs, micro)
    scatters = make_scatters(slab, scatter_refs, micro)
    slab.greet()

    def fill(m):
        own = slab.rows(gathered.at[m], slab.mine[0])
        for start in range(0, half_rows, 32):
            own[pl.ds(start, 32)] = low(grad_ref[m, pl.ds(start, 32)])

    open_gathers(gathers, fill)
    small_ref[...] = jnp.zeros_like(small_ref)
    bias_ref[...] = jnp.zeros_like(bias_ref)
    load_packed.wait()
    widen(packed, wide)

    def head(h, part=0):
        return slice(part * pair + h * LANES, part * pair + (h + 1) * LANES)

    for m in range(micro):
        load_qkv[m].wait()
        shut[m] = shut_keys(lengths[m], own_rows, 2 * half_rows, (seq, LANES), 0)
        for h in range(heads):
            turned[m, h] = low(qkv[m, :, head(h, 1)].astype(jnp.float32).T)

    def mix_grads(m):
        def block(i):
            rows = step_rows(i, TILE)
            grad_mixed[m, rows] = low(dot(gathered[m, rows], wide[:, 3 * pair :], 1, 0))

        repeat(seq // TILE, block)

    def attend(m, h):
        def block(i):
            rows = step_rows(i, LANES)
            queries = qkv[m, rows, head(h)]
            grads = grad_mixed[m, rows, head(h)]
            scores = dot(qkv[m, :, head(h, 1)], queries, 1, 1) * (score_scale * LOG2E) + shut[m]
            probs = jnp.exp2(scores - lse[m, h, rows].T[0:1])
            grad_probs = dot(qkv[m, :, head(h, 2)], grads, 1, 1)
            inner = jnp.sum(grad_probs * probs, axis=0, keepdims=True)
            low_probs[:, rows] = low(probs)
            grad_scores[:, rows] = low(probs * (grad_probs - inner))

        repeat(seq // LANES, block)
        grad_keys = dot(grad_scores[...], qkv[m, :, head(h)], 1, 0)
        grad_qkv[m, :, head(h, 1)] = low(grad_keys * score_scale)
        grad_qkv[m, :, head(h, 2)] = low(dot(low_probs[...], grad_mixed[m, :, head(h)], 1, 0))
        turn = dot(turned[m, h], grad_scores[...], 1, 0).T
        grad_qkv[m, :, head(h)] = low(turn * score_scale)

    def back_project(m, rows):
        grads = grad_qkv[m, rows]
        terms[m, rows] = low(dot(grads, wide[:, : 3 * pair], 1, 1))
        for j, part in enumerate((0, 2)):
            piece = grads[:, part * pair : (part + 1) * pair].astype(jnp.float32)
            bias_ref[j : j + 1] += jnp.sum(piece, axis=0, keepdims=True)

    def stacked(ref, cols=slice(None)):
        return ref[:, :, cols].reshape(micro * seq, -1)

    def weight_grads(first, last):
        def block(i):
            cols = step_rows(i, LANES)
            front = dot(stacked(normed, cols), stacked(grad_qkv), 0, 0)
            back = dot(stacked(gathered, cols), stacked(mixed), 0, 0)
            total = low(jnp.concatenate([front, back], axis=1))
            pieces = [total[:, h * LANES : h * LANES + HEAD] for h in range(4 * heads)]
            grads_ref[cols] = jnp.concatenate(pieces, axis=1)

        repeat(last - first, lambda i: block(first + i))

    def close(m):
        scatters[m].finish()
        for rows in scatters[m].blocks():
            grad_normed = scatters[m].total(rows)
            back, gain_terms = norm_back(
                rows_ref[m, rows].astype(jnp.float32), vec[0:1], grad_normed
            )
            out_ref[m, rows] = low(grad_ref[m, rows] + back)
            for j, item in enumerate((gain_terms, grad_normed)):
                small_ref[j : j + 1] += jnp.sum(item, axis=0, keepdims=True)

    gathers[0].to_mate()
    gathers[0].finish()
    mix_grads(0)
    attend(0, 0)
    gathers[1].forward()
    for h in range(1, heads):
        attend(0, h)
    gathers[1].to_mate()
    chip_rows(slab, True, lambda rows: back_project(0, rows))
    scatters[0].mate_far()
    scatters[0].far_hop()
    chip_rows(slab, False, lambda rows: back_project(0, rows))
    scatters[0].mate_near()
    gathers[1].finish()
    scatters[0].second_hop()
    mix_grads(1)
    scatters[0].first_hop()
    for h in range(heads):
        attend(1, h)
    chip_rows(slab, True, lambda rows: back_project(1, rows))
    scatters[1].mate_far()
    scatters[1].far_hop()
    chip_rows(slab, False, lambda rows: back_project(1, rows))
    scatters[1].mate_near()
    close(0)
    scatters[1].second_hop()
    for load in load_rest:
        load.wait()
    blocks = width // LANES
    weight_grads(0, blocks // 3)
    scatters[1].first_hop()
    weight_grads(blocks // 3, blocks)
    close(1)


def any_spec():
    return pl.BlockSpec(memory_space=pl.ANY)


def vmem_spec():
    return pl.BlockSpec(memory_space=pltpu.VMEM)


def shape_of(shape, dtype):
    return jax.ShapeDtypeStruct(shape, dtype)


def params(collective):
    return pltpu.CompilerParams(
        collective_id=collective, has_side_effects=True, vmem_limit_bytes=VMEM_BYTES
    )


def smem_spec():
    return pl.BlockSpec(memory_space=pltpu.SMEM)


def attn_forward(rows_low, vectors, bias, packed, at, layer, lengths, own_rows, given=None, grads=None):
    micro, half_rows, width = rows_low.shape
    seq = 8 * half_rows
    pair = bias.shape[2] // 3
    heads = pair // LANES
    low_type, high_type = jnp.bfloat16, jnp.float32
    hidden, lse, normed, qkv, mixed = pl.pallas_call(
        functools.partial(attn_forward_kernel, given is not None, at, layer, own_rows),
        out_shape=[
            shape_of((micro, half_rows, width), high_type),
            shape_of((micro, heads, seq, LANES), high_type),
            shape_of((micro, seq, width), low_type),
            shape_of((micro, seq, 3 * pair), low_type),
            shape_of((micro, seq, pair), low_type),
        ],
        in_specs=[vmem_spec()] * 3 + [smem_spec(), any_spec(), any_spec(), vmem_spec()],
        out_specs=[vmem_spec()] * 2 + [any_spec()] * 3,
        scratch_shapes=gather_scratch(micro, seq, width)
        + scatter_scratch(micro, seq, half_rows, width)
        + [
            pltpu.VMEM((width, 4 * heads * HEAD), low_type),
            pltpu.VMEM((width, 4 * pair), low_type),
            pltpu.VMEM((micro, seq, 3 * pair), low_type),
            pltpu.VMEM((micro, seq, pair), low_type),
            pltpu.SemaphoreType.DMA,
            pltpu.SemaphoreType.DMA((6,)),
            pltpu.SemaphoreType.DMA((micro,)),
            pltpu.VMEM((micro, seq if given is not None else 32, width), low_type),
            pltpu.SemaphoreType.DMA((micro, 3)),
            pltpu.SemaphoreType.DMA((micro, 3)),
        ],
        compiler_params=params(0 if given is None else 6),
        cost_estimate=COST,
        name="attn_forward",
    )(
        rows_low,
        vectors,
        bias,
        lengths,
        packed,
        packed if given is None else given,
        rows_low if grads is None else grads,
    )
    if given is None:
        return hidden, (normed, qkv, lse, mixed)
    return hidden, (given, qkv, lse, mixed), normed


def ffn_forward(hidden, vectors, up_biases, packed, at, layer, half_ff):
    micro, half_rows, width = hidden.shape
    seq = 8 * half_rows
    ff = up_biases.shape[2]
    packed_cols = 2 * ff - LANES
    low_type, high_type = jnp.bfloat16, jnp.float32
    out, second, upper = pl.pallas_call(
        functools.partial(ffn_forward_kernel, half_ff, at, layer),
        out_shape=[
            shape_of((micro, half_rows, width), low_type),
            shape_of((micro, seq, width), low_type),
            shape_of((micro, seq, ff), high_type),
        ],
        in_specs=[vmem_spec()] * 3 + [any_spec()],
        out_specs=[vmem_spec()] + [any_spec()] * 2,
        scratch_shapes=gather_scratch(micro, seq, width)
        + scatter_scratch(micro, seq, half_rows, width)
        + [
            pltpu.VMEM((width, packed_cols), low_type),
            pltpu.VMEM((width, 2 * LANES), low_type),
            pltpu.VMEM((micro, seq, ff), high_type),
            pltpu.SemaphoreType.DMA,
            pltpu.SemaphoreType.DMA((4,)),
        ],
        compiler_params=params(1),
        cost_estimate=COST,
        name="ffn_forward",
    )(hidden, vectors, up_biases, packed)
    return out, (second, upper)


def ffn_turn(hidden, grad_low, given, vectors, up_biases, packed, at, layer, half_ff):
    micro, half_rows, width = hidden.shape
    seq = 8 * half_rows
    ff = up_biases.shape[2]
    low_type, high_type = jnp.bfloat16, jnp.float32
    out, grad_hidden, grads, small, up_bias = pl.pallas_call(
        functools.partial(ffn_turn_kernel, half_ff, at, layer),
        out_shape=[
            shape_of((micro, half_rows, width), low_type),
            shape_of((micro, half_rows, width), high_type),
            shape_of((width, 2 * ff - LANES), low_type),
            shape_of((8, width), high_type),
            shape_of((8, ff), high_type),
        ],
        in_specs=[vmem_spec()] * 4 + [any_spec()] * 2,
        out_specs=[vmem_spec()] * 5,
        scratch_shapes=gather_scratch(micro, seq, width)
        + scatter_scratch(micro, seq, half_rows, width)
        + scatter_scratch(micro, seq, half_rows, width)
        + [
            pltpu.VMEM((width, 2 * ff - LANES), low_type),
            pltpu.VMEM((width, 2 * LANES), low_type),
            pltpu.VMEM((micro, seq, width), low_type),
            pltpu.VMEM((micro, seq, ff), low_type),
            pltpu.VMEM((micro, seq, ff), low_type),
            pltpu.SemaphoreType.DMA,
            pltpu.SemaphoreType.DMA((micro,)),
        ],
        compiler_params=params(7),
        cost_estimate=COST,
        name="ffn_turn",
    )(hidden, grad_low, vectors, up_biases, given, packed)
    return out, grad_hidden, grads, small, up_bias[:1]


def ffn_backward(grad_low, hidden, kept, vectors, packed, at, layer, half_ff):
    second, upper = kept
    micro, half_rows, width = hidden.shape
    seq, ff = upper.shape[1:]
    low_type, high_type = jnp.bfloat16, jnp.float32
    grad_hidden, grads, small, up_bias = pl.pallas_call(
        functools.partial(ffn_backward_kernel, half_ff, at, layer),
        out_shape=[
            shape_of((micro, half_rows, width), high_type),
            shape_of((width, 2 * ff - LANES), low_type),
            shape_of((8, width), high_type),
            shape_of((8, ff), high_type),
        ],
        in_specs=[vmem_spec()] * 3 + [any_spec()] * 3,
        out_specs=[vmem_spec()] * 4,
        scratch_shapes=gather_scratch(micro, seq, width)
        + scatter_scratch(micro, seq, half_rows, width)
        + [
            pltpu.VMEM((width, 2 * ff - LANES), low_type),
            pltpu.VMEM((width, 2 * LANES), low_type),
            pltpu.VMEM((micro, seq, width), low_type),
            pltpu.VMEM((micro, seq, ff), high_type),
            pltpu.VMEM((micro, seq, ff), low_type),
            pltpu.VMEM((micro, seq, ff), low_type),
            pltpu.SemaphoreType.DMA((1 + 2 * micro,)),
        ],
        compiler_params=params(2),
        cost_estimate=COST,
        name="ffn_backward",
    )(grad_low, hidden, vectors, second, upper, packed)
    return grad_hidden, grads, small, up_bias[:1]


def attn_backward(grad_hidden, rows_low, kept, vectors, packed, at, layer, lengths, own_rows):
    normed, qkv, lse, mixed = kept
    micro, half_rows, width = grad_hidden.shape
    seq, pair = mixed.shape[1:]
    heads = pair // LANES
    low_type, high_type = jnp.bfloat16, jnp.float32
    out, grads, small, bias = pl.pallas_call(
        functools.partial(attn_backward_kernel, at, layer, own_rows),
        out_shape=[
            shape_of((micro, half_rows, width), low_type),
            shape_of((width, 4 * heads * HEAD), low_type),
            shape_of((8, width), high_type),
            shape_of((8, pair), high_type),
        ],
        in_specs=[vmem_spec()] * 4 + [smem_spec()] + [any_spec()] * 4,
        out_specs=[vmem_spec()] * 4,
        scratch_shapes=gather_scratch(micro, seq, width)
        + scatter_scratch(micro, seq, half_rows, width)
        + [
            pltpu.VMEM((width, 4 * heads * HEAD), low_type),
            pltpu.VMEM((width, 4 * pair), low_type),
            pltpu.VMEM((micro, seq, width), low_type),
            pltpu.VMEM((micro, seq, 3 * pair), low_type),
            pltpu.VMEM((micro, seq, pair), low_type),
            pltpu.VMEM((micro, seq, pair), low_type),
            pltpu.VMEM((micro, seq, 3 * pair), low_type),
            pltpu.VMEM((micro, heads, LANES, seq), low_type),
            pltpu.VMEM((micro, seq, LANES), high_type),
            pltpu.VMEM((seq, seq), low_type),
            pltpu.VMEM((seq, seq), low_type),
            pltpu.SemaphoreType.DMA((1 + 3 * micro,)),
        ],
        compiler_params=params(3 + 5 * layer),
        cost_estimate=COST,
        name="attn_backward",
    )(grad_hidden, rows_low, vectors, lse, lengths, normed, qkv, mixed, packed)
    return out, grads, small, bias


def slab_peers():
    section, tensor = lax.axis_index("section"), lax.axis_index("tensor")
    peers = []
    for role in range(1, 8):
        far, step = role // 4, role % 4
        other = section + far * (1 - 2 * section)
        to = (other, lax.rem(tensor + step, 4))
        source = (other, lax.rem(tensor + 4 - step, 4))
        peers.append((role, to, source))
    return peers


def column_peers(count):
    here = lax.axis_index("dp")
    return [
        (step, lax.rem(here + step, count), lax.rem(here + count - step, count))
        for step in range(1, count)
    ]


def greet_all(count):
    barrier = pltpu.get_barrier_semaphore()
    for _, to, _ in slab_peers():
        pl.semaphore_signal(barrier, inc=1, device_id=named(to), device_id_type=MESH)
    for _, to, _ in column_peers(count):
        pl.semaphore_signal(barrier, inc=1, device_id={"dp": to}, device_id_type=MESH)
    pl.semaphore_wait(barrier, 7 + count - 1)


def remote(src, dst, send_sem, recv_sem, peer):
    return pltpu.make_async_remote_copy(
        src_ref=src,
        dst_ref=dst,
        send_sem=send_sem,
        recv_sem=recv_sem,
        device_id=peer,
        device_id_type=MESH,
    )


def prologue_kernel(
    count, heads, qkv_ref, out_ref_t, up_ref_in, down_ref_t, gains_ref, shifts_ref, up_bias, rows_ref,
    first_hbm, normed_hbm, attn_ref, ff_hbm, out_ref, up_ref, bias_ref,
    attn_parts, ff_parts, up_halves, mine_ref, all_rows, line, ff_line, column, slab, up_got,
    rows_send, rows_recv, column_send, column_recv, slab_send, slab_recv, swap_send, swap_recv,
    right_send, right_recv, left_send, left_recv, out_sems,
):
    section, tensor, here = (lax.axis_index(name) for name in ("section", "tensor", "dp"))
    width = out_ref.shape[2]
    chunk = width // (4 * count)
    rows = attn_parts.shape[1]
    micro, own_rows = rows_ref.shape[:2]
    pieces = swap_send.shape[0] - 2
    size = rows // pieces
    other = {"section": 1 - section}
    pair = heads * LANES
    pair_cols = heads * HEAD
    half_ff = up_ref_in.shape[1] // 2
    main = half_ff // LANES * LANES
    extra = half_ff - main
    greet_all(count)
    for half in range(2):
        span = slice(half * pair_cols, (half + 1) * pair_cols)
        parts = [qkv_ref[k, :, span] for k in range(3)] + [out_ref_t[:, span]]
        attn_parts[half] = jnp.concatenate(parts, axis=1)
    keep_slot = jnp.where(section == 0, here, count)
    send_slot = jnp.where(section == 0, here, count)
    got_slot = jnp.where(section == 0, count, here)
    sent = []
    for p in range(pieces):
        span = pl.ds(p * size, size)
        copy = remote(
            attn_parts.at[1 - section, span],
            line.at[send_slot, span],
            swap_send.at[p],
            swap_recv.at[p],
            other,
        )
        copy.start()
        sent.append(copy)
    line[keep_slot] = attn_parts[section]
    mine_ref[...] = jnp.zeros_like(mine_ref)
    gains = gains_ref.shape[0]
    mine_ref[:gains, :chunk] = gains_ref[...]
    mine_ref[gains:, :chunk] = shifts_ref[...]
    column[here] = mine_ref[...]
    for step, to, _ in column_peers(count):
        copy = remote(
            mine_ref, column.at[here], column_send.at[step], column_recv.at[step], {"dp": to}
        )
        copy.start()
        sent.append(copy)

    def swapped(p):
        got = line.at[got_slot, pl.ds(p * size, size)]
        remote(got, got, swap_send.at[p], swap_recv.at[p], other).wait_recv()

    def hop(step, p, way, finish=False):
        origin = here - way * step
        sends, recvs = (right_send, right_recv) if way == 1 else (left_send, left_recv)
        inside = (origin >= 0) if way == 1 else (origin < count)
        onward = (here + 1 < count) if way == 1 else (here > 0)
        slot = line.at[jnp.clip(origin, 0, count - 1), pl.ds(p * size, size)]
        target = jnp.clip(here + way, 0, count - 1)
        if step > 0 and not finish:

            @pl.when(inside)
            def _():
                remote(slot, slot, sends.at[step, p], recvs.at[step, p], {"dp": target}).wait_recv()

        if step + 1 < count:

            @pl.when(inside & onward)
            def _():
                copy = remote(
                    slot, slot, sends.at[step, p], recvs.at[step + 1, p], {"dp": target}
                )
                if finish:
                    copy.wait_send()
                else:
                    copy.start()

    def hops(step):
        for p in range(pieces):
            for way in (1, -1):
                hop(step, p, way)

    for p in range(pieces):

        @pl.when(section == 1)
        def _():
            swapped(p)

        for way in (1, -1):
            hop(0, p, way)
    for step, _, source in column_peers(count):
        slot = column.at[source]
        remote(slot, slot, column_send.at[step], column_recv.at[step], {"dp": source}).wait_recv()
    for role, to, _ in slab_peers():
        copy = remote(
            column, slab.at[section, tensor], slab_send.at[role], slab_recv.at[role], named(to)
        )
        copy.start()
        sent.append(copy)
    slab[section, tensor] = column[...]
    blank = jnp.zeros((rows, LANES - 2 * extra), jnp.bfloat16)
    up_halves[...] = jnp.zeros_like(up_halves)
    for half in range(2):
        start = half * half_ff
        up_halves[half, :, :half_ff] = up_bias[:, start : start + half_ff]
        ff_parts[half, :, :main] = up_ref_in[:, start : start + main]
        ff_parts[half, :, main : 2 * main] = down_ref_t[:, start : start + main]
        span = slice(start + main, start + half_ff)
        ff_parts[half, :, 2 * main :] = jnp.concatenate(
            [up_ref_in[:, span], down_ref_t[:, span], blank], axis=1
        )
    ff_swap = remote(
        ff_parts.at[1 - section],
        ff_line.at[section],
        swap_send.at[pieces],
        swap_recv.at[pieces],
        other,
    )
    up_swap = remote(
        up_halves.at[1 - section],
        up_got.at[section],
        swap_send.at[pieces + 1],
        swap_recv.at[pieces + 1],
        other,
    )
    up_swap.start()
    for role, _, source in slab_peers():
        slot = slab.at[source[0], source[1]]
        remote(slot, slot, slab_send.at[role], slab_recv.at[role], named(source)).wait_recv()
    ff_swap.start()
    for layer in range(2):
        for part in range(4 * count):
            piece = slab[layer, part % 4, part // 4]
            out_ref[layer, :, part * chunk : (part + 1) * chunk] = piece[:, :chunk]
    tiles = TileGather(all_rows, rows_send, rows_recv)
    for m in range(micro):
        own = tiles.tile(m, tensor)
        for begin in range(0, own_rows, 32):
            end = min(begin + 32, own_rows)
            block = rows_ref[m, begin:end].astype(jnp.float32)
            own[begin:end] = low(layer_norm(block, out_ref[0, 0:1], out_ref[0, 2:3]))
        own[own_rows:] = jnp.zeros((tiles.tile_rows - own_rows, width), jnp.bfloat16)
    tiles.start()
    hops(1)
    start = (2 * tensor + section) * pair_cols
    for layer in range(2):
        turned = pltpu.roll(out_ref[layer], lax.rem(width - start, width), 1)
        empty = jnp.zeros((1, LANES - HEAD), jnp.float32)
        for part, row in ((0, 3), (2, 4)):
            for h in range(heads):
                at = part * pair + h * LANES
                piece = turned[row : row + 1, h * HEAD : (h + 1) * HEAD]
                bias_ref[layer, :, at : at + LANES] = jnp.concatenate([piece, empty], 1)
        bias_ref[layer, :, pair : 2 * pair] = jnp.zeros((1, pair), jnp.float32)
    up_ref[section] = up_halves[section]
    outs = []

    def put(src, dst, i):
        copy = pltpu.make_async_copy(src, dst, out_sems.at[i])
        copy.start()
        outs.append(copy)

    ff_line_out = ff_hbm.at[section]
    put(ff_parts.at[section], ff_line_out, count)
    for step in range(2, count):
        hops(step)
        if step == 2:
            tiles.pass_on()
    if count <= 2:
        tiles.pass_on()
    for p in range(pieces):

        @pl.when(section == 0)
        def _():
            swapped(p)

    for at in range(count):
        put(line.at[at], first_hbm.at[pl.ds(at * rows, rows)], at)
    attn_ref[...] = line[count]
    got = up_got.at[1 - section]
    remote(got, got, swap_send.at[pieces + 1], swap_recv.at[pieces + 1], other).wait_recv()
    up_ref[1 - section] = up_got[1 - section]
    tiles.finish()
    put(all_rows, normed_hbm, count + 2)
    ff_got = ff_line.at[1 - section]
    remote(ff_got, ff_got, swap_send.at[pieces], swap_recv.at[pieces], other).wait_recv()
    put(ff_got, ff_hbm.at[1 - section], count + 1)
    for step in range(count):
        for p in range(pieces):
            for way in (1, -1):
                hop(step, p, way, True)
    for copy in sent + [ff_swap, up_swap]:
        copy.wait_send()
    tiles.drain()
    for copy in outs:
        copy.wait()


def prologue(qkv, out_t, up, down_t, gains, shifts, up_bias, rows_low, count, heads, tile_rows):
    part_rows = qkv.shape[1]
    micro, _, width = rows_low.shape
    vector_rows = gains.shape[0] + shifts.shape[0]
    half_ff = up.shape[1] // 2
    ff_wide = round_up(half_ff, LANES)
    attn_shape = (part_rows, 4 * heads * HEAD)
    ff_shape = (2, part_rows, 2 * ff_wide - LANES)
    all_rows = (micro, 4 * tile_rows, width)
    pieces = 3 if part_rows % 96 == 0 else 1
    low_type, high_type = jnp.bfloat16, jnp.float32
    dma = pltpu.SemaphoreType.DMA
    return pl.pallas_call(
        functools.partial(prologue_kernel, count, heads),
        out_shape=[
            shape_of((count * part_rows, attn_shape[1]), low_type),
            shape_of(all_rows, low_type),
            shape_of(attn_shape, low_type),
            shape_of(ff_shape, low_type),
            shape_of((2, vector_rows, width), high_type),
            shape_of((2, 1, ff_wide), high_type),
            shape_of((2, 1, 3 * heads * LANES), high_type),
        ],
        in_specs=[vmem_spec()] * 8,
        out_specs=[any_spec()] * 2 + [vmem_spec(), any_spec()] + [vmem_spec()] * 3,
        scratch_shapes=[
            pltpu.VMEM((2,) + attn_shape, low_type),
            pltpu.VMEM(ff_shape, low_type),
            pltpu.VMEM((2, 1, ff_wide), high_type),
            pltpu.VMEM((vector_rows, LANES), high_type),
            pltpu.VMEM(all_rows, low_type),
            pltpu.VMEM((count + 1,) + attn_shape, low_type),
            pltpu.VMEM(ff_shape, low_type),
            pltpu.VMEM((count, vector_rows, LANES), high_type),
            pltpu.VMEM((2, 4, count, vector_rows, LANES), high_type),
            pltpu.VMEM((2, 1, ff_wide), high_type),
            dma((micro, 3)),
            dma((micro, 3)),
            dma((count,)),
            dma((count,)),
            dma((8,)),
            dma((8,)),
            dma((pieces + 2,)),
            dma((pieces + 2,)),
            dma((count, pieces)),
            dma((count, pieces)),
            dma((count, pieces)),
            dma((count, pieces)),
            dma((count + 3,)),
        ],
        compiler_params=params(4),
        cost_estimate=COST,
        name="prologue",
    )(qkv, out_t, up, down_t, gains, shifts, up_bias, rows_low)


def home_kernel(
    count, chunk, attn_zero, attn_one, ff_zero, ff_one, biases_in, ups_in,
    ff_sums_hbm, attn_sum_hbm, rows_hbm,
    out_ref, up_ref, ff_got_hbm, attn_got_hbm, rows_got_hbm,
    parts, ups, slab, column, up_pair, up_column, total,
    column_send, column_recv, slab_send, slab_recv, up_sems, up_column_send, up_column_recv, far_send, far_recv,
):
    section, tensor, here = (lax.axis_index(name) for name in ("section", "tensor", "dp"))
    width = attn_zero.shape[1]
    heads = biases_in.shape[2] // LANES
    other = {"section": 1 - section}
    greet_all(count)
    parts[...] = jnp.zeros_like(parts)
    start = (2 * tensor + section) * (heads * HEAD)
    for layer, (attn, ff) in enumerate(((attn_zero, ff_zero), (attn_one, ff_one))):
        bias = biases_in[layer]
        blank = jnp.zeros((8, width - heads * HEAD), jnp.float32)
        pieces = [bias[:, h * LANES : h * LANES + HEAD] for h in range(heads)]
        placed = pltpu.roll(jnp.concatenate(pieces + [blank], 1), start, 1)
        whole = jnp.concatenate(
            [attn[0:1], ff[0:1], attn[1:2], placed[0:2], ff[3:4], ff[1:2], ff[2:3]], axis=0
        )
        for part in range(4 * count):
            piece = whole[:, part * chunk : (part + 1) * chunk]
            parts[layer, part % 4, part // 4, :, :chunk] = piece
        ups[layer] = ups_in[layer]
    sent = []

    def send(src, dst, send_sem, recv_sem, peer):
        copy = remote(src, dst, send_sem, recv_sem, peer)
        copy.start()
        sent.append(copy)

    send(ups.at[1 - section], up_pair.at[section], up_sems.at[0], up_sems.at[1], other)
    for role, to, _ in slab_peers():
        send(
            parts.at[to[0], to[1]], slab.at[role], slab_send.at[role], slab_recv.at[role], named(to)
        )
    up_pair[section] = ups[section]
    value = parts[section, tensor]
    for role, _, source in slab_peers():
        slot = slab.at[role]
        remote(slot, slot, slab_send.at[role], slab_recv.at[role], named(source)).wait_recv()
        value = value + slab[role]
    total[...] = value
    for step, to, _ in column_peers(count):
        send(total.at[to], column.at[step], column_send.at[step], column_recv.at[step], {"dp": to})
    got = up_pair.at[1 - section]
    remote(got, got, up_sems.at[0], up_sems.at[1], other).wait_recv()
    for step, to, _ in column_peers(count):
        send(
            up_pair, up_column.at[here], up_column_send.at[step], up_column_recv.at[step], {"dp": to}
        )
    far = (
        (ff_sums_hbm.at[1 - section], ff_got_hbm),
        (rows_hbm.at[1 - section], rows_got_hbm),
    )
    for k, (src, dst) in enumerate(far):
        send(src, dst, far_send.at[k], far_recv.at[k], other)

    @pl.when(section == 0)
    def _():
        remote(attn_sum_hbm, attn_got_hbm, far_send.at[2], far_recv.at[2], other).start()

    up_column[here] = up_pair[...]
    result = total[here]
    for step, _, source in column_peers(count):
        slot = column.at[step]
        remote(slot, slot, column_send.at[step], column_recv.at[step], {"dp": source}).wait_recv()
        result = result + column[step]
    out_ref[...] = result
    for step, _, source in column_peers(count):
        slot = up_column.at[source]
        remote(
            slot, slot, up_column_send.at[step], up_column_recv.at[step], {"dp": source}
        ).wait_recv()
    value = up_column[0]
    for at in range(1, count):
        value = value + up_column[at]
    up_ref[...] = value
    for k, (_, dst) in enumerate(far):
        remote(dst, dst, far_send.at[k], far_recv.at[k], other).wait_recv()
    last = remote(attn_sum_hbm, attn_got_hbm, far_send.at[2], far_recv.at[2], other)

    @pl.when(section == 0)
    def _():
        last.wait_send()

    @pl.when(section == 1)
    def _():
        last.wait_recv()

    for copy in sent:
        copy.wait_send()


def home(attn_small, ff_small, bias_grads, up_grads, ff_sums, attn_sum, rows, count, chunk):
    vector_rows, lanes = 8, LANES
    up_shape = up_grads.shape[1:]
    dma = pltpu.SemaphoreType.DMA
    high_type = jnp.float32
    return pl.pallas_call(
        functools.partial(home_kernel, count, chunk),
        out_shape=[
            shape_of((vector_rows, lanes), high_type),
            shape_of((2,) + up_shape, high_type),
            shape_of(ff_sums.shape[1:], ff_sums.dtype),
            shape_of(attn_sum.shape, attn_sum.dtype),
            shape_of(rows.shape[1:], rows.dtype),
        ],
        in_specs=[vmem_spec()] * 6 + [any_spec()] * 3,
        out_specs=[vmem_spec()] * 2 + [any_spec()] * 3,
        scratch_shapes=[
            pltpu.VMEM((2, 4, count, vector_rows, lanes), high_type),
            pltpu.VMEM((2,) + up_shape, high_type),
            pltpu.VMEM((8, count, vector_rows, lanes), high_type),
            pltpu.VMEM((count, vector_rows, lanes), high_type),
            pltpu.VMEM((2,) + up_shape, high_type),
            pltpu.VMEM((count, 2) + up_shape, high_type),
            pltpu.VMEM((count, vector_rows, lanes), high_type),
            dma((count,)),
            dma((count,)),
            dma((8,)),
            dma((8,)),
            dma((2,)),
            dma((count,)),
            dma((count,)),
            dma((3,)),
            dma((3,)),
        ],
        compiler_params=params(5),
        cost_estimate=COST,
        name="home",
    )(*attn_small, *ff_small, bias_grads, up_grads, ff_sums, attn_sum, rows)


def shards(
    section_input,
    final_cotangent,
    lengths,
    qkv_weight,
    out_weight,
    up_weight,
    down_weight,
    norm_gains,
    biases,
    up_bias,
):
    here = lax.axis_index("section")
    sections = lax.axis_size("section")
    micro, _, own_rows, _ = section_input.shape
    head_cols = qkv_weight.shape[3]
    pair_cols = head_cols // sections
    heads = pair_cols // HEAD
    ff_cols = up_weight.shape[2]
    half_ff = ff_cols // sections
    half_rows = round_up(-(-own_rows // sections), 32)
    full_rows = half_rows * sections

    def by_layer(mine, other):
        return [jnp.where(here == 0, mine, other), jnp.where(here == 0, other, mine)]

    part_rows = qkv_weight.shape[2]
    count = lax.axis_size("dp")
    chunk = norm_gains.shape[2]
    main = half_ff // LANES * LANES
    first, normed, attn_part, ff_two, vectors, up_biases, bias_qv = prologue(
        qkv_weight[0],
        out_weight[0].T,
        up_weight[0],
        down_weight[0].T,
        norm_gains[0],
        biases[0],
        up_bias,
        section_input[:, 0],
        count,
        heads,
        full_rows,
    )

    def gather_column(part):
        return lax.all_gather(part, "dp", axis=0, tiled=True)

    ff_first = gather_column(ff_two[0])
    attn_packed = [(first, 0), (gather_column(attn_part), 0)]
    ff_packed = [(ff_first, 0), (gather_column(ff_two[1]), 0)]
    lengths_here = lengths.reshape(micro)

    def my_rows(value):
        padded = jnp.pad(value[:, 0], [(0, 0), (0, full_rows - own_rows), (0, 0)])
        return lax.dynamic_slice_in_dim(padded, here * half_rows, half_rows, 1)

    def whole_rows(first, second, got):
        low_half, high_half = by_layer(jnp.where(here == 0, first, second), got)
        return jnp.concatenate([low_half, high_half], 1)[:, None, :own_rows]

    def send_home(value, layer):
        return lax.ppermute(value, "section", [(1 - layer, layer)])

    rows = my_rows(section_input)
    inputs, hiddens, attn_kept = [], [], []
    for layer in range(2):
        inputs.append(rows)
        operands = (rows, vectors, bias_qv, *attn_packed[layer], layer, lengths_here, own_rows)
        if layer == 0:
            hidden, kept, grads_all = attn_forward(*operands, normed, final_cotangent[:, 0])
        else:
            hidden, kept = attn_forward(*operands)
        hiddens.append(hidden)
        attn_kept.append(kept)
        if layer == 0:
            rows, ff_kept = ffn_forward(hidden, vectors, up_biases, *ff_packed[0], 0, half_ff)

    attn_sums, ff_sums, up_sums, input_grads = {}, {}, {}, {}
    attn_small, ff_small, bias_grads = {}, {}, {}
    for layer in (1, 0):
        if layer == 1:
            last, grad_hidden, ff_grad, ff_small[1], up_sums[1] = ffn_turn(
                hiddens[1],
                my_rows(final_cotangent),
                grads_all,
                vectors,
                up_biases,
                *ff_packed[1],
                1,
                half_ff,
            )
        else:
            grad_hidden, ff_grad, ff_small[0], up_sums[0] = ffn_backward(
                grads, hiddens[0], ff_kept, vectors, *ff_packed[0], 0, half_ff
            )
        ff_sums[layer] = lax.psum_scatter(ff_grad, "dp", scatter_dimension=0, tiled=True)
        grads, attn_grad, attn_small[layer], bias_grads[layer] = attn_backward(
            grad_hidden,
            inputs[layer],
            attn_kept[layer],
            vectors,
            *attn_packed[layer],
            layer,
            lengths_here,
            own_rows,
        )
        attn_sums[layer] = lax.psum_scatter(attn_grad, "dp", scatter_dimension=0, tiled=True)
        input_grads[layer] = grads

    out_got = [send_home(rows, 0), send_home(last, 1)]
    section_output = whole_rows(rows, last, jnp.where(here == 0, out_got[0], out_got[1]))
    small_mine, up_total, ff_got, attn_got, rows_got = home(
        [attn_small[0], attn_small[1]],
        [ff_small[0], ff_small[1]],
        jnp.stack([bias_grads[0], bias_grads[1]]),
        jnp.stack([up_sums[0], up_sums[1]]),
        jnp.stack([ff_sums[0], ff_sums[1]]),
        attn_sums[1],
        jnp.stack([input_grads[0], input_grads[1]]),
        count,
        chunk,
    )
    small_mine = small_mine[None, :, :chunk]
    up_total = up_total[:, :, :half_ff].reshape(1, ff_cols)
    input_grad = whole_rows(input_grads[0], input_grads[1], rows_got)

    def own_layer(sums, got):
        return by_layer(jnp.where(here == 0, sums[0], sums[1]), got)

    attn_got = jnp.where(here == 0, send_home(attn_sums[0], 0), attn_got)
    attn_total = jnp.stack(own_layer(attn_sums, attn_got), 1).astype(jnp.float32)
    attn_total = attn_total.reshape(part_rows, sections, 4, pair_cols)
    attn_total = jnp.moveaxis(attn_total, 2, 0).reshape(4, part_rows, head_cols)
    ff_halves = own_layer(ff_sums, ff_got)
    rest_cols = half_ff - main

    def ff_piece(index):
        pieces = []
        for half in ff_halves:
            pieces.append(half[:, index * main : (index + 1) * main])
            start = 2 * main + index * rest_cols
            pieces.append(half[:, start : start + rest_cols])
        return jnp.concatenate(pieces, 1).astype(jnp.float32)

    ff_total = [ff_piece(0), ff_piece(1)]

    gains = norm_gains.shape[1]
    return (
        section_output[None],
        input_grad[None],
        attn_total[None, :3],
        attn_total[3].T[None],
        ff_total[0][None],
        ff_total[1].T[None],
        small_mine[:, :gains],
        small_mine[:, gains:],
        up_total,
    )


def solution(mesh):
    in_specs = (
        P(None, "dp", "tensor", None),
        P(None, "dp", "tensor", None),
        P(None, "dp"),
        P("section", None, "dp", "tensor"),
        P("section", "tensor", "dp"),
        P("section", "dp", "tensor"),
        P("section", "tensor", "dp"),
        P("section", None, ("dp", "tensor")),
        P("section", None, ("dp", "tensor")),
        P("section", "tensor"),
    )
    out_specs = (
        P("section", None, "dp", "tensor", None),
        P("section", None, "dp", "tensor", None),
        P("section", None, "dp", "tensor"),
        P("section", "tensor", "dp"),
        P("section", "dp", "tensor"),
        P("section", "tensor", "dp"),
        P("section", None, ("dp", "tensor")),
        P("section", None, ("dp", "tensor")),
        P("section", "tensor"),
    )
    return jax.shard_map(shards, mesh=mesh, in_specs=in_specs, out_specs=out_specs, check_vma=False)
```

time: 865 us -> 664 us (0.77)
  waiting for transfers between devices: 326 us -> 168 us
  blocking collectives: 56.8 us -> 0 us
  Pallas kernels: 399 us -> 441 us
  local copies, waits for them, and re-layouts: 35.8 us -> 18.7 us
    unnamed x10 -> x7, waiting for transfers between devices: 108 us -> 3.1 us
    all_gather x2 -> x0, blocking collectives: 48 us -> none  [the longest x1 43.7 us: shards(): vectors = lax.all_gather(small, EVERY, axis=0, tiled=False)]
    pallas_call x8 -> x9, Pallas kernels: 399 us -> 441 us  [the longest x2 110 us: attn_backward(): pl.pallas_call(functools.partial(attn_backward_kernel, at, layer, own_row...]
    ppermute x7 -> x3, waiting for transfers between devices: 34.4 us -> 5.24 us  [send_home(): return lax.ppermute(value, 'section', [(1 - layer, layer)])]
    reduce_scatter x2, waiting for transfers between devices: 68.1 us -> 47.4 us  [shards(): lax.psum_scatter(attn_grad, 'dp', scatter_dimension=0, tiled=True)]
    slice x19 -> x4, local copies, waits for them, and re-layouts: 13.3 us -> 4.37 us  [the longest x1 2.53 us: shards(): ff_packed = [(ff_first, 0), (gather_column(ff_two[1]), 0)]]
    psum x1 -> x0, blocking collectives: 8.76 us -> none  [shards(): up_all = lax.psum(jnp.stack([up_sums[0], up_sums[1]])[:, :half_ff], 'dp')]
  transfers between devices with their start and end apart: 16 -> 10, of which waited for: 8 -> 7; matrix products, arithmetic and copies ran while one was open for 3% -> 2% of each run, Pallas kernels for 17% -> 27%
where the time goes in v2:
time: 664 us; the launch traced here: 661 us
  Pallas kernels  441 us (66%)
  waiting for transfers between devices  168 us (25%)
  local copies, waits for them, and re-layouts  18.7 us (3%)
  between operations  14.7 us (2%)
  other arithmetic  10.7 us (2%)
  starting transfers between devices  7.91 us (1%)
    pallas_call x2, Pallas kernels, attn_backward(): pl.pallas_call(functools.partial(attn_backward_kernel, at, layer, own_row...  110 us
    reduce_scatter x2, waiting for transfers between devices, shards(): lax.psum_scatter(ff_grad, 'dp', scatter_dimension=0, tiled=True)  107 us
    pallas_call x2, Pallas kernels, attn_forward(): pl.pallas_call(functools.partial(attn_forward_kernel, given is not None,...  96.7 us
    pallas_call x1, Pallas kernels, ffn_turn(): pl.pallas_call(functools.partial(ffn_turn_kernel, half_ff, at, layer), ou...  63.6 us
    reduce_scatter x2, waiting for transfers between devices, shards(): lax.psum_scatter(attn_grad, 'dp', scatter_dimension=0, tiled=True)  47.4 us
    pallas_call x1, Pallas kernels, prologue(): pl.pallas_call(functools.partial(prologue_kernel, count, heads), out_shap...  46.9 us
    pallas_call x1, Pallas kernels, ffn_backward(): pl.pallas_call(functools.partial(ffn_backward_kernel, half_ff, at, layer)...  41.9 us
    pallas_call x1, Pallas kernels, ffn_forward(): pl.pallas_call(functools.partial(ffn_forward_kernel, half_ff, at, layer),...  40.9 us
  transfers between devices with their start and end apart: 10, of which 7 were waited for; matrix products, arithmetic and copies ran while one was open for 2% of the time, Pallas kernels for 27%

profile of v2, /device:TPU:0, one launch (start us, length us, event | category | flops | bytes accessed | tf_op | source)
XLA Modules:
  0.0 660.9 jit_solution(17770757569081998606)
XLA Ops:
  7.2 1.8 copy.25
  9.0 1.3 copy.35
  10.3 46.9 %prologue.1 = (bf16[1152,576]{1,0:T(8,128)(2,1)}, bf16[2,768,1152]{2,1,0:T(8,128)(2,1)}, bf16[288,576]{1,0:T(8,128)(2,1)}, bf16[2,288,1152]{2,1,0:T(8,128)(2,1)}...) custom-call(bf16[3,288,288]{2,1,0:T(8,128)(2,1)} %bitcast.78, bf16[288,288]{1,0:T(8,128)(2,1)} %bitcast.71, ...), custom_call_target="tpu_custom_call" | custom-call | flops 20000000000 | bytes 100000000 | tf_op jit(solution)/shard_map/prologue/pallas_call | solution.py:1474
  57.2 2.5 fusion.2
  62.6 47.3 %attn_forward.2 = (f32[2,96,1152]{2,1,0:T(8,128)}, f32[2,2,768,128]{3,2,1,0:T(8,128)}, bf16[2,768,1152]{2,1,0:T(8,128)(2,1)}, bf16[2,768,768]{2,1,0:T(8,128)(2,1)}, bf16[2,768,256]{2,1,0:T(8,128)(2,1)}) custom-call(bf16[2,96,1152]{2,1,0:T(8,128)(2,1)} %pad_dynamic-slice_fusion.1.rows_ref, f32[2,8,1152]{2,1,0:T(8,128)} %get-tuple-element.51.vectors, ...), custom_call_target="tpu_custom_call" | custom-call | flops 20000000000 | bytes 100000000 | tf_op jit(solution)/shard_map/attn_forward/pallas_call | solution.py:1039
  110.7 3.7 all-gather.8.cloned.1.call-done
  114.4 40.9 %ffn_forward.1 = (bf16[2,96,1152]{2,1,0:T(8,128)(2,1)}, bf16[2,768,1152]{2,1,0:T(8,128)(2,1)}, f32[2,768,640]{2,1,0:T(8,128)}) custom-call(f32[2,96,1152]{2,1,0:T(8,128)} %get-tuple-element.55.hidden_ref, f32[2,8,1152]{2,1,0:T(8,128)} %get-tuple-element.51.vectors, f32[2,1,640]{2,1,0:T(1,128)} %get-tuple-element.56.up_biases, bf16[1152,1152]{1,0:T(8,128)(2,1)} %bitcast.75), custom_call_target="tpu_custom_call" | custom-call | flops 20000000000 | bytes 100000000 | tf_op jit(solution)/shard_map/ffn_forward/pallas_call | solution.py:1087
  155.4 49.4 %attn_forward.3 = (f32[2,96,1152]{2,1,0:T(8,128)}, f32[2,2,768,128]{3,2,1,0:T(8,128)}, bf16[2,768,1152]{2,1,0:T(8,128)(2,1)}, bf16[2,768,768]{2,1,0:T(8,128)(2,1)}, bf16[2,768,256]{2,1,0:T(8,128)(2,1)}) custom-call(bf16[2,96,1152]{2,1,0:T(8,128)(2,1)} %get-tuple-element.58.rows_ref.grads_ref, f32[2,8,1152]{2,1,0:T(8,128)} %get-tuple-element.51.vectors, ...), custom_call_target="tpu_custom_call" | custom-call | flops 20000000000 | bytes 100000000 | tf_op jit(solution)/shard_map/attn_forward/pallas_call | solution.py:1039
  204.8 1.7 all-gather.10.cloned.1.call-done
  206.5 63.6 %ffn_turn.1 = (bf16[2,96,1152]{2,1,0:T(8,128)(2,1)}, f32[2,96,1152]{2,1,0:T(8,128)}, bf16[1152,1152]{1,0:T(8,128)(2,1)}, f32[8,1152]{1,0:T(8,128)}, f32[8,640]{1,0:T(8,128)}) custom-call(f32[2,96,1152]{2,1,0:T(8,128)} %get-tuple-element.60.hidden_ref, bf16[2,96,1152]{2,1,0:T(8,128)(2,1)} %pad_dynamic-slice_fusion.grad_ref, ...), custom_call_target="tpu_custom_call" | custom-call | flops 20000000000 | bytes 100000000 | tf_op jit(solution)/shard_map/ffn_turn/pallas_call | solution.py:1117
  270.1 55.8 %attn_backward.2 = (bf16[2,96,1152]{2,1,0:T(8,128)(2,1)}, bf16[1152,576]{1,0:T(8,128)(2,1)}, f32[8,1152]{1,0:T(8,128)}, f32[8,256]{1,0:T(8,128)}) custom-call(f32[2,96,1152]{2,1,0:T(8,128)} %get-tuple-element.63.grad_ref, bf16[2,96,1152]{2,1,0:T(8,128)(2,1)} %get-tuple-element.58.rows_ref.grads_ref, f32[2,8,1152]{2,1,0:T(8,128)} %get-tuple-element.51.vectors, ...), custom_call_target="tpu_custom_call" | custom-call | flops 20000000000 | bytes 100000000 | tf_op jit(solution)/shard_map/attn_backward/pallas_call | solution.py:1186
  325.9 41.9 %ffn_backward.1 = (f32[2,96,1152]{2,1,0:T(8,128)}, bf16[1152,1152]{1,0:T(8,128)(2,1)}, f32[8,1152]{1,0:T(8,128)}, f32[8,640]{1,0:T(8,128)}) custom-call(bf16[2,96,1152]{2,1,0:T(8,128)(2,1)} %get-tuple-element.68.grad_ref, f32[2,96,1152]{2,1,0:T(8,128)} %get-tuple-element.55.hidden_ref, f32[2,8,1152]{2,1,0:T(8,128)} %get-tuple-element.51.vectors, ...), custom_call_target="tpu_custom_call" | custom-call | flops 20000000000 | bytes 100000000 | tf_op jit(solution)/shard_map/ffn_backward/pallas_call | solution.py:1152
  367.8 54.6 %attn_backward.3 = (bf16[2,96,1152]{2,1,0:T(8,128)(2,1)}, bf16[1152,576]{1,0:T(8,128)(2,1)}, f32[8,1152]{1,0:T(8,128)}, f32[8,256]{1,0:T(8,128)}) custom-call(f32[2,96,1152]{2,1,0:T(8,128)} %get-tuple-element.71.grad_ref, bf16[2,96,1152]{2,1,0:T(8,128)(2,1)} %pad_dynamic-slice_fusion.1.rows_ref, f32[2,8,1152]{2,1,0:T(8,128)} %get-tuple-element.51.vectors, ...), custom_call_target="tpu_custom_call" | custom-call | flops 20000000000 | bytes 100000000 | tf_op jit(solution)/shard_map/attn_backward/pallas_call | solution.py:1186
  424.4 1.3 collective-permute-start
  425.7 4.6 collective-permute-start.1
  433.0 1.0 pad_maximum_fusion.1.rows_hbm
  434.0 5.2 collective-permute-done.1
  439.3 1.0 fusion.1
  440.3 14.1 %reduce-scatter.11.cloned.1.call-done = bf16[288,576]{1,0:T(8,128)(2,1)} async-done(((bf16[1152,576]{1,0:T(8,128)(2,1)}), bf16[288,576]{1,0:T(8,128)(2,1)}) %reduce-scatter.11.cloned.1.call-update) | async-done | bytes 331792 | tf_op jit(solution)/shard_map/reduce_scatter | solution.py:1760
  454.4 1.3 collective-permute-start.2
  455.7 52.5 %reduce-scatter.5.cloned.1.call-done = bf16[288,1152]{1,0:T(8,128)(2,1)} async-done(((bf16[1152,1152]{1,0:T(8,128)(2,1)}), bf16[288,1152]{1,0:T(8,128)(2,1)}) %reduce-scatter.5.cloned.1.call-update) | async-done | bytes 663568 | tf_op jit(solution)/shard_map/reduce_scatter | solution.py:1749
  508.1 54.5 %reduce-scatter.7.cloned.1.call-done = bf16[288,1152]{1,0:T(8,128)(2,1)} async-done(((bf16[1152,1152]{1,0:T(8,128)(2,1)}), bf16[288,1152]{1,0:T(8,128)(2,1)}) %reduce-scatter.7.cloned.1.call-update) | async-done | bytes 663568 | tf_op jit(solution)/shard_map/reduce_scatter | solution.py:1749
  562.7 2.5 pad_maximum_fusion.ff_sums_hbm
  565.2 33.3 %reduce-scatter.9.cloned.1.call-done.attn_sum_hbm = bf16[288,576]{1,0:T(8,128)(2,1)} async-done(((bf16[1152,576]{1,0:T(8,128)(2,1)}), bf16[288,576]{1,0:T(8,128)(2,1)}) %reduce-scatter.9.cloned.1.call-update) | async-done | bytes 331792 | tf_op jit(solution)/shard_map/reduce_scatter | solution.py:1760
  598.5 40.3 %home.1 = (f32[8,128]{1,0:T(8,128)}, f32[2,1,640]{2,1,0:T(1,128)}, bf16[288,1152]{1,0:T(8,128)(2,1)}, bf16[288,576]{1,0:T(8,128)(2,1)}, bf16[2,96,1152]{2,1,0:T(8,128)(2,1)}) custom-call(f32[8,1152]{1,0:T(8,128)} %get-tuple-element.76.attn_zero, f32[8,1152]{1,0:T(8,128)} %get-tuple-element.77.attn_one, f32[8,1152]{1,0:T(8,128)} %get-tuple-element.78.ff_zero, ...), custom_call_target="tpu_custom_call" | custom-call | flops 20000000000 | bytes 100000000 | tf_op jit(solution)/shard_map/home/pallas_call | solution.py:1619
  638.8 1.3 broadcast_select_fusion
  640.9 1.0 fusion.4
  644.7 1.5 concatenate.35
  646.2 1.1 convert_bitcast_fusion.1
  647.4 1.3 concatenate.34
  648.7 1.1 convert_element_type.16
  650.0 1.6 copy.31
  (85 shorter events, 14.3 us)
Async XLA Ops:
  7.2 107.2 %all-gather.8.cloned.1.call-start = ((), (), s32[]{:S(2)}) async-start(), calls=%async_computation.9 | async-start | bytes 3317760 | tf_op jit(solution)/shard_map/all_gather | solution.py:1699
  57.2 4.6 copy-start.7
  59.7 95.6 %all-gather.6.cloned.1.call-start = ((), (), s32[]{:S(2)}) async-start(), calls=%async_computation.4 | async-start | bytes 1843200 | tf_op jit(solution)/shard_map/all_gather | solution.py:1699
  60.5 146.0 %all-gather.10.cloned.1.call-start = ((), (), s32[]{:S(2)}) async-start(), calls=%async_computation.10 | async-start | bytes 3317760 | tf_op jit(solution)/shard_map/all_gather | solution.py:1699
  61.2 393.1 %reduce-scatter.11.cloned.1.call-start = ((), (), s32[]{:S(2)}) async-start(), calls=%async_computation.8 | async-start | bytes 1843200 | tf_op jit(solution)/shard_map/reduce_scatter | solution.py:1760
  62.6 47.3 %copy-start.8 = (bf16[2,1,184,1152]{3,2,1,0:T(8,128)(2,1)S(1)}, bf16[2,1,184,1152]{3,2,1,0:T(8,128)(2,1)}, u32[]{:S(2)}) copy-start(bf16[2,1,184,1152]{3,2,1,0:T(8,128)(2,1)} %param.11) | copy-start | bytes 2543620
  422.5 85.7 %reduce-scatter.5.cloned.1.call-start = ((), (), s32[]{:S(2)}) async-start(), calls=%async_computation.5 | async-start | bytes 3317760 | tf_op jit(solution)/shard_map/reduce_scatter | solution.py:1749
  423.0 139.6 %reduce-scatter.7.cloned.1.call-start = ((), (), s32[]{:S(2)}) async-start(), calls=%async_computation.6 | async-start | bytes 3317760 | tf_op jit(solution)/shard_map/reduce_scatter | solution.py:1749
  423.1 1.3 copy-start.10
  423.1 2.6 copy-start.11
  423.1 9.3 %copy-start.18 = (f32[8,256]{1,0:T(8,128)S(1)}, f32[8,256]{1,0:T(8,128)}, u32[]{:S(2)}) copy-start(f32[8,256]{1,0:T(8,128)} %get-tuple-element.81) | copy-start | bytes 24580
  423.1 9.2 %copy-start.19 = (f32[8,256]{1,0:T(8,128)S(1)}, f32[8,256]{1,0:T(8,128)}, u32[]{:S(2)}) copy-start(f32[8,256]{1,0:T(8,128)} %get-tuple-element.80) | copy-start | bytes 24580
  423.1 9.8 %copy-start.3 = (bf16[2,96,1152]{2,1,0:T(8,128)(2,1)S(1)}, bf16[2,96,1152]{2,1,0:T(8,128)(2,1)}, u32[]{:S(2)}) copy-start(bf16[2,96,1152]{2,1,0:T(8,128)(2,1)} %get-tuple-element.68.grad_ref) | copy-start | bytes 1327108
  423.1 9.8 %copy-start.4 = (bf16[2,96,1152]{2,1,0:T(8,128)(2,1)S(1)}, bf16[2,96,1152]{2,1,0:T(8,128)(2,1)}, u32[]{:S(2)}) copy-start(bf16[2,96,1152]{2,1,0:T(8,128)(2,1)} %get-tuple-element.75) | copy-start | bytes 1327108
  423.6 174.9 %reduce-scatter.9.cloned.1.call-start = ((), (), s32[]{:S(2)}) async-start(), calls=%async_computation.7 | async-start | bytes 1843200 | tf_op jit(solution)/shard_map/reduce_scatter | solution.py:1760
  424.4 14.8 %collective-permute-start = (bf16[2,96,1152]{2,1,0:T(8,128)(2,1)S(1)}, bf16[2,96,1152]{2,1,0:T(8,128)(2,1)S(1)}, u32[]{:S(2)}, u32[]{:S(2)}) collective-permute-start(bf16[2,96,1152]{2,1,0:T(8,128)(2,1)S(1)} %copy-done.10), channel_id=1, source_target_pairs={{16,0},{17,1},{18,2},{19,3},{20,4},{21,5},{22,6},{23,7},{24,8},{25... | collective-permute-start | bytes 1327112 | tf_op jit(solution)/shard_map/ppermute | solution.py:1715
  425.7 13.5 %collective-permute-start.1 = (bf16[2,96,1152]{2,1,0:T(8,128)(2,1)S(1)}, bf16[2,96,1152]{2,1,0:T(8,128)(2,1)S(1)}, u32[]{:S(2)}, u32[]{:S(2)}) collective-permute-start(bf16[2,96,1152]{2,1,0:T(8,128)(2,1)S(1)} %copy-done.11), channel_id=1, source_target_pairs={{0,16},{1,17},{2,18},{3,19},{4,20},{5,21},{6,22},{7,23},{8,24},{9,... | collective-permute-start | bytes 1327112 | tf_op jit(solution)/shard_map/ppermute | solution.py:1715
  454.4 187.6 %collective-permute-start.2 = (bf16[288,576]{1,0:T(8,128)(2,1)}, bf16[288,576]{1,0:T(8,128)(2,1)S(1)}, u32[]{:S(2)}, u32[]{:S(2)}) collective-permute-start(bf16[288,576]{1,0:T(8,128)(2,1)} %reduce-scatter.11.cloned.1.call-done), channel_id=1, source_target_pairs={{16,0},{17,1},{18,2},{19,3},{20,4},{21,5},{22,6},{23,7},{24,8},{25... | collective-permute-start | bytes 995336 | tf_op jit(solution)/shard_map/ppermute | solution.py:1715
  598.5 40.3 %copy-start.1 = (bf16[288,1152]{1,0:T(8,128)(2,1)S(1)}, bf16[288,1152]{1,0:T(8,128)(2,1)}, u32[]{:S(2)}) copy-start(bf16[288,1152]{1,0:T(8,128)(2,1)} %reduce-scatter.5.cloned.1.call-done) | copy-start | bytes 1990660
  598.5 40.3 %copy-start.2 = (bf16[288,1152]{1,0:T(8,128)(2,1)S(1)}, bf16[288,1152]{1,0:T(8,128)(2,1)}, u32[]{:S(2)}) copy-start(bf16[288,1152]{1,0:T(8,128)(2,1)} %reduce-scatter.7.cloned.1.call-done) | copy-start | bytes 1990660
  640.1 1.9 copy-start.12
  640.1 1.8 copy-start.13
  640.1 1.8 copy-start.14
  642.8 1.4 copy-start
  642.8 1.4 copy-start.21
  642.8 1.9 copy-start.16
  642.8 1.9 copy-start.17
  644.7 2.7 copy-start.5
  644.7 2.7 copy-start.6
  644.7 2.7 copy-start.15
  647.4 2.5 slice-start
  650.0 1.6 copy-start.9
  (1 other events, 0.7 us)
Sparse Core Ops, SparseCore 0:
  59.9 54.5 all-gather.7
  116.0 34.0 all-gather.5
  152.3 54.2 all-gather.9
  422.6 31.7 reduce-scatter.10
  456.5 51.5 reduce-scatter.4
  510.3 52.3 reduce-scatter.6
  565.0 33.4 reduce-scatter.8

commit v3 on v2

--- a/solution.py
+++ b/solution.py
@@ -61,6 +61,7 @@
 COST = pl.CostEstimate(flops=20_000_000_000, transcendentals=0, bytes_accessed=100_000_000)
 LOG2E = 1.0 / math.log(2.0)
 TILE = 256
+WIDE = 384
 
 
 class Slab:
@@ -98,13 +99,6 @@
         start = pl.multiple_of((2 * at[1] + at[0]) * self.half_rows, self.half_rows)
         return ref.at[pl.ds(start, self.half_rows)]
 
-    def tile(self, tensor):
-        size = 2 * self.half_rows
-        return pl.ds(pl.multiple_of(tensor * size, size), size)
-
-    def chip_tiles(self, far):
-        return (self.mate_far, self.far) if far else (self.mate_near, self.near)
-
     def greet(self):
         barrier = pltpu.get_barrier_semaphore()
         for peer in (self.first, self.second, self.mate):
@@ -351,17 +345,24 @@
     return jnp.where(live, 0.0, masked_score)
 
 
-def chip_rows(slab, far, compute):
-    first, last = slab.chip_tiles(far)
-    repeat(2, lambda i: compute(slab.tile(first + i * (last - first))))
-
-
-def open_gathers(gathers, fill):
+def chip_rows(slab, far, compute, parts=1):
+    tensor = (slab.far if far else slab.near) - slab.core
+    size = 4 * slab.half_rows // parts
+
+    def one(i):
+        start = tensor * (2 * slab.half_rows) + i * size
+        compute(pl.ds(pl.multiple_of(start, 2 * slab.half_rows), size))
+
+    repeat(parts, one)
+
+
+def open_gathers(gathers, fill, prepare):
     fill(0)
     gathers[0].start()
     fill(1)
     gathers[0].second()
     gathers[1].start()
+    prepare()
     gathers[0].forward()
     gathers[1].second()
 
@@ -460,10 +461,14 @@
             block = rows_ref[m, pl.ds(start, 32)].astype(jnp.float32)
             own[pl.ds(start, 32)] = low(layer_norm(block, vec[0:1], vec[2:3]))
 
-    if not ready:
-        open_gathers(gathers, fill)
-    load.wait()
-    widen(packed, wide)
+    def prepare():
+        load.wait()
+        widen(packed, wide)
+
+    if ready:
+        prepare()
+    else:
+        open_gathers(gathers, fill, prepare)
     keeps = []
 
     def keep(src, dst, i):
@@ -473,11 +478,11 @@
 
     def project(m):
         def block(i):
-            rows = step_rows(i, TILE)
+            rows = step_rows(i, 4 * half_rows)
             out = dot(gathered[m, rows], wide[:, : 3 * pair], 1, 0)
             qkv[m, rows] = low(out + bias)
 
-        repeat(seq // TILE, block)
+        repeat(seq // (4 * half_rows), block)
 
     def attend(m, rows):
         shut = shut_keys(lengths[m], own_rows, 2 * half_rows, (1, seq), 1)
@@ -495,6 +500,8 @@
             lse_ref[m, h, rows] = jnp.broadcast_to(
                 top + jnp.log(total) * LOG2E, (2 * half_rows, LANES)
             )
+
+    def output(m, rows):
         terms[m, rows] = low(dot(mixed[m, rows], wide[:, 3 * pair :], 1, 1))
 
     def close(m):
@@ -515,11 +522,13 @@
     project(0)
     if not ready:
         gathers[1].forward()
-    chip_rows(slab, True, lambda rows: attend(0, rows))
+    chip_rows(slab, True, lambda rows: attend(0, rows), 2)
+    chip_rows(slab, True, lambda rows: output(0, rows))
     scatters[0].mate_far()
     gathered_rows(1)
     scatters[0].far_hop()
-    chip_rows(slab, False, lambda rows: attend(0, rows))
+    chip_rows(slab, False, lambda rows: attend(0, rows), 2)
+    chip_rows(slab, False, lambda rows: output(0, rows))
     scatters[0].mate_near()
     keep(qkv.at[0], qkv_hbm.at[0], 2)
     keep(mixed.at[0], mixed_hbm.at[0], 3)
@@ -528,7 +537,8 @@
     scatters[0].first_hop()
     if ready:
         tiles.pass_on()
-    chip_rows(slab, True, lambda rows: attend(1, rows))
+    chip_rows(slab, True, lambda rows: attend(1, rows), 2)
+    chip_rows(slab, True, lambda rows: output(1, rows))
     scatters[1].mate_far()
     close(0)
     scatters[1].far_hop()
@@ -536,7 +546,8 @@
         tiles.finish()
         for m in range(micro):
             keep(all_grads.at[m], normed_hbm.at[m], m)
-    chip_rows(slab, False, lambda rows: attend(1, rows))
+    chip_rows(slab, False, lambda rows: attend(1, rows), 2)
+    chip_rows(slab, False, lambda rows: output(1, rows))
     scatters[1].mate_near()
     keep(qkv.at[1], qkv_hbm.at[1], 4)
     keep(mixed.at[1], mixed_hbm.at[1], 5)
@@ -574,9 +585,11 @@
             block = hidden_ref[m, pl.ds(start, 32)]
             own[pl.ds(start, 32)] = low(layer_norm(block, vec[1:2], vec[6:7]))
 
-    open_gathers(gathers, fill)
-    load.wait()
-    split_tail(packed, tails, half_ff - ff + LANES)
+    def prepare():
+        load.wait()
+        split_tail(packed, tails, half_ff - ff + LANES)
+
+    open_gathers(gathers, fill, prepare)
     keeps = []
 
     def keep(src, dst, i):
@@ -662,11 +675,13 @@
         for start in range(0, half_rows, 32):
             own[pl.ds(start, 32)] = grad_ref[m, pl.ds(start, 32)]
 
-    open_gathers(gathers, fill)
-    small_ref[...] = jnp.zeros_like(small_ref)
-    up_bias_ref[...] = jnp.zeros_like(up_bias_ref)
-    load_packed.wait()
-    split_tail(packed, tails, extra)
+    def prepare():
+        small_ref[...] = jnp.zeros_like(small_ref)
+        up_bias_ref[...] = jnp.zeros_like(up_bias_ref)
+        load_packed.wait()
+        split_tail(packed, tails, extra)
+
+    open_gathers(gathers, fill, prepare)
 
     def compute(m, rows):
         value = upper[m, rows]
@@ -686,12 +701,12 @@
 
     def weight_grads(first, last):
         def block(i):
-            cols = step_rows(i, LANES)
+            cols = step_rows(i, WIDE)
             up = dot(stacked(second, cols), stacked(grad_upper), 0, 0)
             down = dot(stacked(gathered, cols), stacked(active), 0, 0)
             grads_ref[cols, :main] = low(up[:, :main])
             grads_ref[cols, main : 2 * main] = low(down[:, :main])
-            blank = jnp.zeros((LANES, LANES - 2 * extra), jnp.float32)
+            blank = jnp.zeros((WIDE, LANES - 2 * extra), jnp.float32)
             rest_cols = [up[:, main : main + extra], down[:, main : main + extra], blank]
             grads_ref[cols, 2 * main :] = low(jnp.concatenate(rest_cols, axis=1))
 
@@ -731,7 +746,7 @@
     scatters[1].second_hop()
     for load in load_second:
         load.wait()
-    blocks = width // LANES
+    blocks = width // WIDE
     weight_grads(0, blocks // 3)
     scatters[1].first_hop()
     close(0)
@@ -772,11 +787,13 @@
             block = hidden_ref[m, pl.ds(start, 32)]
             own[pl.ds(start, 32)] = low(layer_norm(block, vec[1:2], vec[6:7]))
 
-    open_gathers(gathers, fill)
-    small_ref[...] = jnp.zeros_like(small_ref)
-    up_bias_ref[...] = jnp.zeros_like(up_bias_ref)
-    load.wait()
-    split_tail(packed, tails, extra)
+    def prepare():
+        small_ref[...] = jnp.zeros_like(small_ref)
+        up_bias_ref[...] = jnp.zeros_like(up_bias_ref)
+        load.wait()
+        split_tail(packed, tails, extra)
+
+    open_gathers(gathers, fill, prepare)
 
     def compute(m, rows):
         value = up_dot(gathered[m, rows], packed, tails) + up_bias[...]
@@ -797,12 +814,12 @@
 
     def weight_grads(first, last):
         def block(i):
-            cols = step_rows(i, LANES)
+            cols = step_rows(i, WIDE)
             up = dot(stacked(gathered, cols), stacked(grad_upper), 0, 0)
             down = dot(stacked(given, cols), stacked(active), 0, 0)
             grads_ref[cols, :main] = low(up[:, :main])
             grads_ref[cols, main : 2 * main] = low(down[:, :main])
-            blank = jnp.zeros((LANES, LANES - 2 * extra), jnp.float32)
+            blank = jnp.zeros((WIDE, LANES - 2 * extra), jnp.float32)
             rest_cols = [up[:, main : main + extra], down[:, main : main + extra], blank]
             grads_ref[cols, 2 * main :] = low(jnp.concatenate(rest_cols, axis=1))
 
@@ -839,24 +856,25 @@
     gathers[1].to_mate()
     backs[0].second_hop()
     gathers[1].finish()
+    scatters[0].far_hop()
+    scatters[0].second_hop()
     loads[1].wait()
     chip_rows(slab, True, lambda rows: compute(1, rows))
     backs[1].mate_far()
     scatters[1].mate_far()
     backs[0].first_hop()
     backs[1].far_hop()
+    scatters[0].first_hop()
     chip_rows(slab, False, lambda rows: compute(1, rows))
     backs[1].mate_near()
     scatters[1].mate_near()
     backs[1].second_hop()
-    for scatter in scatters:
-        scatter.far_hop()
-        scatter.second_hop()
-    blocks = width // LANES
+    scatters[1].far_hop()
+    scatters[1].second_hop()
+    blocks = width // WIDE
     weight_grads(0, blocks // 3)
     backs[1].first_hop()
-    for scatter in scatters:
-        scatter.first_hop()
+    scatters[1].first_hop()
     close_back(0)
     weight_grads(blocks // 3, blocks)
     close_back(1)
@@ -865,15 +883,16 @@
 
 
 def attn_backward_kernel(
-    at, layer, own_rows, grad_ref, rows_ref, vectors, lse, lengths, normed_hbm, qkv_hbm, mixed_hbm, packed_hbm,
-    out_ref, grads_ref, small_ref, bias_ref, *rest
+    at, layer, own_rows, both_ways, grad_ref, rows_ref, vectors, lse, lengths,
+    normed_hbm, qkv_hbm, mixed_hbm, packed_hbm, errand_hbm,
+    out_ref, grads_ref, small_ref, bias_ref, errand_got, *rest
 ):
     micro, half_rows, width = grad_ref.shape
     gathered, gather_refs = rest[0], rest[0:3]
     scatter_refs = rest[3:9]
     terms = rest[3]
     packed, wide, normed, qkv, mixed, grad_mixed, grad_qkv, turned, shut = rest[9:18]
-    low_probs, grad_scores, load_sems = rest[18:]
+    low_probs, grad_scores, high_probs, errand_sems, load_sems = rest[18:]
     vec = vectors.at[layer]
     seq, pair = mixed.shape[1:]
     heads = pair // LANES
@@ -900,41 +919,61 @@
         for start in range(0, half_rows, 32):
             own[pl.ds(start, 32)] = low(grad_ref[m, pl.ds(start, 32)])
 
-    open_gathers(gathers, fill)
-    small_ref[...] = jnp.zeros_like(small_ref)
-    bias_ref[...] = jnp.zeros_like(bias_ref)
-    load_packed.wait()
-    widen(packed, wide)
-
     def head(h, part=0):
         return slice(part * pair + h * LANES, part * pair + (h + 1) * LANES)
 
-    for m in range(micro):
+    def ready_qkv(m):
         load_qkv[m].wait()
-        shut[m] = shut_keys(lengths[m], own_rows, 2 * half_rows, (seq, LANES), 0)
+        shut[...] = shut_keys(lengths[m], own_rows, 2 * half_rows, (seq, LANES), 0)
         for h in range(heads):
             turned[m, h] = low(qkv[m, :, head(h, 1)].astype(jnp.float32).T)
 
+    def find_probs(m, h):
+        def block(i):
+            rows = step_rows(i, TILE)
+            keys, queries = qkv[m, :, head(h, 1)], qkv[m, rows, head(h)]
+            closed = jnp.concatenate([shut[...]] * (TILE // LANES), axis=1)
+            scores = dot(keys, queries, 1, 1) * (score_scale * LOG2E) + closed
+            high_probs[m, h, :, rows] = jnp.exp2(scores - lse[m, h, rows].T[0:1])
+
+        repeat(seq // TILE, block)
+
+    errand = remote(
+        errand_hbm,
+        errand_got,
+        errand_sems.at[0],
+        errand_sems.at[1],
+        {"section": 1 - lax.axis_index("section")},
+    )
+    sends_errand = (lax.axis_index("section") == 0) | both_ways
+    gets_errand = (lax.axis_index("section") == 1) | both_ways
+
+    def prepare():
+        small_ref[...] = jnp.zeros_like(small_ref)
+        bias_ref[...] = jnp.zeros_like(bias_ref)
+        ready_qkv(0)
+        find_probs(0, 0)
+
+    open_gathers(gathers, fill, prepare)
+
     def mix_grads(m):
         def block(i):
-            rows = step_rows(i, TILE)
+            rows = step_rows(i, 4 * half_rows)
             grad_mixed[m, rows] = low(dot(gathered[m, rows], wide[:, 3 * pair :], 1, 0))
 
-        repeat(seq // TILE, block)
+        repeat(seq // (4 * half_rows), block)
 
     def attend(m, h):
         def block(i):
-            rows = step_rows(i, LANES)
-            queries = qkv[m, rows, head(h)]
+            rows = step_rows(i, TILE)
             grads = grad_mixed[m, rows, head(h)]
-            scores = dot(qkv[m, :, head(h, 1)], queries, 1, 1) * (score_scale * LOG2E) + shut[m]
-            probs = jnp.exp2(scores - lse[m, h, rows].T[0:1])
+            probs = high_probs[m, h, :, rows]
             grad_probs = dot(qkv[m, :, head(h, 2)], grads, 1, 1)
             inner = jnp.sum(grad_probs * probs, axis=0, keepdims=True)
             low_probs[:, rows] = low(probs)
             grad_scores[:, rows] = low(probs * (grad_probs - inner))
 
-        repeat(seq // LANES, block)
+        repeat(seq // TILE, block)
         grad_keys = dot(grad_scores[...], qkv[m, :, head(h)], 1, 0)
         grad_qkv[m, :, head(h, 1)] = low(grad_keys * score_scale)
         grad_qkv[m, :, head(h, 2)] = low(dot(low_probs[...], grad_mixed[m, :, head(h)], 1, 0))
@@ -953,7 +992,7 @@
 
     def weight_grads(first, last):
         def block(i):
-            cols = step_rows(i, LANES)
+            cols = step_rows(i, WIDE)
             front = dot(stacked(normed, cols), stacked(grad_qkv), 0, 0)
             back = dot(stacked(gathered, cols), stacked(mixed), 0, 0)
             total = low(jnp.concatenate([front, back], axis=1))
@@ -973,22 +1012,35 @@
             for j, item in enumerate((gain_terms, grad_normed)):
                 small_ref[j : j + 1] += jnp.sum(item, axis=0, keepdims=True)
 
+    load_packed.wait()
+    widen(packed, wide)
+    gathers[1].forward()
     gathers[0].to_mate()
+
+    @pl.when(sends_errand)
+    def _():
+        errand.start()
+
+    for h in range(1, heads):
+        find_probs(0, h)
     gathers[0].finish()
     mix_grads(0)
     attend(0, 0)
-    gathers[1].forward()
+    gathers[1].to_mate()
     for h in range(1, heads):
         attend(0, h)
-    gathers[1].to_mate()
     chip_rows(slab, True, lambda rows: back_project(0, rows))
     scatters[0].mate_far()
+    ready_qkv(1)
+    find_probs(1, 0)
     scatters[0].far_hop()
     chip_rows(slab, False, lambda rows: back_project(0, rows))
     scatters[0].mate_near()
     gathers[1].finish()
+    mix_grads(1)
     scatters[0].second_hop()
-    mix_grads(1)
+    for h in range(1, heads):
+        find_probs(1, h)
     scatters[0].first_hop()
     for h in range(heads):
         attend(1, h)
@@ -1001,11 +1053,19 @@
     scatters[1].second_hop()
     for load in load_rest:
         load.wait()
-    blocks = width // LANES
+    blocks = width // WIDE
     weight_grads(0, blocks // 3)
     scatters[1].first_hop()
     weight_grads(blocks // 3, blocks)
     close(1)
+
+    @pl.when(sends_errand)
+    def _():
+        errand.wait_send()
+
+    @pl.when(gets_errand)
+    def _():
+        errand.wait_recv()
 
 
 def any_spec():
@@ -1177,22 +1237,25 @@
     return grad_hidden, grads, small, up_bias[:1]
 
 
-def attn_backward(grad_hidden, rows_low, kept, vectors, packed, at, layer, lengths, own_rows):
+def attn_backward(
+    grad_hidden, rows_low, kept, vectors, packed, at, layer, lengths, own_rows, errand, both_ways
+):
     normed, qkv, lse, mixed = kept
     micro, half_rows, width = grad_hidden.shape
     seq, pair = mixed.shape[1:]
     heads = pair // LANES
     low_type, high_type = jnp.bfloat16, jnp.float32
-    out, grads, small, bias = pl.pallas_call(
-        functools.partial(attn_backward_kernel, at, layer, own_rows),
+    out, grads, small, bias, got = pl.pallas_call(
+        functools.partial(attn_backward_kernel, at, layer, own_rows, both_ways),
         out_shape=[
             shape_of((micro, half_rows, width), low_type),
             shape_of((width, 4 * heads * HEAD), low_type),
             shape_of((8, width), high_type),
             shape_of((8, pair), high_type),
+            shape_of(errand.shape, errand.dtype),
         ],
-        in_specs=[vmem_spec()] * 4 + [smem_spec()] + [any_spec()] * 4,
-        out_specs=[vmem_spec()] * 4,
+        in_specs=[vmem_spec()] * 4 + [smem_spec()] + [any_spec()] * 5,
+        out_specs=[vmem_spec()] * 4 + [any_spec()],
         scratch_shapes=gather_scratch(micro, seq, width)
         + scatter_scratch(micro, seq, half_rows, width)
         + [
@@ -1204,16 +1267,18 @@
             pltpu.VMEM((micro, seq, pair), low_type),
             pltpu.VMEM((micro, seq, 3 * pair), low_type),
             pltpu.VMEM((micro, heads, LANES, seq), low_type),
-            pltpu.VMEM((micro, seq, LANES), high_type),
+            pltpu.VMEM((seq, LANES), high_type),
             pltpu.VMEM((seq, seq), low_type),
             pltpu.VMEM((seq, seq), low_type),
+            pltpu.VMEM((micro, heads, seq, seq), high_type),
+            pltpu.SemaphoreType.DMA((2,)),
             pltpu.SemaphoreType.DMA((1 + 3 * micro,)),
         ],
         compiler_params=params(3 + 5 * layer),
         cost_estimate=COST,
         name="attn_backward",
-    )(grad_hidden, rows_low, vectors, lse, lengths, normed, qkv, mixed, packed)
-    return out, grads, small, bias
+    )(grad_hidden, rows_low, vectors, lse, lengths, normed, qkv, mixed, packed, errand)
+    return out, grads, small, bias, got
 
 
 def slab_peers():
@@ -1258,7 +1323,7 @@
 
 def prologue_kernel(
     count, heads, qkv_ref, out_ref_t, up_ref_in, down_ref_t, gains_ref, shifts_ref, up_bias, rows_ref,
-    first_hbm, normed_hbm, attn_ref, ff_hbm, out_ref, up_ref, bias_ref,
+    first_hbm, normed_hbm, attn_ref, ff_zero_hbm, ff_one_hbm, out_ref, up_ref, bias_ref,
     attn_parts, ff_parts, up_halves, mine_ref, all_rows, line, ff_line, column, slab, up_got,
     rows_send, rows_recv, column_send, column_recv, slab_send, slab_recv, swap_send, swap_recv,
     right_send, right_recv, left_send, left_recv, out_sems,
@@ -1343,14 +1408,6 @@
             for way in (1, -1):
                 hop(step, p, way)
 
-    for p in range(pieces):
-
-        @pl.when(section == 1)
-        def _():
-            swapped(p)
-
-        for way in (1, -1):
-            hop(0, p, way)
     for step, _, source in column_peers(count):
         slot = column.at[source]
         remote(slot, slot, column_send.at[step], column_recv.at[step], {"dp": source}).wait_recv()
@@ -1361,6 +1418,14 @@
         copy.start()
         sent.append(copy)
     slab[section, tensor] = column[...]
+    for p in range(pieces):
+
+        @pl.when(section == 1)
+        def _():
+            swapped(p)
+
+        for way in (1, -1):
+            hop(0, p, way)
     blank = jnp.zeros((rows, LANES - 2 * extra), jnp.bfloat16)
     up_halves[...] = jnp.zeros_like(up_halves)
     for half in range(2):
@@ -1423,8 +1488,17 @@
         copy.start()
         outs.append(copy)
 
-    ff_line_out = ff_hbm.at[section]
-    put(ff_parts.at[section], ff_line_out, count)
+    def put_ff(src, section_of_first, i):
+        for layer, dst in enumerate((ff_zero_hbm, ff_one_hbm)):
+            here_too = layer if section_of_first == 0 else 1 - layer
+
+            @pl.when(section == here_too)
+            def _():
+                pltpu.make_async_copy(src, dst, out_sems.at[i]).start()
+
+        outs.append(pltpu.make_async_copy(src, ff_zero_hbm, out_sems.at[i]))
+
+    put_ff(ff_parts.at[section], 0, count)
     for step in range(2, count):
         hops(step)
         if step == 2:
@@ -1447,7 +1521,7 @@
     put(all_rows, normed_hbm, count + 2)
     ff_got = ff_line.at[1 - section]
     remote(ff_got, ff_got, swap_send.at[pieces], swap_recv.at[pieces], other).wait_recv()
-    put(ff_got, ff_hbm.at[1 - section], count + 1)
+    put_ff(ff_got, 1, count + 1)
     for step in range(count):
         for p in range(pieces):
             for way in (1, -1):
@@ -1477,13 +1551,14 @@
             shape_of((count * part_rows, attn_shape[1]), low_type),
             shape_of(all_rows, low_type),
             shape_of(attn_shape, low_type),
-            shape_of(ff_shape, low_type),
+            shape_of(ff_shape[1:], low_type),
+            shape_of(ff_shape[1:], low_type),
             shape_of((2, vector_rows, width), high_type),
             shape_of((2, 1, ff_wide), high_type),
             shape_of((2, 1, 3 * heads * LANES), high_type),
         ],
         in_specs=[vmem_spec()] * 8,
-        out_specs=[any_spec()] * 2 + [vmem_spec(), any_spec()] + [vmem_spec()] * 3,
+        out_specs=[any_spec()] * 2 + [vmem_spec()] + [any_spec()] * 2 + [vmem_spec()] * 3,
         scratch_shapes=[
             pltpu.VMEM((2,) + attn_shape, low_type),
             pltpu.VMEM(ff_shape, low_type),
@@ -1517,7 +1592,7 @@
 
 def home_kernel(
     count, chunk, attn_zero, attn_one, ff_zero, ff_one, biases_in, ups_in,
-    ff_sums_hbm, attn_sum_hbm, rows_hbm,
+    ff_sum_hbm, attn_sum_hbm, rows_hbm,
     out_ref, up_ref, ff_got_hbm, attn_got_hbm, rows_got_hbm,
     parts, ups, slab, column, up_pair, up_column, total,
     column_send, column_recv, slab_send, slab_recv, up_sems, up_column_send, up_column_recv, far_send, far_recv,
@@ -1553,6 +1628,13 @@
         send(
             parts.at[to[0], to[1]], slab.at[role], slab_send.at[role], slab_recv.at[role], named(to)
         )
+    far_rows = remote(rows_hbm, rows_got_hbm, far_send.at[0], far_recv.at[0], other)
+    far_ff = remote(ff_sum_hbm, ff_got_hbm, far_send.at[1], far_recv.at[1], other)
+    far_attn = remote(attn_sum_hbm, attn_got_hbm, far_send.at[2], far_recv.at[2], other)
+    one_way = ((far_ff, 1), (far_attn, 0))
+    far_rows.start()
+    for copy, source in one_way:
+        pl.when(section == source)(copy.start)
     up_pair[section] = ups[section]
     value = parts[section, tensor]
     for role, _, source in slab_peers():
@@ -1568,17 +1650,6 @@
         send(
             up_pair, up_column.at[here], up_column_send.at[step], up_column_recv.at[step], {"dp": to}
         )
-    far = (
-        (ff_sums_hbm.at[1 - section], ff_got_hbm),
-        (rows_hbm.at[1 - section], rows_got_hbm),
-    )
-    for k, (src, dst) in enumerate(far):
-        send(src, dst, far_send.at[k], far_recv.at[k], other)
-
-    @pl.when(section == 0)
-    def _():
-        remote(attn_sum_hbm, attn_got_hbm, far_send.at[2], far_recv.at[2], other).start()
-
     up_column[here] = up_pair[...]
     result = total[here]
     for step, _, source in column_peers(count):
@@ -1595,23 +1666,15 @@
     for at in range(1, count):
         value = value + up_column[at]
     up_ref[...] = value
-    for k, (_, dst) in enumerate(far):
-        remote(dst, dst, far_send.at[k], far_recv.at[k], other).wait_recv()
-    last = remote(attn_sum_hbm, attn_got_hbm, far_send.at[2], far_recv.at[2], other)
-
-    @pl.when(section == 0)
-    def _():
-        last.wait_send()
-
-    @pl.when(section == 1)
-    def _():
-        last.wait_recv()
-
+    far_rows.wait()
+    for copy, source in one_way:
+        pl.when(section == source)(copy.wait_send)
+        pl.when(section != source)(copy.wait_recv)
     for copy in sent:
         copy.wait_send()
 
 
-def home(attn_small, ff_small, bias_grads, up_grads, ff_sums, attn_sum, rows, count, chunk):
+def home(attn_small, ff_small, bias_grads, up_grads, ff_sum, attn_sum, rows, count, chunk):
     vector_rows, lanes = 8, LANES
     up_shape = up_grads.shape[1:]
     dma = pltpu.SemaphoreType.DMA
@@ -1621,9 +1684,9 @@
         out_shape=[
             shape_of((vector_rows, lanes), high_type),
             shape_of((2,) + up_shape, high_type),
-            shape_of(ff_sums.shape[1:], ff_sums.dtype),
+            shape_of(ff_sum.shape, ff_sum.dtype),
             shape_of(attn_sum.shape, attn_sum.dtype),
-            shape_of(rows.shape[1:], rows.dtype),
+            shape_of(rows.shape, rows.dtype),
         ],
         in_specs=[vmem_spec()] * 6 + [any_spec()] * 3,
         out_specs=[vmem_spec()] * 2 + [any_spec()] * 3,
@@ -1648,7 +1711,96 @@
         compiler_params=params(5),
         cost_estimate=COST,
         name="home",
-    )(*attn_small, *ff_small, bias_grads, up_grads, ff_sums, attn_sum, rows)
+    )(*attn_small, *ff_small, bias_grads, up_grads, ff_sum, attn_sum, rows)
+
+
+def finish_kernel(
+    ff_zero, ff_one, ff_zero_got, ff_one_got, attn_zero, attn_one, attn_one_got,
+    qkv_ref, out_ref, up_ref, down_ref, attn_zero_got, send_sem, recv_sem,
+):
+    section = lax.axis_index("section")
+    first = section == 0
+    other = {"section": 1 - section}
+    barrier = pltpu.get_barrier_semaphore()
+    pl.semaphore_signal(barrier, inc=1, device_id=other, device_id_type=MESH)
+    pl.semaphore_wait(barrier, 1)
+    copy = remote(attn_zero, attn_zero_got, send_sem, recv_sem, other)
+
+    @pl.when(section == 1)
+    def _():
+        copy.start()
+        attn_zero_got[...] = attn_zero[...]
+
+    rows = up_ref.shape[0]
+    half_ff = up_ref.shape[1] // 2
+    main = half_ff // LANES * LANES
+    extra = half_ff - main
+    pair_cols = qkv_ref.shape[2] // 2
+    size = 96 if rows % 96 == 0 else rows
+
+    def ff_block(i):
+        at = step_rows(i, size)
+        halves = (
+            jnp.where(first, ff_zero[at], ff_one_got[at]),
+            jnp.where(first, ff_zero_got[at], ff_one[at]),
+        )
+        for k, ref in enumerate((up_ref, down_ref)):
+            pieces = []
+            for half in halves:
+                start = 2 * main + k * extra
+                pieces += [half[:, k * main : (k + 1) * main], half[:, start : start + extra]]
+            ref[at] = jnp.concatenate(pieces, axis=1).astype(jnp.float32)
+
+    repeat(rows // size, ff_block)
+
+    @pl.when(first)
+    def _():
+        copy.wait_recv()
+
+    def attn_block(i):
+        at = step_rows(i, size)
+        halves = (
+            jnp.where(first, attn_zero[at], attn_one_got[at]),
+            jnp.where(first, attn_zero_got[at], attn_one[at]),
+        )
+        for k in range(4):
+            span = slice(k * pair_cols, (k + 1) * pair_cols)
+            whole = jnp.concatenate([half[:, span] for half in halves], axis=1)
+            whole = whole.astype(jnp.float32)
+            if k < 3:
+                qkv_ref[k, at] = whole
+            else:
+                out_ref[at] = whole
+
+    repeat(rows // size, attn_block)
+
+    @pl.when(section == 1)
+    def _():
+        copy.wait_send()
+
+
+def finish(ff_sums, ff_got, attn_sums, attn_got, head_cols, ff_cols):
+    rows = ff_sums[0].shape[0]
+    high_type = jnp.float32
+    return pl.pallas_call(
+        finish_kernel,
+        out_shape=[
+            shape_of((3, rows, head_cols), high_type),
+            shape_of((rows, head_cols), high_type),
+            shape_of((rows, ff_cols), high_type),
+            shape_of((rows, ff_cols), high_type),
+        ],
+        in_specs=[vmem_spec()] * 7,
+        out_specs=[vmem_spec()] * 4,
+        scratch_shapes=[
+            pltpu.VMEM(attn_sums[0].shape, attn_sums[0].dtype),
+            pltpu.SemaphoreType.DMA,
+            pltpu.SemaphoreType.DMA,
+        ],
+        compiler_params=params(9),
+        cost_estimate=COST,
+        name="finish",
+    )(*ff_sums, *ff_got, *attn_sums, attn_got)
 
 
 def shards(
@@ -1677,11 +1829,9 @@
     def by_layer(mine, other):
         return [jnp.where(here == 0, mine, other), jnp.where(here == 0, other, mine)]
 
-    part_rows = qkv_weight.shape[2]
     count = lax.axis_size("dp")
     chunk = norm_gains.shape[2]
-    main = half_ff // LANES * LANES
-    first, normed, attn_part, ff_two, vectors, up_biases, bias_qv = prologue(
+    first, normed, attn_part, ff_zero, ff_one, vectors, up_biases, bias_qv = prologue(
         qkv_weight[0],
         out_weight[0].T,
         up_weight[0],
@@ -1698,9 +1848,9 @@
     def gather_column(part):
         return lax.all_gather(part, "dp", axis=0, tiled=True)
 
-    ff_first = gather_column(ff_two[0])
+    ff_first = gather_column(ff_zero)
     attn_packed = [(first, 0), (gather_column(attn_part), 0)]
-    ff_packed = [(ff_first, 0), (gather_column(ff_two[1]), 0)]
+    ff_packed = [(ff_first, 0), (gather_column(ff_one), 0)]
     lengths_here = lengths.reshape(micro)
 
     def my_rows(value):
@@ -1710,9 +1860,6 @@
     def whole_rows(first, second, got):
         low_half, high_half = by_layer(jnp.where(here == 0, first, second), got)
         return jnp.concatenate([low_half, high_half], 1)[:, None, :own_rows]
-
-    def send_home(value, layer):
-        return lax.ppermute(value, "section", [(1 - layer, layer)])
 
     rows = my_rows(section_input)
     inputs, hiddens, attn_kept = [], [], []
@@ -1729,7 +1876,7 @@
             rows, ff_kept = ffn_forward(hidden, vectors, up_biases, *ff_packed[0], 0, half_ff)
 
     attn_sums, ff_sums, up_sums, input_grads = {}, {}, {}, {}
-    attn_small, ff_small, bias_grads = {}, {}, {}
+    attn_small, ff_small, bias_grads, errands = {}, {}, {}, {}
     for layer in (1, 0):
         if layer == 1:
             last, grad_hidden, ff_grad, ff_small[1], up_sums[1] = ffn_turn(
@@ -1747,7 +1894,11 @@
                 grads, hiddens[0], ff_kept, vectors, *ff_packed[0], 0, half_ff
             )
         ff_sums[layer] = lax.psum_scatter(ff_grad, "dp", scatter_dimension=0, tiled=True)
-        grads, attn_grad, attn_small[layer], bias_grads[layer] = attn_backward(
+        if layer == 1:
+            errand, both_ways = jnp.where(here == 0, last, rows), True
+        else:
+            errand, both_ways = ff_sums[1], False
+        grads, attn_grad, attn_small[layer], bias_grads[layer], got = attn_backward(
             grad_hidden,
             inputs[layer],
             attn_kept[layer],
@@ -1756,20 +1907,22 @@
             layer,
             lengths_here,
             own_rows,
+            errand,
+            both_ways,
         )
+        errands[layer] = got
         attn_sums[layer] = lax.psum_scatter(attn_grad, "dp", scatter_dimension=0, tiled=True)
         input_grads[layer] = grads
 
-    out_got = [send_home(rows, 0), send_home(last, 1)]
-    section_output = whole_rows(rows, last, jnp.where(here == 0, out_got[0], out_got[1]))
+    section_output = whole_rows(rows, last, errands[1])
     small_mine, up_total, ff_got, attn_got, rows_got = home(
         [attn_small[0], attn_small[1]],
         [ff_small[0], ff_small[1]],
         jnp.stack([bias_grads[0], bias_grads[1]]),
         jnp.stack([up_sums[0], up_sums[1]]),
-        jnp.stack([ff_sums[0], ff_sums[1]]),
+        ff_sums[0],
         attn_sums[1],
-        jnp.stack([input_grads[0], input_grads[1]]),
+        jnp.where(here == 0, input_grads[1], input_grads[0]),
         count,
         chunk,
     )
@@ -1777,34 +1930,22 @@
     up_total = up_total[:, :, :half_ff].reshape(1, ff_cols)
     input_grad = whole_rows(input_grads[0], input_grads[1], rows_got)
 
-    def own_layer(sums, got):
-        return by_layer(jnp.where(here == 0, sums[0], sums[1]), got)
-
-    attn_got = jnp.where(here == 0, send_home(attn_sums[0], 0), attn_got)
-    attn_total = jnp.stack(own_layer(attn_sums, attn_got), 1).astype(jnp.float32)
-    attn_total = attn_total.reshape(part_rows, sections, 4, pair_cols)
-    attn_total = jnp.moveaxis(attn_total, 2, 0).reshape(4, part_rows, head_cols)
-    ff_halves = own_layer(ff_sums, ff_got)
-    rest_cols = half_ff - main
-
-    def ff_piece(index):
-        pieces = []
-        for half in ff_halves:
-            pieces.append(half[:, index * main : (index + 1) * main])
-            start = 2 * main + index * rest_cols
-            pieces.append(half[:, start : start + rest_cols])
-        return jnp.concatenate(pieces, 1).astype(jnp.float32)
-
-    ff_total = [ff_piece(0), ff_piece(1)]
-
+    qkv_total, out_total, up_grad, down_grad = finish(
+        [ff_sums[0], ff_sums[1]],
+        [ff_got, errands[0]],
+        [attn_sums[0], attn_sums[1]],
+        attn_got,
+        head_cols,
+        ff_cols,
+    )
     gains = norm_gains.shape[1]
     return (
         section_output[None],
         input_grad[None],
-        attn_total[None, :3],
-        attn_total[3].T[None],
-        ff_total[0][None],
-        ff_total[1].T[None],
+        qkv_total[None],
+        out_total.T[None],
+        up_grad[None],
+        down_grad.T[None],
         small_mine[:, :gains],
         small_mine[:, gains:],
         up_total,

time: 664 us -> 497 us (0.75)
  waiting for transfers between devices: 168 us -> 7.8 us
  starting transfers between devices: 7.91 us -> 0.28 us
    reduce_scatter x2, waiting for transfers between devices: 107 us -> 0.01 us  [shards(): lax.psum_scatter(ff_grad, 'dp', scatter_dimension=0, tiled=True)]
    reduce_scatter x2, waiting for transfers between devices: 47.4 us -> 0.01 us  [shards(): lax.psum_scatter(attn_grad, 'dp', scatter_dimension=0, tiled=True)]
    pallas_call x0 -> x1, Pallas kernels: none -> 14.6 us  [finish(): pl.pallas_call(finish_kernel, out_shape=[shape_of((3, rows, head_cols), h...]
    pallas_call x1, Pallas kernels: 40.3 us -> 31.1 us  [home(): pl.pallas_call(functools.partial(home_kernel, count, chunk), out_shape=[s...]
    ppermute x3 -> x0, starting transfers between devices: 7.17 us -> none  [send_home(): return lax.ppermute(value, 'section', [(1 - layer, layer)])]
  transfers between devices with their start and end apart: 10 -> 7, of which waited for: 7 -> 2; matrix products, arithmetic and copies ran while one was open for 2% -> 3% of each run, Pallas kernels for 27% -> 65%
where the time goes in v3:
time: 497 us; the launch traced here: 489 us
  Pallas kernels  442 us (89%)
  local copies, waits for them, and re-layouts  17.9 us (4%)
  between operations  14.8 us (3%)
  waiting for transfers between devices  7.8 us (2%)
  other arithmetic  6.02 us (1%)
    pallas_call x2, Pallas kernels, attn_backward(): pl.pallas_call(functools.partial(attn_backward_kernel, at, layer, own_row...  110 us
    pallas_call x2, Pallas kernels, attn_forward(): pl.pallas_call(functools.partial(attn_forward_kernel, given is not None,...  95.8 us
    pallas_call x1, Pallas kernels, ffn_turn(): pl.pallas_call(functools.partial(ffn_turn_kernel, half_ff, at, layer), ou...  63.9 us
    pallas_call x1, Pallas kernels, prologue(): pl.pallas_call(functools.partial(prologue_kernel, count, heads), out_shap...  44.8 us
    pallas_call x1, Pallas kernels, ffn_backward(): pl.pallas_call(functools.partial(ffn_backward_kernel, half_ff, at, layer)...  41.4 us
    pallas_call x1, Pallas kernels, ffn_forward(): pl.pallas_call(functools.partial(ffn_forward_kernel, half_ff, at, layer),...  41 us
    pallas_call x1, Pallas kernels, home(): pl.pallas_call(functools.partial(home_kernel, count, chunk), out_shape=[s...  31.1 us
    pallas_call x1, Pallas kernels, finish(): pl.pallas_call(finish_kernel, out_shape=[shape_of((3, rows, head_cols), h...  14.6 us
  transfers between devices with their start and end apart: 7, of which 2 were waited for; matrix products, arithmetic and copies ran while one was open for 3% of the time, Pallas kernels for 65%

profile of v3, /device:TPU:0, one launch (start us, length us, event | category | flops | bytes accessed | tf_op | source)
XLA Modules:
  0.0 489.1 jit_solution(14777600669077446149)
XLA Ops:
  7.2 1.3 copy.26
  8.5 1.8 copy.19
  10.3 44.8 %prologue.1 = (bf16[1152,576]{1,0:T(8,128)(2,1)}, bf16[2,768,1152]{2,1,0:T(8,128)(2,1)}, bf16[288,576]{1,0:T(8,128)(2,1)}, bf16[288,1152]{1,0:T(8,128)(2,1)}, bf...) custom-call(bf16[3,288,288]{2,1,0:T(8,128)(2,1)} %bitcast.51, ...), custom_call_target="tpu_custom_call" | custom-call | flops 20000000000 | bytes 100000000 | tf_op jit(solution)/shard_map/prologue/pallas_call | solution.py:1548
  55.2 0.7 all-gather.6.cloned.1.call-update
  56.7 0.8 pad_dynamic-slice_fusion.1.rows_ref
  57.5 47.1 %attn_forward.2 = (f32[2,96,1152]{2,1,0:T(8,128)}, f32[2,2,768,128]{3,2,1,0:T(8,128)}, bf16[2,768,1152]{2,1,0:T(8,128)(2,1)}, bf16[2,768,768]{2,1,0:T(8,128)(2,1)}, bf16[2,768,256]{2,1,0:T(8,128)(2,1)}) custom-call(bf16[2,96,1152]{2,1,0:T(8,128)(2,1)} %pad_dynamic-slice_fusion.1.rows_ref, f32[2,8,1152]{2,1,0:T(8,128)} %get-tuple-element.58.vectors, ...), custom_call_target="tpu_custom_call" | custom-call | flops 20000000000 | bytes 100000000 | tf_op jit(solution)/shard_map/attn_forward/pallas_call | solution.py:1099
  104.6 0.8 pad_dynamic-slice_fusion.grad_ref
  105.5 4.5 all-gather.4.cloned.1.call-done.packed_hbm
  109.9 41.0 %ffn_forward.1 = (bf16[2,96,1152]{2,1,0:T(8,128)(2,1)}, bf16[2,768,1152]{2,1,0:T(8,128)(2,1)}, f32[2,768,640]{2,1,0:T(8,128)}) custom-call(f32[2,96,1152]{2,1,0:T(8,128)} %get-tuple-element.62.hidden_ref, f32[2,8,1152]{2,1,0:T(8,128)} %get-tuple-element.58.vectors, f32[2,1,640]{2,1,0:T(1,128)} %get-tuple-element.63.up_biases, ...), custom_call_target="tpu_custom_call" | custom-call | flops 20000000000 | bytes 100000000 | tf_op jit(solution)/shard_map/ffn_forward/pallas_call | solution.py:1147
  150.9 48.7 %attn_forward.3 = (f32[2,96,1152]{2,1,0:T(8,128)}, f32[2,2,768,128]{3,2,1,0:T(8,128)}, bf16[2,768,1152]{2,1,0:T(8,128)(2,1)}, bf16[2,768,768]{2,1,0:T(8,128)(2,1)}, bf16[2,768,256]{2,1,0:T(8,128)(2,1)}) custom-call(bf16[2,96,1152]{2,1,0:T(8,128)(2,1)} %get-tuple-element.65.rows_ref.grads_ref, f32[2,8,1152]{2,1,0:T(8,128)} %get-tuple-element.58.vectors, ...), custom_call_target="tpu_custom_call" | custom-call | flops 20000000000 | bytes 100000000 | tf_op jit(solution)/shard_map/attn_forward/pallas_call | solution.py:1099
  199.6 1.8 all-gather.8.cloned.1.call-done.packed_hbm
  201.5 63.9 %ffn_turn.1 = (bf16[2,96,1152]{2,1,0:T(8,128)(2,1)}, f32[2,96,1152]{2,1,0:T(8,128)}, bf16[1152,1152]{1,0:T(8,128)(2,1)}, f32[8,1152]{1,0:T(8,128)}, f32[8,640]{1,0:T(8,128)}) custom-call(f32[2,96,1152]{2,1,0:T(8,128)} %get-tuple-element.67.hidden_ref, bf16[2,96,1152]{2,1,0:T(8,128)(2,1)} %pad_dynamic-slice_fusion.grad_ref, ...), custom_call_target="tpu_custom_call" | custom-call | flops 20000000000 | bytes 100000000 | tf_op jit(solution)/shard_map/ffn_turn/pallas_call | solution.py:1177
  265.5 0.9 copy-done.1
  266.5 0.8 broadcast_select_fusion.6.errand_hbm
  267.3 51.1 %attn_backward.2 = (bf16[2,96,1152]{2,1,0:T(8,128)(2,1)}, bf16[1152,576]{1,0:T(8,128)(2,1)}, f32[8,1152]{1,0:T(8,128)}, f32[8,256]{1,0:T(8,128)}, bf16[2,96,1152]{2,1,0:T(8,128)(2,1)}) custom-call(f32[2,96,1152]{2,1,0:T(8,128)} %get-tuple-element.71.grad_ref, bf16[2,96,1152]{2,1,0:T(8,128)(2,1)} %get-tuple-element.65.rows_ref.grads_ref, ...), custom_call_target="tpu_custom_call" | custom-call | flops 20000000000 | bytes 100000000 | tf_op jit(solution)/shard_map/attn_backward/pallas_call | solution.py:1248
  318.5 41.4 %ffn_backward.1 = (f32[2,96,1152]{2,1,0:T(8,128)}, bf16[1152,1152]{1,0:T(8,128)(2,1)}, f32[8,1152]{1,0:T(8,128)}, f32[8,640]{1,0:T(8,128)}) custom-call(bf16[2,96,1152]{2,1,0:T(8,128)(2,1)} %get-tuple-element.77.grad_ref, f32[2,96,1152]{2,1,0:T(8,128)} %get-tuple-element.62.hidden_ref, f32[2,8,1152]{2,1,0:T(8,128)} %get-tuple-element.58.vectors, ...), custom_call_target="tpu_custom_call" | custom-call | flops 20000000000 | bytes 100000000 | tf_op jit(solution)/shard_map/ffn_backward/pallas_call | solution.py:1212
  360.1 0.8 slice_bitcast_fusion.1
  360.9 0.7 slice_bitcast_fusion.2
  362.3 1.0 fusion.1
  363.3 58.6 %attn_backward.3 = (bf16[2,96,1152]{2,1,0:T(8,128)(2,1)}, bf16[1152,576]{1,0:T(8,128)(2,1)}, f32[8,1152]{1,0:T(8,128)}, f32[8,256]{1,0:T(8,128)}, bf16[288,1152]{1,0:T(8,128)(2,1)}) custom-call(f32[2,96,1152]{2,1,0:T(8,128)} %get-tuple-element.80.grad_ref, bf16[2,96,1152]{2,1,0:T(8,128)(2,1)} %pad_dynamic-slice_fusion.1.rows_ref, ...), custom_call_target="tpu_custom_call" | custom-call | flops 20000000000 | bytes 100000000 | tf_op jit(solution)/shard_map/attn_backward/pallas_call | solution.py:1248
  422.0 0.8 broadcast_select_fusion.2.rows_hbm
  423.5 31.1 %home.1 = (f32[8,128]{1,0:T(8,128)}, f32[2,1,640]{2,1,0:T(1,128)}, bf16[288,1152]{1,0:T(8,128)(2,1)}, bf16[288,576]{1,0:T(8,128)(2,1)}, bf16[2,96,1152]{2,1,0:T(8,128)(2,1)}) custom-call(f32[8,1152]{1,0:T(8,128)} %get-tuple-element.86.attn_zero, f32[8,1152]{1,0:T(8,128)} %get-tuple-element.87.attn_one, f32[8,1152]{1,0:T(8,128)} %get-tuple-element.88.ff_zero, ...), custom_call_target="tpu_custom_call" | custom-call | flops 20000000000 | bytes 100000000 | tf_op jit(solution)/shard_map/home/pallas_call | solution.py:1682
  454.5 0.7 slice_bitcast_fusion
  456.4 0.7 slice_reduce_fusion
  457.8 1.1 broadcast_select_fusion.1
  458.9 1.0 fusion
  459.8 14.6 %finish.1 = (f32[3,288,288]{2,1,0:T(8,128)}, f32[288,288]{1,0:T(8,128)}, f32[288,1076]{1,0:T(8,128)}, f32[288,1076]{1,0:T(8,128)}) custom-call(bf16[288,1152]{1,0:T(8,128)(2,1)} %reduce-scatter.7.cloned.1.call-done.ff_sum_hbm.ff_zero, bf16[288,1152]{1,0:T(8,128)(2,1)} %reduce-scatter.5.cloned.1.call-done.errand_hbm.ff_one, ...), custom_call_target="tpu_custom_call" | custom-call | flops 20000000000 | bytes 100000000 | tf_op jit(solution)/shard_map/finish/pallas_call | solution.py:1785
  474.4 2.1 copy.22
  476.5 2.5 copy.30
  479.0 1.1 copy.31
  480.0 0.7 copy-done.5
  480.8 1.1 copy.32
  (47 shorter events, 4.4 us)
Async XLA Ops:
  7.2 102.7 %all-gather.4.cloned.1.call-start = ((), (), s32[]{:S(2)}) async-start(), calls=%async_computation.4 | async-start | bytes 3317760 | tf_op jit(solution)/shard_map/all_gather | solution.py:1849
  55.1 1.6 copy-start.7
  55.1 95.8 %all-gather.6.cloned.1.call-start = ((), (), s32[]{:S(2)}) async-start(), calls=%async_computation.5 | async-start | bytes 1843200 | tf_op jit(solution)/shard_map/all_gather | solution.py:1849
  55.9 145.6 %all-gather.8.cloned.1.call-start = ((), (), s32[]{:S(2)}) async-start(), calls=%async_computation.6 | async-start | bytes 3317760 | tf_op jit(solution)/shard_map/all_gather | solution.py:1849
  56.6 306.7 %reduce-scatter.5.cloned.1.call-start = ((), (), s32[]{:S(2)}) async-start(), calls=%async_computation.7 | async-start | bytes 3317760 | tf_op jit(solution)/shard_map/reduce_scatter | solution.py:1896
  57.5 47.1 %copy-start.8 = (bf16[2,1,184,1152]{3,2,1,0:T(8,128)(2,1)S(1)}, bf16[2,1,184,1152]{3,2,1,0:T(8,128)(2,1)}, u32[]{:S(2)}) copy-start(bf16[2,1,184,1152]{3,2,1,0:T(8,128)(2,1)} %param.11) | copy-start | bytes 2543620
  265.4 1.0 copy-start.1
  265.4 1.1 copy-start.3
  265.4 158.0 %reduce-scatter.9.cloned.1.call-start = ((), (), s32[]{:S(2)}) async-start(), calls=%async_computation.9 | async-start | bytes 1843200 | tf_op jit(solution)/shard_map/reduce_scatter | solution.py:1914
  318.5 105.0 %reduce-scatter.7.cloned.1.call-start = ((), (), s32[]{:S(2)}) async-start(), calls=%async_computation.8 | async-start | bytes 3317760 | tf_op jit(solution)/shard_map/reduce_scatter | solution.py:1896
  360.0 2.2 copy-start.2
  360.0 2.2 copy-start.9
  360.0 99.8 %reduce-scatter.11.cloned.1.call-start = ((), (), s32[]{:S(2)}) async-start(), calls=%async_computation.10 | async-start | bytes 1843200 | tf_op jit(solution)/shard_map/reduce_scatter | solution.py:1914
  363.3 58.7 %copy-start = (bf16[2,96,1152]{2,1,0:T(8,128)(2,1)S(1)}, bf16[2,96,1152]{2,1,0:T(8,128)(2,1)}, u32[]{:S(2)}) copy-start(bf16[2,96,1152]{2,1,0:T(8,128)(2,1)} %get-tuple-element.77.grad_ref) | copy-start | bytes 1327108
  421.9 0.9 copy-start.10
  421.9 0.9 copy-start.11
  423.5 34.3 %copy-start.4 = (bf16[2,96,1152]{2,1,0:T(8,128)(2,1)S(1)}, bf16[2,96,1152]{2,1,0:T(8,128)(2,1)}, u32[]{:S(2)}) copy-start(bf16[2,96,1152]{2,1,0:T(8,128)(2,1)} %get-tuple-element.85) | copy-start | bytes 1327108
  474.4 4.6 copy-start.6
  479.0 1.8 copy-start.5
Sparse Core Ops, SparseCore 0:
  55.3 54.6 all-gather.3
  111.5 34.0 all-gather.5
  147.2 54.2 all-gather.7
  265.5 50.6 reduce-scatter.4
  318.6 33.3 reduce-scatter.8
  360.1 50.7 reduce-scatter.6
  422.9 32.3 reduce-scatter.10

commit v4 on v3

--- a/solution.py
+++ b/solution.py
@@ -73,6 +73,7 @@
         self.core = core
         self.mine = self.around(section, tensor, core)
         self.theirs = self.around(section, tensor + 1 - 2 * core, 1 - core)
+        self.far_role, self.near_role = 1 + core, 2 - core
         self.mate = self.theirs[0]
         over = lax.rem(tensor + 2, 4)
         self.near, self.far = tensor, over
@@ -82,22 +83,24 @@
         self.across_y = self.grid[2]
         self.first, self.second = self.mine[1], self.mine[2]
 
-    @staticmethod
-    def places(section, near, far):
+    def place(self, section, tensor):
+        start = (2 * tensor + section) * self.half_rows
+        return (section, tensor, pl.multiple_of(start, self.half_rows))
+
+    def places(self, section, near, far):
         flip = 1 - section
-        return [(section, near), (flip, near), (section, far), (flip, far)]
-
-    @staticmethod
-    def around(section, tensor, core):
+        return [self.place(*at) for at in ((section, near), (flip, near), (section, far), (flip, far))]
+
+    def around(self, section, tensor, core):
         over = lax.rem(tensor + 2, 4)
         turn = 1 - 2 * section
         first = (section + (1 - core) * turn, tensor + core * (over - tensor))
         second = (section + core * turn, tensor + (1 - core) * (over - tensor))
-        return [(section, tensor), first, second, (1 - section, over)]
+        places = ((section, tensor), first, second, (1 - section, over))
+        return [self.place(*at) for at in places]
 
     def rows(self, ref, at):
-        start = pl.multiple_of((2 * at[1] + at[0]) * self.half_rows, self.half_rows)
-        return ref.at[pl.ds(start, self.half_rows)]
+        return ref.at[pl.ds(at[2], self.half_rows)]
 
     def greet(self):
         barrier = pltpu.get_barrier_semaphore()
@@ -125,17 +128,16 @@
             device_id_type=MESH,
         )
 
-    def send(self, src, dst, role, peer):
-        copy = self.copy(src, dst, role, peer)
-        copy.start()
-        self.sent.append(copy)
+    def send(self, ends, role, peer):
+        self.copy(*ends(), role, peer).start()
+        self.sent.append(lambda: self.copy(*ends(), role, peer))
 
     def arrived(self, dst, role):
         self.copy(dst, dst, role, self.slab.mate).wait_recv()
 
     def drain(self):
         for copy in self.sent:
-            copy.wait_send()
+            copy().wait_send()
 
 
 class Gather(Moves):
@@ -144,8 +146,7 @@
         self.whole = whole
 
     def pass_on(self, at, role, peer):
-        part = self.slab.rows(self.whole, at)
-        self.send(part, part, role, peer)
+        self.send(lambda: (self.slab.rows(self.whole, at),) * 2, role, peer)
 
     def arrive(self, at, role):
         self.arrived(self.slab.rows(self.whole, at), role)
@@ -156,7 +157,7 @@
         self.pass_on(mine[0], 3, self.slab.mate)
 
     def second(self):
-        self.sent.pop(0).wait_send()
+        self.sent.pop(0)().wait_send()
         self.pass_on(self.slab.mine[0], 1, self.slab.mine[2])
 
     def forward(self):
@@ -199,9 +200,8 @@
         )
 
     def send(self, m, index, role, peer):
-        copy = self.copy(m, index, role, peer)
-        copy.start()
-        self.sent.append(copy)
+        self.copy(m, index, role, peer).start()
+        self.sent.append(lambda: self.copy(m, index, role, peer))
 
     def start(self):
         for m in range(self.micro):
@@ -220,7 +220,7 @@
 
     def drain(self):
         for copy in self.sent:
-            copy.wait_send()
+            copy().wait_send()
 
 
 class Scatter(Moves):
@@ -230,14 +230,16 @@
         self.relay, self.from_second, self.from_first = (arrivals.at[k] for k in range(3))
 
     def to_mate(self, at, role):
-        self.send(self.slab.rows(self.terms, at), self.from_mate.at[role], role, self.slab.mate)
+        self.send(
+            lambda: (self.slab.rows(self.terms, at), self.from_mate.at[role]), role, self.slab.mate
+        )
 
     def mate_far(self):
         self.to_mate(self.slab.mate_grid[3], 3)
-        self.to_mate(self.slab.mate_grid[2], 1 + self.slab.core)
+        self.to_mate(self.slab.mate_grid[2], self.slab.far_role)
 
     def mate_near(self):
-        self.to_mate(self.slab.mate_grid[1], 2 - self.slab.core)
+        self.to_mate(self.slab.mate_grid[1], self.slab.near_role)
         self.to_mate(self.slab.mate_grid[0], 0)
 
     def chip_sum(self, k, rows):
@@ -256,7 +258,7 @@
             if ride is not None:
                 value = value + ride[rows].astype(jnp.float32)
             self.outgoing[slot, rows] = low(value)
-        self.send(self.outgoing.at[slot], dst, role, peer)
+        self.send(lambda: (self.outgoing.at[slot], dst), role, peer)
 
     def far_hop(self):
         self.hop(3, 0, self.relay, 4, self.slab.second)
@@ -322,6 +324,10 @@
     ]
 
 
+def step_from(start, i, size):
+    return pl.ds(pl.multiple_of(start + i * size, size), size)
+
+
 def step_rows(i, size):
     return pl.ds(pl.multiple_of(i * size, size), size)
 
@@ -345,15 +351,23 @@
     return jnp.where(live, 0.0, masked_score)
 
 
-def chip_rows(slab, far, compute, parts=1):
-    tensor = (slab.far if far else slab.near) - slab.core
-    size = 4 * slab.half_rows // parts
-
-    def one(i):
-        start = tensor * (2 * slab.half_rows) + i * size
-        compute(pl.ds(pl.multiple_of(start, 2 * slab.half_rows), size))
-
-    repeat(parts, one)
+def stages(count, work, hooks):
+    def body(k):
+        work(k)
+        for at, steps in hooks.items():
+
+            @pl.when(k == at)
+            def _():
+                for step in steps:
+                    step()
+
+    repeat(count, body)
+
+
+def chip_rows(slab, k):
+    far, near = slab.far - slab.core, slab.near - slab.core
+    start = (far + lax.rem(k, 2) * (near - far)) * (2 * slab.half_rows)
+    return pl.multiple_of(start, 2 * slab.half_rows)
 
 
 def open_gathers(gathers, fill, prepare):
@@ -471,9 +485,11 @@
         open_gathers(gathers, fill, prepare)
     keeps = []
 
-    def keep(src, dst, i):
-        copy = pltpu.make_async_copy(src, dst, keep_sems.at[i])
-        copy.start()
+    def keep(src, dst, m, i):
+        def copy():
+            return pltpu.make_async_copy(src.at[m], dst.at[m], keep_sems.at[i])
+
+        copy().start()
         keeps.append(copy)
 
     def project(m):
@@ -516,48 +532,52 @@
             return
         gathers[m].to_mate()
         gathers[m].finish()
-        keep(gathered.at[m], normed_hbm.at[m], m)
+        keep(gathered, normed_hbm, m, m)
+
+    def work(k):
+        m = lax.div(k, 2)
+        start = chip_rows(slab, k)
+        pl.when(lax.rem(k, 2) == 0)(lambda: project(m))
+
+        def piece(i):
+            attend(m, step_from(start, i, 2 * half_rows))
+
+        repeat(2, piece)
+        output(m, pl.ds(start, 4 * half_rows))
+
+    def keep_two(m):
+        keep(qkv, qkv_hbm, m, 2 + 2 * m)
+        keep(mixed, mixed_hbm, m, 3 + 2 * m)
+
+    def grads_on():
+        if ready:
+            tiles.pass_on()
+
+    def grads_in():
+        if ready:
+            tiles.finish()
+            for m in range(micro):
+                keep(all_grads, normed_hbm, m, m)
 
     gathered_rows(0)
-    project(0)
     if not ready:
         gathers[1].forward()
-    chip_rows(slab, True, lambda rows: attend(0, rows), 2)
-    chip_rows(slab, True, lambda rows: output(0, rows))
-    scatters[0].mate_far()
-    gathered_rows(1)
-    scatters[0].far_hop()
-    chip_rows(slab, False, lambda rows: attend(0, rows), 2)
-    chip_rows(slab, False, lambda rows: output(0, rows))
-    scatters[0].mate_near()
-    keep(qkv.at[0], qkv_hbm.at[0], 2)
-    keep(mixed.at[0], mixed_hbm.at[0], 3)
-    project(1)
-    scatters[0].second_hop()
-    scatters[0].first_hop()
-    if ready:
-        tiles.pass_on()
-    chip_rows(slab, True, lambda rows: attend(1, rows), 2)
-    chip_rows(slab, True, lambda rows: output(1, rows))
-    scatters[1].mate_far()
-    close(0)
-    scatters[1].far_hop()
-    if ready:
-        tiles.finish()
-        for m in range(micro):
-            keep(all_grads.at[m], normed_hbm.at[m], m)
-    chip_rows(slab, False, lambda rows: attend(1, rows), 2)
-    chip_rows(slab, False, lambda rows: output(1, rows))
-    scatters[1].mate_near()
-    keep(qkv.at[1], qkv_hbm.at[1], 4)
-    keep(mixed.at[1], mixed_hbm.at[1], 5)
-    scatters[1].second_hop()
-    scatters[1].first_hop()
+    zero, one = scatters
+    stages(
+        4,
+        work,
+        {
+            0: [zero.mate_far, lambda: gathered_rows(1), zero.far_hop],
+            1: [zero.mate_near, lambda: keep_two(0), zero.second_hop, zero.first_hop, grads_on],
+            2: [one.mate_far, lambda: close(0), one.far_hop, grads_in],
+            3: [one.mate_near, lambda: keep_two(1), one.second_hop, one.first_hop],
+        },
+    )
     close(1)
     if ready:
         tiles.drain()
     for copy in keeps:
-        copy.wait()
+        copy().wait()
 
 
 def ffn_forward_kernel(
@@ -592,9 +612,11 @@
     open_gathers(gathers, fill, prepare)
     keeps = []
 
-    def keep(src, dst, i):
-        copy = pltpu.make_async_copy(src, dst, keep_sems.at[i])
-        copy.start()
+    def keep(src, dst, m, i):
+        def copy():
+            return pltpu.make_async_copy(src.at[m], dst.at[m], keep_sems.at[i])
+
+        copy().start()
         keeps.append(copy)
 
     def compute(m, rows):
@@ -608,33 +630,35 @@
         for rows in scatters[m].blocks():
             out_ref[m, rows] = low(hidden_ref[m, rows] + scatters[m].total(rows) + vec[7:8])
 
+    def work(k):
+        compute(lax.div(k, 2), pl.ds(chip_rows(slab, k), 4 * half_rows))
+
     gathers[0].to_mate()
     gathers[0].finish()
-    keep(gathered.at[0], second_hbm.at[0], 0)
-    chip_rows(slab, True, lambda rows: compute(0, rows))
-    scatters[0].mate_far()
-    gathers[1].forward()
-    scatters[0].far_hop()
-    chip_rows(slab, False, lambda rows: compute(0, rows))
-    scatters[0].mate_near()
-    keep(upper.at[0], upper_hbm.at[0], 1)
-    gathers[1].to_mate()
-    scatters[0].second_hop()
-    gathers[1].finish()
-    keep(gathered.at[1], second_hbm.at[1], 2)
-    chip_rows(slab, True, lambda rows: compute(1, rows))
-    scatters[1].mate_far()
-    scatters[0].first_hop()
-    scatters[1].far_hop()
-    chip_rows(slab, False, lambda rows: compute(1, rows))
-    scatters[1].mate_near()
-    keep(upper.at[1], upper_hbm.at[1], 3)
-    scatters[1].second_hop()
+    keep(gathered, second_hbm, 0, 0)
+    zero, one = scatters
+    stages(
+        4,
+        work,
+        {
+            0: [zero.mate_far, gathers[1].forward, zero.far_hop],
+            1: [
+                zero.mate_near,
+                lambda: keep(upper, upper_hbm, 0, 1),
+                gathers[1].to_mate,
+                zero.second_hop,
+                gathers[1].finish,
+                lambda: keep(gathered, second_hbm, 1, 2),
+            ],
+            2: [one.mate_far, zero.first_hop, one.far_hop],
+            3: [one.mate_near, lambda: keep(upper, upper_hbm, 1, 3), one.second_hop],
+        },
+    )
     close(0)
-    scatters[1].first_hop()
+    one.first_hop()
     close(1)
     for copy in keeps:
-        copy.wait()
+        copy().wait()
 
 
 def ffn_backward_kernel(
@@ -699,7 +723,7 @@
     def stacked(ref, cols=slice(None)):
         return ref[:, :, cols].reshape(micro * seq, -1)
 
-    def weight_grads(first, last):
+    def weight_grads(hooks):
         def block(i):
             cols = step_rows(i, WIDE)
             up = dot(stacked(second, cols), stacked(grad_upper), 0, 0)
@@ -710,7 +734,7 @@
             rest_cols = [up[:, main : main + extra], down[:, main : main + extra], blank]
             grads_ref[cols, 2 * main :] = low(jnp.concatenate(rest_cols, axis=1))
 
-        repeat(last - first, lambda i: block(first + i))
+        stages(width // WIDE, block, hooks)
 
     def close(m):
         scatters[m].finish()
@@ -724,33 +748,32 @@
             for j, item in enumerate((gain_terms, grad_normed, grad_rows, branch)):
                 small_ref[j : j + 1] += jnp.sum(item, axis=0, keepdims=True)
 
+    def work(k):
+        compute(lax.div(k, 2), pl.ds(chip_rows(slab, k), 4 * half_rows))
+
     gathers[0].to_mate()
     gathers[0].finish()
     load_upper[0].wait()
-    chip_rows(slab, True, lambda rows: compute(0, rows))
-    scatters[0].mate_far()
-    gathers[1].forward()
-    scatters[0].far_hop()
-    chip_rows(slab, False, lambda rows: compute(0, rows))
-    scatters[0].mate_near()
-    gathers[1].to_mate()
-    scatters[0].second_hop()
-    gathers[1].finish()
-    load_upper[1].wait()
-    chip_rows(slab, True, lambda rows: compute(1, rows))
-    scatters[1].mate_far()
-    scatters[0].first_hop()
-    scatters[1].far_hop()
-    chip_rows(slab, False, lambda rows: compute(1, rows))
-    scatters[1].mate_near()
-    scatters[1].second_hop()
+    zero, one = scatters
+    stages(
+        4,
+        work,
+        {
+            0: [zero.mate_far, gathers[1].forward, zero.far_hop],
+            1: [
+                zero.mate_near,
+                gathers[1].to_mate,
+                zero.second_hop,
+                gathers[1].finish,
+                load_upper[1].wait,
+            ],
+            2: [one.mate_far, zero.first_hop, one.far_hop],
+            3: [one.mate_near, one.second_hop],
+        },
+    )
     for load in load_second:
         load.wait()
-    blocks = width // WIDE
-    weight_grads(0, blocks // 3)
-    scatters[1].first_hop()
-    close(0)
-    weight_grads(blocks // 3, blocks)
+    weight_grads({0: [one.first_hop, lambda: close(0)]})
     close(1)
 
 
@@ -812,7 +835,7 @@
     def stacked(ref, cols=slice(None)):
         return ref[:, :, cols].reshape(micro * seq, -1)
 
-    def weight_grads(first, last):
+    def weight_grads(hooks):
         def block(i):
             cols = step_rows(i, WIDE)
             up = dot(stacked(gathered, cols), stacked(grad_upper), 0, 0)
@@ -823,7 +846,7 @@
             rest_cols = [up[:, main : main + extra], down[:, main : main + extra], blank]
             grads_ref[cols, 2 * main :] = low(jnp.concatenate(rest_cols, axis=1))
 
-        repeat(last - first, lambda i: block(first + i))
+        stages(width // WIDE, block, hooks)
 
     def close_back(m):
         backs[m].finish()
@@ -842,41 +865,46 @@
         for rows in scatters[m].blocks():
             out_ref[m, rows] = low(hidden_ref[m, rows] + scatters[m].total(rows) + vec[7:8])
 
+    def work(k):
+        compute(lax.div(k, 2), pl.ds(chip_rows(slab, k), 4 * half_rows))
+
     gathers[0].to_mate()
     gathers[0].finish()
     loads[0].wait()
-    chip_rows(slab, True, lambda rows: compute(0, rows))
-    backs[0].mate_far()
-    scatters[0].mate_far()
-    gathers[1].forward()
-    backs[0].far_hop()
-    chip_rows(slab, False, lambda rows: compute(0, rows))
-    backs[0].mate_near()
-    scatters[0].mate_near()
-    gathers[1].to_mate()
-    backs[0].second_hop()
-    gathers[1].finish()
-    scatters[0].far_hop()
-    scatters[0].second_hop()
-    loads[1].wait()
-    chip_rows(slab, True, lambda rows: compute(1, rows))
-    backs[1].mate_far()
-    scatters[1].mate_far()
-    backs[0].first_hop()
-    backs[1].far_hop()
-    scatters[0].first_hop()
-    chip_rows(slab, False, lambda rows: compute(1, rows))
-    backs[1].mate_near()
-    scatters[1].mate_near()
-    backs[1].second_hop()
-    scatters[1].far_hop()
-    scatters[1].second_hop()
-    blocks = width // WIDE
-    weight_grads(0, blocks // 3)
-    backs[1].first_hop()
-    scatters[1].first_hop()
-    close_back(0)
-    weight_grads(blocks // 3, blocks)
+    zero, one = scatters
+    back_zero, back_one = backs
+    stages(
+        4,
+        work,
+        {
+            0: [back_zero.mate_far, zero.mate_far, gathers[1].forward, back_zero.far_hop],
+            1: [
+                back_zero.mate_near,
+                zero.mate_near,
+                gathers[1].to_mate,
+                back_zero.second_hop,
+                gathers[1].finish,
+                zero.far_hop,
+                zero.second_hop,
+                loads[1].wait,
+            ],
+            2: [
+                back_one.mate_far,
+                one.mate_far,
+                back_zero.first_hop,
+                back_one.far_hop,
+                zero.first_hop,
+            ],
+            3: [
+                back_one.mate_near,
+                one.mate_near,
+                back_one.second_hop,
+                one.far_hop,
+                one.second_hop,
+            ],
+        },
+    )
+    weight_grads({0: [back_one.first_hop, one.first_hop, lambda: close_back(0)]})
     close_back(1)
     for m in range(micro):
         close(m)
@@ -920,11 +948,11 @@
             own[pl.ds(start, 32)] = low(grad_ref[m, pl.ds(start, 32)])
 
     def head(h, part=0):
-        return slice(part * pair + h * LANES, part * pair + (h + 1) * LANES)
+        return pl.ds(pl.multiple_of(part * pair + h * LANES, LANES), LANES)
 
     def ready_qkv(m):
         load_qkv[m].wait()
-        shut[...] = shut_keys(lengths[m], own_rows, 2 * half_rows, (seq, LANES), 0)
+        shut[m] = shut_keys(lengths[m], own_rows, 2 * half_rows, (seq, LANES), 0)
         for h in range(heads):
             turned[m, h] = low(qkv[m, :, head(h, 1)].astype(jnp.float32).T)
 
@@ -932,11 +960,14 @@
         def block(i):
             rows = step_rows(i, TILE)
             keys, queries = qkv[m, :, head(h, 1)], qkv[m, rows, head(h)]
-            closed = jnp.concatenate([shut[...]] * (TILE // LANES), axis=1)
+            closed = jnp.concatenate([shut[m]] * (TILE // LANES), axis=1)
             scores = dot(keys, queries, 1, 1) * (score_scale * LOG2E) + closed
             high_probs[m, h, :, rows] = jnp.exp2(scores - lse[m, h, rows].T[0:1])
 
         repeat(seq // TILE, block)
+
+    def find_all(k):
+        find_probs(lax.div(k, heads), lax.rem(k, heads))
 
     errand = remote(
         errand_hbm,
@@ -951,10 +982,17 @@
     def prepare():
         small_ref[...] = jnp.zeros_like(small_ref)
         bias_ref[...] = jnp.zeros_like(bias_ref)
-        ready_qkv(0)
-        find_probs(0, 0)
-
-    open_gathers(gathers, fill, prepare)
+        load_packed.wait()
+        widen(packed, wide)
+        for m in range(micro):
+            ready_qkv(m)
+
+    fill(0)
+    gathers[0].start()
+    fill(1)
+    gathers[0].second()
+    gathers[1].start()
+    prepare()
 
     def mix_grads(m):
         def block(i):
@@ -990,7 +1028,7 @@
     def stacked(ref, cols=slice(None)):
         return ref[:, :, cols].reshape(micro * seq, -1)
 
-    def weight_grads(first, last):
+    def weight_grads(hooks):
         def block(i):
             cols = step_rows(i, WIDE)
             front = dot(stacked(normed, cols), stacked(grad_qkv), 0, 0)
@@ -999,7 +1037,7 @@
             pieces = [total[:, h * LANES : h * LANES + HEAD] for h in range(4 * heads)]
             grads_ref[cols] = jnp.concatenate(pieces, axis=1)
 
-        repeat(last - first, lambda i: block(first + i))
+        stages(width // WIDE, block, hooks)
 
     def close(m):
         scatters[m].finish()
@@ -1012,51 +1050,58 @@
             for j, item in enumerate((gain_terms, grad_normed)):
                 small_ref[j : j + 1] += jnp.sum(item, axis=0, keepdims=True)
 
-    load_packed.wait()
-    widen(packed, wide)
-    gathers[1].forward()
-    gathers[0].to_mate()
-
-    @pl.when(sends_errand)
-    def _():
-        errand.start()
-
-    for h in range(1, heads):
-        find_probs(0, h)
+    def start_errand():
+        pl.when(sends_errand)(errand.start)
+
+    stages(
+        2 * heads,
+        find_all,
+        {
+            0: [gathers[0].forward, gathers[1].second],
+            1: [gathers[1].forward, gathers[0].to_mate, start_errand],
+        },
+    )
     gathers[0].finish()
-    mix_grads(0)
-    attend(0, 0)
-    gathers[1].to_mate()
-    for h in range(1, heads):
-        attend(0, h)
-    chip_rows(slab, True, lambda rows: back_project(0, rows))
-    scatters[0].mate_far()
-    ready_qkv(1)
-    find_probs(1, 0)
-    scatters[0].far_hop()
-    chip_rows(slab, False, lambda rows: back_project(0, rows))
-    scatters[0].mate_near()
-    gathers[1].finish()
-    mix_grads(1)
-    scatters[0].second_hop()
-    for h in range(1, heads):
-        find_probs(1, h)
-    scatters[0].first_hop()
-    for h in range(heads):
-        attend(1, h)
-    chip_rows(slab, True, lambda rows: back_project(1, rows))
-    scatters[1].mate_far()
-    scatters[1].far_hop()
-    chip_rows(slab, False, lambda rows: back_project(1, rows))
-    scatters[1].mate_near()
-    close(0)
-    scatters[1].second_hop()
+    zero, one = scatters
+    attend_hooks = {
+        0: [gathers[1].to_mate],
+        heads - 1: [gathers[1].finish],
+        heads: [zero.first_hop],
+    }
+    project_hooks = {
+        0: [zero.mate_far, zero.far_hop],
+        1: [zero.mate_near, zero.second_hop],
+        2: [one.mate_far, one.far_hop],
+        3: [one.mate_near, lambda: close(0), one.second_hop],
+    }
+
+    def hooked(at, hooks):
+        for k, steps in hooks.items():
+
+            @pl.when(at == k)
+            def _():
+                for step in steps:
+                    step()
+
+    def image(m):
+        mix_grads(m)
+
+        def one_head(h):
+            attend(m, h)
+            hooked(m * heads + h, attend_hooks)
+
+        repeat(heads, one_head)
+
+        def one_chip(i):
+            back_project(m, pl.ds(chip_rows(slab, i), 4 * half_rows))
+            hooked(2 * m + i, project_hooks)
+
+        repeat(2, one_chip)
+
+    repeat(micro, image)
     for load in load_rest:
         load.wait()
-    blocks = width // WIDE
-    weight_grads(0, blocks // 3)
-    scatters[1].first_hop()
-    weight_grads(blocks // 3, blocks)
+    weight_grads({0: [one.first_hop]})
     close(1)
 
     @pl.when(sends_errand)
@@ -1267,7 +1312,7 @@
             pltpu.VMEM((micro, seq, pair), low_type),
             pltpu.VMEM((micro, seq, 3 * pair), low_type),
             pltpu.VMEM((micro, heads, LANES, seq), low_type),
-            pltpu.VMEM((seq, LANES), high_type),
+            pltpu.VMEM((micro, seq, LANES), high_type),
             pltpu.VMEM((seq, seq), low_type),
             pltpu.VMEM((seq, seq), low_type),
             pltpu.VMEM((micro, heads, seq, seq), high_type),
@@ -1714,93 +1759,72 @@
     )(*attn_small, *ff_small, bias_grads, up_grads, ff_sum, attn_sum, rows)
 
 
-def finish_kernel(
-    ff_zero, ff_one, ff_zero_got, ff_one_got, attn_zero, attn_one, attn_one_got,
-    qkv_ref, out_ref, up_ref, down_ref, attn_zero_got, send_sem, recv_sem,
-):
-    section = lax.axis_index("section")
-    first = section == 0
-    other = {"section": 1 - section}
-    barrier = pltpu.get_barrier_semaphore()
-    pl.semaphore_signal(barrier, inc=1, device_id=other, device_id_type=MESH)
-    pl.semaphore_wait(barrier, 1)
-    copy = remote(attn_zero, attn_zero_got, send_sem, recv_sem, other)
-
-    @pl.when(section == 1)
-    def _():
-        copy.start()
-        attn_zero_got[...] = attn_zero[...]
-
-    rows = up_ref.shape[0]
+def ff_finish_kernel(zero, one, zero_got, one_got, up_ref, down_ref):
+    first = lax.axis_index("section") == 0
+    halves = (
+        jnp.where(first, zero[...], one_got[...]),
+        jnp.where(first, zero_got[...], one[...]),
+    )
     half_ff = up_ref.shape[1] // 2
     main = half_ff // LANES * LANES
     extra = half_ff - main
+    for k in range(2):
+        pieces = []
+        for half in halves:
+            start = 2 * main + k * extra
+            pieces += [half[:, k * main : (k + 1) * main], half[:, start : start + extra]]
+        whole = jnp.concatenate(pieces, axis=1).astype(jnp.float32)
+        if k == 0:
+            up_ref[...] = whole
+        else:
+            down_ref[...] = whole.T
+
+
+def ff_finish(sums, got, ff_cols):
+    rows = sums[0].shape[0]
+    return pl.pallas_call(
+        ff_finish_kernel,
+        out_shape=[
+            shape_of((rows, ff_cols), jnp.float32),
+            shape_of((ff_cols, rows), jnp.float32),
+        ],
+        in_specs=[vmem_spec()] * 4,
+        out_specs=[vmem_spec()] * 2,
+        compiler_params=pltpu.CompilerParams(vmem_limit_bytes=VMEM_BYTES),
+        cost_estimate=COST,
+        name="ff_finish",
+    )(*sums, *got)
+
+
+def attn_finish_kernel(zero, one, zero_got, one_got, qkv_ref, out_ref):
+    first = lax.axis_index("section") == 0
+    halves = (
+        jnp.where(first, zero[...], one_got[...]),
+        jnp.where(first, zero_got[...], one[...]),
+    )
     pair_cols = qkv_ref.shape[2] // 2
-    size = 96 if rows % 96 == 0 else rows
-
-    def ff_block(i):
-        at = step_rows(i, size)
-        halves = (
-            jnp.where(first, ff_zero[at], ff_one_got[at]),
-            jnp.where(first, ff_zero_got[at], ff_one[at]),
-        )
-        for k, ref in enumerate((up_ref, down_ref)):
-            pieces = []
-            for half in halves:
-                start = 2 * main + k * extra
-                pieces += [half[:, k * main : (k + 1) * main], half[:, start : start + extra]]
-            ref[at] = jnp.concatenate(pieces, axis=1).astype(jnp.float32)
-
-    repeat(rows // size, ff_block)
-
-    @pl.when(first)
-    def _():
-        copy.wait_recv()
-
-    def attn_block(i):
-        at = step_rows(i, size)
-        halves = (
-            jnp.where(first, attn_zero[at], attn_one_got[at]),
-            jnp.where(first, attn_zero_got[at], attn_one[at]),
-        )
-        for k in range(4):
-            span = slice(k * pair_cols, (k + 1) * pair_cols)
-            whole = jnp.concatenate([half[:, span] for half in halves], axis=1)
-            whole = whole.astype(jnp.float32)
-            if k < 3:
-                qkv_ref[k, at] = whole
-            else:
-                out_ref[at] = whole
-
-    repeat(rows // size, attn_block)
-
-    @pl.when(section == 1)
-    def _():
-        copy.wait_send()
-
-
-def finish(ff_sums, ff_got, attn_sums, attn_got, head_cols, ff_cols):
-    rows = ff_sums[0].shape[0]
-    high_type = jnp.float32
+    for k in range(4):
+        span = slice(k * pair_cols, (k + 1) * pair_cols)
+        whole = jnp.concatenate([half[:, span] for half in halves], axis=1).astype(jnp.float32)
+        if k < 3:
+            qkv_ref[k] = whole
+        else:
+            out_ref[...] = whole.T
+
+
+def attn_finish(sums, got, head_cols):
+    rows = sums[0].shape[0]
     return pl.pallas_call(
-        finish_kernel,
+        attn_finish_kernel,
         out_shape=[
-            shape_of((3, rows, head_cols), high_type),
-            shape_of((rows, head_cols), high_type),
-            shape_of((rows, ff_cols), high_type),
-            shape_of((rows, ff_cols), high_type),
+            shape_of((3, rows, head_cols), jnp.float32),
+            shape_of((head_cols, rows), jnp.float32),
         ],
-        in_specs=[vmem_spec()] * 7,
-        out_specs=[vmem_spec()] * 4,
-        scratch_shapes=[
-            pltpu.VMEM(attn_sums[0].shape, attn_sums[0].dtype),
-            pltpu.SemaphoreType.DMA,
-            pltpu.SemaphoreType.DMA,
-        ],
-        compiler_params=params(9),
-        cost_estimate=COST,
-        name="finish",
-    )(*ff_sums, *ff_got, *attn_sums, attn_got)
+        in_specs=[vmem_spec()] * 4,
+        out_specs=[vmem_spec()] * 2,
+        compiler_params=pltpu.CompilerParams(vmem_limit_bytes=VMEM_BYTES),
+        name="attn_finish",
+    )(*sums, *got)
 
 
 def shards(
@@ -1930,22 +1954,19 @@
     up_total = up_total[:, :, :half_ff].reshape(1, ff_cols)
     input_grad = whole_rows(input_grads[0], input_grads[1], rows_got)
 
-    qkv_total, out_total, up_grad, down_grad = finish(
-        [ff_sums[0], ff_sums[1]],
-        [ff_got, errands[0]],
-        [attn_sums[0], attn_sums[1]],
-        attn_got,
-        head_cols,
-        ff_cols,
+    attn_zero_got = lax.ppermute(attn_sums[0], "section", [(1, 0)])
+    up_grad, down_grad = ff_finish([ff_sums[0], ff_sums[1]], [ff_got, errands[0]], ff_cols)
+    qkv_total, out_total = attn_finish(
+        [attn_sums[0], attn_sums[1]], [attn_zero_got, attn_got], head_cols
     )
     gains = norm_gains.shape[1]
     return (
         section_output[None],
         input_grad[None],
         qkv_total[None],
-        out_total.T[None],
+        out_total[None],
         up_grad[None],
-        down_grad.T[None],
+        down_grad[None],
         small_mine[:, :gains],
         small_mine[:, gains:],
         up_total,

time: 497 us -> 477 us (0.960)
  Pallas kernels: 442 us -> 423 us
  waiting for transfers between devices: 7.8 us -> 14.9 us
    pallas_call x1 -> x2, Pallas kernels: 14.6 us -> 6.59 us  [the longest x1 3.84 us: ff_finish(): pl.pallas_call(ff_finish_kernel, out_shape=[shape_of((rows, ff_cols), jnp...]
    pallas_call x1, Pallas kernels: 63.9 us -> 57.6 us  [ffn_turn(): pl.pallas_call(functools.partial(ffn_turn_kernel, half_ff, at, layer), ou...]
    ppermute x0 -> x1, waiting for transfers between devices: none -> 6.14 us  [shards(): attn_zero_got = lax.ppermute(attn_sums[0], 'section', [(1, 0)])]
    unnamed x31 -> x28, local copies, waits for them, and re-layouts: 12.1 us -> 8.47 us
  transfers between devices with their start and end apart: 7 -> 8, of which waited for: 2 -> 3; matrix products, arithmetic and copies ran while one was open for 3% -> 3% of each run, Pallas kernels for 65% -> 67%
where the time goes in v4:
time: 477 us; the launch traced here: 474 us
  Pallas kernels  423 us (89%)
  waiting for transfers between devices  14.9 us (3%)
  between operations  14.6 us (3%)
  local copies, waits for them, and re-layouts  13.5 us (3%)
  other arithmetic  6.02 us (1%)
    pallas_call x2, Pallas kernels, attn_backward(): pl.pallas_call(functools.partial(attn_backward_kernel, at, layer, own_row...  105 us
    pallas_call x2, Pallas kernels, attn_forward(): pl.pallas_call(functools.partial(attn_forward_kernel, given is not None,...  94 us
    pallas_call x1, Pallas kernels, ffn_turn(): pl.pallas_call(functools.partial(ffn_turn_kernel, half_ff, at, layer), ou...  57.6 us
    pallas_call x1, Pallas kernels, prologue(): pl.pallas_call(functools.partial(prologue_kernel, count, heads), out_shap...  44.8 us
    pallas_call x1, Pallas kernels, ffn_backward(): pl.pallas_call(functools.partial(ffn_backward_kernel, half_ff, at, layer)...  42.1 us
    pallas_call x1, Pallas kernels, ffn_forward(): pl.pallas_call(functools.partial(ffn_forward_kernel, half_ff, at, layer),...  41.6 us
    pallas_call x1, Pallas kernels, home(): pl.pallas_call(functools.partial(home_kernel, count, chunk), out_shape=[s...  30.8 us
  transfers between devices with their start and end apart: 8, of which 3 were waited for; matrix products, arithmetic and copies ran while one was open for 3% of the time, Pallas kernels for 67%

profile of v4, /device:TPU:0, one launch (start us, length us, event | category | flops | bytes accessed | tf_op | source)
XLA Modules:
  0.0 473.7 jit_solution(10397803154956345793)
XLA Ops:
  7.2 1.3 copy.26
  8.5 1.8 copy.19
  10.3 44.8 %prologue.1 = (bf16[1152,576]{1,0:T(8,128)(2,1)}, bf16[2,768,1152]{2,1,0:T(8,128)(2,1)}, bf16[288,576]{1,0:T(8,128)(2,1)}, bf16[288,1152]{1,0:T(8,128)(2,1)}, bf...) custom-call(bf16[3,288,288]{2,1,0:T(8,128)(2,1)} %bitcast.45, ...), custom_call_target="tpu_custom_call" | custom-call | flops 20000000000 | bytes 100000000 | tf_op jit(solution)/shard_map/prologue/pallas_call | solution.py:1593
  55.2 0.7 all-gather.6.cloned.1.call-update
  57.0 0.8 pad_dynamic-slice_fusion.1.rows_ref
  57.8 47.3 %attn_forward.2 = (f32[2,96,1152]{2,1,0:T(8,128)}, f32[2,2,768,128]{3,2,1,0:T(8,128)}, bf16[2,768,1152]{2,1,0:T(8,128)(2,1)}, bf16[2,768,768]{2,1,0:T(8,128)(2,1)}, bf16[2,768,256]{2,1,0:T(8,128)(2,1)}) custom-call(bf16[2,96,1152]{2,1,0:T(8,128)(2,1)} %pad_dynamic-slice_fusion.1.rows_ref, f32[2,8,1152]{2,1,0:T(8,128)} %get-tuple-element.58.vectors, ...), custom_call_target="tpu_custom_call" | custom-call | flops 20000000000 | bytes 100000000 | tf_op jit(solution)/shard_map/attn_forward/pallas_call | solution.py:1144
  105.2 0.8 pad_dynamic-slice_fusion.grad_ref
  106.0 4.0 all-gather.4.cloned.1.call-done.packed_hbm
  110.0 41.6 %ffn_forward.1 = (bf16[2,96,1152]{2,1,0:T(8,128)(2,1)}, bf16[2,768,1152]{2,1,0:T(8,128)(2,1)}, f32[2,768,640]{2,1,0:T(8,128)}) custom-call(f32[2,96,1152]{2,1,0:T(8,128)} %get-tuple-element.62.hidden_ref, f32[2,8,1152]{2,1,0:T(8,128)} %get-tuple-element.58.vectors, f32[2,1,640]{2,1,0:T(1,128)} %get-tuple-element.63.up_biases, ...), custom_call_target="tpu_custom_call" | custom-call | flops 20000000000 | bytes 100000000 | tf_op jit(solution)/shard_map/ffn_forward/pallas_call | solution.py:1192
  151.6 46.7 %attn_forward.3 = (f32[2,96,1152]{2,1,0:T(8,128)}, f32[2,2,768,128]{3,2,1,0:T(8,128)}, bf16[2,768,1152]{2,1,0:T(8,128)(2,1)}, bf16[2,768,768]{2,1,0:T(8,128)(2,1)}, bf16[2,768,256]{2,1,0:T(8,128)(2,1)}) custom-call(bf16[2,96,1152]{2,1,0:T(8,128)(2,1)} %get-tuple-element.65.rows_ref.grads_ref, f32[2,8,1152]{2,1,0:T(8,128)} %get-tuple-element.58.vectors, ...), custom_call_target="tpu_custom_call" | custom-call | flops 20000000000 | bytes 100000000 | tf_op jit(solution)/shard_map/attn_forward/pallas_call | solution.py:1144
  198.3 3.2 all-gather.8.cloned.1.call-done.packed_hbm
  201.5 57.6 %ffn_turn.1 = (bf16[2,96,1152]{2,1,0:T(8,128)(2,1)}, f32[2,96,1152]{2,1,0:T(8,128)}, bf16[1152,1152]{1,0:T(8,128)(2,1)}, f32[8,1152]{1,0:T(8,128)}, f32[8,640]{1,0:T(8,128)}) custom-call(f32[2,96,1152]{2,1,0:T(8,128)} %get-tuple-element.67.hidden_ref, bf16[2,96,1152]{2,1,0:T(8,128)(2,1)} %pad_dynamic-slice_fusion.grad_ref, ...), custom_call_target="tpu_custom_call" | custom-call | flops 20000000000 | bytes 100000000 | tf_op jit(solution)/shard_map/ffn_turn/pallas_call | solution.py:1222
  259.2 0.9 copy-done.1
  260.2 0.8 broadcast_select_fusion.6.errand_hbm
  261.1 49.0 %attn_backward.2 = (bf16[2,96,1152]{2,1,0:T(8,128)(2,1)}, bf16[1152,576]{1,0:T(8,128)(2,1)}, f32[8,1152]{1,0:T(8,128)}, f32[8,256]{1,0:T(8,128)}, bf16[2,96,1152]{2,1,0:T(8,128)(2,1)}) custom-call(f32[2,96,1152]{2,1,0:T(8,128)} %get-tuple-element.71.grad_ref, bf16[2,96,1152]{2,1,0:T(8,128)(2,1)} %get-tuple-element.65.rows_ref.grads_ref, ...), custom_call_target="tpu_custom_call" | custom-call | flops 20000000000 | bytes 100000000 | tf_op jit(solution)/shard_map/attn_backward/pallas_call | solution.py:1293
  310.1 42.1 %ffn_backward.1 = (f32[2,96,1152]{2,1,0:T(8,128)}, bf16[1152,1152]{1,0:T(8,128)(2,1)}, f32[8,1152]{1,0:T(8,128)}, f32[8,640]{1,0:T(8,128)}) custom-call(bf16[2,96,1152]{2,1,0:T(8,128)(2,1)} %get-tuple-element.77.grad_ref, f32[2,96,1152]{2,1,0:T(8,128)} %get-tuple-element.62.hidden_ref, f32[2,8,1152]{2,1,0:T(8,128)} %get-tuple-element.58.vectors, ...), custom_call_target="tpu_custom_call" | custom-call | flops 20000000000 | bytes 100000000 | tf_op jit(solution)/shard_map/ffn_backward/pallas_call | solution.py:1257
  352.5 0.7 slice_bitcast_fusion.1
  353.3 0.7 slice_bitcast_fusion.2
  354.7 1.0 fusion.1
  355.7 56.2 %attn_backward.3 = (bf16[2,96,1152]{2,1,0:T(8,128)(2,1)}, bf16[1152,576]{1,0:T(8,128)(2,1)}, f32[8,1152]{1,0:T(8,128)}, f32[8,256]{1,0:T(8,128)}, bf16[288,1152]{1,0:T(8,128)(2,1)}) custom-call(f32[2,96,1152]{2,1,0:T(8,128)} %get-tuple-element.80.grad_ref, bf16[2,96,1152]{2,1,0:T(8,128)(2,1)} %pad_dynamic-slice_fusion.1.rows_ref, ...), custom_call_target="tpu_custom_call" | custom-call | flops 20000000000 | bytes 100000000 | tf_op jit(solution)/shard_map/attn_backward/pallas_call | solution.py:1293
  411.9 0.8 broadcast_select_fusion.2.rows_hbm
  413.4 30.8 %home.1 = (f32[8,128]{1,0:T(8,128)}, f32[2,1,640]{2,1,0:T(1,128)}, bf16[288,1152]{1,0:T(8,128)(2,1)}, bf16[288,576]{1,0:T(8,128)(2,1)}, bf16[2,96,1152]{2,1,0:T(8,128)(2,1)}) custom-call(f32[8,1152]{1,0:T(8,128)} %get-tuple-element.86.attn_zero, f32[8,1152]{1,0:T(8,128)} %get-tuple-element.87.attn_one, f32[8,1152]{1,0:T(8,128)} %get-tuple-element.88.ff_zero, ...), custom_call_target="tpu_custom_call" | custom-call | flops 20000000000 | bytes 100000000 | tf_op jit(solution)/shard_map/home/pallas_call | solution.py:1727
  444.2 0.7 slice_bitcast_fusion
  446.0 1.1 broadcast_select_fusion.1
  447.2 3.8 ff_finish.1
  451.0 1.3 collective-permute-start
  452.3 0.7 reshape.25
  453.0 3.0 copy.22
  456.0 1.0 fusion
  457.0 6.1 %collective-permute-done.zero_got = bf16[288,576]{1,0:T(8,128)(2,1)S(1)} collective-permute-done((bf16[288,576]{1,0:T(8,128)(2,1)}, bf16[288,576]{1,0:T(8,128)(2,1)S(1)}, u32[]{:S(2)}, u32[]{:S(2)}) %collective-permute-start) | collective-permute-done | bytes 331808 | tf_op jit(solution)/shard_map/ppermute | solution.py:1957
  463.1 0.7 copy-done.8
  463.9 2.8 attn_finish.1
  (47 shorter events, 4.3 us)
Async XLA Ops:
  7.2 102.8 %all-gather.4.cloned.1.call-start = ((), (), s32[]{:S(2)}) async-start(), calls=%async_computation.4 | async-start | bytes 3317760 | tf_op jit(solution)/shard_map/all_gather | solution.py:1873
  55.1 1.9 copy-start.5
  55.2 96.5 %all-gather.6.cloned.1.call-start = ((), (), s32[]{:S(2)}) async-start(), calls=%async_computation.5 | async-start | bytes 1843200 | tf_op jit(solution)/shard_map/all_gather | solution.py:1873
  55.9 145.6 %all-gather.8.cloned.1.call-start = ((), (), s32[]{:S(2)}) async-start(), calls=%async_computation.6 | async-start | bytes 3317760 | tf_op jit(solution)/shard_map/all_gather | solution.py:1873
  56.6 299.1 %reduce-scatter.5.cloned.1.call-start = ((), (), s32[]{:S(2)}) async-start(), calls=%async_computation.7 | async-start | bytes 3317760 | tf_op jit(solution)/shard_map/reduce_scatter | solution.py:1920
  57.8 47.3 %copy-start.6 = (bf16[2,1,184,1152]{3,2,1,0:T(8,128)(2,1)S(1)}, bf16[2,1,184,1152]{3,2,1,0:T(8,128)(2,1)}, u32[]{:S(2)}) copy-start(bf16[2,1,184,1152]{3,2,1,0:T(8,128)(2,1)} %param.11) | copy-start | bytes 2543620
  259.1 1.0 copy-start.1
  259.1 1.1 copy-start.3
  259.1 154.3 %reduce-scatter.9.cloned.1.call-start = ((), (), s32[]{:S(2)}) async-start(), calls=%async_computation.9 | async-start | bytes 1843200 | tf_op jit(solution)/shard_map/reduce_scatter | solution.py:1938
  310.1 103.3 %reduce-scatter.7.cloned.1.call-start = ((), (), s32[]{:S(2)}) async-start(), calls=%async_computation.8 | async-start | bytes 3317760 | tf_op jit(solution)/shard_map/reduce_scatter | solution.py:1920
  352.2 2.4 copy-start.2
  352.2 2.4 copy-start.7
  352.3 98.7 %reduce-scatter.11.cloned.1.call-start = ((), (), s32[]{:S(2)}) async-start(), calls=%async_computation.10 | async-start | bytes 1843200 | tf_op jit(solution)/shard_map/reduce_scatter | solution.py:1938
  355.7 56.2 %copy-start = (bf16[2,96,1152]{2,1,0:T(8,128)(2,1)S(1)}, bf16[2,96,1152]{2,1,0:T(8,128)(2,1)}, u32[]{:S(2)}) copy-start(bf16[2,96,1152]{2,1,0:T(8,128)(2,1)} %get-tuple-element.77.grad_ref) | copy-start | bytes 1327108
  411.9 0.9 copy-start.9
  411.9 0.9 copy-start.10
  413.4 32.6 %copy-start.4 = (bf16[2,96,1152]{2,1,0:T(8,128)(2,1)S(1)}, bf16[2,96,1152]{2,1,0:T(8,128)(2,1)}, u32[]{:S(2)}) copy-start(bf16[2,96,1152]{2,1,0:T(8,128)(2,1)} %get-tuple-element.85) | copy-start | bytes 1327108
  447.2 5.1 %copy-start.11 = (f32[2,1,640]{2,1,0:T(1,128)S(1)}, f32[2,1,640]{2,1,0:T(1,128)}, u32[]{:S(2)}) copy-start(f32[2,1,640]{2,1,0:T(1,128)} %get-tuple-element.106) | copy-start | bytes 15364
  451.0 12.1 %collective-permute-start = (bf16[288,576]{1,0:T(8,128)(2,1)}, bf16[288,576]{1,0:T(8,128)(2,1)S(1)}, u32[]{:S(2)}, u32[]{:S(2)}) collective-permute-start(bf16[288,576]{1,0:T(8,128)(2,1)} %reduce-scatter.11.cloned.1.call-done.zero), channel_id=1, source_target_pairs={{16,0},{17,1},{18,2},{19,3},{20,4},{21,5},{22,6},{23,7},{24,8},{25... | collective-permute-start | bytes 995336 | tf_op jit(solution)/shard_map/ppermute | solution.py:1957
  463.1 0.7 copy-start.8
Sparse Core Ops, SparseCore 0:
  55.3 54.6 all-gather.3
  111.5 34.0 all-gather.5
  147.2 54.2 all-gather.7
  259.3 50.6 reduce-scatter.4
  312.1 33.4 reduce-scatter.8
  352.4 50.7 reduce-scatter.6
  412.9 32.2 reduce-scatter.10

commit v5 on v4

--- a/solution.py
+++ b/solution.py
@@ -969,13 +969,19 @@
     def find_all(k):
         find_probs(lax.div(k, heads), lax.rem(k, heads))
 
-    errand = remote(
-        errand_hbm,
-        errand_got,
-        errand_sems.at[0],
-        errand_sems.at[1],
-        {"section": 1 - lax.axis_index("section")},
-    )
+    span = errand_hbm.shape[0]
+    cut = round_up(span // 2, 16) if span > 16 else span // 2
+    errands = []
+    for k, part in enumerate((pl.ds(0, cut), pl.ds(cut, span - cut))):
+        errands.append(
+            remote(
+                errand_hbm.at[part],
+                errand_got.at[part],
+                errand_sems.at[0, k],
+                errand_sems.at[1, k],
+                {"section": 1 - lax.axis_index("section")},
+            )
+        )
     sends_errand = (lax.axis_index("section") == 0) | both_ways
     gets_errand = (lax.axis_index("section") == 1) | both_ways
 
@@ -1050,15 +1056,15 @@
             for j, item in enumerate((gain_terms, grad_normed)):
                 small_ref[j : j + 1] += jnp.sum(item, axis=0, keepdims=True)
 
-    def start_errand():
-        pl.when(sends_errand)(errand.start)
+    def start_errand(k):
+        pl.when(sends_errand)(errands[k].start)
 
     stages(
         2 * heads,
         find_all,
         {
             0: [gathers[0].forward, gathers[1].second],
-            1: [gathers[1].forward, gathers[0].to_mate, start_errand],
+            1: [gathers[1].forward, gathers[0].to_mate, lambda: start_errand(0)],
         },
     )
     gathers[0].finish()
@@ -1066,7 +1072,7 @@
     attend_hooks = {
         0: [gathers[1].to_mate],
         heads - 1: [gathers[1].finish],
-        heads: [zero.first_hop],
+        heads: [zero.first_hop, lambda: start_errand(1)],
     }
     project_hooks = {
         0: [zero.mate_far, zero.far_hop],
@@ -1104,13 +1110,9 @@
     weight_grads({0: [one.first_hop]})
     close(1)
 
-    @pl.when(sends_errand)
-    def _():
-        errand.wait_send()
-
-    @pl.when(gets_errand)
-    def _():
-        errand.wait_recv()
+    for errand in errands:
+        pl.when(sends_errand)(errand.wait_send)
+        pl.when(gets_errand)(errand.wait_recv)
 
 
 def any_spec():
@@ -1316,7 +1318,7 @@
             pltpu.VMEM((seq, seq), low_type),
             pltpu.VMEM((seq, seq), low_type),
             pltpu.VMEM((micro, heads, seq, seq), high_type),
-            pltpu.SemaphoreType.DMA((2,)),
+            pltpu.SemaphoreType.DMA((2, 2)),
             pltpu.SemaphoreType.DMA((1 + 3 * micro,)),
         ],
         compiler_params=params(3 + 5 * layer),
@@ -1367,7 +1369,7 @@
 
 
 def prologue_kernel(
-    count, heads, qkv_ref, out_ref_t, up_ref_in, down_ref_t, gains_ref, shifts_ref, up_bias, rows_ref,
+    count, heads, qkv_ref, out_ref_in, up_ref_in, down_ref_t, gains_ref, shifts_ref, up_bias, rows_ref,
     first_hbm, normed_hbm, attn_ref, ff_zero_hbm, ff_one_hbm, out_ref, up_ref, bias_ref,
     attn_parts, ff_parts, up_halves, mine_ref, all_rows, line, ff_line, column, slab, up_got,
     rows_send, rows_recv, column_send, column_recv, slab_send, slab_recv, swap_send, swap_recv,
@@ -1387,9 +1389,10 @@
     main = half_ff // LANES * LANES
     extra = half_ff - main
     greet_all(count)
+    out_turned = low(out_ref_in[...].astype(jnp.float32).T)
     for half in range(2):
         span = slice(half * pair_cols, (half + 1) * pair_cols)
-        parts = [qkv_ref[k, :, span] for k in range(3)] + [out_ref_t[:, span]]
+        parts = [qkv_ref[k, :, span] for k in range(3)] + [out_turned[:, span]]
         attn_parts[half] = jnp.concatenate(parts, axis=1)
     keep_slot = jnp.where(section == 0, here, count)
     send_slot = jnp.where(section == 0, here, count)
@@ -1410,7 +1413,8 @@
     mine_ref[...] = jnp.zeros_like(mine_ref)
     gains = gains_ref.shape[0]
     mine_ref[:gains, :chunk] = gains_ref[...]
-    mine_ref[gains:, :chunk] = shifts_ref[...]
+    for i in range(shifts_ref.shape[0]):
+        mine_ref[gains + i : gains + i + 1, :chunk] = shifts_ref[i]
     column[here] = mine_ref[...]
     for step, to, _ in column_peers(count):
         copy = remote(
@@ -1578,7 +1582,7 @@
         copy.wait()
 
 
-def prologue(qkv, out_t, up, down_t, gains, shifts, up_bias, rows_low, count, heads, tile_rows):
+def prologue(qkv, out, up, down_t, gains, shifts, up_bias, rows_low, count, heads, tile_rows):
     part_rows = qkv.shape[1]
     micro, _, width = rows_low.shape
     vector_rows = gains.shape[0] + shifts.shape[0]
@@ -1632,7 +1636,7 @@
         compiler_params=params(4),
         cost_estimate=COST,
         name="prologue",
-    )(qkv, out_t, up, down_t, gains, shifts, up_bias, rows_low)
+    )(qkv, out, up, down_t, gains, shifts, up_bias, rows_low)
 
 
 def home_kernel(
@@ -1774,10 +1778,7 @@
             start = 2 * main + k * extra
             pieces += [half[:, k * main : (k + 1) * main], half[:, start : start + extra]]
         whole = jnp.concatenate(pieces, axis=1).astype(jnp.float32)
-        if k == 0:
-            up_ref[...] = whole
-        else:
-            down_ref[...] = whole.T
+        (up_ref, down_ref)[k][...] = whole
 
 
 def ff_finish(sums, got, ff_cols):
@@ -1786,7 +1787,7 @@
         ff_finish_kernel,
         out_shape=[
             shape_of((rows, ff_cols), jnp.float32),
-            shape_of((ff_cols, rows), jnp.float32),
+            shape_of((rows, ff_cols), jnp.float32),
         ],
         in_specs=[vmem_spec()] * 4,
         out_specs=[vmem_spec()] * 2,
@@ -1857,11 +1858,11 @@
     chunk = norm_gains.shape[2]
     first, normed, attn_part, ff_zero, ff_one, vectors, up_biases, bias_qv = prologue(
         qkv_weight[0],
-        out_weight[0].T,
+        out_weight[0],
         up_weight[0],
         down_weight[0].T,
         norm_gains[0],
-        biases[0],
+        biases.transpose(1, 0, 2),
         up_bias,
         section_input[:, 0],
         count,
@@ -1950,12 +1951,15 @@
         count,
         chunk,
     )
+    attn_zero_got = lax.ppermute(attn_sums[0], "section", [(1, 0)])
+    up_grad, down_grad = ff_finish([ff_sums[0], ff_sums[1]], [ff_got, errands[0]], ff_cols)
+    small_mine, up_total, rows_got, up_grad = lax.optimization_barrier(
+        (small_mine, up_total, rows_got, up_grad)
+    )
     small_mine = small_mine[None, :, :chunk]
     up_total = up_total[:, :, :half_ff].reshape(1, ff_cols)
     input_grad = whole_rows(input_grads[0], input_grads[1], rows_got)
 
-    attn_zero_got = lax.ppermute(attn_sums[0], "section", [(1, 0)])
-    up_grad, down_grad = ff_finish([ff_sums[0], ff_sums[1]], [ff_got, errands[0]], ff_cols)
     qkv_total, out_total = attn_finish(
         [attn_sums[0], attn_sums[1]], [attn_zero_got, attn_got], head_cols
     )
@@ -1966,7 +1970,7 @@
         qkv_total[None],
         out_total[None],
         up_grad[None],
-        down_grad[None],
+        down_grad.T[None],
         small_mine[:, :gains],
         small_mine[:, gains:],
         up_total,

time: 477 us -> 469 us (0.983)
  local copies, waits for them, and re-layouts: 13.5 us -> 6.78 us
    unnamed x28 -> x29, local copies, waits for them, and re-layouts: 8.47 us -> 2.42 us
    pallas_call x2, Pallas kernels: 105 us -> 100 us  [attn_backward(): pl.pallas_call(functools.partial(attn_backward_kernel, at, layer, own_row...]
  transfers between devices with their start and end apart: 8 -> 8, of which waited for: 3 -> 3; matrix products, arithmetic and copies ran while one was open for 3% -> 2% of each run, Pallas kernels for 67% -> 67%
where the time goes in v5:
time: 469 us; the launch traced here: 466 us
  Pallas kernels  420 us (90%)
  waiting for transfers between devices  17.9 us (4%)
  between operations  14.6 us (3%)
  local copies, waits for them, and re-layouts  6.78 us (1%)
  other arithmetic  5.01 us (1%)
    pallas_call x2, Pallas kernels, attn_backward(): pl.pallas_call(functools.partial(attn_backward_kernel, at, layer, own_row...  100 us
    pallas_call x2, Pallas kernels, attn_forward(): pl.pallas_call(functools.partial(attn_forward_kernel, given is not None,...  94 us
    pallas_call x1, Pallas kernels, ffn_turn(): pl.pallas_call(functools.partial(ffn_turn_kernel, half_ff, at, layer), ou...  57.6 us
    pallas_call x1, Pallas kernels, prologue(): pl.pallas_call(functools.partial(prologue_kernel, count, heads), out_shap...  45 us
    pallas_call x1, Pallas kernels, ffn_backward(): pl.pallas_call(functools.partial(ffn_backward_kernel, half_ff, at, layer)...  42 us
    pallas_call x1, Pallas kernels, ffn_forward(): pl.pallas_call(functools.partial(ffn_forward_kernel, half_ff, at, layer),...  41.6 us
    pallas_call x1, Pallas kernels, home(): pl.pallas_call(functools.partial(home_kernel, count, chunk), out_shape=[s...  32.9 us
  transfers between devices with their start and end apart: 8, of which 3 were waited for; matrix products, arithmetic and copies ran while one was open for 2% of the time, Pallas kernels for 67%

profile of v5, /device:TPU:0, one launch (start us, length us, event | category | flops | bytes accessed | tf_op | source)
XLA Modules:
  0.0 466.2 jit_solution(3061048732802090771)
XLA Ops:
  7.2 45.0 %prologue.1 = (bf16[1152,576]{1,0:T(8,128)(2,1)}, bf16[2,768,1152]{2,1,0:T(8,128)(2,1)}, bf16[288,576]{1,0:T(8,128)(2,1)}, bf16[288,1152]{1,0:T(8,128)(2,1)}, bf...) custom-call(bf16[3,288,288]{2,1,0:T(8,128)(2,1)} %bitcast.40, ...), custom_call_target="tpu_custom_call" | custom-call | flops 20000000000 | bytes 100000000 | tf_op jit(solution)/shard_map/prologue/pallas_call | solution.py:1597
  52.3 0.7 all-gather.6.cloned.1.call-update
  53.0 0.7 all-gather.8.cloned.1.call-update
  54.1 0.8 pad_dynamic-slice_fusion.1.rows_ref
  54.9 47.3 %attn_forward.2 = (f32[2,96,1152]{2,1,0:T(8,128)}, f32[2,2,768,128]{3,2,1,0:T(8,128)}, bf16[2,768,1152]{2,1,0:T(8,128)(2,1)}, bf16[2,768,768]{2,1,0:T(8,128)(2,1)}, bf16[2,768,256]{2,1,0:T(8,128)(2,1)}) custom-call(bf16[2,96,1152]{2,1,0:T(8,128)(2,1)} %pad_dynamic-slice_fusion.1.rows_ref, f32[2,8,1152]{2,1,0:T(8,128)} %get-tuple-element.62.vectors, ...), custom_call_target="tpu_custom_call" | custom-call | flops 20000000000 | bytes 100000000 | tf_op jit(solution)/shard_map/attn_forward/pallas_call | solution.py:1146
  102.2 0.8 pad_dynamic-slice_fusion.grad_ref
  103.0 4.0 all-gather.4.cloned.1.call-done.packed_hbm
  107.1 41.6 %ffn_forward.1 = (bf16[2,96,1152]{2,1,0:T(8,128)(2,1)}, bf16[2,768,1152]{2,1,0:T(8,128)(2,1)}, f32[2,768,640]{2,1,0:T(8,128)}) custom-call(f32[2,96,1152]{2,1,0:T(8,128)} %get-tuple-element.66.hidden_ref, f32[2,8,1152]{2,1,0:T(8,128)} %get-tuple-element.62.vectors, f32[2,1,640]{2,1,0:T(1,128)} %get-tuple-element.67.up_biases, ...), custom_call_target="tpu_custom_call" | custom-call | flops 20000000000 | bytes 100000000 | tf_op jit(solution)/shard_map/ffn_forward/pallas_call | solution.py:1194
  148.7 46.7 %attn_forward.3 = (f32[2,96,1152]{2,1,0:T(8,128)}, f32[2,2,768,128]{3,2,1,0:T(8,128)}, bf16[2,768,1152]{2,1,0:T(8,128)(2,1)}, bf16[2,768,768]{2,1,0:T(8,128)(2,1)}, bf16[2,768,256]{2,1,0:T(8,128)(2,1)}) custom-call(bf16[2,96,1152]{2,1,0:T(8,128)(2,1)} %get-tuple-element.69.rows_ref.grads_ref, f32[2,8,1152]{2,1,0:T(8,128)} %get-tuple-element.62.vectors, ...), custom_call_target="tpu_custom_call" | custom-call | flops 20000000000 | bytes 100000000 | tf_op jit(solution)/shard_map/attn_forward/pallas_call | solution.py:1146
  195.4 3.3 all-gather.8.cloned.1.call-done.packed_hbm
  198.6 57.6 %ffn_turn.1 = (bf16[2,96,1152]{2,1,0:T(8,128)(2,1)}, f32[2,96,1152]{2,1,0:T(8,128)}, bf16[1152,1152]{1,0:T(8,128)(2,1)}, f32[8,1152]{1,0:T(8,128)}, f32[8,640]{1,0:T(8,128)}) custom-call(f32[2,96,1152]{2,1,0:T(8,128)} %get-tuple-element.71.hidden_ref, bf16[2,96,1152]{2,1,0:T(8,128)(2,1)} %pad_dynamic-slice_fusion.grad_ref, ...), custom_call_target="tpu_custom_call" | custom-call | flops 20000000000 | bytes 100000000 | tf_op jit(solution)/shard_map/ffn_turn/pallas_call | solution.py:1224
  256.3 0.9 copy-done.1
  257.3 0.8 broadcast_select_fusion.6.errand_hbm
  258.1 50.6 %attn_backward.2 = (bf16[2,96,1152]{2,1,0:T(8,128)(2,1)}, bf16[1152,576]{1,0:T(8,128)(2,1)}, f32[8,1152]{1,0:T(8,128)}, f32[8,256]{1,0:T(8,128)}, bf16[2,96,1152]{2,1,0:T(8,128)(2,1)}) custom-call(f32[2,96,1152]{2,1,0:T(8,128)} %get-tuple-element.75.grad_ref, bf16[2,96,1152]{2,1,0:T(8,128)(2,1)} %get-tuple-element.69.rows_ref.grads_ref, ...), custom_call_target="tpu_custom_call" | custom-call | flops 20000000000 | bytes 100000000 | tf_op jit(solution)/shard_map/attn_backward/pallas_call | solution.py:1295
  308.8 42.0 %ffn_backward.1 = (f32[2,96,1152]{2,1,0:T(8,128)}, bf16[1152,1152]{1,0:T(8,128)(2,1)}, f32[8,1152]{1,0:T(8,128)}, f32[8,640]{1,0:T(8,128)}) custom-call(bf16[2,96,1152]{2,1,0:T(8,128)(2,1)} %get-tuple-element.81.grad_ref, f32[2,96,1152]{2,1,0:T(8,128)} %get-tuple-element.66.hidden_ref, f32[2,8,1152]{2,1,0:T(8,128)} %get-tuple-element.62.vectors, ...), custom_call_target="tpu_custom_call" | custom-call | flops 20000000000 | bytes 100000000 | tf_op jit(solution)/shard_map/ffn_backward/pallas_call | solution.py:1259
  351.1 0.7 slice_bitcast_fusion.1
  351.8 0.7 slice_bitcast_fusion.2
  352.6 0.6 pad_maximum_fusion.3.ups_in
  353.3 1.0 fusion.1
  354.3 49.8 %attn_backward.3 = (bf16[2,96,1152]{2,1,0:T(8,128)(2,1)}, bf16[1152,576]{1,0:T(8,128)(2,1)}, f32[8,1152]{1,0:T(8,128)}, f32[8,256]{1,0:T(8,128)}, bf16[288,1152]{1,0:T(8,128)(2,1)}) custom-call(f32[2,96,1152]{2,1,0:T(8,128)} %get-tuple-element.84.grad_ref, bf16[2,96,1152]{2,1,0:T(8,128)(2,1)} %pad_dynamic-slice_fusion.1.rows_ref, ...), custom_call_target="tpu_custom_call" | custom-call | flops 20000000000 | bytes 100000000 | tf_op jit(solution)/shard_map/attn_backward/pallas_call | solution.py:1295
  404.2 0.8 broadcast_select_fusion.2.rows_hbm
  405.0 0.6 pad_maximum_fusion.2.biases_in
  405.6 32.9 %home.1 = (f32[8,128]{1,0:T(8,128)}, f32[2,1,640]{2,1,0:T(1,128)}, bf16[288,1152]{1,0:T(8,128)(2,1)}, bf16[288,576]{1,0:T(8,128)(2,1)}, bf16[2,96,1152]{2,1,0:T(8,128)(2,1)}) custom-call(f32[8,1152]{1,0:T(8,128)} %get-tuple-element.90.attn_zero, f32[8,1152]{1,0:T(8,128)} %get-tuple-element.91.attn_one, f32[8,1152]{1,0:T(8,128)} %get-tuple-element.92.ff_zero, ...), custom_call_target="tpu_custom_call" | custom-call | flops 20000000000 | bytes 100000000 | tf_op jit(solution)/shard_map/home/pallas_call | solution.py:1731
  438.6 3.6 ff_finish.1
  442.2 0.6 slice.29
  442.7 0.6 copy.21
  443.5 1.3 collective-permute-start
  444.8 0.7 reshape.25
  445.5 1.0 fusion
  446.4 9.2 %collective-permute-done.zero_got = bf16[288,576]{1,0:T(8,128)(2,1)S(1)} collective-permute-done((bf16[288,576]{1,0:T(8,128)(2,1)}, bf16[288,576]{1,0:T(8,128)(2,1)S(1)}, u32[]{:S(2)}, u32[]{:S(2)}) %collective-permute-start) | collective-permute-done | bytes 331808 | tf_op jit(solution)/shard_map/ppermute | solution.py:1954
  455.6 0.7 copy-done.9
  456.3 2.8 attn_finish.1
  (48 shorter events, 1.4 us)
Async XLA Ops:
  7.2 99.9 %all-gather.4.cloned.1.call-start = ((), (), s32[]{:S(2)}) async-start(), calls=%async_computation.4 | async-start | bytes 3317760 | tf_op jit(solution)/shard_map/all_gather | solution.py:1874
  52.2 1.9 copy-start.5
  52.2 96.5 %all-gather.6.cloned.1.call-start = ((), (), s32[]{:S(2)}) async-start(), calls=%async_computation.5 | async-start | bytes 1843200 | tf_op jit(solution)/shard_map/all_gather | solution.py:1874
  53.0 145.6 %all-gather.8.cloned.1.call-start = ((), (), s32[]{:S(2)}) async-start(), calls=%async_computation.6 | async-start | bytes 3317760 | tf_op jit(solution)/shard_map/all_gather | solution.py:1874
  53.7 300.6 %reduce-scatter.5.cloned.1.call-start = ((), (), s32[]{:S(2)}) async-start(), calls=%async_computation.7 | async-start | bytes 3317760 | tf_op jit(solution)/shard_map/reduce_scatter | solution.py:1921
  54.9 47.4 %copy-start.6 = (bf16[2,1,184,1152]{3,2,1,0:T(8,128)(2,1)S(1)}, bf16[2,1,184,1152]{3,2,1,0:T(8,128)(2,1)}, u32[]{:S(2)}) copy-start(bf16[2,1,184,1152]{3,2,1,0:T(8,128)(2,1)} %param.11) | copy-start | bytes 2543620
  256.2 1.0 copy-start.1
  256.2 1.1 copy-start.3
  256.2 149.4 %reduce-scatter.9.cloned.1.call-start = ((), (), s32[]{:S(2)}) async-start(), calls=%async_computation.9 | async-start | bytes 1843200 | tf_op jit(solution)/shard_map/reduce_scatter | solution.py:1939
  308.7 96.9 %reduce-scatter.7.cloned.1.call-start = ((), (), s32[]{:S(2)}) async-start(), calls=%async_computation.8 | async-start | bytes 3317760 | tf_op jit(solution)/shard_map/reduce_scatter | solution.py:1921
  350.8 2.4 copy-start.2
  350.8 2.4 copy-start.7
  350.8 92.6 %reduce-scatter.11.cloned.1.call-start = ((), (), s32[]{:S(2)}) async-start(), calls=%async_computation.10 | async-start | bytes 1843200 | tf_op jit(solution)/shard_map/reduce_scatter | solution.py:1939
  354.3 49.9 %copy-start = (bf16[2,96,1152]{2,1,0:T(8,128)(2,1)S(1)}, bf16[2,96,1152]{2,1,0:T(8,128)(2,1)}, u32[]{:S(2)}) copy-start(bf16[2,96,1152]{2,1,0:T(8,128)(2,1)} %get-tuple-element.81.grad_ref) | copy-start | bytes 1327108
  404.1 0.9 copy-start.10
  404.1 0.9 copy-start.11
  438.5 3.6 copy-start.13
  438.5 4.8 %copy-start.4 = (bf16[2,96,1152]{2,1,0:T(8,128)(2,1)S(1)}, bf16[2,96,1152]{2,1,0:T(8,128)(2,1)}, u32[]{:S(2)}) copy-start(bf16[2,96,1152]{2,1,0:T(8,128)(2,1)} %get-tuple-element.89) | copy-start | bytes 1327108
  438.5 4.8 %copy-start.8 = (bf16[2,96,1152]{2,1,0:T(8,128)(2,1)S(1)}, bf16[2,96,1152]{2,1,0:T(8,128)(2,1)}, u32[]{:S(2)}) copy-start(bf16[2,96,1152]{2,1,0:T(8,128)(2,1)} %get-tuple-element.106) | copy-start | bytes 1327108
  442.1 2.6 copy-start.12
  443.5 12.1 %collective-permute-start = (bf16[288,576]{1,0:T(8,128)(2,1)}, bf16[288,576]{1,0:T(8,128)(2,1)S(1)}, u32[]{:S(2)}, u32[]{:S(2)}) collective-permute-start(bf16[288,576]{1,0:T(8,128)(2,1)} %reduce-scatter.11.cloned.1.call-done.zero), channel_id=1, source_target_pairs={{16,0},{17,1},{18,2},{19,3},{20,4},{21,5},{22,6},{23,7},{24,8},{25... | collective-permute-start | bytes 995336 | tf_op jit(solution)/shard_map/ppermute | solution.py:1954
  455.6 0.7 copy-start.9
Sparse Core Ops, SparseCore 0:
  52.3 54.6 all-gather.3
  108.6 34.0 all-gather.5
  144.3 54.2 all-gather.7
  256.3 50.6 reduce-scatter.4
  309.2 33.5 reduce-scatter.8
  351.0 50.7 reduce-scatter.6
  405.1 34.6 reduce-scatter.10

commit v6 on v5

--- a/solution.py
+++ b/solution.py
@@ -203,10 +203,9 @@
         self.copy(m, index, role, peer).start()
         self.sent.append(lambda: self.copy(m, index, role, peer))
 
-    def start(self):
-        for m in range(self.micro):
-            self.send(m, self.tensor, 0, self.over)
-            self.send(m, self.tensor, 1, self.mate)
+    def start(self, m):
+        self.send(m, self.tensor, 0, self.over)
+        self.send(m, self.tensor, 1, self.mate)
 
     def pass_on(self):
         for m in range(self.micro):
@@ -467,7 +466,7 @@
             count = grads_ref.shape[1]
             own[:count] = grads_ref[m]
             own[count:] = jnp.zeros((tiles.tile_rows - count, width), jnp.bfloat16)
-        tiles.start()
+            tiles.start(m)
 
     def fill(m):
         own = slab.rows(gathered.at[m], slab.mine[0])
@@ -912,7 +911,7 @@
 
 def attn_backward_kernel(
     at, layer, own_rows, both_ways, grad_ref, rows_ref, vectors, lse, lengths,
-    normed_hbm, qkv_hbm, mixed_hbm, packed_hbm, errand_hbm,
+    normed_hbm, qkv_hbm, mixed_hbm, packed_hbm, errand_hbm, errand_one_hbm,
     out_ref, grads_ref, small_ref, bias_ref, errand_got, *rest
 ):
     micro, half_rows, width = grad_ref.shape
@@ -974,16 +973,19 @@
     errands = []
     for k, part in enumerate((pl.ds(0, cut), pl.ds(cut, span - cut))):
         errands.append(
-            remote(
-                errand_hbm.at[part],
-                errand_got.at[part],
-                errand_sems.at[0, k],
-                errand_sems.at[1, k],
-                {"section": 1 - lax.axis_index("section")},
-            )
+            [
+                remote(
+                    source.at[part],
+                    errand_got.at[part],
+                    errand_sems.at[0, k],
+                    errand_sems.at[1, k],
+                    {"section": 1 - lax.axis_index("section")},
+                )
+                for source in (errand_hbm, errand_one_hbm)
+            ]
         )
-    sends_errand = (lax.axis_index("section") == 0) | both_ways
-    gets_errand = (lax.axis_index("section") == 1) | both_ways
+    first_section = lax.axis_index("section") == 0
+    sends_errand, gets_errand = first_section | both_ways, ~first_section | both_ways
 
     def prepare():
         small_ref[...] = jnp.zeros_like(small_ref)
@@ -1057,7 +1059,9 @@
                 small_ref[j : j + 1] += jnp.sum(item, axis=0, keepdims=True)
 
     def start_errand(k):
-        pl.when(sends_errand)(errands[k].start)
+        pl.when(first_section)(errands[k][0].start)
+        if both_ways:
+            pl.when(~first_section)(errands[k][1].start)
 
     stages(
         2 * heads,
@@ -1110,7 +1114,7 @@
     weight_grads({0: [one.first_hop]})
     close(1)
 
-    for errand in errands:
+    for errand, _ in errands:
         pl.when(sends_errand)(errand.wait_send)
         pl.when(gets_errand)(errand.wait_recv)
 
@@ -1248,7 +1252,7 @@
         cost_estimate=COST,
         name="ffn_turn",
     )(hidden, grad_low, vectors, up_biases, given, packed)
-    return out, grad_hidden, grads, small, up_bias[:1]
+    return out, grad_hidden, grads, small, up_bias
 
 
 def ffn_backward(grad_low, hidden, kept, vectors, packed, at, layer, half_ff):
@@ -1281,7 +1285,7 @@
         cost_estimate=COST,
         name="ffn_backward",
     )(grad_low, hidden, vectors, second, upper, packed)
-    return grad_hidden, grads, small, up_bias[:1]
+    return grad_hidden, grads, small, up_bias
 
 
 def attn_backward(
@@ -1299,9 +1303,9 @@
             shape_of((width, 4 * heads * HEAD), low_type),
             shape_of((8, width), high_type),
             shape_of((8, pair), high_type),
-            shape_of(errand.shape, errand.dtype),
+            shape_of(errand[0].shape, errand[0].dtype),
         ],
-        in_specs=[vmem_spec()] * 4 + [smem_spec()] + [any_spec()] * 5,
+        in_specs=[vmem_spec()] * 4 + [smem_spec()] + [any_spec()] * 6,
         out_specs=[vmem_spec()] * 4 + [any_spec()],
         scratch_shapes=gather_scratch(micro, seq, width)
         + scatter_scratch(micro, seq, half_rows, width)
@@ -1324,7 +1328,7 @@
         compiler_params=params(3 + 5 * layer),
         cost_estimate=COST,
         name="attn_backward",
-    )(grad_hidden, rows_low, vectors, lse, lengths, normed, qkv, mixed, packed, errand)
+    )(grad_hidden, rows_low, vectors, lse, lengths, normed, qkv, mixed, packed, *errand)
     return out, grads, small, bias, got
 
 
@@ -1467,14 +1471,31 @@
         copy.start()
         sent.append(copy)
     slab[section, tensor] = column[...]
-    for p in range(pieces):
-
-        @pl.when(section == 1)
-        def _():
-            swapped(p)
-
+
+    def set_out(p):
+        pl.when(section == 1)(lambda: swapped(p))
         for way in (1, -1):
             hop(0, p, way)
+
+    set_out(0)
+    for role, _, source in slab_peers():
+        slot = slab.at[source[0], source[1]]
+        remote(slot, slot, slab_send.at[role], slab_recv.at[role], named(source)).wait_recv()
+    for layer in range(2):
+        for part in range(4 * count):
+            piece = slab[layer, part % 4, part // 4]
+            out_ref[layer, :, part * chunk : (part + 1) * chunk] = piece[:, :chunk]
+    tiles = TileGather(all_rows, rows_send, rows_recv)
+    for m in range(micro):
+        own = tiles.tile(m, tensor)
+        for begin in range(0, own_rows, 32):
+            end = min(begin + 32, own_rows)
+            block = rows_ref[m, begin:end].astype(jnp.float32)
+            own[begin:end] = low(layer_norm(block, out_ref[0, 0:1], out_ref[0, 2:3]))
+        own[own_rows:] = jnp.zeros((tiles.tile_rows - own_rows, width), jnp.bfloat16)
+        tiles.start(m)
+    for p in range(1, pieces):
+        set_out(p)
     blank = jnp.zeros((rows, LANES - 2 * extra), jnp.bfloat16)
     up_halves[...] = jnp.zeros_like(up_halves)
     for half in range(2):
@@ -1501,23 +1522,7 @@
         other,
     )
     up_swap.start()
-    for role, _, source in slab_peers():
-        slot = slab.at[source[0], source[1]]
-        remote(slot, slot, slab_send.at[role], slab_recv.at[role], named(source)).wait_recv()
     ff_swap.start()
-    for layer in range(2):
-        for part in range(4 * count):
-            piece = slab[layer, part % 4, part // 4]
-            out_ref[layer, :, part * chunk : (part + 1) * chunk] = piece[:, :chunk]
-    tiles = TileGather(all_rows, rows_send, rows_recv)
-    for m in range(micro):
-        own = tiles.tile(m, tensor)
-        for begin in range(0, own_rows, 32):
-            end = min(begin + 32, own_rows)
-            block = rows_ref[m, begin:end].astype(jnp.float32)
-            own[begin:end] = low(layer_norm(block, out_ref[0, 0:1], out_ref[0, 2:3]))
-        own[own_rows:] = jnp.zeros((tiles.tile_rows - own_rows, width), jnp.bfloat16)
-    tiles.start()
     hops(1)
     start = (2 * tensor + section) * pair_cols
     for layer in range(2):
@@ -1640,21 +1645,22 @@
 
 
 def home_kernel(
-    count, chunk, attn_zero, attn_one, ff_zero, ff_one, biases_in, ups_in,
-    ff_sum_hbm, attn_sum_hbm, rows_hbm,
+    count, chunk, attn_zero, attn_one, ff_zero, ff_one, bias_zero, bias_one, up_zero, up_one,
+    ff_sum_hbm, attn_sum_hbm, rows_zero_hbm, rows_one_hbm,
     out_ref, up_ref, ff_got_hbm, attn_got_hbm, rows_got_hbm,
     parts, ups, slab, column, up_pair, up_column, total,
     column_send, column_recv, slab_send, slab_recv, up_sems, up_column_send, up_column_recv, far_send, far_recv,
 ):
     section, tensor, here = (lax.axis_index(name) for name in ("section", "tensor", "dp"))
     width = attn_zero.shape[1]
-    heads = biases_in.shape[2] // LANES
+    heads = bias_zero.shape[1] // LANES
+    biases_in, ups_in = (bias_zero, bias_one), (up_zero, up_one)
     other = {"section": 1 - section}
     greet_all(count)
     parts[...] = jnp.zeros_like(parts)
     start = (2 * tensor + section) * (heads * HEAD)
     for layer, (attn, ff) in enumerate(((attn_zero, ff_zero), (attn_one, ff_one))):
-        bias = biases_in[layer]
+        bias = biases_in[layer][...]
         blank = jnp.zeros((8, width - heads * HEAD), jnp.float32)
         pieces = [bias[:, h * LANES : h * LANES + HEAD] for h in range(heads)]
         placed = pltpu.roll(jnp.concatenate(pieces + [blank], 1), start, 1)
@@ -1664,7 +1670,7 @@
         for part in range(4 * count):
             piece = whole[:, part * chunk : (part + 1) * chunk]
             parts[layer, part % 4, part // 4, :, :chunk] = piece
-        ups[layer] = ups_in[layer]
+        ups[layer] = ups_in[layer][0:1]
     sent = []
 
     def send(src, dst, send_sem, recv_sem, peer):
@@ -1677,11 +1683,13 @@
         send(
             parts.at[to[0], to[1]], slab.at[role], slab_send.at[role], slab_recv.at[role], named(to)
         )
-    far_rows = remote(rows_hbm, rows_got_hbm, far_send.at[0], far_recv.at[0], other)
+    far_rows = remote(rows_zero_hbm, rows_got_hbm, far_send.at[0], far_recv.at[0], other)
+    far_rows_one = remote(rows_one_hbm, rows_got_hbm, far_send.at[0], far_recv.at[0], other)
     far_ff = remote(ff_sum_hbm, ff_got_hbm, far_send.at[1], far_recv.at[1], other)
     far_attn = remote(attn_sum_hbm, attn_got_hbm, far_send.at[2], far_recv.at[2], other)
     one_way = ((far_ff, 1), (far_attn, 0))
-    far_rows.start()
+    pl.when(section == 1)(far_rows.start)
+    pl.when(section == 0)(far_rows_one.start)
     for copy, source in one_way:
         pl.when(section == source)(copy.start)
     up_pair[section] = ups[section]
@@ -1725,7 +1733,7 @@
 
 def home(attn_small, ff_small, bias_grads, up_grads, ff_sum, attn_sum, rows, count, chunk):
     vector_rows, lanes = 8, LANES
-    up_shape = up_grads.shape[1:]
+    up_shape = (1, up_grads[0].shape[1])
     dma = pltpu.SemaphoreType.DMA
     high_type = jnp.float32
     return pl.pallas_call(
@@ -1735,9 +1743,9 @@
             shape_of((2,) + up_shape, high_type),
             shape_of(ff_sum.shape, ff_sum.dtype),
             shape_of(attn_sum.shape, attn_sum.dtype),
-            shape_of(rows.shape, rows.dtype),
+            shape_of(rows[0].shape, rows[0].dtype),
         ],
-        in_specs=[vmem_spec()] * 6 + [any_spec()] * 3,
+        in_specs=[vmem_spec()] * 8 + [any_spec()] * 4,
         out_specs=[vmem_spec()] * 2 + [any_spec()] * 3,
         scratch_shapes=[
             pltpu.VMEM((2, 4, count, vector_rows, lanes), high_type),
@@ -1760,7 +1768,7 @@
         compiler_params=params(5),
         cost_estimate=COST,
         name="home",
-    )(*attn_small, *ff_small, bias_grads, up_grads, ff_sum, attn_sum, rows)
+    )(*attn_small, *ff_small, *bias_grads, *up_grads, ff_sum, attn_sum, *rows)
 
 
 def ff_finish_kernel(zero, one, zero_got, one_got, up_ref, down_ref):
@@ -1920,9 +1928,9 @@
             )
         ff_sums[layer] = lax.psum_scatter(ff_grad, "dp", scatter_dimension=0, tiled=True)
         if layer == 1:
-            errand, both_ways = jnp.where(here == 0, last, rows), True
+            errand, both_ways = (last, rows), True
         else:
-            errand, both_ways = ff_sums[1], False
+            errand, both_ways = (ff_sums[1], ff_sums[1]), False
         grads, attn_grad, attn_small[layer], bias_grads[layer], got = attn_backward(
             grad_hidden,
             inputs[layer],
@@ -1939,23 +1947,23 @@
         attn_sums[layer] = lax.psum_scatter(attn_grad, "dp", scatter_dimension=0, tiled=True)
         input_grads[layer] = grads
 
-    section_output = whole_rows(rows, last, errands[1])
     small_mine, up_total, ff_got, attn_got, rows_got = home(
         [attn_small[0], attn_small[1]],
         [ff_small[0], ff_small[1]],
-        jnp.stack([bias_grads[0], bias_grads[1]]),
-        jnp.stack([up_sums[0], up_sums[1]]),
+        [bias_grads[0], bias_grads[1]],
+        [up_sums[0], up_sums[1]],
         ff_sums[0],
         attn_sums[1],
-        jnp.where(here == 0, input_grads[1], input_grads[0]),
+        [input_grads[0], input_grads[1]],
         count,
         chunk,
     )
     attn_zero_got = lax.ppermute(attn_sums[0], "section", [(1, 0)])
     up_grad, down_grad = ff_finish([ff_sums[0], ff_sums[1]], [ff_got, errands[0]], ff_cols)
-    small_mine, up_total, rows_got, up_grad = lax.optimization_barrier(
-        (small_mine, up_total, rows_got, up_grad)
-    )
+    small_mine, up_total, rows_got, out_got, up_grad = lax.optimization_barrier(
+        (small_mine, up_total, rows_got, errands[1], up_grad)
+    )
+    section_output = whole_rows(rows, last, out_got)
     small_mine = small_mine[None, :, :chunk]
     up_total = up_total[:, :, :half_ff].reshape(1, ff_cols)
     input_grad = whole_rows(input_grads[0], input_grads[1], rows_got)

time: 469 us -> 462 us (0.985)
  transfers between devices with their start and end apart: 8 -> 8, of which waited for: 3 -> 4; matrix products, arithmetic and copies ran while one was open for 2% -> 1% of each run, Pallas kernels for 67% -> 68%
where the time goes in v6:
time: 462 us; the launch traced here: 460 us
  Pallas kernels  418 us (90%)
  waiting for transfers between devices  18.2 us (4%)
  between operations  14.6 us (3%)
  local copies, waits for them, and re-layouts  5.37 us (1%)
    pallas_call x2, Pallas kernels, attn_backward(): pl.pallas_call(functools.partial(attn_backward_kernel, at, layer, own_row...  99.9 us
    pallas_call x2, Pallas kernels, attn_forward(): pl.pallas_call(functools.partial(attn_forward_kernel, given is not None,...  92.4 us
    pallas_call x1, Pallas kernels, ffn_turn(): pl.pallas_call(functools.partial(ffn_turn_kernel, half_ff, at, layer), ou...  57.6 us
    pallas_call x1, Pallas kernels, prologue(): pl.pallas_call(functools.partial(prologue_kernel, count, heads), out_shap...  46.8 us
    pallas_call x1, Pallas kernels, ffn_backward(): pl.pallas_call(functools.partial(ffn_backward_kernel, half_ff, at, layer)...  42 us
    pallas_call x1, Pallas kernels, ffn_forward(): pl.pallas_call(functools.partial(ffn_forward_kernel, half_ff, at, layer),...  41.6 us
    pallas_call x1, Pallas kernels, home(): pl.pallas_call(functools.partial(home_kernel, count, chunk), out_shape=[s...  31.3 us
  transfers between devices with their start and end apart: 8, of which 4 were waited for; matrix products, arithmetic and copies ran while one was open for 1% of the time, Pallas kernels for 68%

profile of v6, /device:TPU:0, one launch (start us, length us, event | category | flops | bytes accessed | tf_op | source)
XLA Modules:
  0.0 459.5 jit_solution(15670457355782483048)
XLA Ops:
  7.2 46.8 %prologue.1 = (bf16[1152,576]{1,0:T(8,128)(2,1)}, bf16[2,768,1152]{2,1,0:T(8,128)(2,1)}, bf16[288,576]{1,0:T(8,128)(2,1)}, bf16[288,1152]{1,0:T(8,128)(2,1)}, bf...) custom-call(bf16[3,288,288]{2,1,0:T(8,128)(2,1)} %bitcast.32, ...), custom_call_target="tpu_custom_call" | custom-call | flops 20000000000 | bytes 100000000 | tf_op jit(solution)/shard_map/prologue/pallas_call | solution.py:1602
  54.2 0.7 all-gather.6.cloned.1.call-update
  54.9 0.7 all-gather.8.cloned.1.call-update
  55.6 0.3 reduce-scatter.5.cloned.1.call-start
  55.9 0.8 pad_dynamic-slice_fusion.1.rows_ref
  56.8 45.7 %attn_forward.2 = (f32[2,96,1152]{2,1,0:T(8,128)}, f32[2,2,768,128]{3,2,1,0:T(8,128)}, bf16[2,768,1152]{2,1,0:T(8,128)(2,1)}, bf16[2,768,768]{2,1,0:T(8,128)(2,1)}, bf16[2,768,256]{2,1,0:T(8,128)(2,1)}) custom-call(bf16[2,96,1152]{2,1,0:T(8,128)(2,1)} %pad_dynamic-slice_fusion.1.rows_ref, f32[2,8,1152]{2,1,0:T(8,128)} %get-tuple-element.63.vectors, ...), custom_call_target="tpu_custom_call" | custom-call | flops 20000000000 | bytes 100000000 | tf_op jit(solution)/shard_map/attn_forward/pallas_call | solution.py:1150
  102.5 0.8 pad_dynamic-slice_fusion.grad_ref
  103.3 4.8 %all-gather.4.cloned.1.call-done.packed_hbm = bf16[1152,1152]{1,0:T(8,128)(2,1)} async-done(((bf16[288,1152]{1,0:T(8,128)(2,1)}), bf16[1152,1152]{1,0:T(8,128)(2,1)}) %all-gather.4.cloned.1.call-update) | async-done | bytes 2654224 | tf_op jit(solution)/shard_map/all_gather | solution.py:1882
  108.1 41.6 %ffn_forward.1 = (bf16[2,96,1152]{2,1,0:T(8,128)(2,1)}, bf16[2,768,1152]{2,1,0:T(8,128)(2,1)}, f32[2,768,640]{2,1,0:T(8,128)}) custom-call(f32[2,96,1152]{2,1,0:T(8,128)} %get-tuple-element.67.hidden_ref, f32[2,8,1152]{2,1,0:T(8,128)} %get-tuple-element.63.vectors, f32[2,1,640]{2,1,0:T(1,128)} %get-tuple-element.68.up_biases, ...), custom_call_target="tpu_custom_call" | custom-call | flops 20000000000 | bytes 100000000 | tf_op jit(solution)/shard_map/ffn_forward/pallas_call | solution.py:1198
  149.8 46.7 %attn_forward.3 = (f32[2,96,1152]{2,1,0:T(8,128)}, f32[2,2,768,128]{3,2,1,0:T(8,128)}, bf16[2,768,1152]{2,1,0:T(8,128)(2,1)}, bf16[2,768,768]{2,1,0:T(8,128)(2,1)}, bf16[2,768,256]{2,1,0:T(8,128)(2,1)}) custom-call(bf16[2,96,1152]{2,1,0:T(8,128)(2,1)} %get-tuple-element.70.rows_ref.grads_ref.errand_one_hbm, f32[2,8,1152]{2,1,0:T(8,128)} %get-tuple-element.63.vectors, ...), custom_call_target="tpu_custom_call" | custom-call | flops 20000000000 | bytes 100000000 | tf_op jit(solution)/shard_map/attn_forward/pallas_call | solution.py:1150
  196.4 3.2 all-gather.8.cloned.1.call-done.packed_hbm
  199.6 57.6 %ffn_turn.1 = (bf16[2,96,1152]{2,1,0:T(8,128)(2,1)}, f32[2,96,1152]{2,1,0:T(8,128)}, bf16[1152,1152]{1,0:T(8,128)(2,1)}, f32[8,1152]{1,0:T(8,128)}, f32[8,640]{1,0:T(8,128)}) custom-call(f32[2,96,1152]{2,1,0:T(8,128)} %get-tuple-element.72.hidden_ref, bf16[2,96,1152]{2,1,0:T(8,128)(2,1)} %pad_dynamic-slice_fusion.grad_ref, ...), custom_call_target="tpu_custom_call" | custom-call | flops 20000000000 | bytes 100000000 | tf_op jit(solution)/shard_map/ffn_turn/pallas_call | solution.py:1228
  257.3 50.5 %attn_backward.2 = (bf16[2,96,1152]{2,1,0:T(8,128)(2,1)}, bf16[1152,576]{1,0:T(8,128)(2,1)}, f32[8,1152]{1,0:T(8,128)}, f32[8,256]{1,0:T(8,128)}, bf16[2,96,1152]{2,1,0:T(8,128)(2,1)}) custom-call(f32[2,96,1152]{2,1,0:T(8,128)} %get-tuple-element.76.grad_ref, bf16[2,96,1152]{2,1,0:T(8,128)(2,1)} %get-tuple-element.70.rows_ref.grads_ref.errand_one_hbm, ...), custom_call_target="tpu_custom_call" | custom-call | flops 20000000000 | bytes 100000000 | tf_op jit(solution)/shard_map/attn_backward/pallas_call | solution.py:1299
  307.9 42.0 %ffn_backward.1 = (f32[2,96,1152]{2,1,0:T(8,128)}, bf16[1152,1152]{1,0:T(8,128)(2,1)}, f32[8,1152]{1,0:T(8,128)}, f32[8,640]{1,0:T(8,128)}) custom-call(bf16[2,96,1152]{2,1,0:T(8,128)(2,1)} %get-tuple-element.81.grad_ref.rows_one_hbm, f32[2,96,1152]{2,1,0:T(8,128)} %get-tuple-element.67.hidden_ref, f32[2,8,1152]{2,1,0:T(8,128)} %get-tuple-element.63.vectors, ...), custom_call_target="tpu_custom_call" | custom-call | flops 20000000000 | bytes 100000000 | tf_op jit(solution)/shard_map/ffn_backward/pallas_call | solution.py:1263
  350.0 0.0 reduce-scatter.11.cloned.1.call-start
  350.0 49.4 %attn_backward.3 = (bf16[2,96,1152]{2,1,0:T(8,128)(2,1)}, bf16[1152,576]{1,0:T(8,128)(2,1)}, f32[8,1152]{1,0:T(8,128)}, f32[8,256]{1,0:T(8,128)}, bf16[288,1152]{1,0:T(8,128)(2,1)}) custom-call(f32[2,96,1152]{2,1,0:T(8,128)} %get-tuple-element.84.grad_ref, bf16[2,96,1152]{2,1,0:T(8,128)(2,1)} %pad_dynamic-slice_fusion.1.rows_ref, ...), custom_call_target="tpu_custom_call" | custom-call | flops 20000000000 | bytes 100000000 | tf_op jit(solution)/shard_map/attn_backward/pallas_call | solution.py:1299
  399.5 1.4 reduce-scatter.7.cloned.1.call-done.ff_sum_hbm.zero
  400.9 31.3 %home.1 = (f32[8,128]{1,0:T(8,128)}, f32[2,1,640]{2,1,0:T(1,128)}, bf16[288,1152]{1,0:T(8,128)(2,1)}, bf16[288,576]{1,0:T(8,128)(2,1)}, bf16[2,96,1152]{2,1,0:T(8,128)(2,1)}) custom-call(f32[8,1152]{1,0:T(8,128)} %get-tuple-element.89.attn_zero, f32[8,1152]{1,0:T(8,128)} %get-tuple-element.90.attn_one, f32[8,1152]{1,0:T(8,128)} %get-tuple-element.91.ff_zero, ...), custom_call_target="tpu_custom_call" | custom-call | flops 20000000000 | bytes 100000000 | tf_op jit(solution)/shard_map/home/pallas_call | solution.py:1739
  432.2 3.6 ff_finish.1
  435.9 0.1 broadcast_select_fusion.4
  436.0 0.8 copy-done.4
  436.9 0.1 copy-done.6
  437.0 0.1 copy-done.7
  437.1 0.1 broadcast_select_fusion.1
  437.3 1.3 collective-permute-start
  438.6 0.6 slice.21
  439.2 0.6 copy.21
  439.8 0.7 reshape.25
  440.4 1.3 fusion
  441.8 7.2 %collective-permute-done.zero_got = bf16[288,576]{1,0:T(8,128)(2,1)S(1)} collective-permute-done((bf16[288,576]{1,0:T(8,128)(2,1)}, bf16[288,576]{1,0:T(8,128)(2,1)S(1)}, u32[]{:S(2)}, u32[]{:S(2)}) %collective-permute-start) | collective-permute-done | bytes 331808 | tf_op jit(solution)/shard_map/ppermute | solution.py:1961
  448.9 0.7 copy-done.8
  449.7 2.8 attn_finish.1
  (35 shorter events, 0.4 us)
Async XLA Ops:
  7.2 100.9 %all-gather.4.cloned.1.call-start = ((), (), s32[]{:S(2)}) async-start(), calls=%async_computation.4 | async-start | bytes 3317760 | tf_op jit(solution)/shard_map/all_gather | solution.py:1882
  54.1 1.9 copy-start
  54.1 95.7 %all-gather.6.cloned.1.call-start = ((), (), s32[]{:S(2)}) async-start(), calls=%async_computation.5 | async-start | bytes 1843200 | tf_op jit(solution)/shard_map/all_gather | solution.py:1882
  54.9 144.8 %all-gather.8.cloned.1.call-start = ((), (), s32[]{:S(2)}) async-start(), calls=%async_computation.6 | async-start | bytes 3317760 | tf_op jit(solution)/shard_map/all_gather | solution.py:1882
  55.6 294.4 %reduce-scatter.5.cloned.1.call-start = ((), (), s32[]{:S(2)}) async-start(), calls=%async_computation.7 | async-start | bytes 3317760 | tf_op jit(solution)/shard_map/reduce_scatter | solution.py:1929
  56.8 45.7 %copy-start.1 = (bf16[2,1,184,1152]{3,2,1,0:T(8,128)(2,1)S(1)}, bf16[2,1,184,1152]{3,2,1,0:T(8,128)(2,1)}, u32[]{:S(2)}) copy-start(bf16[2,1,184,1152]{3,2,1,0:T(8,128)(2,1)} %param.11) | copy-start | bytes 2543620
  257.2 142.3 %reduce-scatter.9.cloned.1.call-start = ((), (), s32[]{:S(2)}) async-start(), calls=%async_computation.9 | async-start | bytes 1843200 | tf_op jit(solution)/shard_map/reduce_scatter | solution.py:1947
  307.9 93.0 %reduce-scatter.7.cloned.1.call-start = ((), (), s32[]{:S(2)}) async-start(), calls=%async_computation.8 | async-start | bytes 3317760 | tf_op jit(solution)/shard_map/reduce_scatter | solution.py:1929
  350.0 87.3 %reduce-scatter.11.cloned.1.call-start = ((), (), s32[]{:S(2)}) async-start(), calls=%async_computation.10 | async-start | bytes 1843200 | tf_op jit(solution)/shard_map/reduce_scatter | solution.py:1947
  432.2 3.7 copy-start.10
  432.2 3.7 copy-start.2
  432.2 3.7 copy-start.3
  432.2 3.7 copy-start.5
  435.8 1.0 copy-start.4
  435.8 1.2 copy-start.6
  435.8 1.3 copy-start.7
  435.9 2.7 copy-start.9
  437.3 11.7 %collective-permute-start = (bf16[288,576]{1,0:T(8,128)(2,1)}, bf16[288,576]{1,0:T(8,128)(2,1)S(1)}, u32[]{:S(2)}, u32[]{:S(2)}) collective-permute-start(bf16[288,576]{1,0:T(8,128)(2,1)} %reduce-scatter.11.cloned.1.call-done.zero), channel_id=1, source_target_pairs={{16,0},{17,1},{18,2},{19,3},{20,4},{21,5},{22,6},{23,7},{24,8},{25... | collective-permute-start | bytes 995336 | tf_op jit(solution)/shard_map/ppermute | solution.py:1961
  448.9 0.7 copy-start.8
Sparse Core Ops, SparseCore 0:
  54.2 53.8 all-gather.3
  109.7 34.0 all-gather.5
  145.4 54.2 all-gather.7
  257.4 50.6 reduce-scatter.4
  310.2 33.4 reduce-scatter.8
  350.1 50.7 reduce-scatter.6
  403.2 33.4 reduce-scatter.10

commit v7 on v6

--- a/solution.py
+++ b/solution.py
@@ -650,10 +650,14 @@
                 lambda: keep(gathered, second_hbm, 1, 2),
             ],
             2: [one.mate_far, zero.first_hop, one.far_hop],
-            3: [one.mate_near, lambda: keep(upper, upper_hbm, 1, 3), one.second_hop],
+            3: [
+                one.mate_near,
+                lambda: keep(upper, upper_hbm, 1, 3),
+                lambda: close(0),
+                one.second_hop,
+            ],
         },
     )
-    close(0)
     one.first_hop()
     close(1)
     for copy in keeps:
@@ -767,12 +771,12 @@
                 load_upper[1].wait,
             ],
             2: [one.mate_far, zero.first_hop, one.far_hop],
-            3: [one.mate_near, one.second_hop],
+            3: [one.mate_near, lambda: close(0), one.second_hop],
         },
     )
     for load in load_second:
         load.wait()
-    weight_grads({0: [one.first_hop, lambda: close(0)]})
+    weight_grads({0: [one.first_hop]})
     close(1)
 
 
@@ -897,13 +901,14 @@
             3: [
                 back_one.mate_near,
                 one.mate_near,
+                lambda: close_back(0),
                 back_one.second_hop,
                 one.far_hop,
                 one.second_hop,
             ],
         },
     )
-    weight_grads({0: [back_one.first_hop, one.first_hop, lambda: close_back(0)]})
+    weight_grads({0: [back_one.first_hop, one.first_hop]})
     close_back(1)
     for m in range(micro):
         close(m)
@@ -1076,13 +1081,13 @@
     attend_hooks = {
         0: [gathers[1].to_mate],
         heads - 1: [gathers[1].finish],
-        heads: [zero.first_hop, lambda: start_errand(1)],
+        heads: [zero.second_hop, zero.first_hop, lambda: start_errand(1)],
     }
     project_hooks = {
-        0: [zero.mate_far, zero.far_hop],
-        1: [zero.mate_near, zero.second_hop],
-        2: [one.mate_far, one.far_hop],
-        3: [one.mate_near, lambda: close(0), one.second_hop],
+        0: [zero.mate_far],
+        1: [zero.far_hop, zero.mate_near],
+        2: [one.mate_far],
+        3: [one.far_hop, one.mate_near, lambda: close(0), one.second_hop],
     }
 
     def hooked(at, hooks):

time: 462 us -> 465 us (level)
  no operation moved by 1% of the time
where the time goes in v7:
time: 465 us; the launch traced here: 462 us
  Pallas kernels  422 us (91%)
  waiting for transfers between devices  16.8 us (4%)
  between operations  14.6 us (3%)
  local copies, waits for them, and re-layouts  5.36 us (1%)
    pallas_call x2, Pallas kernels, attn_backward(): pl.pallas_call(functools.partial(attn_backward_kernel, at, layer, own_row...  100 us
    pallas_call x2, Pallas kernels, attn_forward(): pl.pallas_call(functools.partial(attn_forward_kernel, given is not None,...  92.4 us
    pallas_call x1, Pallas kernels, ffn_turn(): pl.pallas_call(functools.partial(ffn_turn_kernel, half_ff, at, layer), ou...  56.9 us
    pallas_call x1, Pallas kernels, prologue(): pl.pallas_call(functools.partial(prologue_kernel, count, heads), out_shap...  46.8 us
    pallas_call x1, Pallas kernels, ffn_backward(): pl.pallas_call(functools.partial(ffn_backward_kernel, half_ff, at, layer)...  43.9 us
    pallas_call x1, Pallas kernels, ffn_forward(): pl.pallas_call(functools.partial(ffn_forward_kernel, half_ff, at, layer),...  43.5 us
    pallas_call x1, Pallas kernels, home(): pl.pallas_call(functools.partial(home_kernel, count, chunk), out_shape=[s...  32 us
  transfers between devices with their start and end apart: 8, of which 4 were waited for; matrix products, arithmetic and copies ran while one was open for 1% of the time, Pallas kernels for 68%

profile of v7, /device:TPU:0, one launch (start us, length us, event | category | flops | bytes accessed | tf_op | source)
XLA Modules:
  0.0 462.5 jit_solution(16064521868493225825)
XLA Ops:
  7.2 46.8 %prologue.1 = (bf16[1152,576]{1,0:T(8,128)(2,1)}, bf16[2,768,1152]{2,1,0:T(8,128)(2,1)}, bf16[288,576]{1,0:T(8,128)(2,1)}, bf16[288,1152]{1,0:T(8,128)(2,1)}, bf...) custom-call(bf16[3,288,288]{2,1,0:T(8,128)(2,1)} %bitcast.32, ...), custom_call_target="tpu_custom_call" | custom-call | flops 20000000000 | bytes 100000000 | tf_op jit(solution)/shard_map/prologue/pallas_call | solution.py:1607
  54.2 0.7 all-gather.6.cloned.1.call-update
  54.9 0.7 all-gather.8.cloned.1.call-update
  55.6 0.3 reduce-scatter.5.cloned.1.call-start
  55.9 0.8 pad_dynamic-slice_fusion.1.rows_ref
  56.8 45.7 %attn_forward.2 = (f32[2,96,1152]{2,1,0:T(8,128)}, f32[2,2,768,128]{3,2,1,0:T(8,128)}, bf16[2,768,1152]{2,1,0:T(8,128)(2,1)}, bf16[2,768,768]{2,1,0:T(8,128)(2,1)}, bf16[2,768,256]{2,1,0:T(8,128)(2,1)}) custom-call(bf16[2,96,1152]{2,1,0:T(8,128)(2,1)} %pad_dynamic-slice_fusion.1.rows_ref, f32[2,8,1152]{2,1,0:T(8,128)} %get-tuple-element.63.vectors, ...), custom_call_target="tpu_custom_call" | custom-call | flops 20000000000 | bytes 100000000 | tf_op jit(solution)/shard_map/attn_forward/pallas_call | solution.py:1155
  102.5 0.8 pad_dynamic-slice_fusion.grad_ref
  103.3 4.8 %all-gather.4.cloned.1.call-done.packed_hbm = bf16[1152,1152]{1,0:T(8,128)(2,1)} async-done(((bf16[288,1152]{1,0:T(8,128)(2,1)}), bf16[1152,1152]{1,0:T(8,128)(2,1)}) %all-gather.4.cloned.1.call-update) | async-done | bytes 2654224 | tf_op jit(solution)/shard_map/all_gather | solution.py:1887
  108.1 43.5 %ffn_forward.1 = (bf16[2,96,1152]{2,1,0:T(8,128)(2,1)}, bf16[2,768,1152]{2,1,0:T(8,128)(2,1)}, f32[2,768,640]{2,1,0:T(8,128)}) custom-call(f32[2,96,1152]{2,1,0:T(8,128)} %get-tuple-element.67.hidden_ref, f32[2,8,1152]{2,1,0:T(8,128)} %get-tuple-element.63.vectors, f32[2,1,640]{2,1,0:T(1,128)} %get-tuple-element.68.up_biases, ...), custom_call_target="tpu_custom_call" | custom-call | flops 20000000000 | bytes 100000000 | tf_op jit(solution)/shard_map/ffn_forward/pallas_call | solution.py:1203
  151.6 46.7 %attn_forward.3 = (f32[2,96,1152]{2,1,0:T(8,128)}, f32[2,2,768,128]{3,2,1,0:T(8,128)}, bf16[2,768,1152]{2,1,0:T(8,128)(2,1)}, bf16[2,768,768]{2,1,0:T(8,128)(2,1)}, bf16[2,768,256]{2,1,0:T(8,128)(2,1)}) custom-call(bf16[2,96,1152]{2,1,0:T(8,128)(2,1)} %get-tuple-element.70.rows_ref.grads_ref.errand_one_hbm, f32[2,8,1152]{2,1,0:T(8,128)} %get-tuple-element.63.vectors, ...), custom_call_target="tpu_custom_call" | custom-call | flops 20000000000 | bytes 100000000 | tf_op jit(solution)/shard_map/attn_forward/pallas_call | solution.py:1155
  198.3 1.3 all-gather.8.cloned.1.call-done.packed_hbm
  199.6 56.9 %ffn_turn.1 = (bf16[2,96,1152]{2,1,0:T(8,128)(2,1)}, f32[2,96,1152]{2,1,0:T(8,128)}, bf16[1152,1152]{1,0:T(8,128)(2,1)}, f32[8,1152]{1,0:T(8,128)}, f32[8,640]{1,0:T(8,128)}) custom-call(f32[2,96,1152]{2,1,0:T(8,128)} %get-tuple-element.72.hidden_ref, bf16[2,96,1152]{2,1,0:T(8,128)(2,1)} %pad_dynamic-slice_fusion.grad_ref, ...), custom_call_target="tpu_custom_call" | custom-call | flops 20000000000 | bytes 100000000 | tf_op jit(solution)/shard_map/ffn_turn/pallas_call | solution.py:1233
  256.6 51.1 %attn_backward.2 = (bf16[2,96,1152]{2,1,0:T(8,128)(2,1)}, bf16[1152,576]{1,0:T(8,128)(2,1)}, f32[8,1152]{1,0:T(8,128)}, f32[8,256]{1,0:T(8,128)}, bf16[2,96,1152]{2,1,0:T(8,128)(2,1)}) custom-call(f32[2,96,1152]{2,1,0:T(8,128)} %get-tuple-element.76.grad_ref, bf16[2,96,1152]{2,1,0:T(8,128)(2,1)} %get-tuple-element.70.rows_ref.grads_ref.errand_one_hbm, ...), custom_call_target="tpu_custom_call" | custom-call | flops 20000000000 | bytes 100000000 | tf_op jit(solution)/shard_map/attn_backward/pallas_call | solution.py:1304
  307.8 43.9 %ffn_backward.1 = (f32[2,96,1152]{2,1,0:T(8,128)}, bf16[1152,1152]{1,0:T(8,128)(2,1)}, f32[8,1152]{1,0:T(8,128)}, f32[8,640]{1,0:T(8,128)}) custom-call(bf16[2,96,1152]{2,1,0:T(8,128)(2,1)} %get-tuple-element.81.grad_ref.rows_one_hbm, f32[2,96,1152]{2,1,0:T(8,128)} %get-tuple-element.67.hidden_ref, f32[2,8,1152]{2,1,0:T(8,128)} %get-tuple-element.63.vectors, ...), custom_call_target="tpu_custom_call" | custom-call | flops 20000000000 | bytes 100000000 | tf_op jit(solution)/shard_map/ffn_backward/pallas_call | solution.py:1268
  351.7 0.0 reduce-scatter.11.cloned.1.call-start
  351.8 49.3 %attn_backward.3 = (bf16[2,96,1152]{2,1,0:T(8,128)(2,1)}, bf16[1152,576]{1,0:T(8,128)(2,1)}, f32[8,1152]{1,0:T(8,128)}, f32[8,256]{1,0:T(8,128)}, bf16[288,1152]{1,0:T(8,128)(2,1)}) custom-call(f32[2,96,1152]{2,1,0:T(8,128)} %get-tuple-element.84.grad_ref, bf16[2,96,1152]{2,1,0:T(8,128)(2,1)} %pad_dynamic-slice_fusion.1.rows_ref, ...), custom_call_target="tpu_custom_call" | custom-call | flops 20000000000 | bytes 100000000 | tf_op jit(solution)/shard_map/attn_backward/pallas_call | solution.py:1304
  401.2 1.3 reduce-scatter.7.cloned.1.call-done.ff_sum_hbm.zero
  402.5 32.0 %home.1 = (f32[8,128]{1,0:T(8,128)}, f32[2,1,640]{2,1,0:T(1,128)}, bf16[288,1152]{1,0:T(8,128)(2,1)}, bf16[288,576]{1,0:T(8,128)(2,1)}, bf16[2,96,1152]{2,1,0:T(8,128)(2,1)}) custom-call(f32[8,1152]{1,0:T(8,128)} %get-tuple-element.89.attn_zero, f32[8,1152]{1,0:T(8,128)} %get-tuple-element.90.attn_one, f32[8,1152]{1,0:T(8,128)} %get-tuple-element.91.ff_zero, ...), custom_call_target="tpu_custom_call" | custom-call | flops 20000000000 | bytes 100000000 | tf_op jit(solution)/shard_map/home/pallas_call | solution.py:1744
  434.5 3.6 ff_finish.1
  438.2 0.1 broadcast_select_fusion.4
  438.3 0.8 copy-done.4
  439.1 0.1 copy-done.6
  439.3 0.1 copy-done.7
  439.4 0.1 broadcast_select_fusion.1
  439.5 1.3 collective-permute-start
  440.9 0.6 slice.21
  441.4 0.6 copy.21
  442.0 0.7 reshape.25
  442.7 1.3 fusion
  444.0 7.9 %collective-permute-done.zero_got = bf16[288,576]{1,0:T(8,128)(2,1)S(1)} collective-permute-done((bf16[288,576]{1,0:T(8,128)(2,1)}, bf16[288,576]{1,0:T(8,128)(2,1)S(1)}, u32[]{:S(2)}, u32[]{:S(2)}) %collective-permute-start) | collective-permute-done | bytes 331808 | tf_op jit(solution)/shard_map/ppermute | solution.py:1966
  451.9 0.7 copy-done.8
  452.6 2.8 attn_finish.1
  (35 shorter events, 0.4 us)
Async XLA Ops:
  7.2 100.9 %all-gather.4.cloned.1.call-start = ((), (), s32[]{:S(2)}) async-start(), calls=%async_computation.4 | async-start | bytes 3317760 | tf_op jit(solution)/shard_map/all_gather | solution.py:1887
  54.1 1.9 copy-start
  54.1 97.5 %all-gather.6.cloned.1.call-start = ((), (), s32[]{:S(2)}) async-start(), calls=%async_computation.5 | async-start | bytes 1843200 | tf_op jit(solution)/shard_map/all_gather | solution.py:1887
  54.9 144.8 %all-gather.8.cloned.1.call-start = ((), (), s32[]{:S(2)}) async-start(), calls=%async_computation.6 | async-start | bytes 3317760 | tf_op jit(solution)/shard_map/all_gather | solution.py:1887
  55.6 296.2 %reduce-scatter.5.cloned.1.call-start = ((), (), s32[]{:S(2)}) async-start(), calls=%async_computation.7 | async-start | bytes 3317760 | tf_op jit(solution)/shard_map/reduce_scatter | solution.py:1934
  56.8 45.7 %copy-start.1 = (bf16[2,1,184,1152]{3,2,1,0:T(8,128)(2,1)S(1)}, bf16[2,1,184,1152]{3,2,1,0:T(8,128)(2,1)}, u32[]{:S(2)}) copy-start(bf16[2,1,184,1152]{3,2,1,0:T(8,128)(2,1)} %param.11) | copy-start | bytes 2543620
  256.6 144.6 %reduce-scatter.9.cloned.1.call-start = ((), (), s32[]{:S(2)}) async-start(), calls=%async_computation.9 | async-start | bytes 1843200 | tf_op jit(solution)/shard_map/reduce_scatter | solution.py:1952
  307.7 94.7 %reduce-scatter.7.cloned.1.call-start = ((), (), s32[]{:S(2)}) async-start(), calls=%async_computation.8 | async-start | bytes 3317760 | tf_op jit(solution)/shard_map/reduce_scatter | solution.py:1934
  351.7 87.8 %reduce-scatter.11.cloned.1.call-start = ((), (), s32[]{:S(2)}) async-start(), calls=%async_computation.10 | async-start | bytes 1843200 | tf_op jit(solution)/shard_map/reduce_scatter | solution.py:1952
  434.5 3.6 copy-start.10
  434.5 3.7 copy-start.2
  434.5 3.7 copy-start.3
  434.5 3.7 copy-start.5
  438.1 1.0 copy-start.4
  438.1 1.1 copy-start.6
  438.1 1.3 copy-start.7
  438.2 2.7 copy-start.9
  439.5 12.3 %collective-permute-start = (bf16[288,576]{1,0:T(8,128)(2,1)}, bf16[288,576]{1,0:T(8,128)(2,1)S(1)}, u32[]{:S(2)}, u32[]{:S(2)}) collective-permute-start(bf16[288,576]{1,0:T(8,128)(2,1)} %reduce-scatter.11.cloned.1.call-done.zero), channel_id=1, source_target_pairs={{16,0},{17,1},{18,2},{19,3},{20,4},{21,5},{22,6},{23,7},{24,8},{25... | collective-permute-start | bytes 995336 | tf_op jit(solution)/shard_map/ppermute | solution.py:1966
  451.9 0.7 copy-start.8
Sparse Core Ops, SparseCore 0:
  54.2 53.8 all-gather.3
  109.7 34.0 all-gather.5
  145.4 54.2 all-gather.7
  256.7 50.6 reduce-scatter.4
  309.5 33.5 reduce-scatter.8
  351.9 50.5 reduce-scatter.6
  404.8 33.4 reduce-scatter.10

commit v8 on v6

--- a/solution.py
+++ b/solution.py
@@ -378,6 +378,11 @@
     prepare()
     gathers[0].forward()
     gathers[1].second()
+
+
+def block_out(src, dst, sems, i):
+    rows = step_rows(i, WIDE)
+    return pltpu.make_async_copy(src.at[rows], dst.at[rows], sems.at[i])
 
 
 def widen(packed, wide):
@@ -662,13 +667,13 @@
 
 def ffn_backward_kernel(
     half_ff, at, layer, grad_ref, hidden_ref, vectors, second_hbm, upper_hbm, packed_hbm,
-    out_ref, grads_ref, small_ref, up_bias_ref, *rest
+    out_ref, grads_hbm, small_ref, up_bias_ref, *rest
 ):
     micro, half_rows, width = hidden_ref.shape
     gathered, gather_refs = rest[0], rest[0:3]
     scatter_refs = rest[3:9]
     terms = rest[3]
-    packed, tails, second, upper, grad_upper, active, load_sems = rest[9:]
+    packed, tails, second, upper, grad_upper, active, load_sems, grads_ref, grads_sems = rest[9:]
     vec = vectors.at[layer]
     seq, ff = upper.shape[1:]
     main = ff - LANES
@@ -732,8 +737,13 @@
             blank = jnp.zeros((WIDE, LANES - 2 * extra), jnp.float32)
             rest_cols = [up[:, main : main + extra], down[:, main : main + extra], blank]
             grads_ref[cols, 2 * main :] = low(jnp.concatenate(rest_cols, axis=1))
+            block_out(grads_ref, grads_hbm, grads_sems, i).start()
 
         stages(width // WIDE, block, hooks)
+
+    def grads_out():
+        for i in range(width // WIDE):
+            block_out(grads_ref, grads_hbm, grads_sems, i).wait()
 
     def close(m):
         scatters[m].finish()
@@ -774,16 +784,17 @@
         load.wait()
     weight_grads({0: [one.first_hop, lambda: close(0)]})
     close(1)
+    grads_out()
 
 
 def ffn_turn_kernel(
     half_ff, at, layer, hidden_ref, grad_ref, vectors, up_biases, given_hbm, packed_hbm,
-    out_ref, grad_out_ref, grads_ref, small_ref, up_bias_ref, *rest
+    out_ref, grad_out_ref, grads_hbm, small_ref, up_bias_ref, *rest
 ):
     micro, half_rows, width = hidden_ref.shape
     gathered, gather_refs = rest[0], rest[0:3]
     terms, back_terms = rest[3], rest[9]
-    packed, tails, given, grad_upper, active, load_sem, given_sems = rest[15:]
+    packed, tails, given, grad_upper, active, load_sem, given_sems, grads_ref, grads_sems = rest[15:]
     vec, up_bias = vectors.at[layer], up_biases.at[layer]
     seq, ff = active.shape[1:]
     main = ff - LANES
@@ -844,8 +855,13 @@
             blank = jnp.zeros((WIDE, LANES - 2 * extra), jnp.float32)
             rest_cols = [up[:, main : main + extra], down[:, main : main + extra], blank]
             grads_ref[cols, 2 * main :] = low(jnp.concatenate(rest_cols, axis=1))
+            block_out(grads_ref, grads_hbm, grads_sems, i).start()
 
         stages(width // WIDE, block, hooks)
+
+    def grads_out():
+        for i in range(width // WIDE):
+            block_out(grads_ref, grads_hbm, grads_sems, i).wait()
 
     def close_back(m):
         backs[m].finish()
@@ -897,29 +913,34 @@
             3: [
                 back_one.mate_near,
                 one.mate_near,
+                lambda: close_back(0),
                 back_one.second_hop,
                 one.far_hop,
                 one.second_hop,
             ],
         },
     )
-    weight_grads({0: [back_one.first_hop, one.first_hop, lambda: close_back(0)]})
+    weight_grads({0: [back_one.first_hop, one.first_hop]})
     close_back(1)
     for m in range(micro):
         close(m)
+    grads_out()
 
 
 def attn_backward_kernel(
-    at, layer, own_rows, both_ways, grad_ref, rows_ref, vectors, lse, lengths,
+    at, layer, own_rows, both_ways, grad_ref, rows_ref, vectors, lse_hbm, lengths,
     normed_hbm, qkv_hbm, mixed_hbm, packed_hbm, errand_hbm, errand_one_hbm,
-    out_ref, grads_ref, small_ref, bias_ref, errand_got, *rest
+    out_ref, grads_hbm, small_ref, bias_ref, errand_got, *rest
 ):
     micro, half_rows, width = grad_ref.shape
     gathered, gather_refs = rest[0], rest[0:3]
     scatter_refs = rest[3:9]
     terms = rest[3]
     packed, wide, normed, qkv, mixed, grad_mixed, grad_qkv, turned, shut = rest[9:18]
-    low_probs, grad_scores, high_probs, errand_sems, load_sems = rest[18:]
+    low_probs, grad_scores, high_probs, errand_sems, load_sems = rest[18:23]
+    grads_ref, grads_sems, lse, lse_sem = rest[23:]
+    load_lse = pltpu.make_async_copy(lse_hbm, lse, lse_sem)
+    load_lse.start()
     vec = vectors.at[layer]
     seq, pair = mixed.shape[1:]
     heads = pair // LANES
@@ -994,6 +1015,7 @@
         widen(packed, wide)
         for m in range(micro):
             ready_qkv(m)
+        load_lse.wait()
 
     fill(0)
     gathers[0].start()
@@ -1044,6 +1066,7 @@
             total = low(jnp.concatenate([front, back], axis=1))
             pieces = [total[:, h * LANES : h * LANES + HEAD] for h in range(4 * heads)]
             grads_ref[cols] = jnp.concatenate(pieces, axis=1)
+            block_out(grads_ref, grads_hbm, grads_sems, i).start()
 
         stages(width // WIDE, block, hooks)
 
@@ -1113,6 +1136,8 @@
         load.wait()
     weight_grads({0: [one.first_hop]})
     close(1)
+    for i in range(width // WIDE):
+        block_out(grads_ref, grads_hbm, grads_sems, i).wait()
 
     for errand, _ in errands:
         pl.when(sends_errand)(errand.wait_send)
@@ -1235,7 +1260,7 @@
             shape_of((8, ff), high_type),
         ],
         in_specs=[vmem_spec()] * 4 + [any_spec()] * 2,
-        out_specs=[vmem_spec()] * 5,
+        out_specs=[vmem_spec()] * 2 + [any_spec()] + [vmem_spec()] * 2,
         scratch_shapes=gather_scratch(micro, seq, width)
         + scatter_scratch(micro, seq, half_rows, width)
         + scatter_scratch(micro, seq, half_rows, width)
@@ -1247,6 +1272,8 @@
             pltpu.VMEM((micro, seq, ff), low_type),
             pltpu.SemaphoreType.DMA,
             pltpu.SemaphoreType.DMA((micro,)),
+            pltpu.VMEM((width, 2 * ff - LANES), low_type),
+            pltpu.SemaphoreType.DMA((width // WIDE,)),
         ],
         compiler_params=params(7),
         cost_estimate=COST,
@@ -1269,7 +1296,7 @@
             shape_of((8, ff), high_type),
         ],
         in_specs=[vmem_spec()] * 3 + [any_spec()] * 3,
-        out_specs=[vmem_spec()] * 4,
+        out_specs=[vmem_spec(), any_spec()] + [vmem_spec()] * 2,
         scratch_shapes=gather_scratch(micro, seq, width)
         + scatter_scratch(micro, seq, half_rows, width)
         + [
@@ -1280,6 +1307,8 @@
             pltpu.VMEM((micro, seq, ff), low_type),
             pltpu.VMEM((micro, seq, ff), low_type),
             pltpu.SemaphoreType.DMA((1 + 2 * micro,)),
+            pltpu.VMEM((width, 2 * ff - LANES), low_type),
+            pltpu.SemaphoreType.DMA((width // WIDE,)),
         ],
         compiler_params=params(2),
         cost_estimate=COST,
@@ -1305,8 +1334,8 @@
             shape_of((8, pair), high_type),
             shape_of(errand[0].shape, errand[0].dtype),
         ],
-        in_specs=[vmem_spec()] * 4 + [smem_spec()] + [any_spec()] * 6,
-        out_specs=[vmem_spec()] * 4 + [any_spec()],
+        in_specs=[vmem_spec()] * 3 + [any_spec(), smem_spec()] + [any_spec()] * 6,
+        out_specs=[vmem_spec(), any_spec()] + [vmem_spec()] * 2 + [any_spec()],
         scratch_shapes=gather_scratch(micro, seq, width)
         + scatter_scratch(micro, seq, half_rows, width)
         + [
@@ -1324,6 +1353,10 @@
             pltpu.VMEM((micro, heads, seq, seq), high_type),
             pltpu.SemaphoreType.DMA((2, 2)),
             pltpu.SemaphoreType.DMA((1 + 3 * micro,)),
+            pltpu.VMEM((width, 4 * heads * HEAD), low_type),
+            pltpu.SemaphoreType.DMA((width // WIDE,)),
+            pltpu.VMEM(lse.shape, high_type),
+            pltpu.SemaphoreType.DMA,
         ],
         compiler_params=params(3 + 5 * layer),
         cost_estimate=COST,

time: 462 us -> 460 us (level)
  no operation moved by 1% of the time
where the time goes in v8:
time: 460 us; the launch traced here: 457 us
  Pallas kernels  415 us (90%)
  waiting for transfers between devices  19.2 us (4%)
  between operations  14.6 us (3%)
  local copies, waits for them, and re-layouts  5.37 us (1%)
    pallas_call x2, Pallas kernels, attn_backward(): pl.pallas_call(functools.partial(attn_backward_kernel, at, layer, own_row...  98 us
    pallas_call x2, Pallas kernels, attn_forward(): pl.pallas_call(functools.partial(attn_forward_kernel, given is not None,...  92.4 us
    pallas_call x1, Pallas kernels, ffn_turn(): pl.pallas_call(functools.partial(ffn_turn_kernel, half_ff, at, layer), ou...  56.2 us
    pallas_call x1, Pallas kernels, prologue(): pl.pallas_call(functools.partial(prologue_kernel, count, heads), out_shap...  46.8 us
    pallas_call x1, Pallas kernels, ffn_backward(): pl.pallas_call(functools.partial(ffn_backward_kernel, half_ff, at, layer)...  41.9 us
    pallas_call x1, Pallas kernels, ffn_forward(): pl.pallas_call(functools.partial(ffn_forward_kernel, half_ff, at, layer),...  41.6 us
    pallas_call x1, Pallas kernels, home(): pl.pallas_call(functools.partial(home_kernel, count, chunk), out_shape=[s...  31.3 us
  transfers between devices with their start and end apart: 8, of which 4 were waited for; matrix products, arithmetic and copies ran while one was open for 1% of the time, Pallas kernels for 68%

profile of v8, /device:TPU:0, one launch (start us, length us, event | category | flops | bytes accessed | tf_op | source)
XLA Modules:
  0.0 457.2 jit_solution(2717276479179619143)
XLA Ops:
  7.2 46.8 %prologue.1 = (bf16[1152,576]{1,0:T(8,128)(2,1)}, bf16[2,768,1152]{2,1,0:T(8,128)(2,1)}, bf16[288,576]{1,0:T(8,128)(2,1)}, bf16[288,1152]{1,0:T(8,128)(2,1)}, bf...) custom-call(bf16[3,288,288]{2,1,0:T(8,128)(2,1)} %bitcast.32, ...), custom_call_target="tpu_custom_call" | custom-call | flops 20000000000 | bytes 100000000 | tf_op jit(solution)/shard_map/prologue/pallas_call | solution.py:1635
  54.2 0.7 all-gather.6.cloned.1.call-update
  54.9 0.7 all-gather.8.cloned.1.call-update
  55.6 0.3 reduce-scatter.5.cloned.1.call-start
  55.9 0.8 pad_dynamic-slice_fusion.1.rows_ref
  56.8 45.7 %attn_forward.2 = (f32[2,96,1152]{2,1,0:T(8,128)}, f32[2,2,768,128]{3,2,1,0:T(8,128)}, bf16[2,768,1152]{2,1,0:T(8,128)(2,1)}, bf16[2,768,768]{2,1,0:T(8,128)(2,1)}, bf16[2,768,256]{2,1,0:T(8,128)(2,1)}) custom-call(bf16[2,96,1152]{2,1,0:T(8,128)(2,1)} %pad_dynamic-slice_fusion.1.rows_ref, f32[2,8,1152]{2,1,0:T(8,128)} %get-tuple-element.63.vectors, ...), custom_call_target="tpu_custom_call" | custom-call | flops 20000000000 | bytes 100000000 | tf_op jit(solution)/shard_map/attn_forward/pallas_call | solution.py:1175
  102.5 0.8 pad_dynamic-slice_fusion.grad_ref
  103.3 4.8 %all-gather.4.cloned.1.call-done.packed_hbm = bf16[1152,1152]{1,0:T(8,128)(2,1)} async-done(((bf16[288,1152]{1,0:T(8,128)(2,1)}), bf16[1152,1152]{1,0:T(8,128)(2,1)}) %all-gather.4.cloned.1.call-update) | async-done | bytes 2654224 | tf_op jit(solution)/shard_map/all_gather | solution.py:1915
  108.1 41.6 %ffn_forward.1 = (bf16[2,96,1152]{2,1,0:T(8,128)(2,1)}, bf16[2,768,1152]{2,1,0:T(8,128)(2,1)}, f32[2,768,640]{2,1,0:T(8,128)}) custom-call(f32[2,96,1152]{2,1,0:T(8,128)} %get-tuple-element.67.hidden_ref, f32[2,8,1152]{2,1,0:T(8,128)} %get-tuple-element.63.vectors, f32[2,1,640]{2,1,0:T(1,128)} %get-tuple-element.68.up_biases, ...), custom_call_target="tpu_custom_call" | custom-call | flops 20000000000 | bytes 100000000 | tf_op jit(solution)/shard_map/ffn_forward/pallas_call | solution.py:1223
  149.8 46.7 %attn_forward.3 = (f32[2,96,1152]{2,1,0:T(8,128)}, f32[2,2,768,128]{3,2,1,0:T(8,128)}, bf16[2,768,1152]{2,1,0:T(8,128)(2,1)}, bf16[2,768,768]{2,1,0:T(8,128)(2,1)}, bf16[2,768,256]{2,1,0:T(8,128)(2,1)}) custom-call(bf16[2,96,1152]{2,1,0:T(8,128)(2,1)} %get-tuple-element.70.rows_ref.grads_ref.errand_one_hbm, f32[2,8,1152]{2,1,0:T(8,128)} %get-tuple-element.63.vectors, ...), custom_call_target="tpu_custom_call" | custom-call | flops 20000000000 | bytes 100000000 | tf_op jit(solution)/shard_map/attn_forward/pallas_call | solution.py:1175
  196.4 3.2 all-gather.8.cloned.1.call-done.packed_hbm
  199.6 56.2 %ffn_turn.1 = (bf16[2,96,1152]{2,1,0:T(8,128)(2,1)}, f32[2,96,1152]{2,1,0:T(8,128)}, bf16[1152,1152]{1,0:T(8,128)(2,1)}, f32[8,1152]{1,0:T(8,128)}, f32[8,640]{1,0:T(8,128)}) custom-call(f32[2,96,1152]{2,1,0:T(8,128)} %get-tuple-element.72.hidden_ref, bf16[2,96,1152]{2,1,0:T(8,128)(2,1)} %pad_dynamic-slice_fusion.grad_ref, ...), custom_call_target="tpu_custom_call" | custom-call | flops 20000000000 | bytes 100000000 | tf_op jit(solution)/shard_map/ffn_turn/pallas_call | solution.py:1253
  255.9 49.5 %attn_backward.2 = (bf16[2,96,1152]{2,1,0:T(8,128)(2,1)}, bf16[1152,576]{1,0:T(8,128)(2,1)}, f32[8,1152]{1,0:T(8,128)}, f32[8,256]{1,0:T(8,128)}, bf16[2,96,1152]{2,1,0:T(8,128)(2,1)}) custom-call(f32[2,96,1152]{2,1,0:T(8,128)} %get-tuple-element.76.grad_ref, bf16[2,96,1152]{2,1,0:T(8,128)(2,1)} %get-tuple-element.70.rows_ref.grads_ref.errand_one_hbm, ...), custom_call_target="tpu_custom_call" | custom-call | flops 20000000000 | bytes 100000000 | tf_op jit(solution)/shard_map/attn_backward/pallas_call | solution.py:1328
  305.5 41.9 %ffn_backward.1 = (f32[2,96,1152]{2,1,0:T(8,128)}, bf16[1152,1152]{1,0:T(8,128)(2,1)}, f32[8,1152]{1,0:T(8,128)}, f32[8,640]{1,0:T(8,128)}) custom-call(bf16[2,96,1152]{2,1,0:T(8,128)(2,1)} %get-tuple-element.81.grad_ref.rows_one_hbm, f32[2,96,1152]{2,1,0:T(8,128)} %get-tuple-element.67.hidden_ref, f32[2,8,1152]{2,1,0:T(8,128)} %get-tuple-element.63.vectors, ...), custom_call_target="tpu_custom_call" | custom-call | flops 20000000000 | bytes 100000000 | tf_op jit(solution)/shard_map/ffn_backward/pallas_call | solution.py:1290
  347.4 0.0 reduce-scatter.11.cloned.1.call-start
  347.5 48.5 %attn_backward.3 = (bf16[2,96,1152]{2,1,0:T(8,128)(2,1)}, bf16[1152,576]{1,0:T(8,128)(2,1)}, f32[8,1152]{1,0:T(8,128)}, f32[8,256]{1,0:T(8,128)}, bf16[288,1152]{1,0:T(8,128)(2,1)}) custom-call(f32[2,96,1152]{2,1,0:T(8,128)} %get-tuple-element.84.grad_ref, bf16[2,96,1152]{2,1,0:T(8,128)(2,1)} %pad_dynamic-slice_fusion.1.rows_ref, ...), custom_call_target="tpu_custom_call" | custom-call | flops 20000000000 | bytes 100000000 | tf_op jit(solution)/shard_map/attn_backward/pallas_call | solution.py:1328
  396.1 2.5 reduce-scatter.7.cloned.1.call-done.ff_sum_hbm.zero
  398.6 31.3 %home.1 = (f32[8,128]{1,0:T(8,128)}, f32[2,1,640]{2,1,0:T(1,128)}, bf16[288,1152]{1,0:T(8,128)(2,1)}, bf16[288,576]{1,0:T(8,128)(2,1)}, bf16[2,96,1152]{2,1,0:T(8,128)(2,1)}) custom-call(f32[8,1152]{1,0:T(8,128)} %get-tuple-element.89.attn_zero, f32[8,1152]{1,0:T(8,128)} %get-tuple-element.90.attn_one, f32[8,1152]{1,0:T(8,128)} %get-tuple-element.91.ff_zero, ...), custom_call_target="tpu_custom_call" | custom-call | flops 20000000000 | bytes 100000000 | tf_op jit(solution)/shard_map/home/pallas_call | solution.py:1772
  429.9 3.6 ff_finish.1
  433.6 0.1 broadcast_select_fusion.4
  433.7 0.8 copy-done.4
  434.5 0.1 copy-done.6
  434.7 0.1 copy-done.7
  434.8 0.1 broadcast_select_fusion.1
  435.0 1.3 collective-permute-start
  436.3 0.6 slice.21
  436.9 0.6 copy.21
  437.4 0.7 reshape.25
  438.1 1.3 fusion
  439.4 7.2 %collective-permute-done.zero_got = bf16[288,576]{1,0:T(8,128)(2,1)S(1)} collective-permute-done((bf16[288,576]{1,0:T(8,128)(2,1)}, bf16[288,576]{1,0:T(8,128)(2,1)S(1)}, u32[]{:S(2)}, u32[]{:S(2)}) %collective-permute-start) | collective-permute-done | bytes 331808 | tf_op jit(solution)/shard_map/ppermute | solution.py:1994
  446.6 0.7 copy-done.8
  447.4 2.8 attn_finish.1
  (35 shorter events, 0.4 us)
Async XLA Ops:
  7.2 100.9 %all-gather.4.cloned.1.call-start = ((), (), s32[]{:S(2)}) async-start(), calls=%async_computation.4 | async-start | bytes 3317760 | tf_op jit(solution)/shard_map/all_gather | solution.py:1915
  54.1 1.9 copy-start
  54.1 95.7 %all-gather.6.cloned.1.call-start = ((), (), s32[]{:S(2)}) async-start(), calls=%async_computation.5 | async-start | bytes 1843200 | tf_op jit(solution)/shard_map/all_gather | solution.py:1915
  54.9 144.8 %all-gather.8.cloned.1.call-start = ((), (), s32[]{:S(2)}) async-start(), calls=%async_computation.6 | async-start | bytes 3317760 | tf_op jit(solution)/shard_map/all_gather | solution.py:1915
  55.6 291.9 %reduce-scatter.5.cloned.1.call-start = ((), (), s32[]{:S(2)}) async-start(), calls=%async_computation.7 | async-start | bytes 3317760 | tf_op jit(solution)/shard_map/reduce_scatter | solution.py:1962
  56.8 45.7 %copy-start.1 = (bf16[2,1,184,1152]{3,2,1,0:T(8,128)(2,1)S(1)}, bf16[2,1,184,1152]{3,2,1,0:T(8,128)(2,1)}, u32[]{:S(2)}) copy-start(bf16[2,1,184,1152]{3,2,1,0:T(8,128)(2,1)} %param.11) | copy-start | bytes 2543620
  255.9 140.2 %reduce-scatter.9.cloned.1.call-start = ((), (), s32[]{:S(2)}) async-start(), calls=%async_computation.9 | async-start | bytes 1843200 | tf_op jit(solution)/shard_map/reduce_scatter | solution.py:1980
  305.5 93.1 %reduce-scatter.7.cloned.1.call-start = ((), (), s32[]{:S(2)}) async-start(), calls=%async_computation.8 | async-start | bytes 3317760 | tf_op jit(solution)/shard_map/reduce_scatter | solution.py:1962
  347.4 87.5 %reduce-scatter.11.cloned.1.call-start = ((), (), s32[]{:S(2)}) async-start(), calls=%async_computation.10 | async-start | bytes 1843200 | tf_op jit(solution)/shard_map/reduce_scatter | solution.py:1980
  429.9 3.7 copy-start.10
  429.9 3.7 copy-start.2
  429.9 3.7 copy-start.3
  429.9 3.7 copy-start.5
  433.5 1.0 copy-start.4
  433.5 1.2 copy-start.6
  433.5 1.3 copy-start.7
  433.6 2.7 copy-start.9
  435.0 11.7 %collective-permute-start = (bf16[288,576]{1,0:T(8,128)(2,1)}, bf16[288,576]{1,0:T(8,128)(2,1)S(1)}, u32[]{:S(2)}, u32[]{:S(2)}) collective-permute-start(bf16[288,576]{1,0:T(8,128)(2,1)} %reduce-scatter.11.cloned.1.call-done.zero), channel_id=1, source_target_pairs={{16,0},{17,1},{18,2},{19,3},{20,4},{21,5},{22,6},{23,7},{24,8},{25... | collective-permute-start | bytes 995336 | tf_op jit(solution)/shard_map/ppermute | solution.py:1994
  446.6 0.7 copy-start.8
Sparse Core Ops, SparseCore 0:
  54.2 53.8 all-gather.3
  109.7 34.0 all-gather.5
  145.4 54.2 all-gather.7
  256.0 50.6 reduce-scatter.4
  308.8 33.5 reduce-scatter.8
  347.5 50.9 reduce-scatter.6
  400.9 33.4 reduce-scatter.10

commit v9 on v8

--- a/solution.py
+++ b/solution.py
@@ -61,7 +61,7 @@
 COST = pl.CostEstimate(flops=20_000_000_000, transcendentals=0, bytes_accessed=100_000_000)
 LOG2E = 1.0 / math.log(2.0)
 TILE = 256
-WIDE = 384
+WIDE = 128
 
 
 class Slab:
@@ -1504,31 +1504,14 @@
         copy.start()
         sent.append(copy)
     slab[section, tensor] = column[...]
-
-    def set_out(p):
-        pl.when(section == 1)(lambda: swapped(p))
+    for p in range(pieces):
+
+        @pl.when(section == 1)
+        def _():
+            swapped(p)
+
         for way in (1, -1):
             hop(0, p, way)
-
-    set_out(0)
-    for role, _, source in slab_peers():
-        slot = slab.at[source[0], source[1]]
-        remote(slot, slot, slab_send.at[role], slab_recv.at[role], named(source)).wait_recv()
-    for layer in range(2):
-        for part in range(4 * count):
-            piece = slab[layer, part % 4, part // 4]
-            out_ref[layer, :, part * chunk : (part + 1) * chunk] = piece[:, :chunk]
-    tiles = TileGather(all_rows, rows_send, rows_recv)
-    for m in range(micro):
-        own = tiles.tile(m, tensor)
-        for begin in range(0, own_rows, 32):
-            end = min(begin + 32, own_rows)
-            block = rows_ref[m, begin:end].astype(jnp.float32)
-            own[begin:end] = low(layer_norm(block, out_ref[0, 0:1], out_ref[0, 2:3]))
-        own[own_rows:] = jnp.zeros((tiles.tile_rows - own_rows, width), jnp.bfloat16)
-        tiles.start(m)
-    for p in range(1, pieces):
-        set_out(p)
     blank = jnp.zeros((rows, LANES - 2 * extra), jnp.bfloat16)
     up_halves[...] = jnp.zeros_like(up_halves)
     for half in range(2):
@@ -1555,7 +1538,24 @@
         other,
     )
     up_swap.start()
+    for role, _, source in slab_peers():
+        slot = slab.at[source[0], source[1]]
+        remote(slot, slot, slab_send.at[role], slab_recv.at[role], named(source)).wait_recv()
     ff_swap.start()
+    for layer in range(2):
+        for part in range(4 * count):
+            piece = slab[layer, part % 4, part // 4]
+            out_ref[layer, :, part * chunk : (part + 1) * chunk] = piece[:, :chunk]
+    tiles = TileGather(all_rows, rows_send, rows_recv)
+    for m in range(micro):
+        own = tiles.tile(m, tensor)
+        for begin in range(0, own_rows, 32):
+            end = min(begin + 32, own_rows)
+            block = rows_ref[m, begin:end].astype(jnp.float32)
+            own[begin:end] = low(layer_norm(block, out_ref[0, 0:1], out_ref[0, 2:3]))
+        own[own_rows:] = jnp.zeros((tiles.tile_rows - own_rows, width), jnp.bfloat16)
+    for m in range(micro):
+        tiles.start(m)
     hops(1)
     start = (2 * tensor + section) * pair_cols
     for layer in range(2):

time: 460 us -> 466 us (1.013)
  Pallas kernels: 415 us -> 421 us
where the time goes in v9:
time: 466 us; the launch traced here: 463 us
  Pallas kernels  421 us (90%)
  waiting for transfers between devices  18.5 us (4%)
  between operations  14.6 us (3%)
  local copies, waits for them, and re-layouts  5.37 us (1%)
    pallas_call x2, Pallas kernels, attn_backward(): pl.pallas_call(functools.partial(attn_backward_kernel, at, layer, own_row...  98.1 us
    pallas_call x2, Pallas kernels, attn_forward(): pl.pallas_call(functools.partial(attn_forward_kernel, given is not None,...  94 us
    pallas_call x1, Pallas kernels, ffn_turn(): pl.pallas_call(functools.partial(ffn_turn_kernel, half_ff, at, layer), ou...  58.9 us
    pallas_call x1, Pallas kernels, ffn_backward(): pl.pallas_call(functools.partial(ffn_backward_kernel, half_ff, at, layer)...  45.6 us
    pallas_call x1, Pallas kernels, prologue(): pl.pallas_call(functools.partial(prologue_kernel, count, heads), out_shap...  45 us
    pallas_call x1, Pallas kernels, ffn_forward(): pl.pallas_call(functools.partial(ffn_forward_kernel, half_ff, at, layer),...  41.6 us
    pallas_call x1, Pallas kernels, home(): pl.pallas_call(functools.partial(home_kernel, count, chunk), out_shape=[s...  31.6 us
  transfers between devices with their start and end apart: 8, of which 4 were waited for; matrix products, arithmetic and copies ran while one was open for 1% of the time, Pallas kernels for 68%

profile of v9, /device:TPU:0, one launch (start us, length us, event | category | flops | bytes accessed | tf_op | source)
XLA Modules:
  0.0 463.1 jit_solution(3419002527192330084)
XLA Ops:
  7.2 45.0 %prologue.1 = (bf16[1152,576]{1,0:T(8,128)(2,1)}, bf16[2,768,1152]{2,1,0:T(8,128)(2,1)}, bf16[288,576]{1,0:T(8,128)(2,1)}, bf16[288,1152]{1,0:T(8,128)(2,1)}, bf...) custom-call(bf16[3,288,288]{2,1,0:T(8,128)(2,1)} %bitcast.32, ...), custom_call_target="tpu_custom_call" | custom-call | flops 20000000000 | bytes 100000000 | tf_op jit(solution)/shard_map/prologue/pallas_call | solution.py:1635
  52.3 0.7 all-gather.6.cloned.1.call-update
  53.0 0.7 all-gather.8.cloned.1.call-update
  53.7 0.5 reduce-scatter.5.cloned.1.call-start
  54.2 0.8 pad_dynamic-slice_fusion.1.rows_ref
  55.1 47.3 %attn_forward.2 = (f32[2,96,1152]{2,1,0:T(8,128)}, f32[2,2,768,128]{3,2,1,0:T(8,128)}, bf16[2,768,1152]{2,1,0:T(8,128)(2,1)}, bf16[2,768,768]{2,1,0:T(8,128)(2,1)}, bf16[2,768,256]{2,1,0:T(8,128)(2,1)}) custom-call(bf16[2,96,1152]{2,1,0:T(8,128)(2,1)} %pad_dynamic-slice_fusion.1.rows_ref, f32[2,8,1152]{2,1,0:T(8,128)} %get-tuple-element.63.vectors, ...), custom_call_target="tpu_custom_call" | custom-call | flops 20000000000 | bytes 100000000 | tf_op jit(solution)/shard_map/attn_forward/pallas_call | solution.py:1175
  102.4 0.8 pad_dynamic-slice_fusion.grad_ref
  103.2 3.9 all-gather.4.cloned.1.call-done.packed_hbm
  107.0 41.6 %ffn_forward.1 = (bf16[2,96,1152]{2,1,0:T(8,128)(2,1)}, bf16[2,768,1152]{2,1,0:T(8,128)(2,1)}, f32[2,768,640]{2,1,0:T(8,128)}) custom-call(f32[2,96,1152]{2,1,0:T(8,128)} %get-tuple-element.67.hidden_ref, f32[2,8,1152]{2,1,0:T(8,128)} %get-tuple-element.63.vectors, f32[2,1,640]{2,1,0:T(1,128)} %get-tuple-element.68.up_biases, ...), custom_call_target="tpu_custom_call" | custom-call | flops 20000000000 | bytes 100000000 | tf_op jit(solution)/shard_map/ffn_forward/pallas_call | solution.py:1223
  148.7 46.7 %attn_forward.3 = (f32[2,96,1152]{2,1,0:T(8,128)}, f32[2,2,768,128]{3,2,1,0:T(8,128)}, bf16[2,768,1152]{2,1,0:T(8,128)(2,1)}, bf16[2,768,768]{2,1,0:T(8,128)(2,1)}, bf16[2,768,256]{2,1,0:T(8,128)(2,1)}) custom-call(bf16[2,96,1152]{2,1,0:T(8,128)(2,1)} %get-tuple-element.70.rows_ref.grads_ref.errand_one_hbm, f32[2,8,1152]{2,1,0:T(8,128)} %get-tuple-element.63.vectors, ...), custom_call_target="tpu_custom_call" | custom-call | flops 20000000000 | bytes 100000000 | tf_op jit(solution)/shard_map/attn_forward/pallas_call | solution.py:1175
  195.4 3.2 all-gather.8.cloned.1.call-done.packed_hbm
  198.6 58.9 %ffn_turn.1 = (bf16[2,96,1152]{2,1,0:T(8,128)(2,1)}, f32[2,96,1152]{2,1,0:T(8,128)}, bf16[1152,1152]{1,0:T(8,128)(2,1)}, f32[8,1152]{1,0:T(8,128)}, f32[8,640]{1,0:T(8,128)}) custom-call(f32[2,96,1152]{2,1,0:T(8,128)} %get-tuple-element.72.hidden_ref, bf16[2,96,1152]{2,1,0:T(8,128)(2,1)} %pad_dynamic-slice_fusion.grad_ref, ...), custom_call_target="tpu_custom_call" | custom-call | flops 20000000000 | bytes 100000000 | tf_op jit(solution)/shard_map/ffn_turn/pallas_call | solution.py:1253
  257.6 49.6 %attn_backward.2 = (bf16[2,96,1152]{2,1,0:T(8,128)(2,1)}, bf16[1152,576]{1,0:T(8,128)(2,1)}, f32[8,1152]{1,0:T(8,128)}, f32[8,256]{1,0:T(8,128)}, bf16[2,96,1152]{2,1,0:T(8,128)(2,1)}) custom-call(f32[2,96,1152]{2,1,0:T(8,128)} %get-tuple-element.76.grad_ref, bf16[2,96,1152]{2,1,0:T(8,128)(2,1)} %get-tuple-element.70.rows_ref.grads_ref.errand_one_hbm, ...), custom_call_target="tpu_custom_call" | custom-call | flops 20000000000 | bytes 100000000 | tf_op jit(solution)/shard_map/attn_backward/pallas_call | solution.py:1328
  307.2 45.6 %ffn_backward.1 = (f32[2,96,1152]{2,1,0:T(8,128)}, bf16[1152,1152]{1,0:T(8,128)(2,1)}, f32[8,1152]{1,0:T(8,128)}, f32[8,640]{1,0:T(8,128)}) custom-call(bf16[2,96,1152]{2,1,0:T(8,128)(2,1)} %get-tuple-element.81.grad_ref.rows_one_hbm, f32[2,96,1152]{2,1,0:T(8,128)} %get-tuple-element.67.hidden_ref, f32[2,8,1152]{2,1,0:T(8,128)} %get-tuple-element.63.vectors, ...), custom_call_target="tpu_custom_call" | custom-call | flops 20000000000 | bytes 100000000 | tf_op jit(solution)/shard_map/ffn_backward/pallas_call | solution.py:1290
  352.9 0.0 reduce-scatter.11.cloned.1.call-start
  353.0 48.5 %attn_backward.3 = (bf16[2,96,1152]{2,1,0:T(8,128)(2,1)}, bf16[1152,576]{1,0:T(8,128)(2,1)}, f32[8,1152]{1,0:T(8,128)}, f32[8,256]{1,0:T(8,128)}, bf16[288,1152]{1,0:T(8,128)(2,1)}) custom-call(f32[2,96,1152]{2,1,0:T(8,128)} %get-tuple-element.84.grad_ref, bf16[2,96,1152]{2,1,0:T(8,128)(2,1)} %pad_dynamic-slice_fusion.1.rows_ref, ...), custom_call_target="tpu_custom_call" | custom-call | flops 20000000000 | bytes 100000000 | tf_op jit(solution)/shard_map/attn_backward/pallas_call | solution.py:1328
  401.6 2.4 reduce-scatter.7.cloned.1.call-done.ff_sum_hbm.zero
  404.0 31.6 %home.1 = (f32[8,128]{1,0:T(8,128)}, f32[2,1,640]{2,1,0:T(1,128)}, bf16[288,1152]{1,0:T(8,128)(2,1)}, bf16[288,576]{1,0:T(8,128)(2,1)}, bf16[2,96,1152]{2,1,0:T(8,128)(2,1)}) custom-call(f32[8,1152]{1,0:T(8,128)} %get-tuple-element.89.attn_zero, f32[8,1152]{1,0:T(8,128)} %get-tuple-element.90.attn_one, f32[8,1152]{1,0:T(8,128)} %get-tuple-element.91.ff_zero, ...), custom_call_target="tpu_custom_call" | custom-call | flops 20000000000 | bytes 100000000 | tf_op jit(solution)/shard_map/home/pallas_call | solution.py:1772
  435.6 3.6 ff_finish.1
  439.3 0.1 broadcast_select_fusion.4
  439.4 0.8 copy-done.4
  440.2 0.1 copy-done.6
  440.4 0.1 copy-done.7
  440.5 0.1 broadcast_select_fusion.1
  440.6 1.3 collective-permute-start
  442.0 0.6 slice.21
  442.5 0.6 copy.21
  443.1 0.7 reshape.25
  443.8 1.3 fusion
  445.1 7.4 %collective-permute-done.zero_got = bf16[288,576]{1,0:T(8,128)(2,1)S(1)} collective-permute-done((bf16[288,576]{1,0:T(8,128)(2,1)}, bf16[288,576]{1,0:T(8,128)(2,1)S(1)}, u32[]{:S(2)}, u32[]{:S(2)}) %collective-permute-start) | collective-permute-done | bytes 331808 | tf_op jit(solution)/shard_map/ppermute | solution.py:1994
  452.5 0.7 copy-done.8
  453.3 2.8 attn_finish.1
  (35 shorter events, 0.4 us)
Async XLA Ops:
  7.2 99.9 %all-gather.4.cloned.1.call-start = ((), (), s32[]{:S(2)}) async-start(), calls=%async_computation.4 | async-start | bytes 3317760 | tf_op jit(solution)/shard_map/all_gather | solution.py:1915
  52.2 2.0 copy-start
  52.2 96.5 %all-gather.6.cloned.1.call-start = ((), (), s32[]{:S(2)}) async-start(), calls=%async_computation.5 | async-start | bytes 1843200 | tf_op jit(solution)/shard_map/all_gather | solution.py:1915
  53.0 145.6 %all-gather.8.cloned.1.call-start = ((), (), s32[]{:S(2)}) async-start(), calls=%async_computation.6 | async-start | bytes 3317760 | tf_op jit(solution)/shard_map/all_gather | solution.py:1915
  53.7 299.3 %reduce-scatter.5.cloned.1.call-start = ((), (), s32[]{:S(2)}) async-start(), calls=%async_computation.7 | async-start | bytes 3317760 | tf_op jit(solution)/shard_map/reduce_scatter | solution.py:1962
  55.1 47.3 %copy-start.1 = (bf16[2,1,184,1152]{3,2,1,0:T(8,128)(2,1)S(1)}, bf16[2,1,184,1152]{3,2,1,0:T(8,128)(2,1)}, u32[]{:S(2)}) copy-start(bf16[2,1,184,1152]{3,2,1,0:T(8,128)(2,1)} %param.11) | copy-start | bytes 2543620
  257.6 144.0 %reduce-scatter.9.cloned.1.call-start = ((), (), s32[]{:S(2)}) async-start(), calls=%async_computation.9 | async-start | bytes 1843200 | tf_op jit(solution)/shard_map/reduce_scatter | solution.py:1980
  307.2 96.8 %reduce-scatter.7.cloned.1.call-start = ((), (), s32[]{:S(2)}) async-start(), calls=%async_computation.8 | async-start | bytes 3317760 | tf_op jit(solution)/shard_map/reduce_scatter | solution.py:1962
  352.9 87.7 %reduce-scatter.11.cloned.1.call-start = ((), (), s32[]{:S(2)}) async-start(), calls=%async_computation.10 | async-start | bytes 1843200 | tf_op jit(solution)/shard_map/reduce_scatter | solution.py:1980
  435.6 3.7 copy-start.10
  435.6 3.7 copy-start.2
  435.6 3.7 copy-start.3
  435.6 3.7 copy-start.5
  439.2 1.0 copy-start.4
  439.2 1.2 copy-start.6
  439.2 1.3 copy-start.7
  439.3 2.7 copy-start.9
  440.6 11.9 %collective-permute-start = (bf16[288,576]{1,0:T(8,128)(2,1)}, bf16[288,576]{1,0:T(8,128)(2,1)S(1)}, u32[]{:S(2)}, u32[]{:S(2)}) collective-permute-start(bf16[288,576]{1,0:T(8,128)(2,1)} %reduce-scatter.11.cloned.1.call-done.zero), channel_id=1, source_target_pairs={{16,0},{17,1},{18,2},{19,3},{20,4},{21,5},{22,6},{23,7},{24,8},{25... | collective-permute-start | bytes 995336 | tf_op jit(solution)/shard_map/ppermute | solution.py:1994
  452.5 0.7 copy-start.8
Sparse Core Ops, SparseCore 0:
  52.4 54.6 all-gather.3
  108.6 34.0 all-gather.5
  144.3 54.2 all-gather.7
  257.7 50.6 reduce-scatter.4
  310.5 33.4 reduce-scatter.8
  353.0 50.9 reduce-scatter.6
  406.3 33.4 reduce-scatter.10
